TPU v7x, 32 devices: a whole 2x2x4 slice. The times are simulated.
32 devices in a mesh: parts: 2 (over y), blk: 4 (over z), rows: 4 (over x, core).
Axes of the slice: x: 2, y: 2, z: 4, core: 2. Of those that a mesh axis runs over, the one named last changes fastest.
Arguments:
- tiles: float32 [16, 1024, 1024], P(('parts', 'blk'), 'rows'), parts along dimension 0, may hold values from -6 to 6
- pairs: int32 [8, 2, 2], P(('parts', 'blk')), parts along dimension 0, may hold values from 0 to 3, as said below
- counts: int32 [8], P(('parts', 'blk')), parts along dimension 0, may hold values from 1 to 2, as said below
Outputs:
- surfaces: float32 [16, 1024, 1024], P(('parts', 'blk'), 'rows'), parts along dimension 0
There are 2 independent parts, one for each index of `parts`. A program takes and returns all parts, laid end to end along the dimension named above; each array names one. Nothing has to cross between parts.
Inputs may be any that keep to these rules, and one draw needn't show every extreme that they name: pairs[b, k] = (a, c) with a < 2; c below 2 names a tile of group b, otherwise a tile of the group half the groups away; slot 0 of every group names a tile of that other group. Slots k < counts[b] of group b are live; some group has all 2 slots live.
All inputs are finite; a program needn't handle non-finite values.
Results may differ from a plain program's by a relative error of at most 0.011.
Values may be sent and summed in bfloat16 or wider, within the bound.
No kernel may reach another device: no remote copies, remote signals or barrier semaphores. Data moves between devices by JAX's collectives and lax.ppermute only.
A program may use at most 64 MiB of HBM per device.

v0:
```python
import math

import jax
import jax.numpy as jnp
from jax import lax
from jax.sharding import PartitionSpec as P

FLOOR = 0.05


def passed_along(value, axis, steps):
    count = lax.axis_size(axis)
    pairs = [(source, (source + steps) % count) for source in range(count)]
    return lax.ppermute(value, axis, pairs)


def dft_tables(length):
    index = jnp.arange(length, dtype=jnp.int32)
    phase = index[:, None] * index[None, :] % length
    angle = 2.0 * math.pi / length * phase.astype(jnp.float32)
    factor = 1.0 / math.sqrt(length)
    return (
        (jnp.cos(angle) * factor).astype(jnp.bfloat16),
        (jnp.sin(angle) * factor).astype(jnp.bfloat16),
    )


def hann(length, first, number):
    index = (first + jnp.arange(number, dtype=jnp.int32)).astype(jnp.float32)
    return 0.5 - 0.5 * jnp.cos(2.0 * math.pi / length * index)


def local(tiles, pairs, counts):
    row_count = lax.axis_size("rows")
    row_index = lax.axis_index("rows")
    tile_rows = tiles.shape[1]
    width = tiles.shape[2]
    height = tile_rows * row_count
    cos_h, sin_h = dft_tables(height)
    cos_w, sin_w = dft_tables(width)
    window = (
        hann(height, row_index * tile_rows, tile_rows)[:, None] * hann(width, 0, width)[None, :]
    )
    shaded = (tiles * window[None]).astype(jnp.bfloat16)
    y_real = jnp.einsum("grn,nv->grv", shaded, cos_w, preferred_element_type=jnp.float32).astype(
        jnp.bfloat16
    )
    y_imag = (-jnp.einsum("grn,nv->grv", shaded, sin_w, preferred_element_type=jnp.float32)).astype(
        jnp.bfloat16
    )
    stacked = jnp.stack([y_real, y_imag], axis=1)
    columns = lax.all_to_all(stacked, "rows", split_axis=3, concat_axis=2, tiled=True)
    f_real = jnp.einsum(
        "ur,grv->guv", cos_h, columns[:, 0], preferred_element_type=jnp.float32
    ) + jnp.einsum("ur,grv->guv", sin_h, columns[:, 1], preferred_element_type=jnp.float32)
    f_imag = jnp.einsum(
        "ur,grv->guv", cos_h, columns[:, 1], preferred_element_type=jnp.float32
    ) - jnp.einsum("ur,grv->guv", sin_h, columns[:, 0], preferred_element_type=jnp.float32)
    spectra = jnp.stack([f_real, f_imag], axis=1).astype(jnp.bfloat16)
    half_turn = lax.axis_size("blk") // 2
    partner = passed_along(spectra, "blk", half_turn)
    combined = jnp.concatenate([spectra, partner], axis=0)
    first = pairs[0, :, 0]
    second = pairs[0, :, 1]
    left = jnp.take(spectra, first, axis=0).astype(jnp.float32)
    right = jnp.take(combined, second, axis=0).astype(jnp.float32)
    cross_real = left[:, 0] * right[:, 0] + left[:, 1] * right[:, 1]
    cross_imag = left[:, 1] * right[:, 0] - left[:, 0] * right[:, 1]
    factor = 1.0 / (jnp.sqrt(cross_real * cross_real + cross_imag * cross_imag) + FLOOR)
    q_real = (cross_real * factor).astype(jnp.bfloat16)
    q_imag = (cross_imag * factor).astype(jnp.bfloat16)
    z_real = jnp.einsum(
        "ru,puv->prv", cos_h, q_real, preferred_element_type=jnp.float32
    ) - jnp.einsum("ru,puv->prv", sin_h, q_imag, preferred_element_type=jnp.float32)
    z_imag = jnp.einsum(
        "ru,puv->prv", sin_h, q_real, preferred_element_type=jnp.float32
    ) + jnp.einsum("ru,puv->prv", cos_h, q_imag, preferred_element_type=jnp.float32)
    half_done = jnp.stack([z_real, z_imag], axis=1).astype(jnp.bfloat16)
    banded = lax.all_to_all(half_done, "rows", split_axis=2, concat_axis=3, tiled=True)
    surface = jnp.einsum(
        "prv,vn->prn", banded[:, 0], cos_w, preferred_element_type=jnp.float32
    ) - jnp.einsum("prv,vn->prn", banded[:, 1], sin_w, preferred_element_type=jnp.float32)
    slot_index = jnp.arange(pairs.shape[1], dtype=jnp.int32)
    live = (slot_index < counts[0]).astype(jnp.float32)
    return surface * live[:, None, None]


def solution(mesh):
    return jax.shard_map(
        local,
        mesh=mesh,
        in_specs=(
            P(("parts", "blk"), "rows", None),
            P(("parts", "blk"), None, None),
            P(("parts", "blk")),
        ),
        out_specs=P(("parts", "blk"), "rows", None),
        check_vma=False,
    )
```

profile of v0, /device:TPU:0, one launch (start us, length us, event | category | flops | bytes accessed | tf_op | source)
XLA Modules:
  0.0 390.9 jit_solution(5445066731936324704)
XLA Ops:
  0.3 18.3 %fusion.55 = bf16[2,1,256,1024]{3,2,0,1:T(8,128)(2,1)S(1)} fusion(f32[2,256,1024]{2,1,0:T(8,128)} %param.3, f32[256,1024]{1,0:T(8,128)S(1)} %broadcast_multiply_fusion), kind=kOutput, calls=%fused_computation.58 | convolution fusion | flops 1092091904 | bytes 4194304 | tf_op jit(solution)/shard_map/grn,nv->grv/dot_general | solution.py:45
  18.6 17.0 %fusion.58 = bf16[2,1,256,1024]{3,2,0,1:T(8,128)(2,1)S(1)} fusion(f32[2,256,1024]{2,1,0:T(8,128)S(1)} %copy-done.5, f32[256,1024]{1,0:T(8,128)S(1)} %broadcast_multiply_fusion), kind=kOutput, calls=%fused_computation.59 | convolution fusion | flops 1092616192 | bytes 4194304 | tf_op jit(solution)/shard_map/grn,nv->grv/dot_general | solution.py:48
  35.8 4.0 %copy.20 = bf16[2,2,256,1024]{2,0,1,3:T(2,128)(2,1)} copy(bf16[2,2,256,1024]{3,2,0,1:T(8,128)(2,1)S(1)} %pad_maximum_fusion.1) | data formatting | bytes 4194304 | tf_op jit(solution)/shard_map/stack | solution.py:51
  39.8 29.9 %all_to_all.36 = bf16[2,2,256,1024]{2,0,1,3:T(2,128)(2,1)S(1)} all-to-all(bf16[2,2,256,1024]{2,0,1,3:T(2,128)(2,1)} %copy.20), channel_id=1, replica_groups=mesh['parts'=2,'blk'=4,'rows'=4] {'rows'}, dimensions={3} | all-to-all | bytes 4194304 | tf_op jit(solution)/shard_map/all_to_all | solution.py:52
  74.2 18.0 %fusion.24 = f32[2,256,1024]{2,1,0:T(8,128)S(1)} fusion(bf16[2,2,1024,256]{2,3,0,1:T(8,128)(2,1)} %all_to_all.29), kind=kOutput, calls=%fused_computation.48 | convolution fusion | flops 1090519040 | bytes 3145728 | tf_op jit(solution)/shard_map/ur,grv->guv/dot_general | solution.py:55
  92.3 16.9 %fusion.22 = f32[2,256,1024]{2,1,0:T(8,128)S(1)} fusion(bf16[2,2,1024,256]{2,3,0,1:T(8,128)(2,1)S(1)} %copy-done.3), kind=kOutput, calls=%fused_computation.47 | convolution fusion | flops 1090519040 | bytes 3145728 | tf_op jit(solution)/shard_map/ur,grv->guv/dot_general | solution.py:58
  109.2 16.8 %fusion.61 = bf16[2,1,1024,256]{2,3,0,1:T(8,128)(2,1)S(1)} fusion(f32[2,256,1024]{2,1,0:T(8,128)S(1)} %fusion.24, bf16[2,2,1024,256]{2,3,0,1:T(8,128)(2,1)S(1)} %copy-done.3), kind=kOutput, calls=%fused_computation.60 | convolution fusion | flops 1091567616 | bytes 4194304 | tf_op jit(solution)/shard_map/ur,grv->guv/dot_general | solution.py:53
  125.9 16.8 %fusion.64 = bf16[2,1,1024,256]{2,3,0,1:T(8,128)(2,1)S(1)} fusion(f32[2,256,1024]{2,1,0:T(8,128)S(1)} %fusion.22, bf16[2,2,1024,256]{2,3,0,1:T(8,128)(2,1)S(1)} %copy-done.3), kind=kOutput, calls=%fused_computation.61 | convolution fusion | flops 1091567616 | bytes 4194304 | tf_op jit(solution)/shard_map/ur,grv->guv/dot_general | solution.py:56
  144.4 3.4 collective-permute-start
  153.0 3.0 copy.23
  158.3 80.1 %collective-permute-done = bf16[2,2,1024,256]{2,3,0,1:T(8,128)(2,1)} collective-permute-done((bf16[2,2,1024,256]{2,3,0,1:T(8,128)(2,1)}, bf16[2,2,1024,256]{2,3,0,1:T(8,128)(2,1)}, u32[]{:S(2)}, u32[]{:S(2)}) %collective-permute-start) | collective-permute-done | bytes 2097184 | tf_op jit(solution)/shard_map/ppermute | solution.py:14
  238.3 3.8 pad_maximum_fusion
  242.2 2.9 gather_fusion.1
  248.9 16.8 %fusion.20 = f32[2,256,1024]{2,1,0:T(8,128)S(1)} fusion(bf16[2,1024,256]{1,2,0:T(8,128)(2,1)S(1)} %get-tuple-element.7), kind=kOutput, calls=%fused_computation.46 | convolution fusion | flops 1090519040 | bytes 3145728 | tf_op jit(solution)/shard_map/ru,puv->prv/dot_general | solution.py:74
  266.6 16.8 %fusion.18 = f32[2,256,1024]{2,1,0:T(8,128)S(1)} fusion(bf16[2,1024,256]{1,2,0:T(8,128)(2,1)S(1)} %fusion.14), kind=kOutput, calls=%fused_computation.45 | convolution fusion | flops 1090519040 | bytes 3145728 | tf_op jit(solution)/shard_map/ru,puv->prv/dot_general | solution.py:75
  283.4 16.7 %fusion.67 = bf16[2,1,1024,256]{2,3,0,1:T(8,128)(2,1)S(1)} fusion(f32[2,256,1024]{2,1,0:T(8,128)S(1)} %fusion.20, bf16[2,1024,256]{1,2,0:T(8,128)(2,1)S(1)} %fusion.14), kind=kOutput, calls=%fused_computation.62 | convolution fusion | flops 1091567616 | bytes 4194304 | tf_op jit(solution)/shard_map/ru,puv->prv/dot_general | solution.py:72
  300.1 16.5 %fusion.70 = bf16[2,1,1024,256]{2,3,0,1:T(8,128)(2,1)S(1)} fusion(f32[2,256,1024]{2,1,0:T(8,128)S(1)} %fusion.18, bf16[2,1024,256]{1,2,0:T(8,128)(2,1)S(1)} %get-tuple-element.7), kind=kOutput, calls=%fused_computation.63 | convolution fusion | flops 1091567616 | bytes 4194304 | tf_op jit(solution)/shard_map/ru,puv->prv/dot_general | solution.py:77
  316.8 4.0 %copy.29 = bf16[2,2,1024,256]{3,0,1,2:T(2,128)(2,1)} copy(bf16[2,2,1024,256]{2,3,0,1:T(8,128)(2,1)S(1)} %pad_maximum_fusion.3) | data formatting | bytes 4194304 | tf_op jit(solution)/shard_map/stack | solution.py:78
  320.9 3.6 all-to-all-start.1
  325.2 25.0 %all-to-all-done.1 = bf16[2,2,1024,256]{3,0,1,2:T(2,128)(2,1)S(1)} async-done(((bf16[2,2,1024,256]{3,0,1,2:T(2,128)(2,1)}), bf16[2,2,1024,256]{3,0,1,2:T(2,128)(2,1)S(1)}, u32[]{:S(2)}, u32[]{:S(2)}) %all-to-all-start.1) | async-done | bytes 2097184 | tf_op jit(solution)/shard_map/all_to_all | solution.py:79
  350.2 2.9 copy.34
  353.1 3.6 all_to_all.33
  356.7 16.5 %fusion.16 = f32[2,256,1024]{2,1,0:T(8,128)S(1)} fusion(bf16[2,2,256,1024]{3,2,0,1:T(8,128)(2,1)S(1)} %all_to_all.33), kind=kOutput, calls=%fused_computation.44 | convolution fusion | flops 1090519040 | bytes 3145728 | tf_op jit(solution)/shard_map/prv,vn->prn/dot_general | solution.py:82
  373.2 17.5 %subtract_multiply_fusion = f32[2,256,1024]{2,1,0:T(8,128)} fusion(f32[2,256,1024]{2,1,0:T(8,128)S(1)} %fusion.16, bf16[2,2,256,1024]{3,2,0,1:T(8,128)(2,1)S(1)} %all_to_all.33, f32[2]{0:T(128)S(1)} %compare_convert_fusion), kind=kOutput, calls=%fused_computation.36 | convolution fusion | flops 1091567616 | bytes 5243392 | tf_op jit(solution)/shard_map/prv,vn->prn/dot_general | solution.py:80
  (33 shorter events, 18.9 us)
Async XLA Ops:
  0.2 18.3 %copy-start.5 = (f32[2,256,1024]{2,1,0:T(8,128)S(1)}, f32[2,256,1024]{2,1,0:T(8,128)}, u32[]{:S(2)}) copy-start(f32[2,256,1024]{2,1,0:T(8,128)} %param.3) | copy-start | bytes 6291460
  74.2 18.1 %copy-start.3 = (bf16[2,2,1024,256]{2,3,0,1:T(8,128)(2,1)S(1)}, bf16[2,2,1024,256]{2,3,0,1:T(8,128)(2,1)}, u32[]{:S(2)}) copy-start(bf16[2,2,1024,256]{2,3,0,1:T(8,128)(2,1)} %all_to_all.29) | copy-start | bytes 6291460
  142.7 5.3 %copy-start.1 = (bf16[2,1,1024,256]{2,3,0,1:T(8,128)(2,1)}, bf16[2,1,1024,256]{2,3,0,1:T(8,128)(2,1)S(1)}, u32[]{:S(2)}) copy-start(bf16[2,1,1024,256]{2,3,0,1:T(8,128)(2,1)S(1)} %fusion.64) | copy-start | bytes 3145732
  142.8 5.1 %copy-start.4 = (s32[1,2,2]{2,1,0:T(2,128)S(1)}, s32[1,2,2]{2,1,0:T(2,128)}, u32[]{:S(2)}) copy-start(s32[1,2,2]{2,1,0:T(2,128)} %param.4) | copy-start | bytes 52
  144.4 93.9 %collective-permute-start = (bf16[2,2,1024,256]{2,3,0,1:T(8,128)(2,1)}, bf16[2,2,1024,256]{2,3,0,1:T(8,128)(2,1)}, u32[]{:S(2)}, u32[]{:S(2)}) collective-permute-start(bf16[2,2,1024,256]{2,3,0,1:T(8,128)(2,1)} %pad_maximum_fusion.2), channel_id=1, source_target_pairs={{0,8},{4,12},{8,0},{12,4},{1,9},{5,13},{9,1},{13,5},{2,10},{6,14},... | collective-permute-start | bytes 6291464 | tf_op jit(solution)/shard_map/ppermute | solution.py:14
  156.0 82.4 %copy-start.2 = (bf16[2,1,1024,256]{2,3,0,1:T(8,128)(2,1)S(1)}, bf16[2,1,1024,256]{2,3,0,1:T(8,128)(2,1)}, u32[]{:S(2)}) copy-start(bf16[2,1,1024,256]{2,3,0,1:T(8,128)(2,1)} %copy-done.1) | copy-start | bytes 3145732
  245.1 2.2 copy-start
  320.9 29.3 %all-to-all-start.1 = ((bf16[2,2,1024,256]{3,0,1,2:T(2,128)(2,1)}), bf16[2,2,1024,256]{3,0,1,2:T(2,128)(2,1)S(1)}, u32[]{:S(2)}, u32[]{:S(2)}) async-start(bf16[2,2,1024,256]{3,0,1,2:T(2,128)(2,1)} %copy.29), calls=%async_computation.1 | async-start | bytes 4194304 | tf_op jit(solution)/shard_map/all_to_all | solution.py:79
where the time goes:
time: 398 us; the launch traced here: 391 us
  matrix products  205 us (52%)
  waiting for transfers between devices  105 us (26%)
  local copies, waits for them, and re-layouts  31.9 us (8%)
  blocking collectives  29.9 us (8%)
  other arithmetic  11.3 us (3%)
  starting transfers between devices  7.01 us (2%)
    ppermute x1, waiting for transfers between devices, passed_along(): return lax.ppermute(value, axis, pairs)  80.1 us
    all_to_all x1, blocking collectives, local(): lax.all_to_all(stacked, 'rows', split_axis=3, concat_axis=2, tiled=True)  29.9 us
    all_to_all x1, waiting for transfers between devices, local(): lax.all_to_all(half_done, 'rows', split_axis=2, concat_axis=3, tiled=True)  25 us
    dot_general x1, matrix products, local(): jnp.einsum('grn,nv->grv', shaded, cos_w, preferred_element_type=jnp.float32)  18.3 us
    dot_general x1, matrix products, local(): jnp.einsum('ur,grv->guv', sin_h, columns[:, 1], preferred_element_type=jn...  18 us
    dot_general x1, matrix products, local(): jnp.einsum('prv,vn->prn', banded[:, 0], cos_w, preferred_element_type=jnp...  17.5 us
    dot_general x1, matrix products, local(): jnp.einsum('grn,nv->grv', shaded, sin_w, preferred_element_type=jnp.float32)  17 us
    dot_general x1, matrix products, local(): jnp.einsum('ur,grv->guv', sin_h, columns[:, 0], preferred_element_type=jn...  16.9 us
  transfers between devices with their start and end apart: 2, of which 2 were waited for; matrix products, arithmetic and copies ran while one was open for 3% of the time, Pallas kernels for 0%

commit v1 on v0

v1 whole, which is shorter than its diff:
```python
import math

import jax
import jax.numpy as jnp
import numpy as np
from jax import lax
from jax.experimental import pallas as pl
from jax.experimental.pallas import tpu as pltpu

FLOOR = 0.05
VMEM_LIMIT = 56 * 1024 * 1024


def hann(length, first, number):
    index = (first + jnp.arange(number, dtype=jnp.int32)).astype(jnp.float32)
    return 0.5 - 0.5 * jnp.cos(2.0 * math.pi / length * index)


def width_table(width, owners):
    half = width // 2
    phase = np.arange(half)[:, None] * np.arange(width)[None, :] % width
    angle = 2.0 * math.pi / width * phase
    factor = 1.0 / math.sqrt(width)
    cosine = np.cos(angle) * factor
    sine = -np.sin(angle) * factor
    sine[0] = np.where(np.arange(width) % 2 == 0, factor, -factor)
    shape = (owners, half // owners, width)
    table = np.stack([cosine.reshape(shape), sine.reshape(shape)], axis=1)
    return table.reshape(width, width).astype(jnp.bfloat16)


def height_table(height):
    fine = 32
    coarse = height // fine
    column = np.arange(height)[None, :]
    rough = 2.0 * math.pi / height * (np.arange(coarse)[:, None] * fine * column % height)
    small = 2.0 * math.pi / height * (np.arange(fine)[:, None] * column % height)
    factor = 1.0 / math.sqrt(height)
    rc = jnp.asarray(np.cos(rough) * factor, jnp.float32)[:, None, :]
    rs = jnp.asarray(np.sin(rough) * factor, jnp.float32)[:, None, :]
    sc = jnp.asarray(np.cos(small), jnp.float32)[None, :, :]
    ss = jnp.asarray(np.sin(small), jnp.float32)[None, :, :]
    cosine = (rc * sc - rs * ss).reshape(height, height)
    sine = (rs * sc + rc * ss).reshape(height, height)
    return jnp.concatenate([cosine, sine], axis=1).astype(jnp.bfloat16)


def params():
    return pltpu.CompilerParams(vmem_limit_bytes=VMEM_LIMIT)


def row_transform(tiles, down, across, table, scalars, peers):
    count, rows, width = tiles.shape
    span = table.shape[0] // 2
    block = span // peers

    def body(s_ref, tile_ref, down_ref, across_ref, table_ref, *refs):
        outs, work = refs[:-1], refs[-1]
        window = down_ref[...] * across_ref[...]
        shaded = (tile_ref[0] * window).astype(jnp.bfloat16)
        y = lax.dot_general(
            table_ref[...], shaded, (((1,), (1,)), ((), ())), preferred_element_type=jnp.float32
        )
        work[...] = y.astype(jnp.bfloat16)
        me = s_ref[1]
        for k in range(peers):
            start = pl.multiple_of((me ^ k) * block, block)
            outs[k][0] = work[pl.ds(start, block), :]

    return pl.pallas_call(
        body,
        grid_spec=pltpu.PrefetchScalarGridSpec(
            num_scalar_prefetch=1,
            grid=(count,),
            in_specs=[
                pl.BlockSpec((1, rows, width), lambda t, s: (t, 0, 0)),
                pl.BlockSpec((rows, 1), lambda t, s: (0, 0)),
                pl.BlockSpec((1, width), lambda t, s: (0, 0)),
                pl.BlockSpec((span, width), lambda t, s: (s[0], 0)),
            ],
            out_specs=[pl.BlockSpec((1, block, rows), lambda t, s: (t, 0, 0))] * peers,
            scratch_shapes=[pltpu.VMEM((span, rows), jnp.bfloat16)],
        ),
        out_shape=[jax.ShapeDtypeStruct((count, block, rows), jnp.bfloat16)] * peers,
        compiler_params=params(),
        name="row_transform",
    )(scalars, tiles, down, across, table)


def gather_rows(s_ref, pieces, table_ref):
    me = s_ref[1]
    total = None
    for k, piece in enumerate(pieces):
        count, block, rows = piece.shape
        start = pl.multiple_of((me ^ k) * rows, rows)
        term = jnp.dot(
            piece[...].reshape(count * block, rows),
            table_ref[pl.ds(start, rows), :],
            preferred_element_type=jnp.float32,
        )
        total = term if total is None else total + term
    return total


def store_spectra(s_ref, total, spectra, edge, first):
    block = spectra.shape[2]
    height = spectra.shape[3]
    row = lax.broadcasted_iota(jnp.int32, (block, height), 0)
    packed = (row == 0) & (s_ref[2] == 1)
    for t in range(total.shape[0] // (2 * block)):
        real = total[2 * t * block : (2 * t + 1) * block]
        imag = total[(2 * t + 1) * block : (2 * t + 2) * block]
        cr, sr = real[:, :height], real[:, height:]
        ci, si = imag[:, :height], imag[:, height:]
        spectra[first + t, 0] = jnp.where(packed, cr, cr + si).astype(jnp.bfloat16)
        spectra[first + t, 1] = jnp.where(packed, -sr, ci - sr).astype(jnp.bfloat16)
        edge[first + t, 0] = ci[:16].astype(jnp.bfloat16)
        edge[first + t, 1] = (-si[:16]).astype(jnp.bfloat16)


def normalised(left_real, left_imag, right_real, right_imag):
    lr = left_real.astype(jnp.float32)
    li = left_imag.astype(jnp.float32)
    rr = right_real.astype(jnp.float32)
    ri = right_imag.astype(jnp.float32)
    cross_real = lr * rr + li * ri
    cross_imag = li * rr - lr * ri
    factor = 1.0 / (jnp.sqrt(cross_real * cross_real + cross_imag * cross_imag) + FLOOR)
    return (
        (cross_real * factor).astype(jnp.bfloat16),
        (cross_imag * factor).astype(jnp.bfloat16),
    )


def correlate(s_ref, base, spectra, edge, table_ref, phases, outs):
    block = spectra.shape[2]
    height = spectra.shape[3]
    slots = outs[0].shape[0]
    rows = outs[0].shape[2]
    lead = lax.broadcasted_iota(jnp.int32, (16, height), 0)
    packed = (lead == 0) & (s_ref[2] == 1)
    for p in range(slots):
        a = s_ref[base + 2 * p]
        c = s_ref[base + 2 * p + 1]
        q_real, q_imag = normalised(spectra[a, 0], spectra[a, 1], spectra[c, 0], spectra[c, 1])
        e_real, e_imag = normalised(edge[a, 0], edge[a, 1], edge[c, 0], edge[c, 1])
        phases[2 * p] = q_real
        phases[2 * p + 1] = q_imag
        top_real = q_real[:16].astype(jnp.float32)
        top_imag = q_imag[:16].astype(jnp.float32)
        mixed_real = jnp.where(packed, top_real - e_imag.astype(jnp.float32), top_real)
        mixed_imag = jnp.where(packed, top_imag + e_real.astype(jnp.float32), top_imag)
        phases[2 * p, :16] = mixed_real.astype(jnp.bfloat16)
        phases[2 * p + 1, :16] = mixed_imag.astype(jnp.bfloat16)
    row = lax.broadcasted_iota(jnp.int32, (block, rows), 0)
    twice = jnp.where((row == 0) & (s_ref[2] == 1), 1.0, 2.0)
    flat = phases[...].reshape(2 * slots * block, height)
    me = s_ref[1]
    for k in range(len(outs)):
        start = pl.multiple_of((me ^ k) * rows, rows)
        c_part = jnp.dot(
            flat, table_ref[:, pl.ds(start, rows)], preferred_element_type=jnp.float32
        )
        start = pl.multiple_of(height + (me ^ k) * rows, rows)
        s_part = jnp.dot(
            flat, table_ref[:, pl.ds(start, rows)], preferred_element_type=jnp.float32
        )
        for p in range(slots):
            re = slice(2 * p * block, (2 * p + 1) * block)
            im = slice((2 * p + 1) * block, (2 * p + 2) * block)
            outs[k][p, :block] = ((c_part[re] - s_part[im]) * twice).astype(jnp.bfloat16)
            outs[k][p, block:] = ((s_part[re] + c_part[im]) * twice).astype(jnp.bfloat16)


def own_spectra(scalars, pieces, table):
    peers = len(pieces)
    count, double, rows = pieces[0].shape
    height = table.shape[0]

    def body(s_ref, *refs):
        inputs, table_ref = refs[:peers], refs[peers]
        spectra, edge = refs[peers + 1 :]
        store_spectra(s_ref, gather_rows(s_ref, inputs, table_ref), spectra, edge, 0)

    return pl.pallas_call(
        body,
        in_specs=[pl.BlockSpec(memory_space=pltpu.SMEM)]
        + [pl.BlockSpec(memory_space=pltpu.VMEM)] * (peers + 1),
        out_specs=[pl.BlockSpec(memory_space=pltpu.VMEM)] * 2,
        out_shape=[
            jax.ShapeDtypeStruct((count, 2, double // 2, height), jnp.bfloat16),
            jax.ShapeDtypeStruct((count, 2, 16, height), jnp.bfloat16),
        ],
        compiler_params=params(),
        name="own_spectra",
    )(scalars, *pieces, table)


def partner_slots(scalars, pieces, table, spectra, edge, slots):
    peers = len(pieces)
    count, double, rows = pieces[0].shape
    height = table.shape[0]
    block = double // 2

    def body(s_ref, *refs):
        inputs, table_ref, own_ref, own_edge = refs[:peers], *refs[peers : peers + 3]
        outs = refs[peers + 3 : 2 * peers + 3]
        every, edges, phases = refs[2 * peers + 3 :]
        every[:count] = own_ref[...]
        edges[:count] = own_edge[...]
        store_spectra(s_ref, gather_rows(s_ref, inputs, table_ref), every, edges, count)
        correlate(s_ref, 3 + 2 * slots, every, edges, table_ref, phases, outs)

    return pl.pallas_call(
        body,
        in_specs=[pl.BlockSpec(memory_space=pltpu.SMEM)]
        + [pl.BlockSpec(memory_space=pltpu.VMEM)] * (peers + 3),
        out_specs=[pl.BlockSpec(memory_space=pltpu.VMEM)] * (peers + 2),
        out_shape=[jax.ShapeDtypeStruct((slots, double, rows), jnp.bfloat16)] * peers
        + [
            jax.ShapeDtypeStruct((2 * count, 2, block, height), jnp.bfloat16),
            jax.ShapeDtypeStruct((2 * count, 2, 16, height), jnp.bfloat16),
        ],
        scratch_shapes=[pltpu.VMEM((2 * slots, block, height), jnp.bfloat16)],
        compiler_params=params(),
        name="partner_slots",
    )(scalars, *pieces, table, spectra, edge)


def own_slots(scalars, table, spectra, edge, peers, slots):
    block, height = spectra.shape[2:]
    rows = height // peers

    def body(s_ref, table_ref, every, edges, *refs):
        correlate(s_ref, 3, every, edges, table_ref, refs[-1], refs[:-1])

    return pl.pallas_call(
        body,
        in_specs=[pl.BlockSpec(memory_space=pltpu.SMEM)]
        + [pl.BlockSpec(memory_space=pltpu.VMEM)] * 3,
        out_specs=[pl.BlockSpec(memory_space=pltpu.VMEM)] * peers,
        out_shape=[jax.ShapeDtypeStruct((slots, 2 * block, rows), jnp.bfloat16)] * peers,
        scratch_shapes=[pltpu.VMEM((2 * slots, block, height), jnp.bfloat16)],
        compiler_params=params(),
        name="own_slots",
    )(scalars, table, spectra, edge)


def surfaces_of(scalars, own, other, table):
    peers = len(own)
    slots, double, rows = own[0].shape
    width = table.shape[0]
    span = peers * double

    def body(s_ref, *refs):
        own_refs, other_refs = refs[:peers], refs[peers : 2 * peers]
        table_ref, out_ref, work = refs[2 * peers :]
        half = s_ref[0]
        me = s_ref[1]
        for k in range(peers):
            place = (me ^ k) * double
            here = pl.multiple_of(half * span + place, double)
            there = pl.multiple_of((1 - half) * span + place, double)
            work[pl.ds(here, double), :] = own_refs[k][0]
            work[pl.ds(there, double), :] = other_refs[k][0]
        surface = lax.dot_general(
            work[...], table_ref[...], (((0,), (0,)), ((), ())), preferred_element_type=jnp.float32
        )
        live = pl.program_id(0) < s_ref[2]
        out_ref[0] = jnp.where(live, surface, 0.0)

    piece = pl.BlockSpec((1, double, rows), lambda p, s: (p, 0, 0))
    return pl.pallas_call(
        body,
        grid_spec=pltpu.PrefetchScalarGridSpec(
            num_scalar_prefetch=1,
            grid=(slots,),
            in_specs=[piece] * (2 * peers) + [pl.BlockSpec((width, width), lambda p, s: (0, 0))],
            out_specs=pl.BlockSpec((1, rows, width), lambda p, s: (p, 0, 0)),
            scratch_shapes=[pltpu.VMEM((width, rows), jnp.bfloat16)],
        ),
        out_shape=jax.ShapeDtypeStruct((slots, rows, width), jnp.float32),
        compiler_params=params(),
        name="surfaces",
    )(scalars, *own, *other, table)


def local(tiles, pairs, counts):
    groups = lax.axis_size("blk")
    peers = lax.axis_size("rows")
    group = lax.axis_index("blk")
    me = lax.axis_index("rows")
    count, rows, width = tiles.shape
    slots = pairs.shape[1]
    height = rows * peers
    turn = groups // 2
    half = group // turn
    axes = ("blk", "rows")

    def across(value, k):
        moves = [
            (b * peers + r, (b + turn) % groups * peers + (r ^ k))
            for b in range(groups)
            for r in range(peers)
        ]
        return lax.ppermute(value, axes, moves)

    def along(value, k):
        return lax.ppermute(value, "rows", [(r, r ^ k) for r in range(peers)])

    table_w = jnp.asarray(width_table(width, 2 * peers))
    down = hann(height, me * rows, rows)[:, None]
    sideways = hann(width, 0, width)[None, :]

    first = jnp.stack([1 - half, me])
    sent = row_transform(tiles, down, sideways, table_w, first, peers)
    arrived = [across(sent[k], k) for k in range(peers)]
    kept = row_transform(tiles, down, sideways, table_w, jnp.stack([half, me]), peers)
    mine = [kept[0]] + [along(kept[k], k) for k in range(1, peers)]

    table_h = height_table(height)
    theirs = across(pairs, 0)
    packed = ((half == 0) & (me == 0)).astype(jnp.int32)
    their_pairs = jnp.stack([theirs[0, :, 0] + count, (theirs[0, :, 1] + count) % (2 * count)], 1)
    scalars = jnp.concatenate(
        [jnp.stack([half, me, packed]), pairs.reshape(-1), their_pairs.reshape(-1)]
    )
    spectra, edge = own_spectra(scalars, mine, table_h)
    *back, spectra, edge = partner_slots(scalars, arrived, table_h, spectra, edge, slots)
    other = [across(back[k], k) for k in range(peers)]
    out = own_slots(scalars, table_h, spectra, edge, peers, slots)
    own = [out[0]] + [along(out[k], k) for k in range(1, peers)]
    return surfaces_of(jnp.stack([half, me, counts[0]]), own, other, table_w)


def solution(mesh):
    from jax.sharding import PartitionSpec as P

    return jax.shard_map(
        local,
        mesh=mesh,
        in_specs=(
            P(("parts", "blk"), "rows", None),
            P(("parts", "blk"), None, None),
            P(("parts", "blk")),
        ),
        out_specs=P(("parts", "blk"), "rows", None),
        check_vma=False,
    )
```

time: 398 us -> 85.6 us (0.22); the launches traced: 391 us -> 85.4 us
  matrix products: 205 us -> 0 us
  waiting for transfers between devices: 105 us -> 22.6 us
  blocking collectives: 29.9 us -> 0 us
  Pallas kernels: 0 us -> 29.8 us
  local copies, waits for them, and re-layouts: 31.9 us -> 2.91 us
  starting transfers between devices: 7.01 us -> 22.1 us
  other arithmetic: 11.3 us -> 7.15 us
    dot_general x12 -> x0, matrix products: 205 us -> none  [the longest x1 18.3 us: local(): jnp.einsum('grn,nv->grv', shaded, cos_w, preferred_element_type=jnp.float32)]
    ppermute x1 -> x15, waiting for transfers between devices: 80.1 us -> 22.6 us  [the longest x9 20 us: across(): return lax.ppermute(value, axes, moves)]
    all_to_all x1 -> x0, blocking collectives: 29.9 us -> none  [local(): lax.all_to_all(stacked, 'rows', split_axis=3, concat_axis=2, tiled=True)]
    pallas_call x0 -> x6, Pallas kernels: none -> 29.8 us  [the longest x2 8.48 us: row_transform(): pl.pallas_call(body, grid_spec=pltpu.PrefetchScalarGridSpec(num_scalar_pr...]
    all_to_all x1 -> x0, waiting for transfers between devices: 25 us -> none  [local(): lax.all_to_all(half_done, 'rows', split_axis=2, concat_axis=3, tiled=True)]
    ppermute x1 -> x15, starting transfers between devices: 3.4 us -> 22.1 us  [the longest x9 15.8 us: across(): return lax.ppermute(value, axes, moves)]
    all_to_all x4 -> x0, local copies, waits for them, and re-layouts: 11 us -> none  [the longest x2 6.57 us: local(): lax.all_to_all(half_done, 'rows', split_axis=2, concat_axis=3, tiled=True)]
    another operation x3 -> x1, local copies, waits for them, and re-layouts: 11 us -> 0.1 us  [local(): jnp.stack([theirs[0, :, 0] + count, (theirs[0, :, 1] + count) % (2 * coun...]
  transfers between devices with their start and end apart: 2 -> 15, of which waited for: 2 -> 6; matrix products, arithmetic and copies ran while one was open for 3% -> 9% of each run, Pallas kernels for 0% -> 15%
where the time goes in v1:
time: 85.6 us; the launch traced here: 85.4 us
  Pallas kernels  29.8 us (35%)
  waiting for transfers between devices  22.6 us (26%)
  starting transfers between devices  22.1 us (26%)
  other arithmetic  7.15 us (8%)
  local copies, waits for them, and re-layouts  2.91 us (3%)
    ppermute x9, waiting for transfers between devices, across(): return lax.ppermute(value, axes, moves)  20 us
    ppermute x9, starting transfers between devices, across(): return lax.ppermute(value, axes, moves)  15.8 us
    pallas_call x2, Pallas kernels, row_transform(): pl.pallas_call(body, grid_spec=pltpu.PrefetchScalarGridSpec(num_scalar_pr...  8.48 us
    pallas_call x1, Pallas kernels, partner_slots(): pl.pallas_call(body, in_specs=[pl.BlockSpec(memory_space=pltpu.SMEM)] + [...  6.57 us
    ppermute x6, starting transfers between devices, along(): return lax.ppermute(value, 'rows', [(r, r ^ k) for r in range(peers)])  6.22 us
    pallas_call x1, Pallas kernels, surfaces_of(): pl.pallas_call(body, grid_spec=pltpu.PrefetchScalarGridSpec(num_scalar_pr...  5.21 us
    pallas_call x1, Pallas kernels, own_slots(): pl.pallas_call(body, in_specs=[pl.BlockSpec(memory_space=pltpu.SMEM)] + [...  4.98 us
    pallas_call x1, Pallas kernels, own_spectra(): pl.pallas_call(body, in_specs=[pl.BlockSpec(memory_space=pltpu.SMEM)] + [...  4.55 us
  transfers between devices with their start and end apart: 15, of which 6 were waited for; matrix products, arithmetic and copies ran while one was open for 9% of the time, Pallas kernels for 15%

profile of v1, /device:TPU:0, one launch (start us, length us, event | category | flops | bytes accessed | tf_op | source)
XLA Modules:
  0.0 85.4 jit_solution(1116013284356713896)
XLA Ops:
  0.0 4.0 %collective-permute-start = (s32[1,2,2]{2,1,0:T(2,128)}, s32[1,2,2]{2,1,0:T(2,128)S(1)}, u32[]{:S(2)}, u32[]{:S(2)}) collective-permute-start(s32[1,2,2]{2,1,0:T(2,128)} %param.9), channel_id=1, source_target_pairs={{0,8},{1,9},{2,10},{3,11},{4,12},{5,13},{6,14},{7,15},{8,0},{9,1},... | collective-permute-start | bytes 56 | tf_op jit(solution)/shard_map/ppermute | solution.py:306
  4.0 0.7 multiply_subtract_fusion.1.across_ref
  4.8 1.1 %multiply_subtract_fusion.down_ref = f32[256,1]{1,0:T(8,128)} fusion(s32[]{:T(128)S(6)} %mul.113), kind=kLoop, calls=%fused_computation.3 | loop fusion | flops 1280 | bytes 1028 | tf_op jit(solution)/shard_map/sub | solution.py:16
  6.6 4.3 %row_transform.2 = (bf16[2,128,256]{2,1,0:T(8,128)(2,1)}, bf16[2,128,256]{2,1,0:T(8,128)(2,1)}, bf16[2,128,256]{2,1,0:T(8,128)(2,1)}, bf16[2,128,256]{2,1,0:T(8,128)(2,1)}) custom-call(s32[2]{0:T(128)} %get-tuple-element.49.s_ref, f32[2,256,1024]{2,1,0:T(8,128)} %tile_ref.3, f32[256,1]{1,0:T(8,128)} %multiply_subtract_fusion.down_ref, ...), custom_call_target="tpu_custom_call" | custom-call | tf_op jit(solution)/shard_map/row_transform/pallas_call | solution.py:70
  10.9 1.8 %collective-permute-start.2 = (bf16[2,128,256]{2,1,0:T(8,128)(2,1)}, bf16[2,128,256]{2,1,0:T(8,128)(2,1)S(1)}, u32[]{:S(2)}, u32[]{:S(2)}) collective-permute-start(bf16[2,128,256]{2,1,0:T(8,128)(2,1)} %get-tuple-element.26), channel_id=1, source_target_pairs={{0,9},{1,8},{2,11},{3,10},{4,13},{5,12},{6,15},{7,14},{8,1},{9,0},... | collective-permute-start | bytes 393224 | tf_op jit(solution)/shard_map/ppermute | solution.py:306
  12.7 4.2 %row_transform.3 = (bf16[2,128,256]{2,1,0:T(8,128)(2,1)}, bf16[2,128,256]{2,1,0:T(8,128)(2,1)}, bf16[2,128,256]{2,1,0:T(8,128)(2,1)}, bf16[2,128,256]{2,1,0:T(8,128)(2,1)}) custom-call(s32[2]{0:T(128)} %get-tuple-element.50.s_ref, f32[2,256,1024]{2,1,0:T(8,128)} %tile_ref.3, f32[256,1]{1,0:T(8,128)} %multiply_subtract_fusion.down_ref, ...), custom_call_target="tpu_custom_call" | custom-call | tf_op jit(solution)/shard_map/row_transform/pallas_call | solution.py:70
  16.8 1.2 %collective-permute-start.5 = (bf16[2,128,256]{2,1,0:T(8,128)(2,1)}, bf16[2,128,256]{2,1,0:T(8,128)(2,1)S(1)}, u32[]{:S(2)}, u32[]{:S(2)}) collective-permute-start(bf16[2,128,256]{2,1,0:T(8,128)(2,1)} %get-tuple-element.30), channel_id=1, source_target_pairs={{0,1},{1,0},{2,3},{3,2},{4,5},{5,4},{6,7},{7,6},{8,9},{9,8},{10,11... | collective-permute-start | bytes 393224 | tf_op jit(solution)/shard_map/ppermute | solution.py:309
  18.1 1.5 %collective-permute-start.6 = (bf16[2,128,256]{2,1,0:T(8,128)(2,1)}, bf16[2,128,256]{2,1,0:T(8,128)(2,1)S(1)}, u32[]{:S(2)}, u32[]{:S(2)}) collective-permute-start(bf16[2,128,256]{2,1,0:T(8,128)(2,1)} %get-tuple-element.31), channel_id=1, source_target_pairs={{0,2},{1,3},{2,0},{3,1},{4,6},{5,7},{6,4},{7,5},{8,10},{9,11},{10,... | collective-permute-start | bytes 393224 | tf_op jit(solution)/shard_map/ppermute | solution.py:309
  19.6 1.4 %subtract_convert_fusion = (bf16[32,32,1024]{2,1,0:T(8,128)(2,1)S(1)}, bf16[32,32,1024]{2,1,0:T(8,128)(2,1)S(1)}) fusion(f32[32,1024]{1,0:T(8,128)S(1)} %copy-done.2, f32[32,1024]{1,0:T(8,128)S(1)} %copy-done.3, f32[32,1024]{1,0:T(8,128)S(1)} %copy-done.4, f32[32,1024]{1,0:T(8,128)S(1)} %copy-done.5), kind=kLoop, calls=%fused_computation.2 | loop fusion | flops 8388608 | bytes 4718592 | tf_op jit(solution)/shard_map/convert.4
  21.0 2.4 %pad_maximum_fusion.refs_4_.table_ref = bf16[1024,2048]{1,0:T(8,128)(2,1)} fusion(bf16[1024,1024]{1,0:T(8,128)(2,1)S(1)} %bitcast.10, bf16[1024,1024]{1,0:T(8,128)(2,1)S(1)} %bitcast.9), kind=kLoop, calls=%fused_computation | loop fusion | flops 8388608 | bytes 8388608 | tf_op jit(solution)/shard_map/concatenate | solution.py:45
  23.8 3.0 %collective-permute-start.4 = (bf16[2,128,256]{2,1,0:T(8,128)(2,1)S(1)}, bf16[2,128,256]{2,1,0:T(8,128)(2,1)S(1)}, u32[]{:S(2)}, u32[]{:S(2)}) collective-permute-start(bf16[2,128,256]{2,1,0:T(8,128)(2,1)S(1)} %copy-done.18), channel_id=1, source_target_pairs={{0,11},{1,10},{2,9},{3,8},{4,15},{5,14},{6,13},{7,12},{8,3},{9,2},... | collective-permute-start | bytes 393224 | tf_op jit(solution)/shard_map/ppermute | solution.py:306
  26.8 1.2 %collective-permute-start.7 = (bf16[2,128,256]{2,1,0:T(8,128)(2,1)S(1)}, bf16[2,128,256]{2,1,0:T(8,128)(2,1)S(1)}, u32[]{:S(2)}, u32[]{:S(2)}) collective-permute-start(bf16[2,128,256]{2,1,0:T(8,128)(2,1)S(1)} %copy-done.20), channel_id=1, source_target_pairs={{0,3},{1,2},{2,1},{3,0},{4,7},{5,6},{6,5},{7,4},{8,11},{9,10},{10,... | collective-permute-start | bytes 393224 | tf_op jit(solution)/shard_map/ppermute | solution.py:309
  28.8 2.6 %collective-permute-done.7.refs_3_ = bf16[2,128,256]{2,1,0:T(8,128)(2,1)S(1)} collective-permute-done((bf16[2,128,256]{2,1,0:T(8,128)(2,1)S(1)}, bf16[2,128,256]{2,1,0:T(8,128)(2,1)S(1)}, u32[]{:S(2)}, u32[]{:S(2)}) %collective-permute-start.7) | collective-permute-done | bytes 131104 | tf_op jit(solution)/shard_map/ppermute | solution.py:309
  32.1 4.6 %own_spectra.1 = (bf16[2,2,64,1024]{3,2,1,0:T(8,128)(2,1)}, bf16[2,2,16,1024]{3,2,1,0:T(8,128)(2,1)}) custom-call(s32[11]{0:T(128)} %concatenate.7.s_ref, bf16[2,128,256]{2,1,0:T(8,128)(2,1)} %get-tuple-element.29.refs_0_, bf16[2,128,256]{2,1,0:T(8,128)(2,1)} %copy-done.6, bf16[2,128,256]{2,1,0:T(8,128)(2,1)} %copy-done.8, bf16[2,128,256]{2,1,0:T(8,128)(2,1)} %copy-done.17, ...), custom_call_target="tpu_custom_call" | custom-call | tf_op jit(solution)/shard_map/own_spectra/pallas_call | solution.py:185
  38.5 6.6 %partner_slots.1 = (bf16[2,128,256]{2,1,0:T(8,128)(2,1)}, bf16[2,128,256]{2,1,0:T(8,128)(2,1)}, bf16[2,128,256]{2,1,0:T(8,128)(2,1)}, bf16[2,128,256]{2,1,0:T(8,...) custom-call(s32[11]{0:T(128)} %concatenate.7.s_ref, bf16[2,128,256]{2,1,0:T(8,128)(2,1)} %copy-done, ...), custom_call_target="tpu_custom_call" | custom-call | tf_op jit(solution)/shard_map/partner_slots/pallas_call | solution.py:214
  45.1 5.0 %own_slots.1 = (bf16[2,128,256]{2,1,0:T(8,128)(2,1)}, bf16[2,128,256]{2,1,0:T(8,128)(2,1)}, bf16[2,128,256]{2,1,0:T(8,128)(2,1)}, bf16[2,128,256]{2,1,0:T(8,128)(2,1)}) custom-call(s32[11]{0:T(128)} %concatenate.7.s_ref, bf16[1024,2048]{1,0:T(8,128)(2,1)} %pad_maximum_fusion.refs_4_.table_ref, bf16[4,2,64,1024]{3,2,1,0:T(8,128)(2,1)} %get-tuple-element.35.every, ...), custom_call_target="tpu_custom_call" | custom-call | tf_op jit(solution)/shard_map/own_slots/pallas_call | solution.py:237
  50.1 0.9 %collective-permute-start.8 = (bf16[2,128,256]{2,1,0:T(8,128)(2,1)}, bf16[2,128,256]{2,1,0:T(8,128)(2,1)S(1)}, u32[]{:S(2)}, u32[]{:S(2)}) collective-permute-start(bf16[2,128,256]{2,1,0:T(8,128)(2,1)} %get-tuple-element.38), channel_id=1, source_target_pairs={{0,1},{1,0},{2,3},{3,2},{4,5},{5,4},{6,7},{7,6},{8,9},{9,8},{10,11... | collective-permute-start | bytes 393224 | tf_op jit(solution)/shard_map/ppermute | solution.py:309
  51.5 0.8 collective-permute-start.10
  52.4 3.5 %collective-permute-start.11 = (bf16[2,128,256]{2,1,0:T(8,128)(2,1)S(1)}, bf16[2,128,256]{2,1,0:T(8,128)(2,1)S(1)}, u32[]{:S(2)}, u32[]{:S(2)}) collective-permute-start(bf16[2,128,256]{2,1,0:T(8,128)(2,1)S(1)} %copy-done.24), channel_id=1, source_target_pairs={{0,8},{1,9},{2,10},{3,11},{4,12},{5,13},{6,14},{7,15},{8,0},{9,1},... | collective-permute-start | bytes 393224 | tf_op jit(solution)/shard_map/ppermute | solution.py:306
  55.9 2.8 %collective-permute-start.13 = (bf16[2,128,256]{2,1,0:T(8,128)(2,1)S(1)}, bf16[2,128,256]{2,1,0:T(8,128)(2,1)S(1)}, u32[]{:S(2)}, u32[]{:S(2)}) collective-permute-start(bf16[2,128,256]{2,1,0:T(8,128)(2,1)S(1)} %copy-done.22), channel_id=1, source_target_pairs={{0,10},{1,11},{2,8},{3,9},{4,14},{5,15},{6,12},{7,13},{8,2},{9,3},... | collective-permute-start | bytes 393224 | tf_op jit(solution)/shard_map/ppermute | solution.py:306
  60.7 13.1 %collective-permute-done.12.refs_5_ = bf16[2,128,256]{2,1,0:T(8,128)(2,1)S(1)} collective-permute-done((bf16[2,128,256]{2,1,0:T(8,128)(2,1)S(1)}, bf16[2,128,256]{2,1,0:T(8,128)(2,1)S(1)}, u32[]{:S(2)}, u32[]{:S(2)}) %collective-permute-start.12) | collective-permute-done | bytes 131104 | tf_op jit(solution)/shard_map/ppermute | solution.py:306
  73.8 3.2 %collective-permute-done.13.refs_6_ = bf16[2,128,256]{2,1,0:T(8,128)(2,1)S(1)} collective-permute-done((bf16[2,128,256]{2,1,0:T(8,128)(2,1)S(1)}, bf16[2,128,256]{2,1,0:T(8,128)(2,1)S(1)}, u32[]{:S(2)}, u32[]{:S(2)}) %collective-permute-start.13) | collective-permute-done | bytes 131104 | tf_op jit(solution)/shard_map/ppermute | solution.py:306
  77.0 2.5 %collective-permute-done.14.refs_7_ = bf16[2,128,256]{2,1,0:T(8,128)(2,1)S(1)} collective-permute-done((bf16[2,128,256]{2,1,0:T(8,128)(2,1)S(1)}, bf16[2,128,256]{2,1,0:T(8,128)(2,1)S(1)}, u32[]{:S(2)}, u32[]{:S(2)}) %collective-permute-start.14) | collective-permute-done | bytes 131104 | tf_op jit(solution)/shard_map/ppermute | solution.py:306
  80.2 5.2 %surfaces.1 = f32[2,256,1024]{2,1,0:T(8,128)} custom-call(s32[3]{0:T(128)} %pad_add_fusion.1.s_ref, bf16[2,128,256]{2,1,0:T(8,128)(2,1)} %get-tuple-element.37.refs_0_, bf16[2,128,256]{2,1,0:T(8,128)(2,1)} %copy-done.9, bf16[2,128,256]{2,1,0:T(8,128)(2,1)} %copy-done.11, bf16[2,128,256]{2,1,0:T(8,128)(2,1)} %copy-done.12, bf16[2,128,256]{2,1,0:T(8,128)(2,1)} %copy-done.13, ...), custom_call_target="tpu_custom_call" | custom-call | tf_op jit(solution)/shard_map/surfaces/pallas_call | solution.py:273
  (77 shorter events, 6.9 us)
Async XLA Ops:
  0.0 23.5 %collective-permute-start = (s32[1,2,2]{2,1,0:T(2,128)}, s32[1,2,2]{2,1,0:T(2,128)S(1)}, u32[]{:S(2)}, u32[]{:S(2)}) collective-permute-start(s32[1,2,2]{2,1,0:T(2,128)} %param.9), channel_id=1, source_target_pairs={{0,8},{1,9},{2,10},{3,11},{4,12},{5,13},{6,14},{7,15},{8,0},{9,1},... | collective-permute-start | bytes 56 | tf_op jit(solution)/shard_map/ppermute | solution.py:306
  6.5 13.0 %copy-start.2 = (f32[32,1024]{1,0:T(8,128)S(1)}, f32[32,1024]{1,0:T(8,128)}, u32[]{:S(2)}) copy-start(f32[32,1024]{1,0:T(8,128)} %constant.61.clone) | copy-start | bytes 393220
  6.5 13.0 %copy-start.3 = (f32[32,1024]{1,0:T(8,128)S(1)}, f32[32,1024]{1,0:T(8,128)}, u32[]{:S(2)}) copy-start(f32[32,1024]{1,0:T(8,128)} %constant.59.clone) | copy-start | bytes 393220
  6.5 13.0 %copy-start.4 = (f32[32,1024]{1,0:T(8,128)S(1)}, f32[32,1024]{1,0:T(8,128)}, u32[]{:S(2)}) copy-start(f32[32,1024]{1,0:T(8,128)} %constant.60.clone) | copy-start | bytes 393220
  6.5 13.0 %copy-start.5 = (f32[32,1024]{1,0:T(8,128)S(1)}, f32[32,1024]{1,0:T(8,128)}, u32[]{:S(2)}) copy-start(f32[32,1024]{1,0:T(8,128)} %constant.58.clone) | copy-start | bytes 393220
  10.9 25.8 %collective-permute-start.1 = (bf16[2,128,256]{2,1,0:T(8,128)(2,1)}, bf16[2,128,256]{2,1,0:T(8,128)(2,1)S(1)}, u32[]{:S(2)}, u32[]{:S(2)}) collective-permute-start(bf16[2,128,256]{2,1,0:T(8,128)(2,1)} %get-tuple-element.25), channel_id=1, source_target_pairs={{0,8},{1,9},{2,10},{3,11},{4,12},{5,13},{6,14},{7,15},{8,0},{9,1},... | collective-permute-start | bytes 393224 | tf_op jit(solution)/shard_map/ppermute | solution.py:306
  10.9 25.8 %collective-permute-start.2 = (bf16[2,128,256]{2,1,0:T(8,128)(2,1)}, bf16[2,128,256]{2,1,0:T(8,128)(2,1)S(1)}, u32[]{:S(2)}, u32[]{:S(2)}) collective-permute-start(bf16[2,128,256]{2,1,0:T(8,128)(2,1)} %get-tuple-element.26), channel_id=1, source_target_pairs={{0,9},{1,8},{2,11},{3,10},{4,13},{5,12},{6,15},{7,14},{8,1},{9,0},... | collective-permute-start | bytes 393224 | tf_op jit(solution)/shard_map/ppermute | solution.py:306
  16.8 6.9 %collective-permute-start.5 = (bf16[2,128,256]{2,1,0:T(8,128)(2,1)}, bf16[2,128,256]{2,1,0:T(8,128)(2,1)S(1)}, u32[]{:S(2)}, u32[]{:S(2)}) collective-permute-start(bf16[2,128,256]{2,1,0:T(8,128)(2,1)} %get-tuple-element.30), channel_id=1, source_target_pairs={{0,1},{1,0},{2,3},{3,2},{4,5},{5,4},{6,7},{7,6},{8,9},{9,8},{10,11... | collective-permute-start | bytes 393224 | tf_op jit(solution)/shard_map/ppermute | solution.py:309
  18.1 8.7 %collective-permute-start.6 = (bf16[2,128,256]{2,1,0:T(8,128)(2,1)}, bf16[2,128,256]{2,1,0:T(8,128)(2,1)S(1)}, u32[]{:S(2)}, u32[]{:S(2)}) collective-permute-start(bf16[2,128,256]{2,1,0:T(8,128)(2,1)} %get-tuple-element.31), channel_id=1, source_target_pairs={{0,2},{1,3},{2,0},{3,1},{4,6},{5,7},{6,4},{7,5},{8,10},{9,11},{10,... | collective-permute-start | bytes 393224 | tf_op jit(solution)/shard_map/ppermute | solution.py:309
  23.5 13.8 %collective-permute-start.3 = (bf16[2,128,256]{2,1,0:T(8,128)(2,1)S(1)}, bf16[2,128,256]{2,1,0:T(8,128)(2,1)S(1)}, u32[]{:S(2)}, u32[]{:S(2)}) collective-permute-start(bf16[2,128,256]{2,1,0:T(8,128)(2,1)S(1)} %copy-done.19), channel_id=1, source_target_pairs={{0,10},{1,11},{2,8},{3,9},{4,14},{5,15},{6,12},{7,13},{8,2},{9,3},... | collective-permute-start | bytes 393224 | tf_op jit(solution)/shard_map/ppermute | solution.py:306
  23.8 14.0 %collective-permute-start.4 = (bf16[2,128,256]{2,1,0:T(8,128)(2,1)S(1)}, bf16[2,128,256]{2,1,0:T(8,128)(2,1)S(1)}, u32[]{:S(2)}, u32[]{:S(2)}) collective-permute-start(bf16[2,128,256]{2,1,0:T(8,128)(2,1)S(1)} %copy-done.18), channel_id=1, source_target_pairs={{0,11},{1,10},{2,9},{3,8},{4,15},{5,14},{6,13},{7,12},{8,3},{9,2},... | collective-permute-start | bytes 393224 | tf_op jit(solution)/shard_map/ppermute | solution.py:306
  26.8 4.7 %collective-permute-start.7 = (bf16[2,128,256]{2,1,0:T(8,128)(2,1)S(1)}, bf16[2,128,256]{2,1,0:T(8,128)(2,1)S(1)}, u32[]{:S(2)}, u32[]{:S(2)}) collective-permute-start(bf16[2,128,256]{2,1,0:T(8,128)(2,1)S(1)} %copy-done.20), channel_id=1, source_target_pairs={{0,3},{1,2},{2,1},{3,0},{4,7},{5,6},{6,5},{7,4},{8,11},{9,10},{10,... | collective-permute-start | bytes 393224 | tf_op jit(solution)/shard_map/ppermute | solution.py:309
  45.1 13.6 %copy-start.21 = (bf16[2,128,256]{2,1,0:T(8,128)(2,1)S(1)}, bf16[2,128,256]{2,1,0:T(8,128)(2,1)}, u32[]{:S(2)}) copy-start(bf16[2,128,256]{2,1,0:T(8,128)(2,1)} %get-tuple-element.44) | copy-start | bytes 393220
  50.1 5.8 %collective-permute-start.8 = (bf16[2,128,256]{2,1,0:T(8,128)(2,1)}, bf16[2,128,256]{2,1,0:T(8,128)(2,1)S(1)}, u32[]{:S(2)}, u32[]{:S(2)}) collective-permute-start(bf16[2,128,256]{2,1,0:T(8,128)(2,1)} %get-tuple-element.38), channel_id=1, source_target_pairs={{0,1},{1,0},{2,3},{3,2},{4,5},{5,4},{6,7},{7,6},{8,9},{9,8},{10,11... | collective-permute-start | bytes 393224 | tf_op jit(solution)/shard_map/ppermute | solution.py:309
  51.0 7.7 %collective-permute-start.9 = (bf16[2,128,256]{2,1,0:T(8,128)(2,1)}, bf16[2,128,256]{2,1,0:T(8,128)(2,1)S(1)}, u32[]{:S(2)}, u32[]{:S(2)}) collective-permute-start(bf16[2,128,256]{2,1,0:T(8,128)(2,1)} %get-tuple-element.39), channel_id=1, source_target_pairs={{0,2},{1,3},{2,0},{3,1},{4,6},{5,7},{6,4},{7,5},{8,10},{9,11},{10,... | collective-permute-start | bytes 393224 | tf_op jit(solution)/shard_map/ppermute | solution.py:309
  51.5 9.1 %collective-permute-start.10 = (bf16[2,128,256]{2,1,0:T(8,128)(2,1)}, bf16[2,128,256]{2,1,0:T(8,128)(2,1)S(1)}, u32[]{:S(2)}, u32[]{:S(2)}) collective-permute-start(bf16[2,128,256]{2,1,0:T(8,128)(2,1)} %get-tuple-element.40), channel_id=1, source_target_pairs={{0,3},{1,2},{2,1},{3,0},{4,7},{5,6},{6,5},{7,4},{8,11},{9,10},{10,... | collective-permute-start | bytes 393224 | tf_op jit(solution)/shard_map/ppermute | solution.py:309
  52.4 8.3 %collective-permute-start.11 = (bf16[2,128,256]{2,1,0:T(8,128)(2,1)S(1)}, bf16[2,128,256]{2,1,0:T(8,128)(2,1)S(1)}, u32[]{:S(2)}, u32[]{:S(2)}) collective-permute-start(bf16[2,128,256]{2,1,0:T(8,128)(2,1)S(1)} %copy-done.24), channel_id=1, source_target_pairs={{0,8},{1,9},{2,10},{3,11},{4,12},{5,13},{6,14},{7,15},{8,0},{9,1},... | collective-permute-start | bytes 393224 | tf_op jit(solution)/shard_map/ppermute | solution.py:306
  55.8 17.9 %collective-permute-start.12 = (bf16[2,128,256]{2,1,0:T(8,128)(2,1)S(1)}, bf16[2,128,256]{2,1,0:T(8,128)(2,1)S(1)}, u32[]{:S(2)}, u32[]{:S(2)}) collective-permute-start(bf16[2,128,256]{2,1,0:T(8,128)(2,1)S(1)} %copy-done.23), channel_id=1, source_target_pairs={{0,9},{1,8},{2,11},{3,10},{4,13},{5,12},{6,15},{7,14},{8,1},{9,0},... | collective-permute-start | bytes 393224 | tf_op jit(solution)/shard_map/ppermute | solution.py:306
  55.9 23.6 %copy-start.9 = (bf16[2,128,256]{2,1,0:T(8,128)(2,1)}, bf16[2,128,256]{2,1,0:T(8,128)(2,1)S(1)}, u32[]{:S(2)}) copy-start(bf16[2,128,256]{2,1,0:T(8,128)(2,1)S(1)} %collective-permute-done.8.refs_1_) | copy-start | bytes 393220
  55.9 21.1 %collective-permute-start.13 = (bf16[2,128,256]{2,1,0:T(8,128)(2,1)S(1)}, bf16[2,128,256]{2,1,0:T(8,128)(2,1)S(1)}, u32[]{:S(2)}, u32[]{:S(2)}) collective-permute-start(bf16[2,128,256]{2,1,0:T(8,128)(2,1)S(1)} %copy-done.22), channel_id=1, source_target_pairs={{0,10},{1,11},{2,8},{3,9},{4,14},{5,15},{6,12},{7,13},{8,2},{9,3},... | collective-permute-start | bytes 393224 | tf_op jit(solution)/shard_map/ppermute | solution.py:306
  58.7 20.8 %copy-start.11 = (bf16[2,128,256]{2,1,0:T(8,128)(2,1)}, bf16[2,128,256]{2,1,0:T(8,128)(2,1)S(1)}, u32[]{:S(2)}) copy-start(bf16[2,128,256]{2,1,0:T(8,128)(2,1)S(1)} %collective-permute-done.9.refs_2_) | copy-start | bytes 393220
  58.7 20.8 %collective-permute-start.14 = (bf16[2,128,256]{2,1,0:T(8,128)(2,1)S(1)}, bf16[2,128,256]{2,1,0:T(8,128)(2,1)S(1)}, u32[]{:S(2)}, u32[]{:S(2)}) collective-permute-start(bf16[2,128,256]{2,1,0:T(8,128)(2,1)S(1)} %copy-done.21), channel_id=1, source_target_pairs={{0,11},{1,10},{2,9},{3,8},{4,15},{5,14},{6,13},{7,12},{8,3},{9,2},... | collective-permute-start | bytes 393224 | tf_op jit(solution)/shard_map/ppermute | solution.py:306
  60.6 18.9 %copy-start.12 = (bf16[2,128,256]{2,1,0:T(8,128)(2,1)}, bf16[2,128,256]{2,1,0:T(8,128)(2,1)S(1)}, u32[]{:S(2)}) copy-start(bf16[2,128,256]{2,1,0:T(8,128)(2,1)S(1)} %collective-permute-done.10.refs_3_) | copy-start | bytes 393220
  60.7 18.9 %copy-start.13 = (bf16[2,128,256]{2,1,0:T(8,128)(2,1)}, bf16[2,128,256]{2,1,0:T(8,128)(2,1)S(1)}, u32[]{:S(2)}) copy-start(bf16[2,128,256]{2,1,0:T(8,128)(2,1)S(1)} %collective-permute-done.11.refs_4_) | copy-start | bytes 393220
  (17 other events, 68.1 us)

commit v2 on v1

--- a/solution.py
+++ b/solution.py
@@ -11,9 +11,12 @@
 VMEM_LIMIT = 56 * 1024 * 1024
 
 
-def hann(length, first, number):
-    index = (first + jnp.arange(number, dtype=jnp.int32)).astype(jnp.float32)
-    return 0.5 - 0.5 * jnp.cos(2.0 * math.pi / length * index)
+def hann(length):
+    return np.asarray(0.5 - 0.5 * np.cos(2.0 * math.pi / length * np.arange(length)), np.float32)
+
+
+def scalar(value):
+    return jnp.reshape(value, (1,)).astype(jnp.int32)
 
 
 def width_table(width, owners):
@@ -45,50 +48,63 @@
     return jnp.concatenate([cosine, sine], axis=1).astype(jnp.bfloat16)
 
 
+def cost(flops, moved):
+    return pl.CostEstimate(flops=flops, transcendentals=0, bytes_accessed=moved)
+
+
 def params():
     return pltpu.CompilerParams(vmem_limit_bytes=VMEM_LIMIT)
 
 
-def row_transform(tiles, down, across, table, scalars, peers):
+def row_transform(tiles, down, across, table, half, me, peers, apart):
     count, rows, width = tiles.shape
     span = table.shape[0] // 2
     block = span // peers
 
-    def body(s_ref, tile_ref, down_ref, across_ref, table_ref, *refs):
+    def body(half_ref, me_ref, tile_ref, down_ref, across_ref, table_ref, *refs):
         outs, work = refs[:-1], refs[-1]
-        window = down_ref[...] * across_ref[...]
+        window = down_ref[...].T[:, :1] * across_ref[...]
         shaded = (tile_ref[0] * window).astype(jnp.bfloat16)
         y = lax.dot_general(
             table_ref[...], shaded, (((1,), (1,)), ((), ())), preferred_element_type=jnp.float32
         )
+        if not apart:
+            outs[0][:, 0] = y.astype(jnp.bfloat16).reshape(peers, block, rows)
+            return
         work[...] = y.astype(jnp.bfloat16)
-        me = s_ref[1]
+        me = me_ref[0]
         for k in range(peers):
             start = pl.multiple_of((me ^ k) * block, block)
             outs[k][0] = work[pl.ds(start, block), :]
 
+    if apart:
+        out_specs = [pl.BlockSpec((1, block, rows), lambda t, half, me: (t, 0, 0))] * peers
+        out_shape = [jax.ShapeDtypeStruct((count, block, rows), jnp.bfloat16)] * peers
+    else:
+        out_specs = [pl.BlockSpec((peers, 1, block, rows), lambda t, half, me: (0, t, 0, 0))]
+        out_shape = [jax.ShapeDtypeStruct((peers, count, block, rows), jnp.bfloat16)]
     return pl.pallas_call(
         body,
         grid_spec=pltpu.PrefetchScalarGridSpec(
-            num_scalar_prefetch=1,
+            num_scalar_prefetch=2,
             grid=(count,),
             in_specs=[
-                pl.BlockSpec((1, rows, width), lambda t, s: (t, 0, 0)),
-                pl.BlockSpec((rows, 1), lambda t, s: (0, 0)),
-                pl.BlockSpec((1, width), lambda t, s: (0, 0)),
-                pl.BlockSpec((span, width), lambda t, s: (s[0], 0)),
+                pl.BlockSpec((1, rows, width), lambda t, half, me: (t, 0, 0)),
+                pl.BlockSpec((8, rows), lambda t, half, me: (0, me[0])),
+                pl.BlockSpec((1, width), lambda t, half, me: (0, 0)),
+                pl.BlockSpec((span, width), lambda t, half, me: (half[0], 0)),
             ],
-            out_specs=[pl.BlockSpec((1, block, rows), lambda t, s: (t, 0, 0))] * peers,
+            out_specs=out_specs,
             scratch_shapes=[pltpu.VMEM((span, rows), jnp.bfloat16)],
         ),
-        out_shape=[jax.ShapeDtypeStruct((count, block, rows), jnp.bfloat16)] * peers,
-        compiler_params=params(),
+        out_shape=out_shape,
+        compiler_params=params(),
+        cost_estimate=cost(2 * count * rows * width * span, 4 * tiles.size + 2 * span * width),
         name="row_transform",
-    )(scalars, tiles, down, across, table)
-
-
-def gather_rows(s_ref, pieces, table_ref):
-    me = s_ref[1]
+    )(scalar(half), scalar(me), tiles, down, across, table)
+
+
+def gather_rows(pieces, table_ref, me):
     total = None
     for k, piece in enumerate(pieces):
         count, block, rows = piece.shape
@@ -132,11 +148,10 @@
     )
 
 
-def correlate(s_ref, base, spectra, edge, table_ref, phases, outs):
+def correlate(s_ref, me, base, spectra, edge, table_ref, phases, outs):
     block = spectra.shape[2]
     height = spectra.shape[3]
-    slots = outs[0].shape[0]
-    rows = outs[0].shape[2]
+    slots, _, rows = outs[0].shape
     lead = lax.broadcasted_iota(jnp.int32, (16, height), 0)
     packed = (lead == 0) & (s_ref[2] == 1)
     for p in range(slots):
@@ -155,7 +170,6 @@
     row = lax.broadcasted_iota(jnp.int32, (block, rows), 0)
     twice = jnp.where((row == 0) & (s_ref[2] == 1), 1.0, 2.0)
     flat = phases[...].reshape(2 * slots * block, height)
-    me = s_ref[1]
     for k in range(len(outs)):
         start = pl.multiple_of((me ^ k) * rows, rows)
         c_part = jnp.dot(
@@ -173,27 +187,26 @@
 
 
 def own_spectra(scalars, pieces, table):
-    peers = len(pieces)
-    count, double, rows = pieces[0].shape
+    peers, count, double, rows = pieces.shape
     height = table.shape[0]
 
-    def body(s_ref, *refs):
-        inputs, table_ref = refs[:peers], refs[peers]
-        spectra, edge = refs[peers + 1 :]
-        store_spectra(s_ref, gather_rows(s_ref, inputs, table_ref), spectra, edge, 0)
+    def body(s_ref, pieces_ref, table_ref, spectra, edge):
+        inputs = [pieces_ref.at[k] for k in range(peers)]
+        store_spectra(s_ref, gather_rows(inputs, table_ref, 0), spectra, edge, 0)
 
     return pl.pallas_call(
         body,
         in_specs=[pl.BlockSpec(memory_space=pltpu.SMEM)]
-        + [pl.BlockSpec(memory_space=pltpu.VMEM)] * (peers + 1),
+        + [pl.BlockSpec(memory_space=pltpu.VMEM)] * 2,
         out_specs=[pl.BlockSpec(memory_space=pltpu.VMEM)] * 2,
         out_shape=[
             jax.ShapeDtypeStruct((count, 2, double // 2, height), jnp.bfloat16),
             jax.ShapeDtypeStruct((count, 2, 16, height), jnp.bfloat16),
         ],
         compiler_params=params(),
+        cost_estimate=cost(4 * count * double * height * height, 8 * height * height),
         name="own_spectra",
-    )(scalars, *pieces, table)
+    )(scalars, pieces, table)
 
 
 def partner_slots(scalars, pieces, table, spectra, edge, slots):
@@ -204,25 +217,26 @@
 
     def body(s_ref, *refs):
         inputs, table_ref, own_ref, own_edge = refs[:peers], *refs[peers : peers + 3]
-        outs = refs[peers + 3 : 2 * peers + 3]
-        every, edges, phases = refs[2 * peers + 3 :]
+        outs = [refs[peers + 3 + k // 2].at[k % 2] for k in range(peers)]
+        every, edges, phases = refs[-3:]
         every[:count] = own_ref[...]
         edges[:count] = own_edge[...]
-        store_spectra(s_ref, gather_rows(s_ref, inputs, table_ref), every, edges, count)
-        correlate(s_ref, 3 + 2 * slots, every, edges, table_ref, phases, outs)
+        store_spectra(s_ref, gather_rows(inputs, table_ref, s_ref[1]), every, edges, count)
+        correlate(s_ref, s_ref[1], 3 + 2 * slots, every, edges, table_ref, phases, outs)
 
     return pl.pallas_call(
         body,
         in_specs=[pl.BlockSpec(memory_space=pltpu.SMEM)]
         + [pl.BlockSpec(memory_space=pltpu.VMEM)] * (peers + 3),
-        out_specs=[pl.BlockSpec(memory_space=pltpu.VMEM)] * (peers + 2),
-        out_shape=[jax.ShapeDtypeStruct((slots, double, rows), jnp.bfloat16)] * peers
+        out_specs=[pl.BlockSpec(memory_space=pltpu.VMEM)] * (peers // 2 + 2),
+        out_shape=[jax.ShapeDtypeStruct((2, slots, double, rows), jnp.bfloat16)] * (peers // 2)
         + [
             jax.ShapeDtypeStruct((2 * count, 2, block, height), jnp.bfloat16),
             jax.ShapeDtypeStruct((2 * count, 2, 16, height), jnp.bfloat16),
         ],
         scratch_shapes=[pltpu.VMEM((2 * slots, block, height), jnp.bfloat16)],
         compiler_params=params(),
+        cost_estimate=cost(4 * (count + slots) * double * height * height, 8 * height * height),
         name="partner_slots",
     )(scalars, *pieces, table, spectra, edge)
 
@@ -232,57 +246,95 @@
     rows = height // peers
 
     def body(s_ref, table_ref, every, edges, *refs):
-        correlate(s_ref, 3, every, edges, table_ref, refs[-1], refs[:-1])
+        out_ref, phases = refs
+        outs = [out_ref.at[k] for k in range(peers)]
+        correlate(s_ref, 0, 3, every, edges, table_ref, phases, outs)
 
     return pl.pallas_call(
         body,
         in_specs=[pl.BlockSpec(memory_space=pltpu.SMEM)]
         + [pl.BlockSpec(memory_space=pltpu.VMEM)] * 3,
-        out_specs=[pl.BlockSpec(memory_space=pltpu.VMEM)] * peers,
-        out_shape=[jax.ShapeDtypeStruct((slots, 2 * block, rows), jnp.bfloat16)] * peers,
+        out_specs=pl.BlockSpec(memory_space=pltpu.VMEM),
+        out_shape=jax.ShapeDtypeStruct((peers, slots, 2 * block, rows), jnp.bfloat16),
         scratch_shapes=[pltpu.VMEM((2 * slots, block, height), jnp.bfloat16)],
         compiler_params=params(),
+        cost_estimate=cost(8 * slots * block * height * height, 8 * height * height),
         name="own_slots",
     )(scalars, table, spectra, edge)
 
 
-def surfaces_of(scalars, own, other, table):
-    peers = len(own)
-    slots, double, rows = own[0].shape
+def own_surfaces(half, own, table):
+    peers, slots, double, rows = own.shape
     width = table.shape[0]
     span = peers * double
 
-    def body(s_ref, *refs):
-        own_refs, other_refs = refs[:peers], refs[peers : 2 * peers]
-        table_ref, out_ref, work = refs[2 * peers :]
-        half = s_ref[0]
-        me = s_ref[1]
-        for k in range(peers):
-            place = (me ^ k) * double
-            here = pl.multiple_of(half * span + place, double)
-            there = pl.multiple_of((1 - half) * span + place, double)
-            work[pl.ds(here, double), :] = own_refs[k][0]
-            work[pl.ds(there, double), :] = other_refs[k][0]
-        surface = lax.dot_general(
-            work[...], table_ref[...], (((0,), (0,)), ((), ())), preferred_element_type=jnp.float32
-        )
-        live = pl.program_id(0) < s_ref[2]
-        out_ref[0] = jnp.where(live, surface, 0.0)
-
-    piece = pl.BlockSpec((1, double, rows), lambda p, s: (p, 0, 0))
+    def body(half_ref, own_ref, table_ref, out_ref):
+        out_ref[0] = lax.dot_general(
+            own_ref[:, 0].reshape(span, rows),
+            table_ref[...],
+            (((0,), (0,)), ((), ())),
+            preferred_element_type=jnp.float32,
+        )
+
     return pl.pallas_call(
         body,
         grid_spec=pltpu.PrefetchScalarGridSpec(
             num_scalar_prefetch=1,
             grid=(slots,),
-            in_specs=[piece] * (2 * peers) + [pl.BlockSpec((width, width), lambda p, s: (0, 0))],
-            out_specs=pl.BlockSpec((1, rows, width), lambda p, s: (p, 0, 0)),
-            scratch_shapes=[pltpu.VMEM((width, rows), jnp.bfloat16)],
+            in_specs=[
+                pl.BlockSpec((peers, 1, double, rows), lambda p, half: (0, p, 0, 0)),
+                pl.BlockSpec((span, width), lambda p, half: (half[0], 0)),
+            ],
+            out_specs=pl.BlockSpec((1, rows, width), lambda p, half: (p, 0, 0)),
         ),
         out_shape=jax.ShapeDtypeStruct((slots, rows, width), jnp.float32),
         compiler_params=params(),
+        cost_estimate=cost(2 * slots * rows * width * span, 4 * slots * rows * width),
+        name="own_surfaces",
+    )(scalar(half), own, table)
+
+
+def surfaces_of(half, me, counts, part, came, swapped, table):
+    peers = 2 * len(came)
+    slots, double, rows = swapped[0].shape
+    width = table.shape[0]
+    span = peers * double
+
+    def body(half_ref, me_ref, counts_ref, part_ref, *refs):
+        other_refs = refs[:peers]
+        table_ref, out_ref, work = refs[peers:]
+        for k in range(peers):
+            place = pl.multiple_of((me_ref[0] ^ k) * double, double)
+            piece = other_refs[k][0] if k % 2 else other_refs[k][0, 0]
+            work[pl.ds(place, double), :] = piece
+        rest = lax.dot_general(
+            work[...], table_ref[...], (((0,), (0,)), ((), ())), preferred_element_type=jnp.float32
+        )
+        live = pl.program_id(0) < counts_ref[0]
+        out_ref[0] = jnp.where(live, part_ref[0] + rest, 0.0)
+
+    pair = pl.BlockSpec((1, 1, double, rows), lambda p, half, me, counts: (0, p, 0, 0))
+    piece = pl.BlockSpec((1, double, rows), lambda p, half, me, counts: (p, 0, 0))
+    other = [swapped[k // 2] if k % 2 else came[k // 2] for k in range(peers)]
+    plane = pl.BlockSpec((1, rows, width), lambda p, half, me, counts: (p, 0, 0))
+    return pl.pallas_call(
+        body,
+        grid_spec=pltpu.PrefetchScalarGridSpec(
+            num_scalar_prefetch=3,
+            grid=(slots,),
+            in_specs=[
+                plane,
+                *[pair, piece] * (peers // 2),
+                pl.BlockSpec((span, width), lambda p, half, me, counts: (1 - half[0], 0)),
+            ],
+            out_specs=plane,
+            scratch_shapes=[pltpu.VMEM((span, rows), jnp.bfloat16)],
+        ),
+        out_shape=jax.ShapeDtypeStruct((slots, rows, width), jnp.float32),
+        compiler_params=params(),
+        cost_estimate=cost(2 * slots * rows * width * span, 8 * slots * rows * width),
         name="surfaces",
-    )(scalars, *own, *other, table)
+    )(scalar(half), scalar(me), counts, part, *other, table)
 
 
 def local(tiles, pairs, counts):
@@ -305,18 +357,21 @@
         ]
         return lax.ppermute(value, axes, moves)
 
-    def along(value, k):
-        return lax.ppermute(value, "rows", [(r, r ^ k) for r in range(peers)])
+    def along(blocks):
+        return lax.all_to_all(blocks, "rows", split_axis=0, concat_axis=0)
+
+    def swap(value):
+        return lax.ppermute(value, "rows", [(r, r ^ 1) for r in range(peers)])
 
     table_w = jnp.asarray(width_table(width, 2 * peers))
-    down = hann(height, me * rows, rows)[:, None]
-    sideways = hann(width, 0, width)[None, :]
-
-    first = jnp.stack([1 - half, me])
-    sent = row_transform(tiles, down, sideways, table_w, first, peers)
+    down = jnp.asarray(np.tile(hann(height), (8, 1)))
+    sideways = jnp.asarray(hann(width)[None, :])
+
+    sent = row_transform(tiles, down, sideways, table_w, 1 - half, me, peers, True)
     arrived = [across(sent[k], k) for k in range(peers)]
-    kept = row_transform(tiles, down, sideways, table_w, jnp.stack([half, me]), peers)
-    mine = [kept[0]] + [along(kept[k], k) for k in range(1, peers)]
+    *sent, held, pairs = lax.optimization_barrier((*sent, half, pairs))
+    (kept,) = row_transform(tiles, down, sideways, table_w, held, me, peers, False)
+    mine = along(kept)
 
     table_h = height_table(height)
     theirs = across(pairs, 0)
@@ -327,10 +382,10 @@
     )
     spectra, edge = own_spectra(scalars, mine, table_h)
     *back, spectra, edge = partner_slots(scalars, arrived, table_h, spectra, edge, slots)
-    other = [across(back[k], k) for k in range(peers)]
-    out = own_slots(scalars, table_h, spectra, edge, peers, slots)
-    own = [out[0]] + [along(out[k], k) for k in range(1, peers)]
-    return surfaces_of(jnp.stack([half, me, counts[0]]), own, other, table_w)
+    came = [across(back[j], 2 * j) for j in range(peers // 2)]
+    swapped = [swap(value[1]) for value in came]
+    own = along(own_slots(scalars, table_h, spectra, edge, peers, slots))
+    return surfaces_of(half, me, counts, own_surfaces(half, own, table_w), came, swapped, table_w)
 
 
 def solution(mesh):

time: 85.6 us -> 83.3 us (0.973)
  other arithmetic: 7.15 us -> 3.96 us
  starting transfers between devices: 22.1 us -> 20.1 us
  local copies, waits for them, and re-layouts: 2.91 us -> 4.5 us
    all_to_all x0 -> x2, starting transfers between devices: none -> 6.94 us  [along(): return lax.all_to_all(blocks, 'rows', split_axis=0, concat_axis=0)]
    ppermute x6 -> x2, starting transfers between devices: 6.22 us -> 0.14 us  [swap(): return lax.ppermute(value, 'rows', [(r, r ^ 1) for r in range(peers)])]
    all_to_all x0 -> x2, waiting for transfers between devices: none -> 3.48 us  [along(): return lax.all_to_all(blocks, 'rows', split_axis=0, concat_axis=0)]
    pallas_call x0 -> x1, Pallas kernels: none -> 3.2 us  [own_surfaces(): pl.pallas_call(body, grid_spec=pltpu.PrefetchScalarGridSpec(num_scalar_pr...]
    ppermute x9 -> x7, starting transfers between devices: 15.8 us -> 13 us  [across(): return lax.ppermute(value, axes, moves)]
    ppermute x6 -> x2, waiting for transfers between devices: 2.61 us -> 0.01 us  [swap(): return lax.ppermute(value, 'rows', [(r, r ^ 1) for r in range(peers)])]
    sub x2 -> x0, other arithmetic: 1.84 us -> none  [hann(): return 0.5 - 0.5 * jnp.cos(2.0 * math.pi / length * index)]
    unnamed x52 -> x30, local copies, waits for them, and re-layouts: 1.98 us -> 3.63 us
  transfers between devices with their start and end apart: 15 -> 11, of which waited for: 6 -> 5; matrix products, arithmetic and copies ran while one was open for 9% -> 6% of each run, Pallas kernels for 15% -> 20%
where the time goes in v2:
time: 83.3 us; the launch traced here: 83 us
  Pallas kernels  30.4 us (36%)
  waiting for transfers between devices  23.1 us (28%)
  starting transfers between devices  20.1 us (24%)
  local copies, waits for them, and re-layouts  4.5 us (5%)
  other arithmetic  3.96 us (5%)
  between operations  0.85 us (1%)
    ppermute x7, waiting for transfers between devices, across(): return lax.ppermute(value, axes, moves)  19.7 us
    ppermute x7, starting transfers between devices, across(): return lax.ppermute(value, axes, moves)  13 us
    pallas_call x2, Pallas kernels, row_transform(): pl.pallas_call(body, grid_spec=pltpu.PrefetchScalarGridSpec(num_scalar_pr...  7.53 us
    all_to_all x2, starting transfers between devices, along(): return lax.all_to_all(blocks, 'rows', split_axis=0, concat_axis=0)  6.94 us
    pallas_call x1, Pallas kernels, partner_slots(): pl.pallas_call(body, in_specs=[pl.BlockSpec(memory_space=pltpu.SMEM)] + [...  6.57 us
    pallas_call x1, Pallas kernels, own_slots(): pl.pallas_call(body, in_specs=[pl.BlockSpec(memory_space=pltpu.SMEM)] + [...  4.98 us
    pallas_call x1, Pallas kernels, own_spectra(): pl.pallas_call(body, in_specs=[pl.BlockSpec(memory_space=pltpu.SMEM)] + [...  4.48 us
    pallas_call x1, Pallas kernels, surfaces_of(): pl.pallas_call(body, grid_spec=pltpu.PrefetchScalarGridSpec(num_scalar_pr...  3.68 us
  transfers between devices with their start and end apart: 11, of which 5 were waited for; matrix products, arithmetic and copies ran while one was open for 6% of the time, Pallas kernels for 20%

profile of v2, /device:TPU:0, one launch (start us, length us, event | category | flops | bytes accessed | tf_op | source)
XLA Modules:
  0.0 83.0 jit_solution(15834030087190751625)
XLA Ops:
  0.0 3.8 %row_transform.2 = (bf16[2,128,256]{2,1,0:T(8,128)(2,1)}, bf16[2,128,256]{2,1,0:T(8,128)(2,1)}, bf16[2,128,256]{2,1,0:T(8,128)(2,1)}, bf16[2,128,256]{2,1,0:T(8,128)(2,1)}) custom-call(s32[1]{0:T(128)} %bitcast.3.half_ref, s32[1]{0:T(128)} %bitcast.1.me_ref, f32[2,256,1024]{2,1,0:T(8,128)} %tile_ref.3, f32[8,1024]{1,0:T(8,128)} %constant.54.clone.down_ref, ...), custom_call_target="tpu_custom_call" | custom-call | flops 536870912 | bytes 3145728 | tf_op jit(solution)/shard_map/row_transform/pallas_call | solution.py:86
  3.9 4.1 %collective-permute-start.1 = (bf16[2,128,256]{2,1,0:T(8,128)(2,1)}, bf16[2,128,256]{2,1,0:T(8,128)(2,1)S(1)}, u32[]{:S(2)}, u32[]{:S(2)}) collective-permute-start(bf16[2,128,256]{2,1,0:T(8,128)(2,1)} %get-tuple-element.17), channel_id=1, source_target_pairs={{0,8},{1,9},{2,10},{3,11},{4,12},{5,13},{6,14},{7,15},{8,0},{9,1},... | collective-permute-start | bytes 393224 | tf_op jit(solution)/shard_map/ppermute | solution.py:358
  7.9 3.0 %collective-permute-start.3 = (bf16[2,128,256]{2,1,0:T(8,128)(2,1)}, bf16[2,128,256]{2,1,0:T(8,128)(2,1)S(1)}, u32[]{:S(2)}, u32[]{:S(2)}) collective-permute-start(bf16[2,128,256]{2,1,0:T(8,128)(2,1)} %get-tuple-element.19), channel_id=1, source_target_pairs={{0,10},{1,11},{2,8},{3,9},{4,14},{5,15},{6,12},{7,13},{8,2},{9,3},... | collective-permute-start | bytes 393224 | tf_op jit(solution)/shard_map/ppermute | solution.py:358
  11.6 2.6 %collective-permute-start = (s32[1,2,2]{2,1,0:T(2,128)S(1)}, s32[1,2,2]{2,1,0:T(2,128)S(1)}, u32[]{:S(2)}, u32[]{:S(2)}) collective-permute-start(s32[1,2,2]{2,1,0:T(2,128)S(1)} %copy-done.14), channel_id=1, source_target_pairs={{0,8},{1,9},{2,10},{3,11},{4,12},{5,13},{6,14},{7,15},{8,0},{9,1},... | collective-permute-start | bytes 56 | tf_op jit(solution)/shard_map/ppermute | solution.py:358
  14.1 3.7 %row_transform.3 = bf16[4,2,128,256]{3,2,1,0:T(8,128)(2,1)} custom-call(s32[1]{0:T(128)} %bitcast.6.half_ref, s32[1]{0:T(128)} %bitcast.1.me_ref, f32[2,256,1024]{2,1,0:T(8,128)} %tile_ref.3, f32[8,1024]{1,0:T(8,128)} %constant.54.clone.down_ref, f32[1,1024]{1,0:T(1,128)} %constant.55.clone.across_ref, bf16[1024,1024]{1,0:T(8,128)(2,1)} %constant.53.clone.table_ref.refs_4_), custom_call_target="tpu_custom_call" | custom-call | flops 536870912 | bytes 3145728 | tf_op jit(solution)/shard_map/row_transform/pallas_call | solution.py:86
  17.8 3.5 %all-to-all-start = ((bf16[4,2,128,256]{3,2,1,0:T(8,128)(2,1)}), bf16[4,2,128,256]{3,2,1,0:T(8,128)(2,1)S(1)}, u32[]{:S(2)}, u32[]{:S(2)}) async-start(bf16[4,2,128,256]{3,2,1,0:T(8,128)(2,1)} %row_transform.3), calls=%async_computation | async-start | bytes 1048576 | tf_op jit(solution)/shard_map/all_to_all | solution.py:361
  21.4 1.4 %subtract_convert_fusion = (bf16[32,32,1024]{2,1,0:T(8,128)(2,1)S(1)}, bf16[32,32,1024]{2,1,0:T(8,128)(2,1)S(1)}) fusion(f32[32,1024]{1,0:T(8,128)S(1)} %copy-done.4, f32[32,1024]{1,0:T(8,128)S(1)} %copy-done.5, f32[32,1024]{1,0:T(8,128)S(1)} %copy-done.6, f32[32,1024]{1,0:T(8,128)S(1)} %copy-done.7), kind=kLoop, calls=%fused_computation.2 | loop fusion | flops 8388608 | bytes 4718592 | tf_op jit(solution)/shard_map/convert.4
  22.8 2.4 %pad_maximum_fusion.table_ref.refs_4_ = bf16[1024,2048]{1,0:T(8,128)(2,1)} fusion(bf16[1024,1024]{1,0:T(8,128)(2,1)S(1)} %bitcast.15, bf16[1024,1024]{1,0:T(8,128)(2,1)S(1)} %bitcast.14), kind=kLoop, calls=%fused_computation | loop fusion | flops 8388608 | bytes 8388608 | tf_op jit(solution)/shard_map/concatenate | solution.py:48
  25.2 6.2 %collective-permute-done = s32[1,2,2]{2,1,0:T(2,128)S(1)} collective-permute-done((s32[1,2,2]{2,1,0:T(2,128)S(1)}, s32[1,2,2]{2,1,0:T(2,128)S(1)}, u32[]{:S(2)}, u32[]{:S(2)}) %collective-permute-start) | collective-permute-done | bytes 48 | tf_op jit(solution)/shard_map/ppermute | solution.py:358
  31.8 0.6 concatenate.7.s_ref
  32.4 3.4 %all-to-all-done.pieces_ref = bf16[4,2,128,256]{3,2,1,0:T(8,128)(2,1)S(1)} async-done(((bf16[4,2,128,256]{3,2,1,0:T(8,128)(2,1)}), bf16[4,2,128,256]{3,2,1,0:T(8,128)(2,1)S(1)}, u32[]{:S(2)}, u32[]{:S(2)}) %all-to-all-start) | async-done | bytes 524320 | tf_op jit(solution)/shard_map/all_to_all | solution.py:361
  35.7 0.8 copy-done
  36.5 4.5 %own_spectra.1 = (bf16[2,2,64,1024]{3,2,1,0:T(8,128)(2,1)}, bf16[2,2,16,1024]{3,2,1,0:T(8,128)(2,1)}) custom-call(s32[11]{0:T(128)} %concatenate.7.s_ref, bf16[4,2,128,256]{3,2,1,0:T(8,128)(2,1)} %copy-done, bf16[1024,2048]{1,0:T(8,128)(2,1)} %pad_maximum_fusion.table_ref.refs_4_), custom_call_target="tpu_custom_call" | custom-call | flops 1073741824 | bytes 8388608 | tf_op jit(solution)/shard_map/own_spectra/pallas_call | solution.py:197
  41.8 6.6 %partner_slots.1 = (bf16[2,2,128,256]{3,2,1,0:T(8,128)(2,1)}, bf16[2,2,128,256]{3,2,1,0:T(8,128)(2,1)}, bf16[4,2,64,1024]{3,2,1,0:T(8,128)(2,1)}, bf16[4,2,16,1024]{3,2,1,0:T(8,128)(2,1)}) custom-call(s32[11]{0:T(128)} %concatenate.7.s_ref, bf16[2,128,256]{2,1,0:T(8,128)(2,1)} %copy-done.10, bf16[2,128,256]{2,1,0:T(8,128)(2,1)} %copy-done.11, ...), custom_call_target="tpu_custom_call" | custom-call | flops 2147483648 | bytes 8388608 | tf_op jit(solution)/shard_map/partner_slots/pallas_call | solution.py:227
  48.4 2.7 %collective-permute-start.7 = (bf16[2,2,128,256]{3,2,1,0:T(8,128)(2,1)}, bf16[2,2,128,256]{3,2,1,0:T(8,128)(2,1)S(1)}, u32[]{:S(2)}, u32[]{:S(2)}) collective-permute-start(bf16[2,2,128,256]{3,2,1,0:T(8,128)(2,1)} %get-tuple-element.28), channel_id=1, source_target_pairs={{0,10},{1,11},{2,8},{3,9},{4,14},{5,15},{6,12},{7,13},{8,2},{9,3},... | collective-permute-start | bytes 786440 | tf_op jit(solution)/shard_map/ppermute | solution.py:358
  51.1 5.0 %own_slots.1 = bf16[4,2,128,256]{3,2,1,0:T(8,128)(2,1)} custom-call(s32[11]{0:T(128)} %concatenate.7.s_ref, bf16[1024,2048]{1,0:T(8,128)(2,1)} %pad_maximum_fusion.table_ref.refs_4_, bf16[4,2,64,1024]{3,2,1,0:T(8,128)(2,1)} %get-tuple-element.25.every, bf16[4,2,16,1024]{3,2,1,0:T(8,128)(2,1)} %get-tuple-element.26.edges), custom_call_target="tpu_custom_call" | custom-call | flops 1073741824 | bytes 8388608 | tf_op jit(solution)/shard_map/own_slots/pallas_call | solution.py:253
  56.1 3.5 %all-to-all-start.1 = ((bf16[4,2,128,256]{3,2,1,0:T(8,128)(2,1)}), bf16[4,2,128,256]{3,2,1,0:T(8,128)(2,1)S(1)}, u32[]{:S(2)}, u32[]{:S(2)}) async-start(bf16[4,2,128,256]{3,2,1,0:T(8,128)(2,1)} %own_slots.1), calls=%async_computation.1 | async-start | bytes 1048576 | tf_op jit(solution)/shard_map/all_to_all | solution.py:361
  59.6 7.8 %collective-permute-done.5.refs_0_ = bf16[2,2,128,256]{3,2,1,0:T(8,128)(2,1)S(1)} collective-permute-done((bf16[2,2,128,256]{3,2,1,0:T(8,128)(2,1)}, bf16[2,2,128,256]{3,2,1,0:T(8,128)(2,1)S(1)}, u32[]{:S(2)}, u32[]{:S(2)}) %collective-permute-start.5) | collective-permute-done | bytes 262176 | tf_op jit(solution)/shard_map/ppermute | solution.py:358
  67.5 5.6 %collective-permute-done.7.refs_2_ = bf16[2,2,128,256]{3,2,1,0:T(8,128)(2,1)S(1)} collective-permute-done((bf16[2,2,128,256]{3,2,1,0:T(8,128)(2,1)}, bf16[2,2,128,256]{3,2,1,0:T(8,128)(2,1)S(1)}, u32[]{:S(2)}, u32[]{:S(2)}) %collective-permute-start.7) | collective-permute-done | bytes 262176 | tf_op jit(solution)/shard_map/ppermute | solution.py:358
  74.0 0.8 copy-done.1
  74.8 3.2 %own_surfaces.1.part_ref = f32[2,256,1024]{2,1,0:T(8,128)} custom-call(s32[1]{0:T(128)} %bitcast.half_ref, bf16[4,2,128,256]{3,2,1,0:T(8,128)(2,1)} %copy-done.1, bf16[1024,1024]{1,0:T(8,128)(2,1)} %constant.53.clone.table_ref.refs_4_), custom_call_target="tpu_custom_call" | custom-call | flops 536870912 | bytes 2097152 | tf_op jit(solution)/shard_map/own_surfaces/pallas_call | solution.py:279
  78.0 0.6 copy-done.8
  78.7 0.6 copy-done.9
  79.3 3.7 %surfaces.1 = f32[2,256,1024]{2,1,0:T(8,128)} custom-call(s32[1]{0:T(128)} %bitcast.half_ref, s32[1]{0:T(128)} %bitcast.1.me_ref, s32[1]{0:T(128)S(6)} %copy.12.counts_ref, f32[2,256,1024]{2,1,0:T(8,128)} %own_surfaces.1.part_ref, bf16[2,2,128,256]{3,2,1,0:T(8,128)(2,1)} %copy-done.2, bf16[2,128,256]{2,1,0:T(8,128)(2,1)} %copy-done.8, ...), custom_call_target="tpu_custom_call" | custom-call | flops 536870912 | bytes 4194304 | tf_op jit(solution)/shard_map/surfaces/pallas_call | solution.py:320
  (46 shorter events, 2.1 us)
Async XLA Ops:
  0.0 11.6 %copy-start.14 = (s32[1,2,2]{2,1,0:T(2,128)S(1)}, s32[1,2,2]{2,1,0:T(2,128)}, u32[]{:S(2)}) copy-start(s32[1,2,2]{2,1,0:T(2,128)} %param.11) | copy-start | bytes 52
  0.0 21.4 %copy-start.4 = (f32[32,1024]{1,0:T(8,128)S(1)}, f32[32,1024]{1,0:T(8,128)}, u32[]{:S(2)}) copy-start(f32[32,1024]{1,0:T(8,128)} %constant.59.clone) | copy-start | bytes 393220
  0.0 21.4 %copy-start.5 = (f32[32,1024]{1,0:T(8,128)S(1)}, f32[32,1024]{1,0:T(8,128)}, u32[]{:S(2)}) copy-start(f32[32,1024]{1,0:T(8,128)} %constant.57.clone) | copy-start | bytes 393220
  0.0 21.4 %copy-start.6 = (f32[32,1024]{1,0:T(8,128)S(1)}, f32[32,1024]{1,0:T(8,128)}, u32[]{:S(2)}) copy-start(f32[32,1024]{1,0:T(8,128)} %constant.58.clone) | copy-start | bytes 393220
  0.0 21.4 %copy-start.7 = (f32[32,1024]{1,0:T(8,128)S(1)}, f32[32,1024]{1,0:T(8,128)}, u32[]{:S(2)}) copy-start(f32[32,1024]{1,0:T(8,128)} %constant.56.clone) | copy-start | bytes 393220
  3.9 37.2 %collective-permute-start.1 = (bf16[2,128,256]{2,1,0:T(8,128)(2,1)}, bf16[2,128,256]{2,1,0:T(8,128)(2,1)S(1)}, u32[]{:S(2)}, u32[]{:S(2)}) collective-permute-start(bf16[2,128,256]{2,1,0:T(8,128)(2,1)} %get-tuple-element.17), channel_id=1, source_target_pairs={{0,8},{1,9},{2,10},{3,11},{4,12},{5,13},{6,14},{7,15},{8,0},{9,1},... | collective-permute-start | bytes 393224 | tf_op jit(solution)/shard_map/ppermute | solution.py:358
  7.9 33.1 %collective-permute-start.2 = (bf16[2,128,256]{2,1,0:T(8,128)(2,1)}, bf16[2,128,256]{2,1,0:T(8,128)(2,1)S(1)}, u32[]{:S(2)}, u32[]{:S(2)}) collective-permute-start(bf16[2,128,256]{2,1,0:T(8,128)(2,1)} %get-tuple-element.18), channel_id=1, source_target_pairs={{0,9},{1,8},{2,11},{3,10},{4,13},{5,12},{6,15},{7,14},{8,1},{9,0},... | collective-permute-start | bytes 393224 | tf_op jit(solution)/shard_map/ppermute | solution.py:358
  7.9 33.1 %collective-permute-start.3 = (bf16[2,128,256]{2,1,0:T(8,128)(2,1)}, bf16[2,128,256]{2,1,0:T(8,128)(2,1)S(1)}, u32[]{:S(2)}, u32[]{:S(2)}) collective-permute-start(bf16[2,128,256]{2,1,0:T(8,128)(2,1)} %get-tuple-element.19), channel_id=1, source_target_pairs={{0,10},{1,11},{2,8},{3,9},{4,14},{5,15},{6,12},{7,13},{8,2},{9,3},... | collective-permute-start | bytes 393224 | tf_op jit(solution)/shard_map/ppermute | solution.py:358
  11.0 30.1 %collective-permute-start.4 = (bf16[2,128,256]{2,1,0:T(8,128)(2,1)}, bf16[2,128,256]{2,1,0:T(8,128)(2,1)S(1)}, u32[]{:S(2)}, u32[]{:S(2)}) collective-permute-start(bf16[2,128,256]{2,1,0:T(8,128)(2,1)} %get-tuple-element.20), channel_id=1, source_target_pairs={{0,11},{1,10},{2,9},{3,8},{4,15},{5,14},{6,13},{7,12},{8,3},{9,2},... | collective-permute-start | bytes 393224 | tf_op jit(solution)/shard_map/ppermute | solution.py:358
  11.6 19.8 %collective-permute-start = (s32[1,2,2]{2,1,0:T(2,128)S(1)}, s32[1,2,2]{2,1,0:T(2,128)S(1)}, u32[]{:S(2)}, u32[]{:S(2)}) collective-permute-start(s32[1,2,2]{2,1,0:T(2,128)S(1)} %copy-done.14), channel_id=1, source_target_pairs={{0,8},{1,9},{2,10},{3,11},{4,12},{5,13},{6,14},{7,15},{8,0},{9,1},... | collective-permute-start | bytes 56 | tf_op jit(solution)/shard_map/ppermute | solution.py:358
  17.8 17.9 %all-to-all-start = ((bf16[4,2,128,256]{3,2,1,0:T(8,128)(2,1)}), bf16[4,2,128,256]{3,2,1,0:T(8,128)(2,1)S(1)}, u32[]{:S(2)}, u32[]{:S(2)}) async-start(bf16[4,2,128,256]{3,2,1,0:T(8,128)(2,1)} %row_transform.3), calls=%async_computation | async-start | bytes 1048576 | tf_op jit(solution)/shard_map/all_to_all | solution.py:361
  35.7 0.8 copy-start
  41.0 0.7 copy-start.10
  41.0 0.7 copy-start.11
  41.1 0.7 copy-start.12
  41.1 0.8 copy-start.13
  48.4 19.0 %collective-permute-start.5 = (bf16[2,2,128,256]{3,2,1,0:T(8,128)(2,1)}, bf16[2,2,128,256]{3,2,1,0:T(8,128)(2,1)S(1)}, u32[]{:S(2)}, u32[]{:S(2)}) collective-permute-start(bf16[2,2,128,256]{3,2,1,0:T(8,128)(2,1)} %get-tuple-element.27), channel_id=1, source_target_pairs={{0,8},{1,9},{2,10},{3,11},{4,12},{5,13},{6,14},{7,15},{8,0},{9,1},... | collective-permute-start | bytes 786440 | tf_op jit(solution)/shard_map/ppermute | solution.py:358
  48.4 24.7 %collective-permute-start.7 = (bf16[2,2,128,256]{3,2,1,0:T(8,128)(2,1)}, bf16[2,2,128,256]{3,2,1,0:T(8,128)(2,1)S(1)}, u32[]{:S(2)}, u32[]{:S(2)}) collective-permute-start(bf16[2,2,128,256]{3,2,1,0:T(8,128)(2,1)} %get-tuple-element.28), channel_id=1, source_target_pairs={{0,10},{1,11},{2,8},{3,9},{4,14},{5,15},{6,12},{7,13},{8,2},{9,3},... | collective-permute-start | bytes 786440 | tf_op jit(solution)/shard_map/ppermute | solution.py:358
  56.1 17.9 %all-to-all-start.1 = ((bf16[4,2,128,256]{3,2,1,0:T(8,128)(2,1)}), bf16[4,2,128,256]{3,2,1,0:T(8,128)(2,1)S(1)}, u32[]{:S(2)}, u32[]{:S(2)}) async-start(bf16[4,2,128,256]{3,2,1,0:T(8,128)(2,1)} %own_slots.1), calls=%async_computation.1 | async-start | bytes 1048576 | tf_op jit(solution)/shard_map/all_to_all | solution.py:361
  67.4 10.6 %copy-start.2 = (bf16[2,2,128,256]{3,2,1,0:T(8,128)(2,1)}, bf16[2,2,128,256]{3,2,1,0:T(8,128)(2,1)S(1)}, u32[]{:S(2)}) copy-start(bf16[2,2,128,256]{3,2,1,0:T(8,128)(2,1)S(1)} %collective-permute-done.5.refs_0_) | copy-start | bytes 786436
  67.4 10.6 %collective-permute-start.6 = (bf16[2,128,256]{2,1,0:T(8,128)(2,1)S(1)}, bf16[2,128,256]{2,1,0:T(8,128)(2,1)S(1)}, u32[]{:S(2)}, u32[]{:S(2)}) collective-permute-start(bf16[2,128,256]{2,1,0:T(8,128)(2,1)S(1)} %slice_bitcast_fusion.1), channel_id=1, source_target_pairs={{0,1},{1,0},{2,3},{3,2},{4,5},{5,4},{6,7},{7,6},{8,9},{9,8},{10,11... | collective-permute-start | bytes 393224 | tf_op jit(solution)/shard_map/ppermute | solution.py:364
  73.1 4.9 %copy-start.3 = (bf16[2,2,128,256]{3,2,1,0:T(8,128)(2,1)}, bf16[2,2,128,256]{3,2,1,0:T(8,128)(2,1)S(1)}, u32[]{:S(2)}) copy-start(bf16[2,2,128,256]{3,2,1,0:T(8,128)(2,1)S(1)} %collective-permute-done.7.refs_2_) | copy-start | bytes 786436
  73.1 4.9 %collective-permute-start.8 = (bf16[2,128,256]{2,1,0:T(8,128)(2,1)S(1)}, bf16[2,128,256]{2,1,0:T(8,128)(2,1)S(1)}, u32[]{:S(2)}, u32[]{:S(2)}) collective-permute-start(bf16[2,128,256]{2,1,0:T(8,128)(2,1)S(1)} %slice_bitcast_fusion), channel_id=1, source_target_pairs={{0,1},{1,0},{2,3},{3,2},{4,5},{5,4},{6,7},{7,6},{8,9},{9,8},{10,11... | collective-permute-start | bytes 393224 | tf_op jit(solution)/shard_map/ppermute | solution.py:364
  74.0 0.8 copy-start.1
  (2 other events, 1.3 us)

commit v3 on v2

--- a/solution.py
+++ b/solution.py
@@ -377,15 +377,16 @@
     theirs = across(pairs, 0)
     packed = ((half == 0) & (me == 0)).astype(jnp.int32)
     their_pairs = jnp.stack([theirs[0, :, 0] + count, (theirs[0, :, 1] + count) % (2 * count)], 1)
-    scalars = jnp.concatenate(
-        [jnp.stack([half, me, packed]), pairs.reshape(-1), their_pairs.reshape(-1)]
-    )
-    spectra, edge = own_spectra(scalars, mine, table_h)
+    place = jnp.stack([half, me, packed])
+    spectra, edge = own_spectra(place, mine, table_h)
+    scalars = jnp.concatenate([place, pairs.reshape(-1), their_pairs.reshape(-1)])
     *back, spectra, edge = partner_slots(scalars, arrived, table_h, spectra, edge, slots)
     came = [across(back[j], 2 * j) for j in range(peers // 2)]
+    own = along(own_slots(scalars, table_h, spectra, edge, peers, slots))
+    part = own_surfaces(half, own, table_w)
+    came[-1], part = lax.optimization_barrier((came[-1], part))
     swapped = [swap(value[1]) for value in came]
-    own = along(own_slots(scalars, table_h, spectra, edge, peers, slots))
-    return surfaces_of(half, me, counts, own_surfaces(half, own, table_w), came, swapped, table_w)
+    return surfaces_of(half, me, counts, part, came, swapped, table_w)
 
 
 def solution(mesh):

time: 83.3 us -> 80.9 us (0.971)
  the two profiles are of different devices: /device:TPU:0 before, /device:TPU:13 now
where the time goes in v3:
time: 80.9 us; the launch traced here: 80.6 us
  Pallas kernels  30.5 us (38%)
  starting transfers between devices  23.7 us (29%)
  waiting for transfers between devices  16.7 us (21%)
  other arithmetic  4.61 us (6%)
  local copies, waits for them, and re-layouts  4.31 us (5%)
    ppermute x7, starting transfers between devices, across(): return lax.ppermute(value, axes, moves)  13.1 us
    all_to_all x2, waiting for transfers between devices, along(): return lax.all_to_all(blocks, 'rows', split_axis=0, concat_axis=0)  10.7 us
    all_to_all x2, starting transfers between devices, along(): return lax.all_to_all(blocks, 'rows', split_axis=0, concat_axis=0)  9.01 us
    pallas_call x2, Pallas kernels, row_transform(): pl.pallas_call(body, grid_spec=pltpu.PrefetchScalarGridSpec(num_scalar_pr...  7.56 us
    pallas_call x1, Pallas kernels, partner_slots(): pl.pallas_call(body, in_specs=[pl.BlockSpec(memory_space=pltpu.SMEM)] + [...  6.57 us
    ppermute x7, waiting for transfers between devices, across(): return lax.ppermute(value, axes, moves)  5.64 us
    pallas_call x1, Pallas kernels, own_slots(): pl.pallas_call(body, in_specs=[pl.BlockSpec(memory_space=pltpu.SMEM)] + [...  4.98 us
    pallas_call x1, Pallas kernels, own_spectra(): pl.pallas_call(body, in_specs=[pl.BlockSpec(memory_space=pltpu.SMEM)] + [...  4.48 us
  transfers between devices with their start and end apart: 11, of which 4 were waited for; matrix products, arithmetic and copies ran while one was open for 7% of the time, Pallas kernels for 20%

profile of v3, /device:TPU:13, one launch (start us, length us, event | category | flops | bytes accessed | tf_op | source)
XLA Modules:
  0.0 80.6 jit_solution(14303330436396179081)
XLA Ops:
  0.0 3.9 %row_transform.2 = (bf16[2,128,256]{2,1,0:T(8,128)(2,1)}, bf16[2,128,256]{2,1,0:T(8,128)(2,1)}, bf16[2,128,256]{2,1,0:T(8,128)(2,1)}, bf16[2,128,256]{2,1,0:T(8,128)(2,1)}) custom-call(s32[1]{0:T(128)} %bitcast.3.half_ref, s32[1]{0:T(128)} %bitcast.1.me_ref, f32[2,256,1024]{2,1,0:T(8,128)} %tile_ref.3, f32[8,1024]{1,0:T(8,128)} %constant.54.clone.down_ref, ...), custom_call_target="tpu_custom_call" | custom-call | flops 536870912 | bytes 3145728 | tf_op jit(solution)/shard_map/row_transform/pallas_call | solution.py:86
  3.9 2.3 %collective-permute-start.1 = (bf16[2,128,256]{2,1,0:T(8,128)(2,1)}, bf16[2,128,256]{2,1,0:T(8,128)(2,1)S(1)}, u32[]{:S(2)}, u32[]{:S(2)}) collective-permute-start(bf16[2,128,256]{2,1,0:T(8,128)(2,1)} %get-tuple-element.19), channel_id=1, source_target_pairs={{0,8},{1,9},{2,10},{3,11},{4,12},{5,13},{6,14},{7,15},{8,0},{9,1},... | collective-permute-start | bytes 393224 | tf_op jit(solution)/shard_map/ppermute | solution.py:358
  6.2 0.9 %collective-permute-start.2 = (bf16[2,128,256]{2,1,0:T(8,128)(2,1)}, bf16[2,128,256]{2,1,0:T(8,128)(2,1)S(1)}, u32[]{:S(2)}, u32[]{:S(2)}) collective-permute-start(bf16[2,128,256]{2,1,0:T(8,128)(2,1)} %get-tuple-element.20), channel_id=1, source_target_pairs={{0,9},{1,8},{2,11},{3,10},{4,13},{5,12},{6,15},{7,14},{8,1},{9,0},... | collective-permute-start | bytes 393224 | tf_op jit(solution)/shard_map/ppermute | solution.py:358
  7.1 3.2 %collective-permute-start.3 = (bf16[2,128,256]{2,1,0:T(8,128)(2,1)}, bf16[2,128,256]{2,1,0:T(8,128)(2,1)S(1)}, u32[]{:S(2)}, u32[]{:S(2)}) collective-permute-start(bf16[2,128,256]{2,1,0:T(8,128)(2,1)} %get-tuple-element.21), channel_id=1, source_target_pairs={{0,10},{1,11},{2,8},{3,9},{4,14},{5,15},{6,12},{7,13},{8,2},{9,3},... | collective-permute-start | bytes 393224 | tf_op jit(solution)/shard_map/ppermute | solution.py:358
  10.6 1.8 %collective-permute-start = (s32[1,2,2]{2,1,0:T(2,128)S(1)}, s32[1,2,2]{2,1,0:T(2,128)S(1)}, u32[]{:S(2)}, u32[]{:S(2)}) collective-permute-start(s32[1,2,2]{2,1,0:T(2,128)S(1)} %copy-done.15), channel_id=1, source_target_pairs={{0,8},{1,9},{2,10},{3,11},{4,12},{5,13},{6,14},{7,15},{8,0},{9,1},... | collective-permute-start | bytes 56 | tf_op jit(solution)/shard_map/ppermute | solution.py:358
  12.4 3.7 %row_transform.3 = bf16[4,2,128,256]{3,2,1,0:T(8,128)(2,1)} custom-call(s32[1]{0:T(128)} %bitcast.6.half_ref, s32[1]{0:T(128)} %bitcast.1.me_ref, f32[2,256,1024]{2,1,0:T(8,128)} %tile_ref.3, f32[8,1024]{1,0:T(8,128)} %constant.54.clone.down_ref, f32[1,1024]{1,0:T(1,128)} %constant.55.clone.across_ref, bf16[1024,1024]{1,0:T(8,128)(2,1)} %constant.53.clone.table_ref.refs_4_), custom_call_target="tpu_custom_call" | custom-call | flops 536870912 | bytes 3145728 | tf_op jit(solution)/shard_map/row_transform/pallas_call | solution.py:86
  16.1 4.4 %all-to-all-start = ((bf16[4,2,128,256]{3,2,1,0:T(8,128)(2,1)}), bf16[4,2,128,256]{3,2,1,0:T(8,128)(2,1)S(1)}, u32[]{:S(2)}, u32[]{:S(2)}) async-start(bf16[4,2,128,256]{3,2,1,0:T(8,128)(2,1)} %row_transform.3), calls=%async_computation | async-start | bytes 1048576 | tf_op jit(solution)/shard_map/all_to_all | solution.py:361
  20.6 1.4 %subtract_convert_fusion = (bf16[32,32,1024]{2,1,0:T(8,128)(2,1)S(1)}, bf16[32,32,1024]{2,1,0:T(8,128)(2,1)S(1)}) fusion(f32[32,1024]{1,0:T(8,128)S(1)} %copy-done.4, f32[32,1024]{1,0:T(8,128)S(1)} %copy-done.5, f32[32,1024]{1,0:T(8,128)S(1)} %copy-done.6, f32[32,1024]{1,0:T(8,128)S(1)} %copy-done.7), kind=kLoop, calls=%fused_computation.2 | loop fusion | flops 8388608 | bytes 4718592 | tf_op jit(solution)/shard_map/convert.4
  22.0 2.4 %pad_maximum_fusion.table_ref.refs_4_ = bf16[1024,2048]{1,0:T(8,128)(2,1)} fusion(bf16[1024,1024]{1,0:T(8,128)(2,1)S(1)} %bitcast.15, bf16[1024,1024]{1,0:T(8,128)(2,1)S(1)} %bitcast.14), kind=kLoop, calls=%fused_computation | loop fusion | flops 8388608 | bytes 8388608 | tf_op jit(solution)/shard_map/concatenate | solution.py:48
  25.0 4.3 %collective-permute-done = s32[1,2,2]{2,1,0:T(2,128)S(1)} collective-permute-done((s32[1,2,2]{2,1,0:T(2,128)S(1)}, s32[1,2,2]{2,1,0:T(2,128)S(1)}, u32[]{:S(2)}, u32[]{:S(2)}) %collective-permute-start) | collective-permute-done | bytes 48 | tf_op jit(solution)/shard_map/ppermute | solution.py:358
  29.7 0.7 concatenate.8.s_ref
  30.4 0.8 copy-done
  31.2 4.5 %own_spectra.1 = (bf16[2,2,64,1024]{3,2,1,0:T(8,128)(2,1)}, bf16[2,2,16,1024]{3,2,1,0:T(8,128)(2,1)}) custom-call(s32[3]{0:T(128)} %pad_add_fusion.1.s_ref, bf16[4,2,128,256]{3,2,1,0:T(8,128)(2,1)} %copy-done, bf16[1024,2048]{1,0:T(8,128)(2,1)} %pad_maximum_fusion.table_ref.refs_4_), custom_call_target="tpu_custom_call" | custom-call | flops 1073741824 | bytes 8388608 | tf_op jit(solution)/shard_map/own_spectra/pallas_call | solution.py:197
  36.5 6.6 %partner_slots.1 = (bf16[2,2,128,256]{3,2,1,0:T(8,128)(2,1)}, bf16[2,2,128,256]{3,2,1,0:T(8,128)(2,1)}, bf16[4,2,64,1024]{3,2,1,0:T(8,128)(2,1)}, bf16[4,2,16,1024]{3,2,1,0:T(8,128)(2,1)}) custom-call(s32[11]{0:T(128)} %concatenate.8.s_ref, bf16[2,128,256]{2,1,0:T(8,128)(2,1)} %copy-done.11, bf16[2,128,256]{2,1,0:T(8,128)(2,1)} %copy-done.12, ...), custom_call_target="tpu_custom_call" | custom-call | flops 2147483648 | bytes 8388608 | tf_op jit(solution)/shard_map/partner_slots/pallas_call | solution.py:227
  43.0 3.8 %collective-permute-start.6 = (bf16[2,2,128,256]{3,2,1,0:T(8,128)(2,1)}, bf16[2,2,128,256]{3,2,1,0:T(8,128)(2,1)S(1)}, u32[]{:S(2)}, u32[]{:S(2)}) collective-permute-start(bf16[2,2,128,256]{3,2,1,0:T(8,128)(2,1)} %get-tuple-element.31), channel_id=1, source_target_pairs={{0,8},{1,9},{2,10},{3,11},{4,12},{5,13},{6,14},{7,15},{8,0},{9,1},... | collective-permute-start | bytes 786440 | tf_op jit(solution)/shard_map/ppermute | solution.py:358
  46.8 5.0 %own_slots.1 = bf16[4,2,128,256]{3,2,1,0:T(8,128)(2,1)} custom-call(s32[11]{0:T(128)} %concatenate.8.s_ref, bf16[1024,2048]{1,0:T(8,128)(2,1)} %pad_maximum_fusion.table_ref.refs_4_, bf16[4,2,64,1024]{3,2,1,0:T(8,128)(2,1)} %get-tuple-element.28.every, bf16[4,2,16,1024]{3,2,1,0:T(8,128)(2,1)} %get-tuple-element.29.edges), custom_call_target="tpu_custom_call" | custom-call | flops 1073741824 | bytes 8388608 | tf_op jit(solution)/shard_map/own_slots/pallas_call | solution.py:253
  51.8 4.6 %all-to-all-start.1 = ((bf16[4,2,128,256]{3,2,1,0:T(8,128)(2,1)}), bf16[4,2,128,256]{3,2,1,0:T(8,128)(2,1)S(1)}, u32[]{:S(2)}, u32[]{:S(2)}) async-start(bf16[4,2,128,256]{3,2,1,0:T(8,128)(2,1)} %own_slots.1), calls=%async_computation.1 | async-start | bytes 1048576 | tf_op jit(solution)/shard_map/all_to_all | solution.py:361
  56.4 0.9 %collective-permute-start.5 = (bf16[2,2,128,256]{3,2,1,0:T(8,128)(2,1)S(1)}, bf16[2,2,128,256]{3,2,1,0:T(8,128)(2,1)S(1)}, u32[]{:S(2)}, u32[]{:S(2)}) collective-permute-start(bf16[2,2,128,256]{3,2,1,0:T(8,128)(2,1)S(1)} %copy-done.10), channel_id=1, source_target_pairs={{0,10},{1,11},{2,8},{3,9},{4,14},{5,15},{6,12},{7,13},{8,2},{9,3},... | collective-permute-start | bytes 786440 | tf_op jit(solution)/shard_map/ppermute | solution.py:358
  57.3 1.3 %collective-permute-done.6.refs_0_ = bf16[2,2,128,256]{3,2,1,0:T(8,128)(2,1)S(1)} collective-permute-done((bf16[2,2,128,256]{3,2,1,0:T(8,128)(2,1)}, bf16[2,2,128,256]{3,2,1,0:T(8,128)(2,1)S(1)}, u32[]{:S(2)}, u32[]{:S(2)}) %collective-permute-start.6) | collective-permute-done | bytes 262176 | tf_op jit(solution)/shard_map/ppermute | solution.py:358
  59.3 10.7 %all-to-all-done.1.own_ref = bf16[4,2,128,256]{3,2,1,0:T(8,128)(2,1)S(1)} async-done(((bf16[4,2,128,256]{3,2,1,0:T(8,128)(2,1)}), bf16[4,2,128,256]{3,2,1,0:T(8,128)(2,1)S(1)}, u32[]{:S(2)}, u32[]{:S(2)}) %all-to-all-start.1) | async-done | bytes 524320 | tf_op jit(solution)/shard_map/all_to_all | solution.py:361
  70.0 0.8 copy-done.1
  70.8 3.2 %own_surfaces.1.part_ref = f32[2,256,1024]{2,1,0:T(8,128)} custom-call(s32[1]{0:T(128)} %bitcast.half_ref, bf16[4,2,128,256]{3,2,1,0:T(8,128)(2,1)} %copy-done.1, bf16[1024,1024]{1,0:T(8,128)(2,1)} %constant.53.clone.table_ref.refs_4_), custom_call_target="tpu_custom_call" | custom-call | flops 536870912 | bytes 2097152 | tf_op jit(solution)/shard_map/own_surfaces/pallas_call | solution.py:279
  74.0 0.9 %collective-permute-start.8 = (bf16[2,128,256]{2,1,0:T(8,128)(2,1)S(1)}, bf16[2,128,256]{2,1,0:T(8,128)(2,1)S(1)}, u32[]{:S(2)}, u32[]{:S(2)}) collective-permute-start(bf16[2,128,256]{2,1,0:T(8,128)(2,1)S(1)} %slice_bitcast_fusion.1), channel_id=1, source_target_pairs={{0,1},{1,0},{2,3},{3,2},{4,5},{5,4},{6,7},{7,6},{8,9},{9,8},{10,11... | collective-permute-start | bytes 393224 | tf_op jit(solution)/shard_map/ppermute | solution.py:364
  76.9 3.7 %surfaces.1 = f32[2,256,1024]{2,1,0:T(8,128)} custom-call(s32[1]{0:T(128)} %bitcast.half_ref, s32[1]{0:T(128)} %bitcast.1.me_ref, s32[1]{0:T(128)S(6)} %copy.12.counts_ref, f32[2,256,1024]{2,1,0:T(8,128)} %own_surfaces.1.part_ref, bf16[2,2,128,256]{3,2,1,0:T(8,128)(2,1)} %copy-done.2, bf16[2,128,256]{2,1,0:T(8,128)(2,1)} %copy-done.8, ...), custom_call_target="tpu_custom_call" | custom-call | flops 536870912 | bytes 4194304 | tf_op jit(solution)/shard_map/surfaces/pallas_call | solution.py:320
  (49 shorter events, 4.1 us)
Async XLA Ops:
  0.0 10.6 %copy-start.15 = (s32[1,2,2]{2,1,0:T(2,128)S(1)}, s32[1,2,2]{2,1,0:T(2,128)}, u32[]{:S(2)}) copy-start(s32[1,2,2]{2,1,0:T(2,128)} %param.11) | copy-start | bytes 52
  0.0 20.6 %copy-start.4 = (f32[32,1024]{1,0:T(8,128)S(1)}, f32[32,1024]{1,0:T(8,128)}, u32[]{:S(2)}) copy-start(f32[32,1024]{1,0:T(8,128)} %constant.59.clone) | copy-start | bytes 393220
  0.0 20.6 %copy-start.5 = (f32[32,1024]{1,0:T(8,128)S(1)}, f32[32,1024]{1,0:T(8,128)}, u32[]{:S(2)}) copy-start(f32[32,1024]{1,0:T(8,128)} %constant.57.clone) | copy-start | bytes 393220
  0.0 20.6 %copy-start.6 = (f32[32,1024]{1,0:T(8,128)S(1)}, f32[32,1024]{1,0:T(8,128)}, u32[]{:S(2)}) copy-start(f32[32,1024]{1,0:T(8,128)} %constant.58.clone) | copy-start | bytes 393220
  0.0 20.6 %copy-start.7 = (f32[32,1024]{1,0:T(8,128)S(1)}, f32[32,1024]{1,0:T(8,128)}, u32[]{:S(2)}) copy-start(f32[32,1024]{1,0:T(8,128)} %constant.56.clone) | copy-start | bytes 393220
  3.9 31.8 %collective-permute-start.1 = (bf16[2,128,256]{2,1,0:T(8,128)(2,1)}, bf16[2,128,256]{2,1,0:T(8,128)(2,1)S(1)}, u32[]{:S(2)}, u32[]{:S(2)}) collective-permute-start(bf16[2,128,256]{2,1,0:T(8,128)(2,1)} %get-tuple-element.19), channel_id=1, source_target_pairs={{0,8},{1,9},{2,10},{3,11},{4,12},{5,13},{6,14},{7,15},{8,0},{9,1},... | collective-permute-start | bytes 393224 | tf_op jit(solution)/shard_map/ppermute | solution.py:358
  6.2 29.5 %collective-permute-start.2 = (bf16[2,128,256]{2,1,0:T(8,128)(2,1)}, bf16[2,128,256]{2,1,0:T(8,128)(2,1)S(1)}, u32[]{:S(2)}, u32[]{:S(2)}) collective-permute-start(bf16[2,128,256]{2,1,0:T(8,128)(2,1)} %get-tuple-element.20), channel_id=1, source_target_pairs={{0,9},{1,8},{2,11},{3,10},{4,13},{5,12},{6,15},{7,14},{8,1},{9,0},... | collective-permute-start | bytes 393224 | tf_op jit(solution)/shard_map/ppermute | solution.py:358
  7.1 28.6 %collective-permute-start.3 = (bf16[2,128,256]{2,1,0:T(8,128)(2,1)}, bf16[2,128,256]{2,1,0:T(8,128)(2,1)S(1)}, u32[]{:S(2)}, u32[]{:S(2)}) collective-permute-start(bf16[2,128,256]{2,1,0:T(8,128)(2,1)} %get-tuple-element.21), channel_id=1, source_target_pairs={{0,10},{1,11},{2,8},{3,9},{4,14},{5,15},{6,12},{7,13},{8,2},{9,3},... | collective-permute-start | bytes 393224 | tf_op jit(solution)/shard_map/ppermute | solution.py:358
  10.4 25.4 %collective-permute-start.4 = (bf16[2,128,256]{2,1,0:T(8,128)(2,1)}, bf16[2,128,256]{2,1,0:T(8,128)(2,1)S(1)}, u32[]{:S(2)}, u32[]{:S(2)}) collective-permute-start(bf16[2,128,256]{2,1,0:T(8,128)(2,1)} %get-tuple-element.22), channel_id=1, source_target_pairs={{0,11},{1,10},{2,9},{3,8},{4,15},{5,14},{6,13},{7,12},{8,3},{9,2},... | collective-permute-start | bytes 393224 | tf_op jit(solution)/shard_map/ppermute | solution.py:358
  10.6 18.7 %collective-permute-start = (s32[1,2,2]{2,1,0:T(2,128)S(1)}, s32[1,2,2]{2,1,0:T(2,128)S(1)}, u32[]{:S(2)}, u32[]{:S(2)}) collective-permute-start(s32[1,2,2]{2,1,0:T(2,128)S(1)} %copy-done.15), channel_id=1, source_target_pairs={{0,8},{1,9},{2,10},{3,11},{4,12},{5,13},{6,14},{7,15},{8,0},{9,1},... | collective-permute-start | bytes 56 | tf_op jit(solution)/shard_map/ppermute | solution.py:358
  16.1 14.3 %all-to-all-start = ((bf16[4,2,128,256]{3,2,1,0:T(8,128)(2,1)}), bf16[4,2,128,256]{3,2,1,0:T(8,128)(2,1)S(1)}, u32[]{:S(2)}, u32[]{:S(2)}) async-start(bf16[4,2,128,256]{3,2,1,0:T(8,128)(2,1)} %row_transform.3), calls=%async_computation | async-start | bytes 1048576 | tf_op jit(solution)/shard_map/all_to_all | solution.py:361
  30.4 0.8 copy-start
  35.7 0.7 copy-start.12
  35.7 0.7 copy-start.13
  35.7 0.7 copy-start.14
  43.0 13.4 %copy-start.10 = (bf16[2,2,128,256]{3,2,1,0:T(8,128)(2,1)S(1)}, bf16[2,2,128,256]{3,2,1,0:T(8,128)(2,1)}, u32[]{:S(2)}) copy-start(bf16[2,2,128,256]{3,2,1,0:T(8,128)(2,1)} %get-tuple-element.27) | copy-start | bytes 786436
  43.0 15.6 %collective-permute-start.6 = (bf16[2,2,128,256]{3,2,1,0:T(8,128)(2,1)}, bf16[2,2,128,256]{3,2,1,0:T(8,128)(2,1)S(1)}, u32[]{:S(2)}, u32[]{:S(2)}) collective-permute-start(bf16[2,2,128,256]{3,2,1,0:T(8,128)(2,1)} %get-tuple-element.31), channel_id=1, source_target_pairs={{0,8},{1,9},{2,10},{3,11},{4,12},{5,13},{6,14},{7,15},{8,0},{9,1},... | collective-permute-start | bytes 786440 | tf_op jit(solution)/shard_map/ppermute | solution.py:358
  51.8 18.2 %all-to-all-start.1 = ((bf16[4,2,128,256]{3,2,1,0:T(8,128)(2,1)}), bf16[4,2,128,256]{3,2,1,0:T(8,128)(2,1)S(1)}, u32[]{:S(2)}, u32[]{:S(2)}) async-start(bf16[4,2,128,256]{3,2,1,0:T(8,128)(2,1)} %own_slots.1), calls=%async_computation.1 | async-start | bytes 1048576 | tf_op jit(solution)/shard_map/all_to_all | solution.py:361
  56.4 17.6 %collective-permute-start.5 = (bf16[2,2,128,256]{3,2,1,0:T(8,128)(2,1)S(1)}, bf16[2,2,128,256]{3,2,1,0:T(8,128)(2,1)S(1)}, u32[]{:S(2)}, u32[]{:S(2)}) collective-permute-start(bf16[2,2,128,256]{3,2,1,0:T(8,128)(2,1)S(1)} %copy-done.10), channel_id=1, source_target_pairs={{0,10},{1,11},{2,8},{3,9},{4,14},{5,15},{6,12},{7,13},{8,2},{9,3},... | collective-permute-start | bytes 786440 | tf_op jit(solution)/shard_map/ppermute | solution.py:358
  58.6 17.3 %copy-start.2 = (bf16[2,2,128,256]{3,2,1,0:T(8,128)(2,1)}, bf16[2,2,128,256]{3,2,1,0:T(8,128)(2,1)S(1)}, u32[]{:S(2)}) copy-start(bf16[2,2,128,256]{3,2,1,0:T(8,128)(2,1)S(1)} %collective-permute-done.6.refs_0_) | copy-start | bytes 786436
  58.6 17.0 %collective-permute-start.7 = (bf16[2,128,256]{2,1,0:T(8,128)(2,1)S(1)}, bf16[2,128,256]{2,1,0:T(8,128)(2,1)S(1)}, u32[]{:S(2)}, u32[]{:S(2)}) collective-permute-start(bf16[2,128,256]{2,1,0:T(8,128)(2,1)S(1)} %slice_bitcast_fusion), channel_id=1, source_target_pairs={{0,1},{1,0},{2,3},{3,2},{4,5},{5,4},{6,7},{7,6},{8,9},{9,8},{10,11... | collective-permute-start | bytes 393224 | tf_op jit(solution)/shard_map/ppermute | solution.py:364
  70.0 0.8 copy-start.1
  74.0 1.9 %copy-start.3 = (bf16[2,2,128,256]{3,2,1,0:T(8,128)(2,1)}, bf16[2,2,128,256]{3,2,1,0:T(8,128)(2,1)S(1)}, u32[]{:S(2)}) copy-start(bf16[2,2,128,256]{3,2,1,0:T(8,128)(2,1)S(1)} %collective-permute-done.5.refs_2_) | copy-start | bytes 786436
  74.0 1.9 %collective-permute-start.8 = (bf16[2,128,256]{2,1,0:T(8,128)(2,1)S(1)}, bf16[2,128,256]{2,1,0:T(8,128)(2,1)S(1)}, u32[]{:S(2)}, u32[]{:S(2)}) collective-permute-start(bf16[2,128,256]{2,1,0:T(8,128)(2,1)S(1)} %slice_bitcast_fusion.1), channel_id=1, source_target_pairs={{0,1},{1,0},{2,3},{3,2},{4,5},{5,4},{6,7},{7,6},{8,9},{9,8},{10,11... | collective-permute-start | bytes 393224 | tf_op jit(solution)/shard_map/ppermute | solution.py:364
  (3 other events, 2.0 us)

commit v4 on v3

--- a/solution.py
+++ b/solution.py
@@ -8,7 +8,7 @@
 from jax.experimental.pallas import tpu as pltpu
 
 FLOOR = 0.05
-VMEM_LIMIT = 56 * 1024 * 1024
+VMEM_LIMIT = 24 * 1024 * 1024
 
 
 def hann(length):

time: 80.9 us -> 77.3 us (0.956)
  the two profiles are of different devices: /device:TPU:13 before, /device:TPU:0 now
where the time goes in v4:
time: 77.3 us; the launch traced here: 76.9 us
  waiting for transfers between devices  22.8 us (29%)
  starting transfers between devices  21.6 us (28%)
  Pallas kernels  15.7 us (20%)
  local copies, waits for them, and re-layouts  11 us (14%)
  other arithmetic  5.07 us (7%)
  between operations  0.79 us (1%)
    ppermute x7, waiting for transfers between devices, across(): return lax.ppermute(value, axes, moves)  19.8 us
    ppermute x7, starting transfers between devices, across(): return lax.ppermute(value, axes, moves)  14.6 us
    unnamed x30, local copies, waits for them, and re-layouts  9.97 us
    all_to_all x2, starting transfers between devices, along(): return lax.all_to_all(blocks, 'rows', split_axis=0, concat_axis=0)  6.94 us
    pallas_call x2, Pallas kernels, row_transform(): pl.pallas_call(body, grid_spec=pltpu.PrefetchScalarGridSpec(num_scalar_pr...  4.28 us
    pallas_call x1, Pallas kernels, partner_slots(): pl.pallas_call(body, in_specs=[pl.BlockSpec(memory_space=pltpu.SMEM)] + [...  3.63 us
    pallas_call x1, Pallas kernels, own_slots(): pl.pallas_call(body, in_specs=[pl.BlockSpec(memory_space=pltpu.SMEM)] + [...  3.03 us
    another operation x1, other arithmetic  2.41 us
  transfers between devices with their start and end apart: 11, of which 5 were waited for; matrix products, arithmetic and copies ran while one was open for 8% of the time, Pallas kernels for 10%

profile of v4, /device:TPU:0, one launch (start us, length us, event | category | flops | bytes accessed | tf_op | source)
XLA Modules:
  0.0 76.9 jit_solution(13875000330097916792)
XLA Ops:
  0.0 1.6 %copy-done.2 = bf16[1024,1024]{1,0:T(8,128)(2,1)S(1)} copy-done((bf16[1024,1024]{1,0:T(8,128)(2,1)S(1)}, bf16[1024,1024]{1,0:T(8,128)(2,1)}, u32[]{:S(2)}) %copy-start.2) | copy-done | bytes 2097176
  1.6 1.6 %copy-done.4 = f32[2,256,1024]{2,1,0:T(8,128)S(1)} copy-done((f32[2,256,1024]{2,1,0:T(8,128)S(1)}, f32[2,256,1024]{2,1,0:T(8,128)}, u32[]{:S(2)}) %copy-start.4) | copy-done | bytes 2097176
  4.7 2.1 %row_transform.2 = (bf16[2,128,256]{2,1,0:T(8,128)(2,1)}, bf16[2,128,256]{2,1,0:T(8,128)(2,1)}, bf16[2,128,256]{2,1,0:T(8,128)(2,1)S(1)}, bf16[2,128,256]{2,1,0:T(8,128)(2,1)S(1)}) custom-call(s32[1]{0:T(128)} %bitcast.3.half_ref, s32[1]{0:T(128)} %bitcast.1.me_ref, f32[2,256,1024]{2,1,0:T(8,128)S(1)} %copy-done.4, f32[8,1024]{1,0:T(8,128)S(1)} %copy-done.6, ...), custom_call_target="tpu_custom_call" | custom-call | flops 536870912 | bytes 3145728 | tf_op jit(solution)/shard_map/row_transform/pallas_call | solution.py:86
  6.8 4.0 %collective-permute-start.1 = (bf16[2,128,256]{2,1,0:T(8,128)(2,1)}, bf16[2,128,256]{2,1,0:T(8,128)(2,1)S(1)}, u32[]{:S(2)}, u32[]{:S(2)}) collective-permute-start(bf16[2,128,256]{2,1,0:T(8,128)(2,1)} %get-tuple-element.19), channel_id=1, source_target_pairs={{0,8},{1,9},{2,10},{3,11},{4,12},{5,13},{6,14},{7,15},{8,0},{9,1},... | collective-permute-start | bytes 393224 | tf_op jit(solution)/shard_map/ppermute | solution.py:358
  10.8 3.0 %collective-permute-start.3 = (bf16[2,128,256]{2,1,0:T(8,128)(2,1)S(1)}, bf16[2,128,256]{2,1,0:T(8,128)(2,1)S(1)}, u32[]{:S(2)}, u32[]{:S(2)}) collective-permute-start(bf16[2,128,256]{2,1,0:T(8,128)(2,1)S(1)} %get-tuple-element.21), channel_id=1, source_target_pairs={{0,10},{1,11},{2,8},{3,9},{4,14},{5,15},{6,12},{7,13},{8,2},{9,3},... | collective-permute-start | bytes 393224 | tf_op jit(solution)/shard_map/ppermute | solution.py:358
  14.4 2.6 %collective-permute-start = (s32[1,2,2]{2,1,0:T(2,128)S(1)}, s32[1,2,2]{2,1,0:T(2,128)S(1)}, u32[]{:S(2)}, u32[]{:S(2)}) collective-permute-start(s32[1,2,2]{2,1,0:T(2,128)S(1)} %copy-done.14), channel_id=1, source_target_pairs={{0,8},{1,9},{2,10},{3,11},{4,12},{5,13},{6,14},{7,15},{8,0},{9,1},... | collective-permute-start | bytes 56 | tf_op jit(solution)/shard_map/ppermute | solution.py:358
  17.0 2.1 %row_transform.3 = bf16[4,2,128,256]{3,2,1,0:T(8,128)(2,1)} custom-call(s32[1]{0:T(128)} %bitcast.6.half_ref, s32[1]{0:T(128)} %bitcast.1.me_ref, f32[2,256,1024]{2,1,0:T(8,128)S(1)} %copy-done.5, f32[8,1024]{1,0:T(8,128)S(1)} %copy-done.7, f32[1,1024]{1,0:T(1,128)S(1)} %copy-done.8, bf16[1024,1024]{1,0:T(8,128)(2,1)S(1)} %copy-done.3), custom_call_target="tpu_custom_call" | custom-call | flops 536870912 | bytes 3145728 | tf_op jit(solution)/shard_map/row_transform/pallas_call | solution.py:86
  19.2 3.5 %all-to-all-start = ((bf16[4,2,128,256]{3,2,1,0:T(8,128)(2,1)}), bf16[4,2,128,256]{3,2,1,0:T(8,128)(2,1)S(1)}, u32[]{:S(2)}, u32[]{:S(2)}) async-start(bf16[4,2,128,256]{3,2,1,0:T(8,128)(2,1)} %row_transform.3), calls=%async_computation | async-start | bytes 1048576 | tf_op jit(solution)/shard_map/all_to_all | solution.py:361
  22.7 2.4 %subtract_convert_fusion = (bf16[32,32,1024]{2,1,0:T(8,128)(2,1)S(1)}, bf16[32,32,1024]{2,1,0:T(8,128)(2,1)S(1)}) fusion(f32[32,1024]{1,0:T(8,128)S(1)} %copy-done.13, f32[32,1024]{1,0:T(8,128)} %constant.57.clone, f32[32,1024]{1,0:T(8,128)} %constant.58.clone, f32[32,1024]{1,0:T(8,128)} %constant.56.clone), kind=kLoop, calls=%fused_computation.2 | loop fusion | flops 8388608 | bytes 4718592 | tf_op jit(solution)/shard_map/convert.4
  25.2 2.4 %pad_maximum_fusion.table_ref.refs_4_ = bf16[1024,2048]{1,0:T(8,128)(2,1)} fusion(bf16[1024,1024]{1,0:T(8,128)(2,1)S(1)} %bitcast.15, bf16[1024,1024]{1,0:T(8,128)(2,1)S(1)} %bitcast.14), kind=kLoop, calls=%fused_computation | loop fusion | flops 8388608 | bytes 8388608 | tf_op jit(solution)/shard_map/concatenate | solution.py:48
  27.6 6.7 %collective-permute-done = s32[1,2,2]{2,1,0:T(2,128)S(1)} collective-permute-done((s32[1,2,2]{2,1,0:T(2,128)S(1)}, s32[1,2,2]{2,1,0:T(2,128)S(1)}, u32[]{:S(2)}, u32[]{:S(2)}) %collective-permute-start) | collective-permute-done | bytes 48 | tf_op jit(solution)/shard_map/ppermute | solution.py:358
  34.8 2.3 %all-to-all-done.pieces_ref = bf16[4,2,128,256]{3,2,1,0:T(8,128)(2,1)S(1)} async-done(((bf16[4,2,128,256]{3,2,1,0:T(8,128)(2,1)}), bf16[4,2,128,256]{3,2,1,0:T(8,128)(2,1)S(1)}, u32[]{:S(2)}, u32[]{:S(2)}) %all-to-all-start) | async-done | bytes 524320 | tf_op jit(solution)/shard_map/all_to_all | solution.py:361
  37.1 2.2 %copy-done = bf16[1024,2048]{1,0:T(8,128)(2,1)S(1)} copy-done((bf16[1024,2048]{1,0:T(8,128)(2,1)S(1)}, bf16[1024,2048]{1,0:T(8,128)(2,1)}, u32[]{:S(2)}) %copy-start) | copy-done | bytes 4194328
  39.3 1.8 %own_spectra.1 = (bf16[2,2,64,1024]{3,2,1,0:T(8,128)(2,1)S(1)}, bf16[2,2,16,1024]{3,2,1,0:T(8,128)(2,1)S(1)}) custom-call(s32[3]{0:T(128)S(1)} %pad_add_fusion.1.s_ref, bf16[4,2,128,256]{3,2,1,0:T(8,128)(2,1)S(1)} %all-to-all-done.pieces_ref, bf16[1024,2048]{1,0:T(8,128)(2,1)S(1)} %copy-done), custom_call_target="tpu_custom_call" | custom-call | flops 1073741824 | bytes 8388608 | tf_op jit(solution)/shard_map/own_spectra/pallas_call | solution.py:197
  42.4 0.9 %copy-done.10 = bf16[2,128,256]{2,1,0:T(8,128)(2,1)S(1)} copy-done((bf16[2,128,256]{2,1,0:T(8,128)(2,1)S(1)}, bf16[2,128,256]{2,1,0:T(8,128)(2,1)}, u32[]{:S(2)}) %copy-start.10) | copy-done | bytes 131096
  43.3 0.9 %copy-done.12 = bf16[2,128,256]{2,1,0:T(8,128)(2,1)S(1)} copy-done((bf16[2,128,256]{2,1,0:T(8,128)(2,1)S(1)}, bf16[2,128,256]{2,1,0:T(8,128)(2,1)}, u32[]{:S(2)}) %copy-start.12) | copy-done | bytes 131096
  44.2 3.6 %partner_slots.1 = (bf16[2,2,128,256]{3,2,1,0:T(8,128)(2,1)}, bf16[2,2,128,256]{3,2,1,0:T(8,128)(2,1)S(1)}, bf16[4,2,64,1024]{3,2,1,0:T(8,128)(2,1)S(1)}, bf16[4,2,16,1024]{3,2,1,0:T(8,128)(2,1)S(1)}) custom-call(s32[11]{0:T(128)S(1)} %concatenate.8.s_ref, bf16[2,128,256]{2,1,0:T(8,128)(2,1)S(1)} %collective-permute-done.1.refs_0_, ...), custom_call_target="tpu_custom_call" | custom-call | flops 2147483648 | bytes 8388608 | tf_op jit(solution)/shard_map/partner_slots/pallas_call | solution.py:227
  47.9 3.0 %own_slots.1 = bf16[4,2,128,256]{3,2,1,0:T(8,128)(2,1)} custom-call(s32[11]{0:T(128)S(1)} %concatenate.8.s_ref, bf16[1024,2048]{1,0:T(8,128)(2,1)S(1)} %copy-done.1, bf16[4,2,64,1024]{3,2,1,0:T(8,128)(2,1)S(1)} %get-tuple-element.28.every, bf16[4,2,16,1024]{3,2,1,0:T(8,128)(2,1)S(1)} %get-tuple-element.29.edges), custom_call_target="tpu_custom_call" | custom-call | flops 1073741824 | bytes 8388608 | tf_op jit(solution)/shard_map/own_slots/pallas_call | solution.py:253
  50.9 3.5 %all-to-all-start.1 = ((bf16[4,2,128,256]{3,2,1,0:T(8,128)(2,1)}), bf16[4,2,128,256]{3,2,1,0:T(8,128)(2,1)S(1)}, u32[]{:S(2)}, u32[]{:S(2)}) async-start(bf16[4,2,128,256]{3,2,1,0:T(8,128)(2,1)} %own_slots.1), calls=%async_computation.1 | async-start | bytes 1048576 | tf_op jit(solution)/shard_map/all_to_all | solution.py:361
  54.4 4.3 %collective-permute-start.5 = (bf16[2,2,128,256]{3,2,1,0:T(8,128)(2,1)S(1)}, bf16[2,2,128,256]{3,2,1,0:T(8,128)(2,1)S(1)}, u32[]{:S(2)}, u32[]{:S(2)}) collective-permute-start(bf16[2,2,128,256]{3,2,1,0:T(8,128)(2,1)S(1)} %get-tuple-element.27), channel_id=1, source_target_pairs={{0,10},{1,11},{2,8},{3,9},{4,14},{5,15},{6,12},{7,13},{8,2},{9,3},... | collective-permute-start | bytes 786440 | tf_op jit(solution)/shard_map/ppermute | solution.py:358
  58.7 8.4 %collective-permute-done.6.refs_0_ = bf16[2,2,128,256]{3,2,1,0:T(8,128)(2,1)S(1)} collective-permute-done((bf16[2,2,128,256]{3,2,1,0:T(8,128)(2,1)}, bf16[2,2,128,256]{3,2,1,0:T(8,128)(2,1)S(1)}, u32[]{:S(2)}, u32[]{:S(2)}) %collective-permute-start.6) | collective-permute-done | bytes 262176 | tf_op jit(solution)/shard_map/ppermute | solution.py:358
  67.7 1.0 %own_surfaces.1.part_ref = f32[2,256,1024]{2,1,0:T(8,128)S(1)} custom-call(s32[1]{0:T(128)} %bitcast.half_ref, bf16[4,2,128,256]{3,2,1,0:T(8,128)(2,1)S(1)} %all-to-all-done.1.own_ref, bf16[1024,1024]{1,0:T(8,128)(2,1)S(1)} %copy-done.3), custom_call_target="tpu_custom_call" | custom-call | flops 536870912 | bytes 2097152 | tf_op jit(solution)/shard_map/own_surfaces/pallas_call | solution.py:279
  68.7 4.7 %collective-permute-done.5.refs_2_ = bf16[2,2,128,256]{3,2,1,0:T(8,128)(2,1)S(1)} collective-permute-done((bf16[2,2,128,256]{3,2,1,0:T(8,128)(2,1)S(1)}, bf16[2,2,128,256]{3,2,1,0:T(8,128)(2,1)S(1)}, u32[]{:S(2)}, u32[]{:S(2)}) %collective-permute-start.5) | collective-permute-done | bytes 262176 | tf_op jit(solution)/shard_map/ppermute | solution.py:358
  74.9 2.0 %surfaces.1 = f32[2,256,1024]{2,1,0:T(8,128)} custom-call(s32[1]{0:T(128)} %bitcast.half_ref, s32[1]{0:T(128)} %bitcast.1.me_ref, s32[1]{0:T(128)S(6)} %copy.12.counts_ref, f32[2,256,1024]{2,1,0:T(8,128)S(1)} %own_surfaces.1.part_ref, bf16[2,2,128,256]{3,2,1,0:T(8,128)(2,1)S(1)} %collective-permute-done.6.refs_0_, ...), custom_call_target="tpu_custom_call" | custom-call | flops 536870912 | bytes 4194304 | tf_op jit(solution)/shard_map/surfaces/pallas_call | solution.py:320
  (47 shorter events, 5.4 us)
Async XLA Ops:
  0.0 17.0 %copy-start.7 = (f32[8,1024]{1,0:T(8,128)S(1)}, f32[8,1024]{1,0:T(8,128)}, u32[]{:S(2)}) copy-start(f32[8,1024]{1,0:T(8,128)} %constant.54.clone.down_ref) | copy-start | bytes 98308
  0.0 14.4 %copy-start.14 = (s32[1,2,2]{2,1,0:T(2,128)S(1)}, s32[1,2,2]{2,1,0:T(2,128)}, u32[]{:S(2)}) copy-start(s32[1,2,2]{2,1,0:T(2,128)} %param.11) | copy-start | bytes 52
  0.0 1.6 %copy-start.2 = (bf16[1024,1024]{1,0:T(8,128)(2,1)S(1)}, bf16[1024,1024]{1,0:T(8,128)(2,1)}, u32[]{:S(2)}) copy-start(bf16[1024,1024]{1,0:T(8,128)(2,1)} %constant.53.clone.table_ref.refs_4_) | copy-start | bytes 6291460
  1.6 1.6 %copy-start.4 = (f32[2,256,1024]{2,1,0:T(8,128)S(1)}, f32[2,256,1024]{2,1,0:T(8,128)}, u32[]{:S(2)}) copy-start(f32[2,256,1024]{2,1,0:T(8,128)} %tile_ref.3) | copy-start | bytes 6291460
  3.2 0.8 copy-start.6
  4.0 0.7 copy-start.8
  4.7 12.4 %copy-start.3 = (bf16[1024,1024]{1,0:T(8,128)(2,1)S(1)}, bf16[1024,1024]{1,0:T(8,128)(2,1)}, u32[]{:S(2)}) copy-start(bf16[1024,1024]{1,0:T(8,128)(2,1)} %constant.53.clone.table_ref.refs_4_) | copy-start | bytes 6291460
  4.7 12.4 %copy-start.5 = (f32[2,256,1024]{2,1,0:T(8,128)S(1)}, f32[2,256,1024]{2,1,0:T(8,128)}, u32[]{:S(2)}) copy-start(f32[2,256,1024]{2,1,0:T(8,128)} %tile_ref.3) | copy-start | bytes 6291460
  4.7 18.1 %copy-start.13 = (f32[32,1024]{1,0:T(8,128)S(1)}, f32[32,1024]{1,0:T(8,128)}, u32[]{:S(2)}) copy-start(f32[32,1024]{1,0:T(8,128)} %constant.59.clone) | copy-start | bytes 393220
  6.8 34.3 %collective-permute-start.1 = (bf16[2,128,256]{2,1,0:T(8,128)(2,1)}, bf16[2,128,256]{2,1,0:T(8,128)(2,1)S(1)}, u32[]{:S(2)}, u32[]{:S(2)}) collective-permute-start(bf16[2,128,256]{2,1,0:T(8,128)(2,1)} %get-tuple-element.19), channel_id=1, source_target_pairs={{0,8},{1,9},{2,10},{3,11},{4,12},{5,13},{6,14},{7,15},{8,0},{9,1},... | collective-permute-start | bytes 393224 | tf_op jit(solution)/shard_map/ppermute | solution.py:358
  10.8 30.3 %collective-permute-start.2 = (bf16[2,128,256]{2,1,0:T(8,128)(2,1)}, bf16[2,128,256]{2,1,0:T(8,128)(2,1)S(1)}, u32[]{:S(2)}, u32[]{:S(2)}) collective-permute-start(bf16[2,128,256]{2,1,0:T(8,128)(2,1)} %get-tuple-element.20), channel_id=1, source_target_pairs={{0,9},{1,8},{2,11},{3,10},{4,13},{5,12},{6,15},{7,14},{8,1},{9,0},... | collective-permute-start | bytes 393224 | tf_op jit(solution)/shard_map/ppermute | solution.py:358
  10.8 30.3 %collective-permute-start.3 = (bf16[2,128,256]{2,1,0:T(8,128)(2,1)S(1)}, bf16[2,128,256]{2,1,0:T(8,128)(2,1)S(1)}, u32[]{:S(2)}, u32[]{:S(2)}) collective-permute-start(bf16[2,128,256]{2,1,0:T(8,128)(2,1)S(1)} %get-tuple-element.21), channel_id=1, source_target_pairs={{0,10},{1,11},{2,8},{3,9},{4,14},{5,15},{6,12},{7,13},{8,2},{9,3},... | collective-permute-start | bytes 393224 | tf_op jit(solution)/shard_map/ppermute | solution.py:358
  13.8 27.9 %collective-permute-start.4 = (bf16[2,128,256]{2,1,0:T(8,128)(2,1)S(1)}, bf16[2,128,256]{2,1,0:T(8,128)(2,1)S(1)}, u32[]{:S(2)}, u32[]{:S(2)}) collective-permute-start(bf16[2,128,256]{2,1,0:T(8,128)(2,1)S(1)} %get-tuple-element.22), channel_id=1, source_target_pairs={{0,11},{1,10},{2,9},{3,8},{4,15},{5,14},{6,13},{7,12},{8,3},{9,2},... | collective-permute-start | bytes 393224 | tf_op jit(solution)/shard_map/ppermute | solution.py:358
  14.4 19.9 %collective-permute-start = (s32[1,2,2]{2,1,0:T(2,128)S(1)}, s32[1,2,2]{2,1,0:T(2,128)S(1)}, u32[]{:S(2)}, u32[]{:S(2)}) collective-permute-start(s32[1,2,2]{2,1,0:T(2,128)S(1)} %copy-done.14), channel_id=1, source_target_pairs={{0,8},{1,9},{2,10},{3,11},{4,12},{5,13},{6,14},{7,15},{8,0},{9,1},... | collective-permute-start | bytes 56 | tf_op jit(solution)/shard_map/ppermute | solution.py:358
  19.2 17.9 %all-to-all-start = ((bf16[4,2,128,256]{3,2,1,0:T(8,128)(2,1)}), bf16[4,2,128,256]{3,2,1,0:T(8,128)(2,1)S(1)}, u32[]{:S(2)}, u32[]{:S(2)}) async-start(bf16[4,2,128,256]{3,2,1,0:T(8,128)(2,1)} %row_transform.3), calls=%async_computation | async-start | bytes 1048576 | tf_op jit(solution)/shard_map/all_to_all | solution.py:361
  37.1 2.2 %copy-start = (bf16[1024,2048]{1,0:T(8,128)(2,1)S(1)}, bf16[1024,2048]{1,0:T(8,128)(2,1)}, u32[]{:S(2)}) copy-start(bf16[1024,2048]{1,0:T(8,128)(2,1)} %pad_maximum_fusion.table_ref.refs_4_) | copy-start | bytes 12582916
  39.3 3.2 %copy-start.1 = (bf16[1024,2048]{1,0:T(8,128)(2,1)S(1)}, bf16[1024,2048]{1,0:T(8,128)(2,1)}, u32[]{:S(2)}) copy-start(bf16[1024,2048]{1,0:T(8,128)(2,1)} %pad_maximum_fusion.table_ref.refs_4_) | copy-start | bytes 12582916
  42.4 0.9 %copy-start.10 = (bf16[2,128,256]{2,1,0:T(8,128)(2,1)S(1)}, bf16[2,128,256]{2,1,0:T(8,128)(2,1)}, u32[]{:S(2)}) copy-start(bf16[2,128,256]{2,1,0:T(8,128)(2,1)} %copy-done.9) | copy-start | bytes 393220
  43.3 0.9 %copy-start.12 = (bf16[2,128,256]{2,1,0:T(8,128)(2,1)S(1)}, bf16[2,128,256]{2,1,0:T(8,128)(2,1)}, u32[]{:S(2)}) copy-start(bf16[2,128,256]{2,1,0:T(8,128)(2,1)} %copy-done.11) | copy-start | bytes 393220
  47.9 19.2 %collective-permute-start.6 = (bf16[2,2,128,256]{3,2,1,0:T(8,128)(2,1)}, bf16[2,2,128,256]{3,2,1,0:T(8,128)(2,1)S(1)}, u32[]{:S(2)}, u32[]{:S(2)}) collective-permute-start(bf16[2,2,128,256]{3,2,1,0:T(8,128)(2,1)} %get-tuple-element.31), channel_id=1, source_target_pairs={{0,8},{1,9},{2,10},{3,11},{4,12},{5,13},{6,14},{7,15},{8,0},{9,1},... | collective-permute-start | bytes 786440 | tf_op jit(solution)/shard_map/ppermute | solution.py:358
  50.9 16.8 %all-to-all-start.1 = ((bf16[4,2,128,256]{3,2,1,0:T(8,128)(2,1)}), bf16[4,2,128,256]{3,2,1,0:T(8,128)(2,1)S(1)}, u32[]{:S(2)}, u32[]{:S(2)}) async-start(bf16[4,2,128,256]{3,2,1,0:T(8,128)(2,1)} %own_slots.1), calls=%async_computation.1 | async-start | bytes 1048576 | tf_op jit(solution)/shard_map/all_to_all | solution.py:361
  54.4 19.1 %collective-permute-start.5 = (bf16[2,2,128,256]{3,2,1,0:T(8,128)(2,1)S(1)}, bf16[2,2,128,256]{3,2,1,0:T(8,128)(2,1)S(1)}, u32[]{:S(2)}, u32[]{:S(2)}) collective-permute-start(bf16[2,2,128,256]{3,2,1,0:T(8,128)(2,1)S(1)} %get-tuple-element.27), channel_id=1, source_target_pairs={{0,10},{1,11},{2,8},{3,9},{4,14},{5,15},{6,12},{7,13},{8,2},{9,3},... | collective-permute-start | bytes 786440 | tf_op jit(solution)/shard_map/ppermute | solution.py:358
  67.7 6.5 %collective-permute-start.7 = (bf16[2,128,256]{2,1,0:T(8,128)(2,1)}, bf16[2,128,256]{2,1,0:T(8,128)(2,1)S(1)}, u32[]{:S(2)}, u32[]{:S(2)}) collective-permute-start(bf16[2,128,256]{2,1,0:T(8,128)(2,1)} %slice_bitcast_fusion), channel_id=1, source_target_pairs={{0,1},{1,0},{2,3},{3,2},{4,5},{5,4},{6,7},{7,6},{8,9},{9,8},{10,11... | collective-permute-start | bytes 393224 | tf_op jit(solution)/shard_map/ppermute | solution.py:364
  73.5 1.4 %collective-permute-start.8 = (bf16[2,128,256]{2,1,0:T(8,128)(2,1)S(1)}, bf16[2,128,256]{2,1,0:T(8,128)(2,1)S(1)}, u32[]{:S(2)}, u32[]{:S(2)}) collective-permute-start(bf16[2,128,256]{2,1,0:T(8,128)(2,1)S(1)} %slice_bitcast_fusion.1), channel_id=1, source_target_pairs={{0,1},{1,0},{2,3},{3,2},{4,5},{5,4},{6,7},{7,6},{8,9},{9,8},{10,11... | collective-permute-start | bytes 393224 | tf_op jit(solution)/shard_map/ppermute | solution.py:364
  (2 other events, 1.3 us)

commit v5 on v4

--- a/solution.py
+++ b/solution.py
@@ -56,33 +56,88 @@
     return pltpu.CompilerParams(vmem_limit_bytes=VMEM_LIMIT)
 
 
-def row_transform(tiles, down, across, table, half, me, peers, apart):
+def shade(tile, down_ref, across_ref):
+    return (tile * (down_ref[...].T[:, :1] * across_ref[...])).astype(jnp.bfloat16)
+
+
+def times_table(table, shaded):
+    y = lax.dot_general(
+        table, shaded, (((1,), (1,)), ((), ())), preferred_element_type=jnp.float32
+    )
+    return y.astype(jnp.bfloat16)
+
+
+def sent_columns(tiles, down, across, table, half, me, peers):
     count, rows, width = tiles.shape
     span = table.shape[0] // 2
     block = span // peers
 
-    def body(half_ref, me_ref, tile_ref, down_ref, across_ref, table_ref, *refs):
-        outs, work = refs[:-1], refs[-1]
-        window = down_ref[...].T[:, :1] * across_ref[...]
-        shaded = (tile_ref[0] * window).astype(jnp.bfloat16)
-        y = lax.dot_general(
-            table_ref[...], shaded, (((1,), (1,)), ((), ())), preferred_element_type=jnp.float32
-        )
-        if not apart:
-            outs[0][:, 0] = y.astype(jnp.bfloat16).reshape(peers, block, rows)
-            return
-        work[...] = y.astype(jnp.bfloat16)
-        me = me_ref[0]
+    def body(half_ref, me_ref, tile_hbm, down_ref, across_ref, table_hbm, *refs):
+        outs = refs[:peers]
+        tile_ref, table_ref, work, done = refs[peers:]
+        t = pl.program_id(0)
+        start = pl.multiple_of((1 - half_ref[0]) * span, span)
+        fetch = pltpu.make_async_copy(
+            table_hbm.at[pl.ds(start, span)], table_ref, done.at[count]
+        )
+        loads = [
+            pltpu.make_async_copy(tile_hbm.at[i], tile_ref.at[i], done.at[i]) for i in range(count)
+        ]
+
+        @pl.when(t == 0)
+        def _():
+            loads[0].start()
+            fetch.start()
+            for load in loads[1:]:
+                load.start()
+            fetch.wait()
+
+        for i in range(count):
+
+            @pl.when(t == i)
+            def _():
+                loads[i].wait()
+                work[...] = times_table(table_ref[...], shade(tile_ref[i], down_ref, across_ref))
+
         for k in range(peers):
-            start = pl.multiple_of((me ^ k) * block, block)
-            outs[k][0] = work[pl.ds(start, block), :]
-
-    if apart:
-        out_specs = [pl.BlockSpec((1, block, rows), lambda t, half, me: (t, 0, 0))] * peers
-        out_shape = [jax.ShapeDtypeStruct((count, block, rows), jnp.bfloat16)] * peers
-    else:
-        out_specs = [pl.BlockSpec((peers, 1, block, rows), lambda t, half, me: (0, t, 0, 0))]
-        out_shape = [jax.ShapeDtypeStruct((peers, count, block, rows), jnp.bfloat16)]
+            place = pl.multiple_of((me_ref[0] ^ k) * block, block)
+            outs[k][0] = work[pl.ds(place, block), :]
+
+    return pl.pallas_call(
+        body,
+        grid_spec=pltpu.PrefetchScalarGridSpec(
+            num_scalar_prefetch=2,
+            grid=(count,),
+            in_specs=[
+                pl.BlockSpec(memory_space=pltpu.HBM),
+                pl.BlockSpec((8, rows), lambda t, half, me: (0, me[0])),
+                pl.BlockSpec((1, width), lambda t, half, me: (0, 0)),
+                pl.BlockSpec(memory_space=pltpu.HBM),
+            ],
+            out_specs=[pl.BlockSpec((1, block, rows), lambda t, half, me: (t, 0, 0))] * peers,
+            scratch_shapes=[
+                pltpu.VMEM((count, rows, width), tiles.dtype),
+                pltpu.VMEM((span, width), table.dtype),
+                pltpu.VMEM((span, rows), jnp.bfloat16),
+                pltpu.SemaphoreType.DMA((count + 1,)),
+            ],
+        ),
+        out_shape=[jax.ShapeDtypeStruct((count, block, rows), jnp.bfloat16)] * peers,
+        compiler_params=params(),
+        cost_estimate=cost(2 * count * rows * width * span, 4 * tiles.size + 2 * span * width),
+        name="sent_columns",
+    )(scalar(half), scalar(me), tiles, down, across, table)
+
+
+def kept_columns(tiles, down, across, table, half, me, peers):
+    count, rows, width = tiles.shape
+    span = table.shape[0] // 2
+    block = span // peers
+
+    def body(half_ref, me_ref, tile_ref, down_ref, across_ref, table_ref, out_ref):
+        y = times_table(table_ref[...], shade(tile_ref[0], down_ref, across_ref))
+        out_ref[:, 0] = y.reshape(peers, block, rows)
+
     return pl.pallas_call(
         body,
         grid_spec=pltpu.PrefetchScalarGridSpec(
@@ -94,13 +149,12 @@
                 pl.BlockSpec((1, width), lambda t, half, me: (0, 0)),
                 pl.BlockSpec((span, width), lambda t, half, me: (half[0], 0)),
             ],
-            out_specs=out_specs,
-            scratch_shapes=[pltpu.VMEM((span, rows), jnp.bfloat16)],
+            out_specs=pl.BlockSpec((peers, 1, block, rows), lambda t, half, me: (0, t, 0, 0)),
         ),
-        out_shape=out_shape,
+        out_shape=jax.ShapeDtypeStruct((peers, count, block, rows), jnp.bfloat16),
         compiler_params=params(),
         cost_estimate=cost(2 * count * rows * width * span, 4 * tiles.size + 2 * span * width),
-        name="row_transform",
+        name="kept_columns",
     )(scalar(half), scalar(me), tiles, down, across, table)
 
 
@@ -218,23 +272,36 @@
     def body(s_ref, *refs):
         inputs, table_ref, own_ref, own_edge = refs[:peers], *refs[peers : peers + 3]
         outs = [refs[peers + 3 + k // 2].at[k % 2] for k in range(peers)]
-        every, edges, phases = refs[-3:]
+        every, edges, phases, landed, done = refs[-5:]
+        loads = [
+            pltpu.make_async_copy(inputs[k], landed.at[k], done.at[k]) for k in range(peers)
+        ]
+        for load in loads:
+            load.start()
         every[:count] = own_ref[...]
         edges[:count] = own_edge[...]
+        for load in loads:
+            load.wait()
+        inputs = [landed.at[k] for k in range(peers)]
         store_spectra(s_ref, gather_rows(inputs, table_ref, s_ref[1]), every, edges, count)
         correlate(s_ref, s_ref[1], 3 + 2 * slots, every, edges, table_ref, phases, outs)
 
     return pl.pallas_call(
         body,
         in_specs=[pl.BlockSpec(memory_space=pltpu.SMEM)]
-        + [pl.BlockSpec(memory_space=pltpu.VMEM)] * (peers + 3),
+        + [pl.BlockSpec(memory_space=pltpu.HBM)] * peers
+        + [pl.BlockSpec(memory_space=pltpu.VMEM)] * 3,
         out_specs=[pl.BlockSpec(memory_space=pltpu.VMEM)] * (peers // 2 + 2),
         out_shape=[jax.ShapeDtypeStruct((2, slots, double, rows), jnp.bfloat16)] * (peers // 2)
         + [
             jax.ShapeDtypeStruct((2 * count, 2, block, height), jnp.bfloat16),
             jax.ShapeDtypeStruct((2 * count, 2, 16, height), jnp.bfloat16),
         ],
-        scratch_shapes=[pltpu.VMEM((2 * slots, block, height), jnp.bfloat16)],
+        scratch_shapes=[
+            pltpu.VMEM((2 * slots, block, height), jnp.bfloat16),
+            pltpu.VMEM((peers, count, double, rows), jnp.bfloat16),
+            pltpu.SemaphoreType.DMA((peers,)),
+        ],
         compiler_params=params(),
         cost_estimate=cost(4 * (count + slots) * double * height * height, 8 * height * height),
         name="partner_slots",
@@ -367,19 +434,21 @@
     down = jnp.asarray(np.tile(hann(height), (8, 1)))
     sideways = jnp.asarray(hann(width)[None, :])
 
-    sent = row_transform(tiles, down, sideways, table_w, 1 - half, me, peers, True)
+    sent = sent_columns(tiles, down, sideways, table_w, half, me, peers)
     arrived = [across(sent[k], k) for k in range(peers)]
-    *sent, held, pairs = lax.optimization_barrier((*sent, half, pairs))
-    (kept,) = row_transform(tiles, down, sideways, table_w, held, me, peers, False)
+    *sent, held = lax.optimization_barrier((*sent, half))
+    kept = kept_columns(tiles, down, sideways, table_w, held, me, peers)
+    kept, pairs = lax.optimization_barrier((kept, pairs))
     mine = along(kept)
 
     table_h = height_table(height)
     theirs = across(pairs, 0)
     packed = ((half == 0) & (me == 0)).astype(jnp.int32)
-    their_pairs = jnp.stack([theirs[0, :, 0] + count, (theirs[0, :, 1] + count) % (2 * count)], 1)
+    their_pairs = theirs[0]
     place = jnp.stack([half, me, packed])
     spectra, edge = own_spectra(place, mine, table_h)
-    scalars = jnp.concatenate([place, pairs.reshape(-1), their_pairs.reshape(-1)])
+    their_pairs, spectra = lax.optimization_barrier((their_pairs, spectra))
+    scalars = jnp.concatenate([place, pairs.reshape(-1), ((their_pairs + count) % (2 * count)).reshape(-1)])
     *back, spectra, edge = partner_slots(scalars, arrived, table_h, spectra, edge, slots)
     came = [across(back[j], 2 * j) for j in range(peers // 2)]
     own = along(own_slots(scalars, table_h, spectra, edge, peers, slots))

time: 77.3 us -> 71.1 us (0.920)
  waiting for transfers between devices: 22.8 us -> 18.3 us
  other arithmetic: 5.07 us -> 3.85 us
  local copies, waits for them, and re-layouts: 11 us -> 9.95 us
    ppermute x7, waiting for transfers between devices: 19.8 us -> 14.8 us  [across(): return lax.ppermute(value, axes, moves)]
    another operation x2 -> x1, other arithmetic: 2.42 us -> 1.37 us
    unnamed x30 -> x24, local copies, waits for them, and re-layouts: 9.97 us -> 9.02 us
  transfers between devices with their start and end apart: 11 -> 11, of which waited for: 5 -> 5; matrix products, arithmetic and copies ran while one was open for 8% -> 7% of each run, Pallas kernels for 10% -> 11%
where the time goes in v5:
time: 71.1 us; the launch traced here: 70.6 us
  starting transfers between devices  21.8 us (31%)
  waiting for transfers between devices  18.3 us (26%)
  Pallas kernels  16 us (23%)
  local copies, waits for them, and re-layouts  9.95 us (14%)
  other arithmetic  3.85 us (5%)
  between operations  0.81 us (1%)
    ppermute x7, waiting for transfers between devices, across(): return lax.ppermute(value, axes, moves)  14.8 us
    ppermute x7, starting transfers between devices, across(): return lax.ppermute(value, axes, moves)  14.8 us
    unnamed x24, local copies, waits for them, and re-layouts  9.02 us
    all_to_all x2, starting transfers between devices, along(): return lax.all_to_all(blocks, 'rows', split_axis=0, concat_axis=0)  6.94 us
    pallas_call x1, Pallas kernels, partner_slots(): pl.pallas_call(body, in_specs=[pl.BlockSpec(memory_space=pltpu.SMEM)] + [...  4.38 us
    pallas_call x1, Pallas kernels, own_slots(): pl.pallas_call(body, in_specs=[pl.BlockSpec(memory_space=pltpu.SMEM)] + [...  2.99 us
    all_to_all x2, waiting for transfers between devices, along(): return lax.all_to_all(blocks, 'rows', split_axis=0, concat_axis=0)  2.8 us
    concatenate x1, other arithmetic, height_table(): return jnp.concatenate([cosine, sine], axis=1).astype(jnp.bfloat16)  2.39 us
  transfers between devices with their start and end apart: 11, of which 5 were waited for; matrix products, arithmetic and copies ran while one was open for 7% of the time, Pallas kernels for 11%

profile of v5, /device:TPU:0, one launch (start us, length us, event | category | flops | bytes accessed | tf_op | source)
XLA Modules:
  0.0 70.6 jit_solution(6490825102192437586)
XLA Ops:
  0.0 1.6 %copy-done.2 = bf16[1024,1024]{1,0:T(8,128)(2,1)S(1)} copy-done((bf16[1024,1024]{1,0:T(8,128)(2,1)S(1)}, bf16[1024,1024]{1,0:T(8,128)(2,1)}, u32[]{:S(2)}) %copy-start.2) | copy-done | bytes 2097176
  1.6 1.6 %copy-done.4 = f32[2,256,1024]{2,1,0:T(8,128)S(1)} copy-done((f32[2,256,1024]{2,1,0:T(8,128)S(1)}, f32[2,256,1024]{2,1,0:T(8,128)}, u32[]{:S(2)}) %copy-start.4) | copy-done | bytes 2097176
  3.2 0.8 %copy-done.5 = f32[8,1024]{1,0:T(8,128)S(1)} copy-done((f32[8,1024]{1,0:T(8,128)S(1)}, f32[8,1024]{1,0:T(8,128)}, u32[]{:S(2)}) %copy-start.5) | copy-done | bytes 32792
  4.7 1.7 %sent_columns.1 = (bf16[2,128,256]{2,1,0:T(8,128)(2,1)S(1)}, bf16[2,128,256]{2,1,0:T(8,128)(2,1)S(1)}, bf16[2,128,256]{2,1,0:T(8,128)(2,1)S(1)}, bf16[2,128,256]{2,1,0:T(8,128)(2,1)S(1)}) custom-call(s32[1]{0:T(128)} %bitcast.half_ref, s32[1]{0:T(128)} %bitcast.1.me_ref, f32[2,256,1024]{2,1,0:T(8,128)S(1)} %copy-done.4, f32[8,1024]{1,0:T(8,128)S(1)} %copy-done.5, ...), custom_call_target="tpu_custom_call" | custom-call | flops 536870912 | bytes 3145728 | tf_op jit(solution)/shard_map/sent_columns/pallas_call | solution.py:106
  6.4 4.1 %collective-permute-start.1 = (bf16[2,128,256]{2,1,0:T(8,128)(2,1)S(1)}, bf16[2,128,256]{2,1,0:T(8,128)(2,1)S(1)}, u32[]{:S(2)}, u32[]{:S(2)}) collective-permute-start(bf16[2,128,256]{2,1,0:T(8,128)(2,1)S(1)} %get-tuple-element.22), channel_id=1, source_target_pairs={{0,8},{1,9},{2,10},{3,11},{4,12},{5,13},{6,14},{7,15},{8,0},{9,1},... | collective-permute-start | bytes 393224 | tf_op jit(solution)/shard_map/ppermute | solution.py:425
  10.5 3.0 %collective-permute-start.3 = (bf16[2,128,256]{2,1,0:T(8,128)(2,1)S(1)}, bf16[2,128,256]{2,1,0:T(8,128)(2,1)S(1)}, u32[]{:S(2)}, u32[]{:S(2)}) collective-permute-start(bf16[2,128,256]{2,1,0:T(8,128)(2,1)S(1)} %get-tuple-element.24), channel_id=1, source_target_pairs={{0,10},{1,11},{2,8},{3,9},{4,14},{5,15},{6,12},{7,13},{8,2},{9,3},... | collective-permute-start | bytes 393224 | tf_op jit(solution)/shard_map/ppermute | solution.py:425
  14.1 2.1 %kept_columns.1 = bf16[4,2,128,256]{3,2,1,0:T(8,128)(2,1)} custom-call(s32[1]{0:T(128)} %bitcast.3.half_ref, s32[1]{0:T(128)} %bitcast.1.me_ref, f32[2,256,1024]{2,1,0:T(8,128)S(1)} %copy-done.4, f32[8,1024]{1,0:T(8,128)S(1)} %copy-done.5, f32[1,1024]{1,0:T(1,128)S(1)} %copy-done.6, bf16[1024,1024]{1,0:T(8,128)(2,1)S(1)} %copy-done.2), custom_call_target="tpu_custom_call" | custom-call | flops 536870912 | bytes 3145728 | tf_op jit(solution)/shard_map/kept_columns/pallas_call | solution.py:141
  16.2 3.5 %all-to-all-start = ((bf16[4,2,128,256]{3,2,1,0:T(8,128)(2,1)}), bf16[4,2,128,256]{3,2,1,0:T(8,128)(2,1)S(1)}, u32[]{:S(2)}, u32[]{:S(2)}) async-start(bf16[4,2,128,256]{3,2,1,0:T(8,128)(2,1)} %kept_columns.1), calls=%async_computation | async-start | bytes 1048576 | tf_op jit(solution)/shard_map/all_to_all | solution.py:428
  19.7 2.7 %collective-permute-start = (s32[1,2,2]{2,1,0:T(2,128)S(1)}, s32[1,2,2]{2,1,0:T(2,128)S(1)}, u32[]{:S(2)}, u32[]{:S(2)}) collective-permute-start(s32[1,2,2]{2,1,0:T(2,128)S(1)} %copy-done.11), channel_id=1, source_target_pairs={{0,8},{1,9},{2,10},{3,11},{4,12},{5,13},{6,14},{7,15},{8,0},{9,1},... | collective-permute-start | bytes 56 | tf_op jit(solution)/shard_map/ppermute | solution.py:425
  22.5 1.4 %subtract_convert_fusion = (bf16[32,32,1024]{2,1,0:T(8,128)(2,1)S(1)}, bf16[32,32,1024]{2,1,0:T(8,128)(2,1)S(1)}) fusion(f32[32,1024]{1,0:T(8,128)S(1)} %copy-done.10, f32[32,1024]{1,0:T(8,128)S(1)} %copy-done.8, f32[32,1024]{1,0:T(8,128)S(1)} %copy-done.9, f32[32,1024]{1,0:T(8,128)S(1)} %copy-done.7), kind=kLoop, calls=%fused_computation.2 | loop fusion | flops 8388608 | bytes 4718592 | tf_op jit(solution)/shard_map/convert.4
  23.9 2.4 %pad_maximum_fusion.table_ref.refs_4_ = bf16[1024,2048]{1,0:T(8,128)(2,1)} fusion(bf16[1024,1024]{1,0:T(8,128)(2,1)S(1)} %bitcast.12, bf16[1024,1024]{1,0:T(8,128)(2,1)S(1)} %bitcast.11), kind=kLoop, calls=%fused_computation | loop fusion | flops 8388608 | bytes 8388608 | tf_op jit(solution)/shard_map/concatenate | solution.py:48
  26.3 2.8 %all-to-all-done.pieces_ref = bf16[4,2,128,256]{3,2,1,0:T(8,128)(2,1)S(1)} async-done(((bf16[4,2,128,256]{3,2,1,0:T(8,128)(2,1)}), bf16[4,2,128,256]{3,2,1,0:T(8,128)(2,1)S(1)}, u32[]{:S(2)}, u32[]{:S(2)}) %all-to-all-start) | async-done | bytes 524320 | tf_op jit(solution)/shard_map/all_to_all | solution.py:428
  29.1 2.2 %copy-done = bf16[1024,2048]{1,0:T(8,128)(2,1)S(1)} copy-done((bf16[1024,2048]{1,0:T(8,128)(2,1)S(1)}, bf16[1024,2048]{1,0:T(8,128)(2,1)}, u32[]{:S(2)}) %copy-start) | copy-done | bytes 4194328
  31.3 1.8 %own_spectra.1 = (bf16[2,2,64,1024]{3,2,1,0:T(8,128)(2,1)S(1)}, bf16[2,2,16,1024]{3,2,1,0:T(8,128)(2,1)S(1)}) custom-call(s32[3]{0:T(128)S(1)} %pad_add_fusion.s_ref, bf16[4,2,128,256]{3,2,1,0:T(8,128)(2,1)S(1)} %all-to-all-done.pieces_ref, bf16[1024,2048]{1,0:T(8,128)(2,1)S(1)} %copy-done), custom_call_target="tpu_custom_call" | custom-call | flops 1073741824 | bytes 8388608 | tf_op jit(solution)/shard_map/own_spectra/pallas_call | solution.py:251
  33.9 2.2 %copy-done.1 = bf16[1024,2048]{1,0:T(8,128)(2,1)S(1)} copy-done((bf16[1024,2048]{1,0:T(8,128)(2,1)S(1)}, bf16[1024,2048]{1,0:T(8,128)(2,1)}, u32[]{:S(2)}) %copy-start.1) | copy-done | bytes 4194328
  36.1 4.4 %partner_slots.1 = (bf16[2,2,128,256]{3,2,1,0:T(8,128)(2,1)}, bf16[2,2,128,256]{3,2,1,0:T(8,128)(2,1)S(1)}, bf16[4,2,64,1024]{3,2,1,0:T(8,128)(2,1)S(1)}, bf16[4,2,16,1024]{3,2,1,0:T(8,128)(2,1)S(1)}) custom-call(s32[11]{0:T(128)S(1)} %concatenate.9.s_ref, bf16[2,128,256]{2,1,0:T(8,128)(2,1)S(1)} %collective-permute-done.1.refs_0_, ...), custom_call_target="tpu_custom_call" | custom-call | flops 2147483648 | bytes 8388608 | tf_op jit(solution)/shard_map/partner_slots/pallas_call | solution.py:289
  40.5 2.1 %collective-permute-start.6 = (bf16[2,2,128,256]{3,2,1,0:T(8,128)(2,1)}, bf16[2,2,128,256]{3,2,1,0:T(8,128)(2,1)S(1)}, u32[]{:S(2)}, u32[]{:S(2)}) collective-permute-start(bf16[2,2,128,256]{3,2,1,0:T(8,128)(2,1)} %get-tuple-element.37), channel_id=1, source_target_pairs={{0,8},{1,9},{2,10},{3,11},{4,12},{5,13},{6,14},{7,15},{8,0},{9,1},... | collective-permute-start | bytes 786440 | tf_op jit(solution)/shard_map/ppermute | solution.py:425
  42.6 3.0 %own_slots.1 = bf16[4,2,128,256]{3,2,1,0:T(8,128)(2,1)} custom-call(s32[11]{0:T(128)S(1)} %concatenate.9.s_ref, bf16[1024,2048]{1,0:T(8,128)(2,1)S(1)} %copy-done.1, bf16[4,2,64,1024]{3,2,1,0:T(8,128)(2,1)S(1)} %get-tuple-element.34.every, bf16[4,2,16,1024]{3,2,1,0:T(8,128)(2,1)S(1)} %get-tuple-element.35.edges), custom_call_target="tpu_custom_call" | custom-call | flops 1073741824 | bytes 8388608 | tf_op jit(solution)/shard_map/own_slots/pallas_call | solution.py:320
  45.6 3.5 %all-to-all-start.1 = ((bf16[4,2,128,256]{3,2,1,0:T(8,128)(2,1)}), bf16[4,2,128,256]{3,2,1,0:T(8,128)(2,1)S(1)}, u32[]{:S(2)}, u32[]{:S(2)}) async-start(bf16[4,2,128,256]{3,2,1,0:T(8,128)(2,1)} %own_slots.1), calls=%async_computation.1 | async-start | bytes 1048576 | tf_op jit(solution)/shard_map/all_to_all | solution.py:428
  49.0 2.3 %collective-permute-start.5 = (bf16[2,2,128,256]{3,2,1,0:T(8,128)(2,1)S(1)}, bf16[2,2,128,256]{3,2,1,0:T(8,128)(2,1)S(1)}, u32[]{:S(2)}, u32[]{:S(2)}) collective-permute-start(bf16[2,2,128,256]{3,2,1,0:T(8,128)(2,1)S(1)} %get-tuple-element.33), channel_id=1, source_target_pairs={{0,10},{1,11},{2,8},{3,9},{4,14},{5,15},{6,12},{7,13},{8,2},{9,3},... | collective-permute-start | bytes 786440 | tf_op jit(solution)/shard_map/ppermute | solution.py:425
  51.4 10.6 %collective-permute-done.6.refs_0_ = bf16[2,2,128,256]{3,2,1,0:T(8,128)(2,1)S(1)} collective-permute-done((bf16[2,2,128,256]{3,2,1,0:T(8,128)(2,1)}, bf16[2,2,128,256]{3,2,1,0:T(8,128)(2,1)S(1)}, u32[]{:S(2)}, u32[]{:S(2)}) %collective-permute-start.6) | collective-permute-done | bytes 262176 | tf_op jit(solution)/shard_map/ppermute | solution.py:425
  62.7 1.0 %own_surfaces.1.part_ref = f32[2,256,1024]{2,1,0:T(8,128)S(1)} custom-call(s32[1]{0:T(128)} %bitcast.half_ref, bf16[4,2,128,256]{3,2,1,0:T(8,128)(2,1)S(1)} %all-to-all-done.1.own_ref, bf16[1024,1024]{1,0:T(8,128)(2,1)S(1)} %copy-done.3), custom_call_target="tpu_custom_call" | custom-call | flops 536870912 | bytes 2097152 | tf_op jit(solution)/shard_map/own_surfaces/pallas_call | solution.py:346
  63.7 3.6 %collective-permute-done.5.refs_2_ = bf16[2,2,128,256]{3,2,1,0:T(8,128)(2,1)S(1)} collective-permute-done((bf16[2,2,128,256]{3,2,1,0:T(8,128)(2,1)S(1)}, bf16[2,2,128,256]{3,2,1,0:T(8,128)(2,1)S(1)}, u32[]{:S(2)}, u32[]{:S(2)}) %collective-permute-start.5) | collective-permute-done | bytes 262176 | tf_op jit(solution)/shard_map/ppermute | solution.py:425
  68.7 2.0 %surfaces.1 = f32[2,256,1024]{2,1,0:T(8,128)} custom-call(s32[1]{0:T(128)} %bitcast.half_ref, s32[1]{0:T(128)} %bitcast.1.me_ref, s32[1]{0:T(128)S(6)} %copy.11.counts_ref, f32[2,256,1024]{2,1,0:T(8,128)S(1)} %own_surfaces.1.part_ref, bf16[2,2,128,256]{3,2,1,0:T(8,128)(2,1)S(1)} %collective-permute-done.6.refs_0_, ...), custom_call_target="tpu_custom_call" | custom-call | flops 536870912 | bytes 4194304 | tf_op jit(solution)/shard_map/surfaces/pallas_call | solution.py:387
  (38 shorter events, 3.7 us)
Async XLA Ops:
  0.0 1.6 %copy-start.2 = (bf16[1024,1024]{1,0:T(8,128)(2,1)S(1)}, bf16[1024,1024]{1,0:T(8,128)(2,1)}, u32[]{:S(2)}) copy-start(bf16[1024,1024]{1,0:T(8,128)(2,1)} %constant.52.clone.table_hbm.table_ref.refs_4_) | copy-start | bytes 6291460
  1.6 1.6 %copy-start.4 = (f32[2,256,1024]{2,1,0:T(8,128)S(1)}, f32[2,256,1024]{2,1,0:T(8,128)}, u32[]{:S(2)}) copy-start(f32[2,256,1024]{2,1,0:T(8,128)} %tile_ref.1) | copy-start | bytes 6291460
  3.2 0.8 %copy-start.5 = (f32[8,1024]{1,0:T(8,128)S(1)}, f32[8,1024]{1,0:T(8,128)}, u32[]{:S(2)}) copy-start(f32[8,1024]{1,0:T(8,128)} %constant.53.clone.down_ref) | copy-start | bytes 98308
  3.9 0.7 copy-start.6
  4.6 15.1 %copy-start.11 = (s32[1,2,2]{2,1,0:T(2,128)S(1)}, s32[1,2,2]{2,1,0:T(2,128)}, u32[]{:S(2)}) copy-start(s32[1,2,2]{2,1,0:T(2,128)} %param.11) | copy-start | bytes 52
  4.6 17.8 %copy-start.7 = (f32[32,1024]{1,0:T(8,128)S(1)}, f32[32,1024]{1,0:T(8,128)}, u32[]{:S(2)}) copy-start(f32[32,1024]{1,0:T(8,128)} %constant.55.clone) | copy-start | bytes 393220
  4.6 17.8 %copy-start.8 = (f32[32,1024]{1,0:T(8,128)S(1)}, f32[32,1024]{1,0:T(8,128)}, u32[]{:S(2)}) copy-start(f32[32,1024]{1,0:T(8,128)} %constant.56.clone) | copy-start | bytes 393220
  4.6 17.8 %copy-start.9 = (f32[32,1024]{1,0:T(8,128)S(1)}, f32[32,1024]{1,0:T(8,128)}, u32[]{:S(2)}) copy-start(f32[32,1024]{1,0:T(8,128)} %constant.57.clone) | copy-start | bytes 393220
  4.6 17.8 %copy-start.10 = (f32[32,1024]{1,0:T(8,128)S(1)}, f32[32,1024]{1,0:T(8,128)}, u32[]{:S(2)}) copy-start(f32[32,1024]{1,0:T(8,128)} %constant.58.clone) | copy-start | bytes 393220
  6.4 27.5 %collective-permute-start.1 = (bf16[2,128,256]{2,1,0:T(8,128)(2,1)S(1)}, bf16[2,128,256]{2,1,0:T(8,128)(2,1)S(1)}, u32[]{:S(2)}, u32[]{:S(2)}) collective-permute-start(bf16[2,128,256]{2,1,0:T(8,128)(2,1)S(1)} %get-tuple-element.22), channel_id=1, source_target_pairs={{0,8},{1,9},{2,10},{3,11},{4,12},{5,13},{6,14},{7,15},{8,0},{9,1},... | collective-permute-start | bytes 393224 | tf_op jit(solution)/shard_map/ppermute | solution.py:425
  10.5 23.4 %collective-permute-start.2 = (bf16[2,128,256]{2,1,0:T(8,128)(2,1)S(1)}, bf16[2,128,256]{2,1,0:T(8,128)(2,1)S(1)}, u32[]{:S(2)}, u32[]{:S(2)}) collective-permute-start(bf16[2,128,256]{2,1,0:T(8,128)(2,1)S(1)} %get-tuple-element.23), channel_id=1, source_target_pairs={{0,9},{1,8},{2,11},{3,10},{4,13},{5,12},{6,15},{7,14},{8,1},{9,0},... | collective-permute-start | bytes 393224 | tf_op jit(solution)/shard_map/ppermute | solution.py:425
  10.5 23.4 %collective-permute-start.3 = (bf16[2,128,256]{2,1,0:T(8,128)(2,1)S(1)}, bf16[2,128,256]{2,1,0:T(8,128)(2,1)S(1)}, u32[]{:S(2)}, u32[]{:S(2)}) collective-permute-start(bf16[2,128,256]{2,1,0:T(8,128)(2,1)S(1)} %get-tuple-element.24), channel_id=1, source_target_pairs={{0,10},{1,11},{2,8},{3,9},{4,14},{5,15},{6,12},{7,13},{8,2},{9,3},... | collective-permute-start | bytes 393224 | tf_op jit(solution)/shard_map/ppermute | solution.py:425
  13.5 20.4 %collective-permute-start.4 = (bf16[2,128,256]{2,1,0:T(8,128)(2,1)S(1)}, bf16[2,128,256]{2,1,0:T(8,128)(2,1)S(1)}, u32[]{:S(2)}, u32[]{:S(2)}) collective-permute-start(bf16[2,128,256]{2,1,0:T(8,128)(2,1)S(1)} %get-tuple-element.25), channel_id=1, source_target_pairs={{0,11},{1,10},{2,9},{3,8},{4,15},{5,14},{6,13},{7,12},{8,3},{9,2},... | collective-permute-start | bytes 393224 | tf_op jit(solution)/shard_map/ppermute | solution.py:425
  16.2 12.9 %all-to-all-start = ((bf16[4,2,128,256]{3,2,1,0:T(8,128)(2,1)}), bf16[4,2,128,256]{3,2,1,0:T(8,128)(2,1)S(1)}, u32[]{:S(2)}, u32[]{:S(2)}) async-start(bf16[4,2,128,256]{3,2,1,0:T(8,128)(2,1)} %kept_columns.1), calls=%async_computation | async-start | bytes 1048576 | tf_op jit(solution)/shard_map/all_to_all | solution.py:428
  19.7 14.0 %collective-permute-start = (s32[1,2,2]{2,1,0:T(2,128)S(1)}, s32[1,2,2]{2,1,0:T(2,128)S(1)}, u32[]{:S(2)}, u32[]{:S(2)}) collective-permute-start(s32[1,2,2]{2,1,0:T(2,128)S(1)} %copy-done.11), channel_id=1, source_target_pairs={{0,8},{1,9},{2,10},{3,11},{4,12},{5,13},{6,14},{7,15},{8,0},{9,1},... | collective-permute-start | bytes 56 | tf_op jit(solution)/shard_map/ppermute | solution.py:425
  29.1 2.2 %copy-start = (bf16[1024,2048]{1,0:T(8,128)(2,1)S(1)}, bf16[1024,2048]{1,0:T(8,128)(2,1)}, u32[]{:S(2)}) copy-start(bf16[1024,2048]{1,0:T(8,128)(2,1)} %pad_maximum_fusion.table_ref.refs_4_) | copy-start | bytes 12582916
  33.9 2.2 %copy-start.1 = (bf16[1024,2048]{1,0:T(8,128)(2,1)S(1)}, bf16[1024,2048]{1,0:T(8,128)(2,1)}, u32[]{:S(2)}) copy-start(bf16[1024,2048]{1,0:T(8,128)(2,1)} %pad_maximum_fusion.table_ref.refs_4_) | copy-start | bytes 12582916
  40.5 22.2 %copy-start.3 = (bf16[1024,1024]{1,0:T(8,128)(2,1)S(1)}, bf16[1024,1024]{1,0:T(8,128)(2,1)}, u32[]{:S(2)}) copy-start(bf16[1024,1024]{1,0:T(8,128)(2,1)} %constant.52.clone.table_hbm.table_ref.refs_4_) | copy-start | bytes 6291460
  40.5 21.5 %collective-permute-start.6 = (bf16[2,2,128,256]{3,2,1,0:T(8,128)(2,1)}, bf16[2,2,128,256]{3,2,1,0:T(8,128)(2,1)S(1)}, u32[]{:S(2)}, u32[]{:S(2)}) collective-permute-start(bf16[2,2,128,256]{3,2,1,0:T(8,128)(2,1)} %get-tuple-element.37), channel_id=1, source_target_pairs={{0,8},{1,9},{2,10},{3,11},{4,12},{5,13},{6,14},{7,15},{8,0},{9,1},... | collective-permute-start | bytes 786440 | tf_op jit(solution)/shard_map/ppermute | solution.py:425
  45.6 17.1 %all-to-all-start.1 = ((bf16[4,2,128,256]{3,2,1,0:T(8,128)(2,1)}), bf16[4,2,128,256]{3,2,1,0:T(8,128)(2,1)S(1)}, u32[]{:S(2)}, u32[]{:S(2)}) async-start(bf16[4,2,128,256]{3,2,1,0:T(8,128)(2,1)} %own_slots.1), calls=%async_computation.1 | async-start | bytes 1048576 | tf_op jit(solution)/shard_map/all_to_all | solution.py:428
  49.0 18.2 %collective-permute-start.5 = (bf16[2,2,128,256]{3,2,1,0:T(8,128)(2,1)S(1)}, bf16[2,2,128,256]{3,2,1,0:T(8,128)(2,1)S(1)}, u32[]{:S(2)}, u32[]{:S(2)}) collective-permute-start(bf16[2,2,128,256]{3,2,1,0:T(8,128)(2,1)S(1)} %get-tuple-element.33), channel_id=1, source_target_pairs={{0,10},{1,11},{2,8},{3,9},{4,14},{5,15},{6,12},{7,13},{8,2},{9,3},... | collective-permute-start | bytes 786440 | tf_op jit(solution)/shard_map/ppermute | solution.py:425
  62.7 5.3 %collective-permute-start.7 = (bf16[2,128,256]{2,1,0:T(8,128)(2,1)}, bf16[2,128,256]{2,1,0:T(8,128)(2,1)S(1)}, u32[]{:S(2)}, u32[]{:S(2)}) collective-permute-start(bf16[2,128,256]{2,1,0:T(8,128)(2,1)} %slice_bitcast_fusion), channel_id=1, source_target_pairs={{0,1},{1,0},{2,3},{3,2},{4,5},{5,4},{6,7},{7,6},{8,9},{9,8},{10,11... | collective-permute-start | bytes 393224 | tf_op jit(solution)/shard_map/ppermute | solution.py:431
  67.3 1.4 %collective-permute-start.8 = (bf16[2,128,256]{2,1,0:T(8,128)(2,1)S(1)}, bf16[2,128,256]{2,1,0:T(8,128)(2,1)S(1)}, u32[]{:S(2)}, u32[]{:S(2)}) collective-permute-start(bf16[2,128,256]{2,1,0:T(8,128)(2,1)S(1)} %slice_bitcast_fusion.1), channel_id=1, source_target_pairs={{0,1},{1,0},{2,3},{3,2},{4,5},{5,4},{6,7},{7,6},{8,9},{9,8},{10,11... | collective-permute-start | bytes 393224 | tf_op jit(solution)/shard_map/ppermute | solution.py:431

commit v6 on v5

--- a/solution.py
+++ b/solution.py
@@ -9,6 +9,7 @@
 
 FLOOR = 0.05
 VMEM_LIMIT = 24 * 1024 * 1024
+FIRST_LIMIT = 60 * 1024 * 1024
 
 
 def hann(length):
@@ -39,21 +40,33 @@
     rough = 2.0 * math.pi / height * (np.arange(coarse)[:, None] * fine * column % height)
     small = 2.0 * math.pi / height * (np.arange(fine)[:, None] * column % height)
     factor = 1.0 / math.sqrt(height)
-    rc = jnp.asarray(np.cos(rough) * factor, jnp.float32)[:, None, :]
-    rs = jnp.asarray(np.sin(rough) * factor, jnp.float32)[:, None, :]
-    sc = jnp.asarray(np.cos(small), jnp.float32)[None, :, :]
-    ss = jnp.asarray(np.sin(small), jnp.float32)[None, :, :]
-    cosine = (rc * sc - rs * ss).reshape(height, height)
-    sine = (rs * sc + rc * ss).reshape(height, height)
-    return jnp.concatenate([cosine, sine], axis=1).astype(jnp.bfloat16)
+    tables = [np.cos(rough) * factor, np.sin(rough) * factor, np.cos(small), np.sin(small)]
+
+    def body(rc_ref, rs_ref, sc_ref, ss_ref, out_ref):
+        sc, ss = sc_ref[...], ss_ref[...]
+        for a in range(coarse):
+            rc, rs = rc_ref[a : a + 1, :], rs_ref[a : a + 1, :]
+            here = slice(a * fine, (a + 1) * fine)
+            out_ref[here, :height] = (rc * sc - rs * ss).astype(jnp.bfloat16)
+            out_ref[here, height:] = (rs * sc + rc * ss).astype(jnp.bfloat16)
+
+    return pl.pallas_call(
+        body,
+        in_specs=[pl.BlockSpec(memory_space=pltpu.VMEM)] * 4,
+        out_specs=pl.BlockSpec(memory_space=pltpu.VMEM),
+        out_shape=jax.ShapeDtypeStruct((height, 2 * height), jnp.bfloat16),
+        compiler_params=params(),
+        cost_estimate=cost(1 << 33, 4 * height * height),
+        name="height_table",
+    )(*[jnp.asarray(table, jnp.float32) for table in tables])
 
 
 def cost(flops, moved):
     return pl.CostEstimate(flops=flops, transcendentals=0, bytes_accessed=moved)
 
 
-def params():
-    return pltpu.CompilerParams(vmem_limit_bytes=VMEM_LIMIT)
+def params(limit=VMEM_LIMIT):
+    return pltpu.CompilerParams(vmem_limit_bytes=limit)
 
 
 def shade(tile, down_ref, across_ref):
@@ -123,7 +136,7 @@
             ],
         ),
         out_shape=[jax.ShapeDtypeStruct((count, block, rows), jnp.bfloat16)] * peers,
-        compiler_params=params(),
+        compiler_params=params(FIRST_LIMIT),
         cost_estimate=cost(2 * count * rows * width * span, 4 * tiles.size + 2 * span * width),
         name="sent_columns",
     )(scalar(half), scalar(me), tiles, down, across, table)
@@ -172,11 +185,16 @@
     return total
 
 
+def holds_packed(place):
+    half_ref, me_ref = place
+    return (half_ref[0] == 0) & (me_ref[0] == 0)
+
+
 def store_spectra(s_ref, total, spectra, edge, first):
     block = spectra.shape[2]
     height = spectra.shape[3]
     row = lax.broadcasted_iota(jnp.int32, (block, height), 0)
-    packed = (row == 0) & (s_ref[2] == 1)
+    packed = (row == 0) & holds_packed(s_ref)
     for t in range(total.shape[0] // (2 * block)):
         real = total[2 * t * block : (2 * t + 1) * block]
         imag = total[(2 * t + 1) * block : (2 * t + 2) * block]
@@ -202,15 +220,14 @@
     )
 
 
-def correlate(s_ref, me, base, spectra, edge, table_ref, phases, outs):
+def correlate(s_ref, me, picks, spectra, edge, table_ref, phases, outs):
     block = spectra.shape[2]
     height = spectra.shape[3]
     slots, _, rows = outs[0].shape
     lead = lax.broadcasted_iota(jnp.int32, (16, height), 0)
-    packed = (lead == 0) & (s_ref[2] == 1)
+    packed = (lead == 0) & holds_packed(s_ref)
     for p in range(slots):
-        a = s_ref[base + 2 * p]
-        c = s_ref[base + 2 * p + 1]
+        a, c = picks[p]
         q_real, q_imag = normalised(spectra[a, 0], spectra[a, 1], spectra[c, 0], spectra[c, 1])
         e_real, e_imag = normalised(edge[a, 0], edge[a, 1], edge[c, 0], edge[c, 1])
         phases[2 * p] = q_real
@@ -222,7 +239,7 @@
         phases[2 * p, :16] = mixed_real.astype(jnp.bfloat16)
         phases[2 * p + 1, :16] = mixed_imag.astype(jnp.bfloat16)
     row = lax.broadcasted_iota(jnp.int32, (block, rows), 0)
-    twice = jnp.where((row == 0) & (s_ref[2] == 1), 1.0, 2.0)
+    twice = jnp.where((row == 0) & holds_packed(s_ref), 1.0, 2.0)
     flat = phases[...].reshape(2 * slots * block, height)
     for k in range(len(outs)):
         start = pl.multiple_of((me ^ k) * rows, rows)
@@ -240,17 +257,17 @@
             outs[k][p, block:] = ((s_part[re] + c_part[im]) * twice).astype(jnp.bfloat16)
 
 
-def own_spectra(scalars, pieces, table):
+def own_spectra(place, pieces, table):
     peers, count, double, rows = pieces.shape
     height = table.shape[0]
 
-    def body(s_ref, pieces_ref, table_ref, spectra, edge):
+    def body(half_ref, me_ref, pieces_ref, table_ref, spectra, edge):
         inputs = [pieces_ref.at[k] for k in range(peers)]
-        store_spectra(s_ref, gather_rows(inputs, table_ref, 0), spectra, edge, 0)
-
-    return pl.pallas_call(
-        body,
-        in_specs=[pl.BlockSpec(memory_space=pltpu.SMEM)]
+        store_spectra((half_ref, me_ref), gather_rows(inputs, table_ref, 0), spectra, edge, 0)
+
+    return pl.pallas_call(
+        body,
+        in_specs=[pl.BlockSpec(memory_space=pltpu.SMEM)] * 2
         + [pl.BlockSpec(memory_space=pltpu.VMEM)] * 2,
         out_specs=[pl.BlockSpec(memory_space=pltpu.VMEM)] * 2,
         out_shape=[
@@ -260,66 +277,61 @@
         compiler_params=params(),
         cost_estimate=cost(4 * count * double * height * height, 8 * height * height),
         name="own_spectra",
-    )(scalars, pieces, table)
-
-
-def partner_slots(scalars, pieces, table, spectra, edge, slots):
+    )(*place, pieces, table)
+
+
+def partner_slots(place, theirs, pieces, table, spectra, edge):
     peers = len(pieces)
     count, double, rows = pieces[0].shape
     height = table.shape[0]
     block = double // 2
-
-    def body(s_ref, *refs):
+    slots = theirs.shape[1]
+
+    def body(half_ref, me_ref, theirs_ref, *refs):
+        s_ref = (half_ref, me_ref)
+        me = me_ref[0]
+        picks = [
+            [(theirs_ref[0, p, i] + count) % (2 * count) for i in range(2)] for p in range(slots)
+        ]
         inputs, table_ref, own_ref, own_edge = refs[:peers], *refs[peers : peers + 3]
         outs = [refs[peers + 3 + k // 2].at[k % 2] for k in range(peers)]
-        every, edges, phases, landed, done = refs[-5:]
-        loads = [
-            pltpu.make_async_copy(inputs[k], landed.at[k], done.at[k]) for k in range(peers)
-        ]
-        for load in loads:
-            load.start()
+        every, edges, phases = refs[-3:]
         every[:count] = own_ref[...]
         edges[:count] = own_edge[...]
-        for load in loads:
-            load.wait()
-        inputs = [landed.at[k] for k in range(peers)]
-        store_spectra(s_ref, gather_rows(inputs, table_ref, s_ref[1]), every, edges, count)
-        correlate(s_ref, s_ref[1], 3 + 2 * slots, every, edges, table_ref, phases, outs)
-
-    return pl.pallas_call(
-        body,
-        in_specs=[pl.BlockSpec(memory_space=pltpu.SMEM)]
-        + [pl.BlockSpec(memory_space=pltpu.HBM)] * peers
-        + [pl.BlockSpec(memory_space=pltpu.VMEM)] * 3,
+        store_spectra(s_ref, gather_rows(inputs, table_ref, me), every, edges, count)
+        correlate(s_ref, me, picks, every, edges, table_ref, phases, outs)
+
+    return pl.pallas_call(
+        body,
+        in_specs=[pl.BlockSpec(memory_space=pltpu.SMEM)] * 3
+        + [pl.BlockSpec(memory_space=pltpu.VMEM)] * (peers + 3),
         out_specs=[pl.BlockSpec(memory_space=pltpu.VMEM)] * (peers // 2 + 2),
         out_shape=[jax.ShapeDtypeStruct((2, slots, double, rows), jnp.bfloat16)] * (peers // 2)
         + [
             jax.ShapeDtypeStruct((2 * count, 2, block, height), jnp.bfloat16),
             jax.ShapeDtypeStruct((2 * count, 2, 16, height), jnp.bfloat16),
         ],
-        scratch_shapes=[
-            pltpu.VMEM((2 * slots, block, height), jnp.bfloat16),
-            pltpu.VMEM((peers, count, double, rows), jnp.bfloat16),
-            pltpu.SemaphoreType.DMA((peers,)),
-        ],
+        scratch_shapes=[pltpu.VMEM((2 * slots, block, height), jnp.bfloat16)],
         compiler_params=params(),
         cost_estimate=cost(4 * (count + slots) * double * height * height, 8 * height * height),
         name="partner_slots",
-    )(scalars, *pieces, table, spectra, edge)
-
-
-def own_slots(scalars, table, spectra, edge, peers, slots):
+    )(*place, theirs, *pieces, table, spectra, edge)
+
+
+def own_slots(place, pairs, table, spectra, edge, peers):
     block, height = spectra.shape[2:]
     rows = height // peers
-
-    def body(s_ref, table_ref, every, edges, *refs):
+    slots = pairs.shape[1]
+
+    def body(half_ref, me_ref, pairs_ref, table_ref, every, edges, *refs):
+        picks = [[pairs_ref[0, p, i] for i in range(2)] for p in range(slots)]
         out_ref, phases = refs
         outs = [out_ref.at[k] for k in range(peers)]
-        correlate(s_ref, 0, 3, every, edges, table_ref, phases, outs)
-
-    return pl.pallas_call(
-        body,
-        in_specs=[pl.BlockSpec(memory_space=pltpu.SMEM)]
+        correlate((half_ref, me_ref), 0, picks, every, edges, table_ref, phases, outs)
+
+    return pl.pallas_call(
+        body,
+        in_specs=[pl.BlockSpec(memory_space=pltpu.SMEM)] * 3
         + [pl.BlockSpec(memory_space=pltpu.VMEM)] * 3,
         out_specs=pl.BlockSpec(memory_space=pltpu.VMEM),
         out_shape=jax.ShapeDtypeStruct((peers, slots, 2 * block, rows), jnp.bfloat16),
@@ -327,7 +339,7 @@
         compiler_params=params(),
         cost_estimate=cost(8 * slots * block * height * height, 8 * height * height),
         name="own_slots",
-    )(scalars, table, spectra, edge)
+    )(*place, pairs, table, spectra, edge)
 
 
 def own_surfaces(half, own, table):
@@ -410,7 +422,6 @@
     group = lax.axis_index("blk")
     me = lax.axis_index("rows")
     count, rows, width = tiles.shape
-    slots = pairs.shape[1]
     height = rows * peers
     turn = groups // 2
     half = group // turn
@@ -443,15 +454,11 @@
 
     table_h = height_table(height)
     theirs = across(pairs, 0)
-    packed = ((half == 0) & (me == 0)).astype(jnp.int32)
-    their_pairs = theirs[0]
-    place = jnp.stack([half, me, packed])
+    place = (scalar(half), scalar(me))
     spectra, edge = own_spectra(place, mine, table_h)
-    their_pairs, spectra = lax.optimization_barrier((their_pairs, spectra))
-    scalars = jnp.concatenate([place, pairs.reshape(-1), ((their_pairs + count) % (2 * count)).reshape(-1)])
-    *back, spectra, edge = partner_slots(scalars, arrived, table_h, spectra, edge, slots)
+    *back, spectra, edge = partner_slots(place, theirs, arrived, table_h, spectra, edge)
     came = [across(back[j], 2 * j) for j in range(peers // 2)]
-    own = along(own_slots(scalars, table_h, spectra, edge, peers, slots))
+    own = along(own_slots(place, pairs, table_h, spectra, edge, peers))
     part = own_surfaces(half, own, table_w)
     came[-1], part = lax.optimization_barrier((came[-1], part))
     swapped = [swap(value[1]) for value in came]

time: 71.1 us -> 71 us (level)
  other arithmetic: 3.85 us -> 0 us
  waiting for transfers between devices: 18.3 us -> 21.8 us
  Pallas kernels: 16 us -> 18.8 us
  local copies, waits for them, and re-layouts: 9.95 us -> 7.3 us
    all_to_all x2, waiting for transfers between devices: 2.8 us -> 7.78 us  [along(): return lax.all_to_all(blocks, 'rows', split_axis=0, concat_axis=0)]
    pallas_call x1, Pallas kernels: 1.72 us -> 4.62 us  [sent_columns(): pl.pallas_call(body, grid_spec=pltpu.PrefetchScalarGridSpec(num_scalar_pr...]
    unnamed x24 -> x22, local copies, waits for them, and re-layouts: 9.02 us -> 6.63 us
    concatenate x1 -> x0, other arithmetic: 2.39 us -> none  [height_table(): return jnp.concatenate([cosine, sine], axis=1).astype(jnp.bfloat16)]
    another operation x2 -> x0, other arithmetic: 1.45 us -> none
    ppermute x7, waiting for transfers between devices: 14.8 us -> 13.4 us  [across(): return lax.ppermute(value, axes, moves)]
    pallas_call x3 -> x4, Pallas kernels: 9.17 us -> 9.05 us  [the longest x1 3.66 us: partner_slots(): pl.pallas_call(body, in_specs=[pl.BlockSpec(memory_space=pltpu.SMEM)] * 3...]
  transfers between devices with their start and end apart: 11 -> 11, of which waited for: 5 -> 4; matrix products, arithmetic and copies ran while one was open for 7% -> 1% of each run, Pallas kernels for 11% -> 12%
where the time goes in v6:
time: 71 us; the launch traced here: 70.6 us
  starting transfers between devices  21.9 us (31%)
  waiting for transfers between devices  21.8 us (31%)
  Pallas kernels  18.8 us (26%)
  local copies, waits for them, and re-layouts  7.3 us (10%)
  between operations  0.8 us (1%)
    ppermute x7, starting transfers between devices, across(): return lax.ppermute(value, axes, moves)  14.9 us
    ppermute x7, waiting for transfers between devices, across(): return lax.ppermute(value, axes, moves)  13.4 us
    all_to_all x2, waiting for transfers between devices, along(): return lax.all_to_all(blocks, 'rows', split_axis=0, concat_axis=0)  7.78 us
    all_to_all x2, starting transfers between devices, along(): return lax.all_to_all(blocks, 'rows', split_axis=0, concat_axis=0)  6.94 us
    unnamed x22, local copies, waits for them, and re-layouts  6.63 us
    pallas_call x1, Pallas kernels, sent_columns(): pl.pallas_call(body, grid_spec=pltpu.PrefetchScalarGridSpec(num_scalar_pr...  4.62 us
    pallas_call x1, Pallas kernels, partner_slots(): pl.pallas_call(body, in_specs=[pl.BlockSpec(memory_space=pltpu.SMEM)] * 3...  3.66 us
    pallas_call x1, Pallas kernels, own_slots(): pl.pallas_call(body, in_specs=[pl.BlockSpec(memory_space=pltpu.SMEM)] * 3...  3.01 us
  transfers between devices with their start and end apart: 11, of which 4 were waited for; matrix products, arithmetic and copies ran while one was open for 1% of the time, Pallas kernels for 12%

profile of v6, /device:TPU:0, one launch (start us, length us, event | category | flops | bytes accessed | tf_op | source)
XLA Modules:
  0.0 70.6 jit_solution(8132155969951366902)
XLA Ops:
  0.0 4.6 %sent_columns.1 = (bf16[2,128,256]{2,1,0:T(8,128)(2,1)}, bf16[2,128,256]{2,1,0:T(8,128)(2,1)}, bf16[2,128,256]{2,1,0:T(8,128)(2,1)}, bf16[2,128,256]{2,1,0:T(8,128)(2,1)}) custom-call(s32[1]{0:T(128)} %bitcast.half_ref, s32[1]{0:T(128)} %bitcast.1.me_ref, f32[2,256,1024]{2,1,0:T(8,128)} %tile_ref.1, f32[8,1024]{1,0:T(8,128)} %constant.36.clone.down_ref, ...), custom_call_target="tpu_custom_call" | custom-call | flops 536870912 | bytes 3145728 | tf_op jit(solution)/shard_map/sent_columns/pallas_call | solution.py:119
  4.6 4.3 %collective-permute-start.1 = (bf16[2,128,256]{2,1,0:T(8,128)(2,1)}, bf16[2,128,256]{2,1,0:T(8,128)(2,1)S(1)}, u32[]{:S(2)}, u32[]{:S(2)}) collective-permute-start(bf16[2,128,256]{2,1,0:T(8,128)(2,1)} %get-tuple-element.20), channel_id=1, source_target_pairs={{0,8},{1,9},{2,10},{3,11},{4,12},{5,13},{6,14},{7,15},{8,0},{9,1},... | collective-permute-start | bytes 393224 | tf_op jit(solution)/shard_map/ppermute | solution.py:436
  8.9 3.0 %collective-permute-start.3 = (bf16[2,128,256]{2,1,0:T(8,128)(2,1)}, bf16[2,128,256]{2,1,0:T(8,128)(2,1)S(1)}, u32[]{:S(2)}, u32[]{:S(2)}) collective-permute-start(bf16[2,128,256]{2,1,0:T(8,128)(2,1)} %get-tuple-element.22), channel_id=1, source_target_pairs={{0,10},{1,11},{2,8},{3,9},{4,14},{5,15},{6,12},{7,13},{8,2},{9,3},... | collective-permute-start | bytes 393224 | tf_op jit(solution)/shard_map/ppermute | solution.py:436
  11.9 0.6 collective-permute-start.4
  12.6 1.6 %copy-done.3 = f32[2,256,1024]{2,1,0:T(8,128)S(1)} copy-done((f32[2,256,1024]{2,1,0:T(8,128)S(1)}, f32[2,256,1024]{2,1,0:T(8,128)}, u32[]{:S(2)}) %copy-start.3) | copy-done | bytes 2097176
  14.2 2.2 %kept_columns.1 = bf16[4,2,128,256]{3,2,1,0:T(8,128)(2,1)} custom-call(s32[1]{0:T(128)} %bitcast.2.half_ref, s32[1]{0:T(128)} %bitcast.1.me_ref, f32[2,256,1024]{2,1,0:T(8,128)S(1)} %copy-done.3, f32[8,1024]{1,0:T(8,128)S(1)} %copy-done.4, f32[1,1024]{1,0:T(1,128)S(1)} %copy-done.5, bf16[1024,1024]{1,0:T(8,128)(2,1)S(1)} %copy-done), custom_call_target="tpu_custom_call" | custom-call | flops 536870912 | bytes 3145728 | tf_op jit(solution)/shard_map/kept_columns/pallas_call | solution.py:154
  16.3 3.5 %all-to-all-start = ((bf16[4,2,128,256]{3,2,1,0:T(8,128)(2,1)}), bf16[4,2,128,256]{3,2,1,0:T(8,128)(2,1)S(1)}, u32[]{:S(2)}, u32[]{:S(2)}) async-start(bf16[4,2,128,256]{3,2,1,0:T(8,128)(2,1)} %kept_columns.1), calls=%async_computation | async-start | bytes 1048576 | tf_op jit(solution)/shard_map/all_to_all | solution.py:439
  19.8 2.6 %collective-permute-start = (s32[1,2,2]{2,1,0:T(2,128)S(1)}, s32[1,2,2]{2,1,0:T(2,128)S(1)}, u32[]{:S(2)}, u32[]{:S(2)}) collective-permute-start(s32[1,2,2]{2,1,0:T(2,128)S(1)} %copy-done.6), channel_id=1, source_target_pairs={{0,8},{1,9},{2,10},{3,11},{4,12},{5,13},{6,14},{7,15},{8,0},{9,1},... | collective-permute-start | bytes 56 | tf_op jit(solution)/shard_map/ppermute | solution.py:436
  22.5 0.9 %copy-done.10 = f32[32,1024]{1,0:T(8,128)S(1)} copy-done((f32[32,1024]{1,0:T(8,128)S(1)}, f32[32,1024]{1,0:T(8,128)}, u32[]{:S(2)}) %copy-start.10) | copy-done | bytes 131096
  23.4 1.1 %height_table.1.table_ref.refs_4_ = bf16[1024,2048]{1,0:T(8,128)(2,1)S(1)} custom-call(f32[32,1024]{1,0:T(8,128)S(1)} %copy-done.7, f32[32,1024]{1,0:T(8,128)S(1)} %copy-done.8, f32[32,1024]{1,0:T(8,128)S(1)} %copy-done.9, f32[32,1024]{1,0:T(8,128)S(1)} %copy-done.10), custom_call_target="tpu_custom_call" | custom-call | flops 8589934592 | bytes 4194304 | tf_op jit(solution)/shard_map/height_table/pallas_call | solution.py:53
  24.5 1.9 %copy-done.1 = bf16[1024,2048]{1,0:T(8,128)(2,1)} copy-done((bf16[1024,2048]{1,0:T(8,128)(2,1)}, bf16[1024,2048]{1,0:T(8,128)(2,1)S(1)}, u32[]{:S(2)}) %copy-start.1) | copy-done | bytes 4194328
  26.4 7.8 %all-to-all-done.pieces_ref = bf16[4,2,128,256]{3,2,1,0:T(8,128)(2,1)S(1)} async-done(((bf16[4,2,128,256]{3,2,1,0:T(8,128)(2,1)}), bf16[4,2,128,256]{3,2,1,0:T(8,128)(2,1)S(1)}, u32[]{:S(2)}, u32[]{:S(2)}) %all-to-all-start) | async-done | bytes 524320 | tf_op jit(solution)/shard_map/all_to_all | solution.py:439
  34.2 2.2 %copy-done.2 = bf16[1024,2048]{1,0:T(8,128)(2,1)S(1)} copy-done((bf16[1024,2048]{1,0:T(8,128)(2,1)S(1)}, bf16[1024,2048]{1,0:T(8,128)(2,1)}, u32[]{:S(2)}) %copy-start.2) | copy-done | bytes 4194328
  36.4 1.2 %own_spectra.1 = (bf16[2,2,64,1024]{3,2,1,0:T(8,128)(2,1)S(1)}, bf16[2,2,16,1024]{3,2,1,0:T(8,128)(2,1)S(1)}) custom-call(s32[1]{0:T(128)} %bitcast.half_ref, s32[1]{0:T(128)} %bitcast.1.me_ref, bf16[4,2,128,256]{3,2,1,0:T(8,128)(2,1)S(1)} %all-to-all-done.pieces_ref, bf16[1024,2048]{1,0:T(8,128)(2,1)S(1)} %copy-done.2), custom_call_target="tpu_custom_call" | custom-call | flops 1073741824 | bytes 8388608 | tf_op jit(solution)/shard_map/own_spectra/pallas_call | solution.py:268
  37.7 3.7 %partner_slots.1 = (bf16[2,2,128,256]{3,2,1,0:T(8,128)(2,1)}, bf16[2,2,128,256]{3,2,1,0:T(8,128)(2,1)S(1)}, bf16[4,2,64,1024]{3,2,1,0:T(8,128)(2,1)S(1)}, bf16[4,2,16,1024]{3,2,1,0:T(8,128)(2,1)S(1)}) custom-call(s32[1]{0:T(128)} %bitcast.half_ref, s32[1]{0:T(128)} %bitcast.1.me_ref, s32[1,2,2]{2,1,0:T(2,128)S(1)} %collective-permute-done.theirs_ref, ...), custom_call_target="tpu_custom_call" | custom-call | flops 2147483648 | bytes 8388608 | tf_op jit(solution)/shard_map/partner_slots/pallas_call | solution.py:304
  41.4 3.0 %own_slots.1 = bf16[4,2,128,256]{3,2,1,0:T(8,128)(2,1)} custom-call(s32[1]{0:T(128)} %bitcast.half_ref, s32[1]{0:T(128)} %bitcast.1.me_ref, s32[1,2,2]{2,1,0:T(2,128)S(1)} %copy-done.6, bf16[1024,2048]{1,0:T(8,128)(2,1)S(1)} %copy-done.2, bf16[4,2,64,1024]{3,2,1,0:T(8,128)(2,1)S(1)} %get-tuple-element.30.every, ...), custom_call_target="tpu_custom_call" | custom-call | flops 1073741824 | bytes 8388608 | tf_op jit(solution)/shard_map/own_slots/pallas_call | solution.py:332
  44.4 3.5 %all-to-all-start.1 = ((bf16[4,2,128,256]{3,2,1,0:T(8,128)(2,1)}), bf16[4,2,128,256]{3,2,1,0:T(8,128)(2,1)S(1)}, u32[]{:S(2)}, u32[]{:S(2)}) async-start(bf16[4,2,128,256]{3,2,1,0:T(8,128)(2,1)} %own_slots.1), calls=%async_computation.1 | async-start | bytes 1048576 | tf_op jit(solution)/shard_map/all_to_all | solution.py:439
  47.9 4.3 %collective-permute-start.5 = (bf16[2,2,128,256]{3,2,1,0:T(8,128)(2,1)S(1)}, bf16[2,2,128,256]{3,2,1,0:T(8,128)(2,1)S(1)}, u32[]{:S(2)}, u32[]{:S(2)}) collective-permute-start(bf16[2,2,128,256]{3,2,1,0:T(8,128)(2,1)S(1)} %get-tuple-element.29), channel_id=1, source_target_pairs={{0,10},{1,11},{2,8},{3,9},{4,14},{5,15},{6,12},{7,13},{8,2},{9,3},... | collective-permute-start | bytes 786440 | tf_op jit(solution)/shard_map/ppermute | solution.py:436
  52.2 10.4 %collective-permute-done.6.refs_0_ = bf16[2,2,128,256]{3,2,1,0:T(8,128)(2,1)S(1)} collective-permute-done((bf16[2,2,128,256]{3,2,1,0:T(8,128)(2,1)}, bf16[2,2,128,256]{3,2,1,0:T(8,128)(2,1)S(1)}, u32[]{:S(2)}, u32[]{:S(2)}) %collective-permute-start.6) | collective-permute-done | bytes 262176 | tf_op jit(solution)/shard_map/ppermute | solution.py:436
  62.7 0.7 slice_bitcast_fusion
  63.3 1.0 %own_surfaces.1.part_ref = f32[2,256,1024]{2,1,0:T(8,128)S(1)} custom-call(s32[1]{0:T(128)} %bitcast.half_ref, bf16[4,2,128,256]{3,2,1,0:T(8,128)(2,1)S(1)} %all-to-all-done.1.own_ref, bf16[1024,1024]{1,0:T(8,128)(2,1)S(1)} %copy-done), custom_call_target="tpu_custom_call" | custom-call | flops 536870912 | bytes 2097152 | tf_op jit(solution)/shard_map/own_surfaces/pallas_call | solution.py:358
  64.3 2.9 %collective-permute-done.5.refs_2_ = bf16[2,2,128,256]{3,2,1,0:T(8,128)(2,1)S(1)} collective-permute-done((bf16[2,2,128,256]{3,2,1,0:T(8,128)(2,1)S(1)}, bf16[2,2,128,256]{3,2,1,0:T(8,128)(2,1)S(1)}, u32[]{:S(2)}, u32[]{:S(2)}) %collective-permute-start.5) | collective-permute-done | bytes 262176 | tf_op jit(solution)/shard_map/ppermute | solution.py:436
  68.0 0.7 collective-permute-done.8.refs_3_
  68.7 2.0 %surfaces.1 = f32[2,256,1024]{2,1,0:T(8,128)} custom-call(s32[1]{0:T(128)} %bitcast.half_ref, s32[1]{0:T(128)} %bitcast.1.me_ref, s32[1]{0:T(128)S(6)} %copy.11.counts_ref, f32[2,256,1024]{2,1,0:T(8,128)S(1)} %own_surfaces.1.part_ref, bf16[2,2,128,256]{3,2,1,0:T(8,128)(2,1)S(1)} %collective-permute-done.6.refs_0_, ...), custom_call_target="tpu_custom_call" | custom-call | flops 536870912 | bytes 4194304 | tf_op jit(solution)/shard_map/surfaces/pallas_call | solution.py:399
  (30 shorter events, 0.1 us)
Async XLA Ops:
  0.0 12.5 %copy-start = (bf16[1024,1024]{1,0:T(8,128)(2,1)S(1)}, bf16[1024,1024]{1,0:T(8,128)(2,1)}, u32[]{:S(2)}) copy-start(bf16[1024,1024]{1,0:T(8,128)(2,1)} %constant.35.clone.table_hbm.table_ref.refs_4_) | copy-start | bytes 6291460
  0.0 12.5 %copy-start.4 = (f32[8,1024]{1,0:T(8,128)S(1)}, f32[8,1024]{1,0:T(8,128)}, u32[]{:S(2)}) copy-start(f32[8,1024]{1,0:T(8,128)} %constant.36.clone.down_ref) | copy-start | bytes 98308
  0.0 12.5 %copy-start.5 = (f32[1,1024]{1,0:T(1,128)S(1)}, f32[1,1024]{1,0:T(1,128)}, u32[]{:S(2)}) copy-start(f32[1,1024]{1,0:T(1,128)} %constant.37.clone.across_ref) | copy-start | bytes 12292
  4.6 33.0 %collective-permute-start.1 = (bf16[2,128,256]{2,1,0:T(8,128)(2,1)}, bf16[2,128,256]{2,1,0:T(8,128)(2,1)S(1)}, u32[]{:S(2)}, u32[]{:S(2)}) collective-permute-start(bf16[2,128,256]{2,1,0:T(8,128)(2,1)} %get-tuple-element.20), channel_id=1, source_target_pairs={{0,8},{1,9},{2,10},{3,11},{4,12},{5,13},{6,14},{7,15},{8,0},{9,1},... | collective-permute-start | bytes 393224 | tf_op jit(solution)/shard_map/ppermute | solution.py:436
  8.9 28.7 %collective-permute-start.2 = (bf16[2,128,256]{2,1,0:T(8,128)(2,1)}, bf16[2,128,256]{2,1,0:T(8,128)(2,1)S(1)}, u32[]{:S(2)}, u32[]{:S(2)}) collective-permute-start(bf16[2,128,256]{2,1,0:T(8,128)(2,1)} %get-tuple-element.21), channel_id=1, source_target_pairs={{0,9},{1,8},{2,11},{3,10},{4,13},{5,12},{6,15},{7,14},{8,1},{9,0},... | collective-permute-start | bytes 393224 | tf_op jit(solution)/shard_map/ppermute | solution.py:436
  8.9 28.8 %collective-permute-start.3 = (bf16[2,128,256]{2,1,0:T(8,128)(2,1)}, bf16[2,128,256]{2,1,0:T(8,128)(2,1)S(1)}, u32[]{:S(2)}, u32[]{:S(2)}) collective-permute-start(bf16[2,128,256]{2,1,0:T(8,128)(2,1)} %get-tuple-element.22), channel_id=1, source_target_pairs={{0,10},{1,11},{2,8},{3,9},{4,14},{5,15},{6,12},{7,13},{8,2},{9,3},... | collective-permute-start | bytes 393224 | tf_op jit(solution)/shard_map/ppermute | solution.py:436
  11.9 25.8 %collective-permute-start.4 = (bf16[2,128,256]{2,1,0:T(8,128)(2,1)}, bf16[2,128,256]{2,1,0:T(8,128)(2,1)S(1)}, u32[]{:S(2)}, u32[]{:S(2)}) collective-permute-start(bf16[2,128,256]{2,1,0:T(8,128)(2,1)} %get-tuple-element.23), channel_id=1, source_target_pairs={{0,11},{1,10},{2,9},{3,8},{4,15},{5,14},{6,13},{7,12},{8,3},{9,2},... | collective-permute-start | bytes 393224 | tf_op jit(solution)/shard_map/ppermute | solution.py:436
  12.6 1.6 %copy-start.3 = (f32[2,256,1024]{2,1,0:T(8,128)S(1)}, f32[2,256,1024]{2,1,0:T(8,128)}, u32[]{:S(2)}) copy-start(f32[2,256,1024]{2,1,0:T(8,128)} %tile_ref.1) | copy-start | bytes 6291460
  14.1 5.6 %copy-start.6 = (s32[1,2,2]{2,1,0:T(2,128)S(1)}, s32[1,2,2]{2,1,0:T(2,128)}, u32[]{:S(2)}) copy-start(s32[1,2,2]{2,1,0:T(2,128)} %pairs_ref) | copy-start | bytes 52
  14.2 8.3 %copy-start.7 = (f32[32,1024]{1,0:T(8,128)S(1)}, f32[32,1024]{1,0:T(8,128)}, u32[]{:S(2)}) copy-start(f32[32,1024]{1,0:T(8,128)} %constant.38.clone.rc_ref) | copy-start | bytes 393220
  14.2 8.3 %copy-start.8 = (f32[32,1024]{1,0:T(8,128)S(1)}, f32[32,1024]{1,0:T(8,128)}, u32[]{:S(2)}) copy-start(f32[32,1024]{1,0:T(8,128)} %constant.39.clone.rs_ref) | copy-start | bytes 393220
  14.2 8.3 %copy-start.9 = (f32[32,1024]{1,0:T(8,128)S(1)}, f32[32,1024]{1,0:T(8,128)}, u32[]{:S(2)}) copy-start(f32[32,1024]{1,0:T(8,128)} %constant.40.clone.sc_ref) | copy-start | bytes 393220
  16.3 17.9 %all-to-all-start = ((bf16[4,2,128,256]{3,2,1,0:T(8,128)(2,1)}), bf16[4,2,128,256]{3,2,1,0:T(8,128)(2,1)S(1)}, u32[]{:S(2)}, u32[]{:S(2)}) async-start(bf16[4,2,128,256]{3,2,1,0:T(8,128)(2,1)} %kept_columns.1), calls=%async_computation | async-start | bytes 1048576 | tf_op jit(solution)/shard_map/all_to_all | solution.py:439
  19.8 17.9 %collective-permute-start = (s32[1,2,2]{2,1,0:T(2,128)S(1)}, s32[1,2,2]{2,1,0:T(2,128)S(1)}, u32[]{:S(2)}, u32[]{:S(2)}) collective-permute-start(s32[1,2,2]{2,1,0:T(2,128)S(1)} %copy-done.6), channel_id=1, source_target_pairs={{0,8},{1,9},{2,10},{3,11},{4,12},{5,13},{6,14},{7,15},{8,0},{9,1},... | collective-permute-start | bytes 56 | tf_op jit(solution)/shard_map/ppermute | solution.py:436
  22.5 0.9 %copy-start.10 = (f32[32,1024]{1,0:T(8,128)S(1)}, f32[32,1024]{1,0:T(8,128)}, u32[]{:S(2)}) copy-start(f32[32,1024]{1,0:T(8,128)} %constant.41.clone.ss_ref) | copy-start | bytes 393220
  24.5 1.9 %copy-start.1 = (bf16[1024,2048]{1,0:T(8,128)(2,1)}, bf16[1024,2048]{1,0:T(8,128)(2,1)S(1)}, u32[]{:S(2)}) copy-start(bf16[1024,2048]{1,0:T(8,128)(2,1)S(1)} %height_table.1.table_ref.refs_4_) | copy-start | bytes 12582916
  34.2 2.2 %copy-start.2 = (bf16[1024,2048]{1,0:T(8,128)(2,1)S(1)}, bf16[1024,2048]{1,0:T(8,128)(2,1)}, u32[]{:S(2)}) copy-start(bf16[1024,2048]{1,0:T(8,128)(2,1)} %copy-done.1) | copy-start | bytes 12582916
  41.4 21.3 %collective-permute-start.6 = (bf16[2,2,128,256]{3,2,1,0:T(8,128)(2,1)}, bf16[2,2,128,256]{3,2,1,0:T(8,128)(2,1)S(1)}, u32[]{:S(2)}, u32[]{:S(2)}) collective-permute-start(bf16[2,2,128,256]{3,2,1,0:T(8,128)(2,1)} %get-tuple-element.33), channel_id=1, source_target_pairs={{0,8},{1,9},{2,10},{3,11},{4,12},{5,13},{6,14},{7,15},{8,0},{9,1},... | collective-permute-start | bytes 786440 | tf_op jit(solution)/shard_map/ppermute | solution.py:436
  44.4 18.9 %all-to-all-start.1 = ((bf16[4,2,128,256]{3,2,1,0:T(8,128)(2,1)}), bf16[4,2,128,256]{3,2,1,0:T(8,128)(2,1)S(1)}, u32[]{:S(2)}, u32[]{:S(2)}) async-start(bf16[4,2,128,256]{3,2,1,0:T(8,128)(2,1)} %own_slots.1), calls=%async_computation.1 | async-start | bytes 1048576 | tf_op jit(solution)/shard_map/all_to_all | solution.py:439
  47.9 19.4 %collective-permute-start.5 = (bf16[2,2,128,256]{3,2,1,0:T(8,128)(2,1)S(1)}, bf16[2,2,128,256]{3,2,1,0:T(8,128)(2,1)S(1)}, u32[]{:S(2)}, u32[]{:S(2)}) collective-permute-start(bf16[2,2,128,256]{3,2,1,0:T(8,128)(2,1)S(1)} %get-tuple-element.29), channel_id=1, source_target_pairs={{0,10},{1,11},{2,8},{3,9},{4,14},{5,15},{6,12},{7,13},{8,2},{9,3},... | collective-permute-start | bytes 786440 | tf_op jit(solution)/shard_map/ppermute | solution.py:436
  63.3 4.7 %collective-permute-start.7 = (bf16[2,128,256]{2,1,0:T(8,128)(2,1)}, bf16[2,128,256]{2,1,0:T(8,128)(2,1)S(1)}, u32[]{:S(2)}, u32[]{:S(2)}) collective-permute-start(bf16[2,128,256]{2,1,0:T(8,128)(2,1)} %slice_bitcast_fusion), channel_id=1, source_target_pairs={{0,1},{1,0},{2,3},{3,2},{4,5},{5,4},{6,7},{7,6},{8,9},{9,8},{10,11... | collective-permute-start | bytes 393224 | tf_op jit(solution)/shard_map/ppermute | solution.py:442
  67.3 1.4 %collective-permute-start.8 = (bf16[2,128,256]{2,1,0:T(8,128)(2,1)S(1)}, bf16[2,128,256]{2,1,0:T(8,128)(2,1)S(1)}, u32[]{:S(2)}, u32[]{:S(2)}) collective-permute-start(bf16[2,128,256]{2,1,0:T(8,128)(2,1)S(1)} %slice_bitcast_fusion.1), channel_id=1, source_target_pairs={{0,1},{1,0},{2,3},{3,2},{4,5},{5,4},{6,7},{7,6},{8,9},{9,8},{10,11... | collective-permute-start | bytes 393224 | tf_op jit(solution)/shard_map/ppermute | solution.py:442

commit v7 on v6

--- a/solution.py
+++ b/solution.py
@@ -101,8 +101,6 @@
         def _():
             loads[0].start()
             fetch.start()
-            for load in loads[1:]:
-                load.start()
             fetch.wait()
 
         for i in range(count):
@@ -110,6 +108,8 @@
             @pl.when(t == i)
             def _():
                 loads[i].wait()
+                if i + 1 < count:
+                    loads[i + 1].start()
                 work[...] = times_table(table_ref[...], shade(tile_ref[i], down_ref, across_ref))
 
         for k in range(peers):
@@ -446,10 +446,11 @@
     sideways = jnp.asarray(hann(width)[None, :])
 
     sent = sent_columns(tiles, down, sideways, table_w, half, me, peers)
-    arrived = [across(sent[k], k) for k in range(peers)]
+    arrived = [across(sent[k], k) for k in range(2)]
     *sent, held = lax.optimization_barrier((*sent, half))
     kept = kept_columns(tiles, down, sideways, table_w, held, me, peers)
-    kept, pairs = lax.optimization_barrier((kept, pairs))
+    *sent, kept, pairs = lax.optimization_barrier((*sent, kept, pairs))
+    arrived += [across(sent[k], k) for k in range(2, peers)]
     mine = along(kept)
 
     table_h = height_table(height)

time: 71 us -> 67.3 us (0.948)
  waiting for transfers between devices: 21.8 us -> 17.1 us
    all_to_all x2, waiting for transfers between devices: 7.78 us -> 0.01 us  [along(): return lax.all_to_all(blocks, 'rows', split_axis=0, concat_axis=0)]
    ppermute x7, waiting for transfers between devices: 13.4 us -> 16.5 us  [across(): return lax.ppermute(value, axes, moves)]
  transfers between devices with their start and end apart: 11 -> 11, of which waited for: 4 -> 4; matrix products, arithmetic and copies ran while one was open for 1% -> 1% of each run, Pallas kernels for 12% -> 13%
where the time goes in v7:
time: 67.3 us; the launch traced here: 67 us
  starting transfers between devices  22.5 us (33%)
  Pallas kernels  19.2 us (29%)
  waiting for transfers between devices  17.1 us (25%)
  local copies, waits for them, and re-layouts  7.3 us (11%)
  between operations  0.78 us (1%)
    ppermute x7, waiting for transfers between devices, across(): return lax.ppermute(value, axes, moves)  16.5 us
    ppermute x7, starting transfers between devices, across(): return lax.ppermute(value, axes, moves)  15.5 us
    all_to_all x2, starting transfers between devices, along(): return lax.all_to_all(blocks, 'rows', split_axis=0, concat_axis=0)  6.94 us
    unnamed x22, local copies, waits for them, and re-layouts  6.63 us
    pallas_call x1, Pallas kernels, sent_columns(): pl.pallas_call(body, grid_spec=pltpu.PrefetchScalarGridSpec(num_scalar_pr...  5.1 us
    pallas_call x1, Pallas kernels, partner_slots(): pl.pallas_call(body, in_specs=[pl.BlockSpec(memory_space=pltpu.SMEM)] * 3...  3.65 us
    pallas_call x1, Pallas kernels, own_slots(): pl.pallas_call(body, in_specs=[pl.BlockSpec(memory_space=pltpu.SMEM)] * 3...  2.99 us
    pallas_call x1, Pallas kernels, kept_columns(): pl.pallas_call(body, grid_spec=pltpu.PrefetchScalarGridSpec(num_scalar_pr...  2.14 us
  transfers between devices with their start and end apart: 11, of which 4 were waited for; matrix products, arithmetic and copies ran while one was open for 1% of the time, Pallas kernels for 13%

profile of v7, /device:TPU:0, one launch (start us, length us, event | category | flops | bytes accessed | tf_op | source)
XLA Modules:
  0.0 67.0 jit_solution(5161802022086422449)
XLA Ops:
  0.0 5.1 %sent_columns.1 = (bf16[2,128,256]{2,1,0:T(8,128)(2,1)}, bf16[2,128,256]{2,1,0:T(8,128)(2,1)}, bf16[2,128,256]{2,1,0:T(8,128)(2,1)}, bf16[2,128,256]{2,1,0:T(8,128)(2,1)}) custom-call(s32[1]{0:T(128)} %bitcast.half_ref, s32[1]{0:T(128)} %bitcast.1.me_ref, f32[2,256,1024]{2,1,0:T(8,128)} %tile_ref.1, f32[8,1024]{1,0:T(8,128)} %constant.36.clone.down_ref, ...), custom_call_target="tpu_custom_call" | custom-call | flops 536870912 | bytes 3145728 | tf_op jit(solution)/shard_map/sent_columns/pallas_call | solution.py:119
  5.1 4.1 %collective-permute-start.1 = (bf16[2,128,256]{2,1,0:T(8,128)(2,1)}, bf16[2,128,256]{2,1,0:T(8,128)(2,1)S(1)}, u32[]{:S(2)}, u32[]{:S(2)}) collective-permute-start(bf16[2,128,256]{2,1,0:T(8,128)(2,1)} %get-tuple-element.24), channel_id=1, source_target_pairs={{0,8},{1,9},{2,10},{3,11},{4,12},{5,13},{6,14},{7,15},{8,0},{9,1},... | collective-permute-start | bytes 393224 | tf_op jit(solution)/shard_map/ppermute | solution.py:436
  9.3 1.6 %copy-done.3 = f32[2,256,1024]{2,1,0:T(8,128)S(1)} copy-done((f32[2,256,1024]{2,1,0:T(8,128)S(1)}, f32[2,256,1024]{2,1,0:T(8,128)}, u32[]{:S(2)}) %copy-start.3) | copy-done | bytes 2097176
  10.9 2.1 %kept_columns.1 = bf16[4,2,128,256]{3,2,1,0:T(8,128)(2,1)} custom-call(s32[1]{0:T(128)} %bitcast.2.half_ref, s32[1]{0:T(128)} %bitcast.1.me_ref, f32[2,256,1024]{2,1,0:T(8,128)S(1)} %copy-done.3, f32[8,1024]{1,0:T(8,128)S(1)} %copy-done.4, f32[1,1024]{1,0:T(1,128)S(1)} %copy-done.5, bf16[1024,1024]{1,0:T(8,128)(2,1)S(1)} %copy-done), custom_call_target="tpu_custom_call" | custom-call | flops 536870912 | bytes 3145728 | tf_op jit(solution)/shard_map/kept_columns/pallas_call | solution.py:154
  13.0 3.5 %all-to-all-start = ((bf16[4,2,128,256]{3,2,1,0:T(8,128)(2,1)}), bf16[4,2,128,256]{3,2,1,0:T(8,128)(2,1)S(1)}, u32[]{:S(2)}, u32[]{:S(2)}) async-start(bf16[4,2,128,256]{3,2,1,0:T(8,128)(2,1)} %kept_columns.1), calls=%async_computation | async-start | bytes 1048576 | tf_op jit(solution)/shard_map/all_to_all | solution.py:439
  16.5 3.5 %collective-permute-start.3 = (bf16[2,128,256]{2,1,0:T(8,128)(2,1)}, bf16[2,128,256]{2,1,0:T(8,128)(2,1)S(1)}, u32[]{:S(2)}, u32[]{:S(2)}) collective-permute-start(bf16[2,128,256]{2,1,0:T(8,128)(2,1)} %get-tuple-element.32), channel_id=1, source_target_pairs={{0,10},{1,11},{2,8},{3,9},{4,14},{5,15},{6,12},{7,13},{8,2},{9,3},... | collective-permute-start | bytes 393224 | tf_op jit(solution)/shard_map/ppermute | solution.py:436
  20.2 2.5 %collective-permute-start = (s32[1,2,2]{2,1,0:T(2,128)S(1)}, s32[1,2,2]{2,1,0:T(2,128)S(1)}, u32[]{:S(2)}, u32[]{:S(2)}) collective-permute-start(s32[1,2,2]{2,1,0:T(2,128)S(1)} %copy-done.6), channel_id=1, source_target_pairs={{0,8},{1,9},{2,10},{3,11},{4,12},{5,13},{6,14},{7,15},{8,0},{9,1},... | collective-permute-start | bytes 56 | tf_op jit(solution)/shard_map/ppermute | solution.py:436
  22.7 0.9 %copy-done.10 = f32[32,1024]{1,0:T(8,128)S(1)} copy-done((f32[32,1024]{1,0:T(8,128)S(1)}, f32[32,1024]{1,0:T(8,128)}, u32[]{:S(2)}) %copy-start.10) | copy-done | bytes 131096
  23.6 1.1 %height_table.1.table_ref.refs_4_ = bf16[1024,2048]{1,0:T(8,128)(2,1)S(1)} custom-call(f32[32,1024]{1,0:T(8,128)S(1)} %copy-done.7, f32[32,1024]{1,0:T(8,128)S(1)} %copy-done.8, f32[32,1024]{1,0:T(8,128)S(1)} %copy-done.9, f32[32,1024]{1,0:T(8,128)S(1)} %copy-done.10), custom_call_target="tpu_custom_call" | custom-call | flops 8589934592 | bytes 4194304 | tf_op jit(solution)/shard_map/height_table/pallas_call | solution.py:53
  24.8 1.9 %copy-done.1 = bf16[1024,2048]{1,0:T(8,128)(2,1)} copy-done((bf16[1024,2048]{1,0:T(8,128)(2,1)}, bf16[1024,2048]{1,0:T(8,128)(2,1)S(1)}, u32[]{:S(2)}) %copy-start.1) | copy-done | bytes 4194328
  26.7 2.2 %copy-done.2 = bf16[1024,2048]{1,0:T(8,128)(2,1)S(1)} copy-done((bf16[1024,2048]{1,0:T(8,128)(2,1)S(1)}, bf16[1024,2048]{1,0:T(8,128)(2,1)}, u32[]{:S(2)}) %copy-start.2) | copy-done | bytes 4194328
  28.9 1.3 %own_spectra.1 = (bf16[2,2,64,1024]{3,2,1,0:T(8,128)(2,1)S(1)}, bf16[2,2,16,1024]{3,2,1,0:T(8,128)(2,1)S(1)}) custom-call(s32[1]{0:T(128)} %bitcast.half_ref, s32[1]{0:T(128)} %bitcast.1.me_ref, bf16[4,2,128,256]{3,2,1,0:T(8,128)(2,1)S(1)} %all-to-all-done.pieces_ref, bf16[1024,2048]{1,0:T(8,128)(2,1)S(1)} %copy-done.2), custom_call_target="tpu_custom_call" | custom-call | flops 1073741824 | bytes 8388608 | tf_op jit(solution)/shard_map/own_spectra/pallas_call | solution.py:268
  30.2 2.9 %collective-permute-done.theirs_ref = s32[1,2,2]{2,1,0:T(2,128)S(1)} collective-permute-done((s32[1,2,2]{2,1,0:T(2,128)S(1)}, s32[1,2,2]{2,1,0:T(2,128)S(1)}, u32[]{:S(2)}, u32[]{:S(2)}) %collective-permute-start) | collective-permute-done | bytes 48 | tf_op jit(solution)/shard_map/ppermute | solution.py:436
  33.0 3.7 %partner_slots.1 = (bf16[2,2,128,256]{3,2,1,0:T(8,128)(2,1)}, bf16[2,2,128,256]{3,2,1,0:T(8,128)(2,1)S(1)}, bf16[4,2,64,1024]{3,2,1,0:T(8,128)(2,1)S(1)}, bf16[4,2,16,1024]{3,2,1,0:T(8,128)(2,1)S(1)}) custom-call(s32[1]{0:T(128)} %bitcast.half_ref, s32[1]{0:T(128)} %bitcast.1.me_ref, s32[1,2,2]{2,1,0:T(2,128)S(1)} %collective-permute-done.theirs_ref, ...), custom_call_target="tpu_custom_call" | custom-call | flops 2147483648 | bytes 8388608 | tf_op jit(solution)/shard_map/partner_slots/pallas_call | solution.py:304
  36.7 3.7 %collective-permute-start.6 = (bf16[2,2,128,256]{3,2,1,0:T(8,128)(2,1)}, bf16[2,2,128,256]{3,2,1,0:T(8,128)(2,1)S(1)}, u32[]{:S(2)}, u32[]{:S(2)}) collective-permute-start(bf16[2,2,128,256]{3,2,1,0:T(8,128)(2,1)} %get-tuple-element.41), channel_id=1, source_target_pairs={{0,8},{1,9},{2,10},{3,11},{4,12},{5,13},{6,14},{7,15},{8,0},{9,1},... | collective-permute-start | bytes 786440 | tf_op jit(solution)/shard_map/ppermute | solution.py:436
  40.4 3.0 %own_slots.1 = bf16[4,2,128,256]{3,2,1,0:T(8,128)(2,1)} custom-call(s32[1]{0:T(128)} %bitcast.half_ref, s32[1]{0:T(128)} %bitcast.1.me_ref, s32[1,2,2]{2,1,0:T(2,128)S(1)} %copy-done.6, bf16[1024,2048]{1,0:T(8,128)(2,1)S(1)} %copy-done.2, bf16[4,2,64,1024]{3,2,1,0:T(8,128)(2,1)S(1)} %get-tuple-element.38.every, ...), custom_call_target="tpu_custom_call" | custom-call | flops 1073741824 | bytes 8388608 | tf_op jit(solution)/shard_map/own_slots/pallas_call | solution.py:332
  43.4 3.5 %all-to-all-start.1 = ((bf16[4,2,128,256]{3,2,1,0:T(8,128)(2,1)}), bf16[4,2,128,256]{3,2,1,0:T(8,128)(2,1)S(1)}, u32[]{:S(2)}, u32[]{:S(2)}) async-start(bf16[4,2,128,256]{3,2,1,0:T(8,128)(2,1)} %own_slots.1), calls=%async_computation.1 | async-start | bytes 1048576 | tf_op jit(solution)/shard_map/all_to_all | solution.py:439
  46.9 1.4 %collective-permute-start.5 = (bf16[2,2,128,256]{3,2,1,0:T(8,128)(2,1)S(1)}, bf16[2,2,128,256]{3,2,1,0:T(8,128)(2,1)S(1)}, u32[]{:S(2)}, u32[]{:S(2)}) collective-permute-start(bf16[2,2,128,256]{3,2,1,0:T(8,128)(2,1)S(1)} %get-tuple-element.37), channel_id=1, source_target_pairs={{0,10},{1,11},{2,8},{3,9},{4,14},{5,15},{6,12},{7,13},{8,2},{9,3},... | collective-permute-start | bytes 786440 | tf_op jit(solution)/shard_map/ppermute | solution.py:436
  48.3 10.3 %collective-permute-done.6.refs_0_ = bf16[2,2,128,256]{3,2,1,0:T(8,128)(2,1)S(1)} collective-permute-done((bf16[2,2,128,256]{3,2,1,0:T(8,128)(2,1)}, bf16[2,2,128,256]{3,2,1,0:T(8,128)(2,1)S(1)}, u32[]{:S(2)}, u32[]{:S(2)}) %collective-permute-start.6) | collective-permute-done | bytes 262176 | tf_op jit(solution)/shard_map/ppermute | solution.py:436
  58.7 0.7 slice_bitcast_fusion
  59.3 1.0 %own_surfaces.1.part_ref = f32[2,256,1024]{2,1,0:T(8,128)S(1)} custom-call(s32[1]{0:T(128)} %bitcast.half_ref, bf16[4,2,128,256]{3,2,1,0:T(8,128)(2,1)S(1)} %all-to-all-done.1.own_ref, bf16[1024,1024]{1,0:T(8,128)(2,1)S(1)} %copy-done), custom_call_target="tpu_custom_call" | custom-call | flops 536870912 | bytes 2097152 | tf_op jit(solution)/shard_map/own_surfaces/pallas_call | solution.py:358
  60.3 3.2 %collective-permute-done.5.refs_2_ = bf16[2,2,128,256]{3,2,1,0:T(8,128)(2,1)S(1)} collective-permute-done((bf16[2,2,128,256]{3,2,1,0:T(8,128)(2,1)S(1)}, bf16[2,2,128,256]{3,2,1,0:T(8,128)(2,1)S(1)}, u32[]{:S(2)}, u32[]{:S(2)}) %collective-permute-start.5) | collective-permute-done | bytes 262176 | tf_op jit(solution)/shard_map/ppermute | solution.py:436
  64.3 0.7 %collective-permute-done.8.refs_3_ = bf16[2,128,256]{2,1,0:T(8,128)(2,1)S(1)} collective-permute-done((bf16[2,128,256]{2,1,0:T(8,128)(2,1)S(1)}, bf16[2,128,256]{2,1,0:T(8,128)(2,1)S(1)}, u32[]{:S(2)}, u32[]{:S(2)}) %collective-permute-start.8) | collective-permute-done | bytes 131104 | tf_op jit(solution)/shard_map/ppermute | solution.py:442
  65.0 1.9 %surfaces.1 = f32[2,256,1024]{2,1,0:T(8,128)} custom-call(s32[1]{0:T(128)} %bitcast.half_ref, s32[1]{0:T(128)} %bitcast.1.me_ref, s32[1]{0:T(128)S(6)} %copy.11.counts_ref, f32[2,256,1024]{2,1,0:T(8,128)S(1)} %own_surfaces.1.part_ref, bf16[2,2,128,256]{3,2,1,0:T(8,128)(2,1)S(1)} %collective-permute-done.6.refs_0_, ...), custom_call_target="tpu_custom_call" | custom-call | flops 536870912 | bytes 4194304 | tf_op jit(solution)/shard_map/surfaces/pallas_call | solution.py:399
  (30 shorter events, 0.3 us)
Async XLA Ops:
  0.0 9.2 %copy-start = (bf16[1024,1024]{1,0:T(8,128)(2,1)S(1)}, bf16[1024,1024]{1,0:T(8,128)(2,1)}, u32[]{:S(2)}) copy-start(bf16[1024,1024]{1,0:T(8,128)(2,1)} %constant.35.clone.table_hbm.table_ref.refs_4_) | copy-start | bytes 6291460
  0.0 9.2 %copy-start.4 = (f32[8,1024]{1,0:T(8,128)S(1)}, f32[8,1024]{1,0:T(8,128)}, u32[]{:S(2)}) copy-start(f32[8,1024]{1,0:T(8,128)} %constant.36.clone.down_ref) | copy-start | bytes 98308
  0.0 9.2 %copy-start.5 = (f32[1,1024]{1,0:T(1,128)S(1)}, f32[1,1024]{1,0:T(1,128)}, u32[]{:S(2)}) copy-start(f32[1,1024]{1,0:T(1,128)} %constant.37.clone.across_ref) | copy-start | bytes 12292
  5.1 27.9 %collective-permute-start.1 = (bf16[2,128,256]{2,1,0:T(8,128)(2,1)}, bf16[2,128,256]{2,1,0:T(8,128)(2,1)S(1)}, u32[]{:S(2)}, u32[]{:S(2)}) collective-permute-start(bf16[2,128,256]{2,1,0:T(8,128)(2,1)} %get-tuple-element.24), channel_id=1, source_target_pairs={{0,8},{1,9},{2,10},{3,11},{4,12},{5,13},{6,14},{7,15},{8,0},{9,1},... | collective-permute-start | bytes 393224 | tf_op jit(solution)/shard_map/ppermute | solution.py:436
  9.2 23.8 %collective-permute-start.2 = (bf16[2,128,256]{2,1,0:T(8,128)(2,1)}, bf16[2,128,256]{2,1,0:T(8,128)(2,1)S(1)}, u32[]{:S(2)}, u32[]{:S(2)}) collective-permute-start(bf16[2,128,256]{2,1,0:T(8,128)(2,1)} %get-tuple-element.25), channel_id=1, source_target_pairs={{0,9},{1,8},{2,11},{3,10},{4,13},{5,12},{6,15},{7,14},{8,1},{9,0},... | collective-permute-start | bytes 393224 | tf_op jit(solution)/shard_map/ppermute | solution.py:436
  9.3 1.6 %copy-start.3 = (f32[2,256,1024]{2,1,0:T(8,128)S(1)}, f32[2,256,1024]{2,1,0:T(8,128)}, u32[]{:S(2)}) copy-start(f32[2,256,1024]{2,1,0:T(8,128)} %tile_ref.1) | copy-start | bytes 6291460
  10.8 9.3 %copy-start.6 = (s32[1,2,2]{2,1,0:T(2,128)S(1)}, s32[1,2,2]{2,1,0:T(2,128)}, u32[]{:S(2)}) copy-start(s32[1,2,2]{2,1,0:T(2,128)} %pairs_ref) | copy-start | bytes 52
  10.8 11.9 %copy-start.7 = (f32[32,1024]{1,0:T(8,128)S(1)}, f32[32,1024]{1,0:T(8,128)}, u32[]{:S(2)}) copy-start(f32[32,1024]{1,0:T(8,128)} %constant.38.clone.rc_ref) | copy-start | bytes 393220
  10.8 11.9 %copy-start.8 = (f32[32,1024]{1,0:T(8,128)S(1)}, f32[32,1024]{1,0:T(8,128)}, u32[]{:S(2)}) copy-start(f32[32,1024]{1,0:T(8,128)} %constant.39.clone.rs_ref) | copy-start | bytes 393220
  10.9 11.9 %copy-start.9 = (f32[32,1024]{1,0:T(8,128)S(1)}, f32[32,1024]{1,0:T(8,128)}, u32[]{:S(2)}) copy-start(f32[32,1024]{1,0:T(8,128)} %constant.40.clone.sc_ref) | copy-start | bytes 393220
  13.0 13.7 %all-to-all-start = ((bf16[4,2,128,256]{3,2,1,0:T(8,128)(2,1)}), bf16[4,2,128,256]{3,2,1,0:T(8,128)(2,1)S(1)}, u32[]{:S(2)}, u32[]{:S(2)}) async-start(bf16[4,2,128,256]{3,2,1,0:T(8,128)(2,1)} %kept_columns.1), calls=%async_computation | async-start | bytes 1048576 | tf_op jit(solution)/shard_map/all_to_all | solution.py:439
  16.5 16.6 %collective-permute-start.3 = (bf16[2,128,256]{2,1,0:T(8,128)(2,1)}, bf16[2,128,256]{2,1,0:T(8,128)(2,1)S(1)}, u32[]{:S(2)}, u32[]{:S(2)}) collective-permute-start(bf16[2,128,256]{2,1,0:T(8,128)(2,1)} %get-tuple-element.32), channel_id=1, source_target_pairs={{0,10},{1,11},{2,8},{3,9},{4,14},{5,15},{6,12},{7,13},{8,2},{9,3},... | collective-permute-start | bytes 393224 | tf_op jit(solution)/shard_map/ppermute | solution.py:436
  20.0 13.1 %collective-permute-start.4 = (bf16[2,128,256]{2,1,0:T(8,128)(2,1)}, bf16[2,128,256]{2,1,0:T(8,128)(2,1)S(1)}, u32[]{:S(2)}, u32[]{:S(2)}) collective-permute-start(bf16[2,128,256]{2,1,0:T(8,128)(2,1)} %get-tuple-element.33), channel_id=1, source_target_pairs={{0,11},{1,10},{2,9},{3,8},{4,15},{5,14},{6,13},{7,12},{8,3},{9,2},... | collective-permute-start | bytes 393224 | tf_op jit(solution)/shard_map/ppermute | solution.py:436
  20.2 12.9 %collective-permute-start = (s32[1,2,2]{2,1,0:T(2,128)S(1)}, s32[1,2,2]{2,1,0:T(2,128)S(1)}, u32[]{:S(2)}, u32[]{:S(2)}) collective-permute-start(s32[1,2,2]{2,1,0:T(2,128)S(1)} %copy-done.6), channel_id=1, source_target_pairs={{0,8},{1,9},{2,10},{3,11},{4,12},{5,13},{6,14},{7,15},{8,0},{9,1},... | collective-permute-start | bytes 56 | tf_op jit(solution)/shard_map/ppermute | solution.py:436
  22.7 0.9 %copy-start.10 = (f32[32,1024]{1,0:T(8,128)S(1)}, f32[32,1024]{1,0:T(8,128)}, u32[]{:S(2)}) copy-start(f32[32,1024]{1,0:T(8,128)} %constant.41.clone.ss_ref) | copy-start | bytes 393220
  24.8 1.9 %copy-start.1 = (bf16[1024,2048]{1,0:T(8,128)(2,1)}, bf16[1024,2048]{1,0:T(8,128)(2,1)S(1)}, u32[]{:S(2)}) copy-start(bf16[1024,2048]{1,0:T(8,128)(2,1)S(1)} %height_table.1.table_ref.refs_4_) | copy-start | bytes 12582916
  26.7 2.2 %copy-start.2 = (bf16[1024,2048]{1,0:T(8,128)(2,1)S(1)}, bf16[1024,2048]{1,0:T(8,128)(2,1)}, u32[]{:S(2)}) copy-start(bf16[1024,2048]{1,0:T(8,128)(2,1)} %copy-done.1) | copy-start | bytes 12582916
  36.7 22.0 %collective-permute-start.6 = (bf16[2,2,128,256]{3,2,1,0:T(8,128)(2,1)}, bf16[2,2,128,256]{3,2,1,0:T(8,128)(2,1)S(1)}, u32[]{:S(2)}, u32[]{:S(2)}) collective-permute-start(bf16[2,2,128,256]{3,2,1,0:T(8,128)(2,1)} %get-tuple-element.41), channel_id=1, source_target_pairs={{0,8},{1,9},{2,10},{3,11},{4,12},{5,13},{6,14},{7,15},{8,0},{9,1},... | collective-permute-start | bytes 786440 | tf_op jit(solution)/shard_map/ppermute | solution.py:436
  43.4 15.9 %all-to-all-start.1 = ((bf16[4,2,128,256]{3,2,1,0:T(8,128)(2,1)}), bf16[4,2,128,256]{3,2,1,0:T(8,128)(2,1)S(1)}, u32[]{:S(2)}, u32[]{:S(2)}) async-start(bf16[4,2,128,256]{3,2,1,0:T(8,128)(2,1)} %own_slots.1), calls=%async_computation.1 | async-start | bytes 1048576 | tf_op jit(solution)/shard_map/all_to_all | solution.py:439
  46.9 16.7 %collective-permute-start.5 = (bf16[2,2,128,256]{3,2,1,0:T(8,128)(2,1)S(1)}, bf16[2,2,128,256]{3,2,1,0:T(8,128)(2,1)S(1)}, u32[]{:S(2)}, u32[]{:S(2)}) collective-permute-start(bf16[2,2,128,256]{3,2,1,0:T(8,128)(2,1)S(1)} %get-tuple-element.37), channel_id=1, source_target_pairs={{0,10},{1,11},{2,8},{3,9},{4,14},{5,15},{6,12},{7,13},{8,2},{9,3},... | collective-permute-start | bytes 786440 | tf_op jit(solution)/shard_map/ppermute | solution.py:436
  59.3 5.0 %collective-permute-start.7 = (bf16[2,128,256]{2,1,0:T(8,128)(2,1)}, bf16[2,128,256]{2,1,0:T(8,128)(2,1)S(1)}, u32[]{:S(2)}, u32[]{:S(2)}) collective-permute-start(bf16[2,128,256]{2,1,0:T(8,128)(2,1)} %slice_bitcast_fusion), channel_id=1, source_target_pairs={{0,1},{1,0},{2,3},{3,2},{4,5},{5,4},{6,7},{7,6},{8,9},{9,8},{10,11... | collective-permute-start | bytes 393224 | tf_op jit(solution)/shard_map/ppermute | solution.py:442
  63.6 1.4 %collective-permute-start.8 = (bf16[2,128,256]{2,1,0:T(8,128)(2,1)S(1)}, bf16[2,128,256]{2,1,0:T(8,128)(2,1)S(1)}, u32[]{:S(2)}, u32[]{:S(2)}) collective-permute-start(bf16[2,128,256]{2,1,0:T(8,128)(2,1)S(1)} %slice_bitcast_fusion.1), channel_id=1, source_target_pairs={{0,1},{1,0},{2,3},{3,2},{4,5},{5,4},{6,7},{7,6},{8,9},{9,8},{10,11... | collective-permute-start | bytes 393224 | tf_op jit(solution)/shard_map/ppermute | solution.py:442

commit v8 on v7

--- a/solution.py
+++ b/solution.py
@@ -80,18 +80,19 @@
     return y.astype(jnp.bfloat16)
 
 
-def sent_columns(tiles, down, across, table, half, me, peers):
+def near_columns(tiles, down, across, table, half, me, peers):
     count, rows, width = tiles.shape
     span = table.shape[0] // 2
     block = span // peers
 
     def body(half_ref, me_ref, tile_hbm, down_ref, across_ref, table_hbm, *refs):
-        outs = refs[:peers]
-        tile_ref, table_ref, work, done = refs[peers:]
+        outs = refs[:2]
+        tile_ref, table_ref, work, done = refs[2:]
         t = pl.program_id(0)
-        start = pl.multiple_of((1 - half_ref[0]) * span, span)
+        me = me_ref[0]
+        start = pl.multiple_of((1 - half_ref[0]) * span + me // 2 * 2 * block, 2 * block)
         fetch = pltpu.make_async_copy(
-            table_hbm.at[pl.ds(start, span)], table_ref, done.at[count]
+            table_hbm.at[pl.ds(start, 2 * block)], table_ref, done.at[count]
         )
         loads = [
             pltpu.make_async_copy(tile_hbm.at[i], tile_ref.at[i], done.at[i]) for i in range(count)
@@ -99,8 +100,9 @@
 
         @pl.when(t == 0)
         def _():
-            loads[0].start()
             fetch.start()
+            for load in loads:
+                load.start()
             fetch.wait()
 
         for i in range(count):
@@ -108,12 +110,10 @@
             @pl.when(t == i)
             def _():
                 loads[i].wait()
-                if i + 1 < count:
-                    loads[i + 1].start()
                 work[...] = times_table(table_ref[...], shade(tile_ref[i], down_ref, across_ref))
 
-        for k in range(peers):
-            place = pl.multiple_of((me_ref[0] ^ k) * block, block)
+        for k in range(2):
+            place = pl.multiple_of((me % 2 ^ k) * block, block)
             outs[k][0] = work[pl.ds(place, block), :]
 
     return pl.pallas_call(
@@ -127,30 +127,41 @@
                 pl.BlockSpec((1, width), lambda t, half, me: (0, 0)),
                 pl.BlockSpec(memory_space=pltpu.HBM),
             ],
-            out_specs=[pl.BlockSpec((1, block, rows), lambda t, half, me: (t, 0, 0))] * peers,
+            out_specs=[pl.BlockSpec((1, block, rows), lambda t, half, me: (t, 0, 0))] * 2,
             scratch_shapes=[
                 pltpu.VMEM((count, rows, width), tiles.dtype),
-                pltpu.VMEM((span, width), table.dtype),
-                pltpu.VMEM((span, rows), jnp.bfloat16),
+                pltpu.VMEM((2 * block, width), table.dtype),
+                pltpu.VMEM((2 * block, rows), jnp.bfloat16),
                 pltpu.SemaphoreType.DMA((count + 1,)),
             ],
         ),
-        out_shape=[jax.ShapeDtypeStruct((count, block, rows), jnp.bfloat16)] * peers,
+        out_shape=[jax.ShapeDtypeStruct((count, block, rows), jnp.bfloat16)] * 2,
         compiler_params=params(FIRST_LIMIT),
-        cost_estimate=cost(2 * count * rows * width * span, 4 * tiles.size + 2 * span * width),
-        name="sent_columns",
+        cost_estimate=cost(4 * count * rows * width * block, 4 * tiles.size + 4 * block * width),
+        name="near_columns",
     )(scalar(half), scalar(me), tiles, down, across, table)
 
 
-def kept_columns(tiles, down, across, table, half, me, peers):
+def rest_columns(tiles, down, across, table, half, me, peers):
     count, rows, width = tiles.shape
     span = table.shape[0] // 2
     block = span // peers
 
-    def body(half_ref, me_ref, tile_ref, down_ref, across_ref, table_ref, out_ref):
-        y = times_table(table_ref[...], shade(tile_ref[0], down_ref, across_ref))
+    def body(half_ref, me_ref, tile_ref, down_ref, across_ref, table_ref, *refs):
+        out_ref, far, work = refs[0], refs[1:-1], refs[-1]
+        half, me = half_ref[0], me_ref[0]
+        shaded = shade(tile_ref[0], down_ref, across_ref)
+        for j in range(1, peers // 2):
+            start = pl.multiple_of((1 - half) * span + (me // 2 ^ j) * 2 * block, 2 * block)
+            work[...] = times_table(table_ref[pl.ds(start, 2 * block), :], shaded)
+            for k in range(2):
+                place = pl.multiple_of((me % 2 ^ k) * block, block)
+                far[2 * j - 2 + k][0] = work[pl.ds(place, block), :]
+        start = pl.multiple_of(half * span, span)
+        y = times_table(table_ref[pl.ds(start, span), :], shaded)
         out_ref[:, 0] = y.reshape(peers, block, rows)
 
+    piece = pl.BlockSpec((1, block, rows), lambda t, half, me: (t, 0, 0))
     return pl.pallas_call(
         body,
         grid_spec=pltpu.PrefetchScalarGridSpec(
@@ -160,14 +171,21 @@
                 pl.BlockSpec((1, rows, width), lambda t, half, me: (t, 0, 0)),
                 pl.BlockSpec((8, rows), lambda t, half, me: (0, me[0])),
                 pl.BlockSpec((1, width), lambda t, half, me: (0, 0)),
-                pl.BlockSpec((span, width), lambda t, half, me: (half[0], 0)),
+                pl.BlockSpec((width, width), lambda t, half, me: (0, 0)),
             ],
-            out_specs=pl.BlockSpec((peers, 1, block, rows), lambda t, half, me: (0, t, 0, 0)),
+            out_specs=[
+                pl.BlockSpec((peers, 1, block, rows), lambda t, half, me: (0, t, 0, 0)),
+                *[piece] * (peers - 2),
+            ],
+            scratch_shapes=[pltpu.VMEM((2 * block, rows), jnp.bfloat16)],
         ),
-        out_shape=jax.ShapeDtypeStruct((peers, count, block, rows), jnp.bfloat16),
-        compiler_params=params(),
-        cost_estimate=cost(2 * count * rows * width * span, 4 * tiles.size + 2 * span * width),
-        name="kept_columns",
+        out_shape=[
+            jax.ShapeDtypeStruct((peers, count, block, rows), jnp.bfloat16),
+            *[jax.ShapeDtypeStruct((count, block, rows), jnp.bfloat16)] * (peers - 2),
+        ],
+        compiler_params=params(),
+        cost_estimate=cost(3 * count * rows * width * span, 4 * tiles.size + 2 * width * width),
+        name="rest_columns",
     )(scalar(half), scalar(me), tiles, down, across, table)
 
 
@@ -220,10 +238,9 @@
     )
 
 
-def correlate(s_ref, me, picks, spectra, edge, table_ref, phases, outs):
-    block = spectra.shape[2]
+def correlate(s_ref, picks, spectra, edge, phases):
+    slots = len(picks)
     height = spectra.shape[3]
-    slots, _, rows = outs[0].shape
     lead = lax.broadcasted_iota(jnp.int32, (16, height), 0)
     packed = (lead == 0) & holds_packed(s_ref)
     for p in range(slots):
@@ -238,10 +255,15 @@
         mixed_imag = jnp.where(packed, top_imag + e_real.astype(jnp.float32), top_imag)
         phases[2 * p, :16] = mixed_real.astype(jnp.bfloat16)
         phases[2 * p + 1, :16] = mixed_imag.astype(jnp.bfloat16)
+
+def invert_columns(s_ref, me, phases, table_ref, outs):
+    _, block, height = phases.shape
+    slots = phases.shape[0] // 2
+    rows = next(iter(outs.values())).shape[2]
     row = lax.broadcasted_iota(jnp.int32, (block, rows), 0)
     twice = jnp.where((row == 0) & holds_packed(s_ref), 1.0, 2.0)
     flat = phases[...].reshape(2 * slots * block, height)
-    for k in range(len(outs)):
+    for k, out in outs.items():
         start = pl.multiple_of((me ^ k) * rows, rows)
         c_part = jnp.dot(
             flat, table_ref[:, pl.ds(start, rows)], preferred_element_type=jnp.float32
@@ -253,8 +275,8 @@
         for p in range(slots):
             re = slice(2 * p * block, (2 * p + 1) * block)
             im = slice((2 * p + 1) * block, (2 * p + 2) * block)
-            outs[k][p, :block] = ((c_part[re] - s_part[im]) * twice).astype(jnp.bfloat16)
-            outs[k][p, block:] = ((s_part[re] + c_part[im]) * twice).astype(jnp.bfloat16)
+            out[p, :block] = ((c_part[re] - s_part[im]) * twice).astype(jnp.bfloat16)
+            out[p, block:] = ((s_part[re] + c_part[im]) * twice).astype(jnp.bfloat16)
 
 
 def own_spectra(place, pieces, table):
@@ -294,52 +316,59 @@
             [(theirs_ref[0, p, i] + count) % (2 * count) for i in range(2)] for p in range(slots)
         ]
         inputs, table_ref, own_ref, own_edge = refs[:peers], *refs[peers : peers + 3]
-        outs = [refs[peers + 3 + k // 2].at[k % 2] for k in range(peers)]
-        every, edges, phases = refs[-3:]
+        near, every, edges, phases = refs[peers + 3 :]
         every[:count] = own_ref[...]
         edges[:count] = own_edge[...]
         store_spectra(s_ref, gather_rows(inputs, table_ref, me), every, edges, count)
-        correlate(s_ref, me, picks, every, edges, table_ref, phases, outs)
+        correlate(s_ref, picks, every, edges, phases)
+        invert_columns(s_ref, me, phases, table_ref, {k: near.at[k] for k in range(2)})
 
     return pl.pallas_call(
         body,
         in_specs=[pl.BlockSpec(memory_space=pltpu.SMEM)] * 3
         + [pl.BlockSpec(memory_space=pltpu.VMEM)] * (peers + 3),
-        out_specs=[pl.BlockSpec(memory_space=pltpu.VMEM)] * (peers // 2 + 2),
-        out_shape=[jax.ShapeDtypeStruct((2, slots, double, rows), jnp.bfloat16)] * (peers // 2)
-        + [
+        out_specs=[pl.BlockSpec(memory_space=pltpu.VMEM)] * 4,
+        out_shape=[
+            jax.ShapeDtypeStruct((2, slots, double, rows), jnp.bfloat16),
             jax.ShapeDtypeStruct((2 * count, 2, block, height), jnp.bfloat16),
             jax.ShapeDtypeStruct((2 * count, 2, 16, height), jnp.bfloat16),
+            jax.ShapeDtypeStruct((2 * slots, block, height), jnp.bfloat16),
         ],
-        scratch_shapes=[pltpu.VMEM((2 * slots, block, height), jnp.bfloat16)],
         compiler_params=params(),
         cost_estimate=cost(4 * (count + slots) * double * height * height, 8 * height * height),
         name="partner_slots",
     )(*place, theirs, *pieces, table, spectra, edge)
 
 
-def own_slots(place, pairs, table, spectra, edge, peers):
+def own_slots(place, pairs, table, spectra, edge, phases, peers):
     block, height = spectra.shape[2:]
     rows = height // peers
     slots = pairs.shape[1]
 
-    def body(half_ref, me_ref, pairs_ref, table_ref, every, edges, *refs):
+    def body(half_ref, me_ref, pairs_ref, table_ref, every, edges, theirs, out_ref, *refs):
+        s_ref = (half_ref, me_ref)
+        far, work = refs[:-1], refs[-1]
         picks = [[pairs_ref[0, p, i] for i in range(2)] for p in range(slots)]
-        out_ref, phases = refs
-        outs = [out_ref.at[k] for k in range(peers)]
-        correlate((half_ref, me_ref), 0, picks, every, edges, table_ref, phases, outs)
+        if far:
+            outs = {k: far[k - 2] for k in range(2, peers)}
+            invert_columns(s_ref, me_ref[0], theirs, table_ref, outs)
+        correlate(s_ref, picks, every, edges, work)
+        invert_columns(s_ref, 0, work, table_ref, {k: out_ref.at[k] for k in range(peers)})
 
     return pl.pallas_call(
         body,
         in_specs=[pl.BlockSpec(memory_space=pltpu.SMEM)] * 3
-        + [pl.BlockSpec(memory_space=pltpu.VMEM)] * 3,
-        out_specs=pl.BlockSpec(memory_space=pltpu.VMEM),
-        out_shape=jax.ShapeDtypeStruct((peers, slots, 2 * block, rows), jnp.bfloat16),
+        + [pl.BlockSpec(memory_space=pltpu.VMEM)] * 4,
+        out_specs=[pl.BlockSpec(memory_space=pltpu.VMEM)] * (peers - 1),
+        out_shape=[
+            jax.ShapeDtypeStruct((peers, slots, 2 * block, rows), jnp.bfloat16),
+            *[jax.ShapeDtypeStruct((slots, 2 * block, rows), jnp.bfloat16)] * (peers - 2),
+        ],
         scratch_shapes=[pltpu.VMEM((2 * slots, block, height), jnp.bfloat16)],
         compiler_params=params(),
         cost_estimate=cost(8 * slots * block * height * height, 8 * height * height),
         name="own_slots",
-    )(*place, pairs, table, spectra, edge)
+    )(*place, pairs, table, spectra, edge, phases)
 
 
 def own_surfaces(half, own, table):
@@ -373,9 +402,9 @@
     )(scalar(half), own, table)
 
 
-def surfaces_of(half, me, counts, part, came, swapped, table):
-    peers = 2 * len(came)
-    slots, double, rows = swapped[0].shape
+def surfaces_of(half, me, counts, part, near, other, table):
+    peers = 1 + len(other)
+    slots, double, rows = other[0].shape
     width = table.shape[0]
     span = peers * double
 
@@ -384,7 +413,7 @@
         table_ref, out_ref, work = refs[peers:]
         for k in range(peers):
             place = pl.multiple_of((me_ref[0] ^ k) * double, double)
-            piece = other_refs[k][0] if k % 2 else other_refs[k][0, 0]
+            piece = other_refs[k][0] if k else other_refs[k][0, 0]
             work[pl.ds(place, double), :] = piece
         rest = lax.dot_general(
             work[...], table_ref[...], (((0,), (0,)), ((), ())), preferred_element_type=jnp.float32
@@ -394,7 +423,6 @@
 
     pair = pl.BlockSpec((1, 1, double, rows), lambda p, half, me, counts: (0, p, 0, 0))
     piece = pl.BlockSpec((1, double, rows), lambda p, half, me, counts: (p, 0, 0))
-    other = [swapped[k // 2] if k % 2 else came[k // 2] for k in range(peers)]
     plane = pl.BlockSpec((1, rows, width), lambda p, half, me, counts: (p, 0, 0))
     return pl.pallas_call(
         body,
@@ -403,7 +431,8 @@
             grid=(slots,),
             in_specs=[
                 plane,
-                *[pair, piece] * (peers // 2),
+                pair,
+                *[piece] * (peers - 1),
                 pl.BlockSpec((span, width), lambda p, half, me, counts: (1 - half[0], 0)),
             ],
             out_specs=plane,
@@ -413,7 +442,7 @@
         compiler_params=params(),
         cost_estimate=cost(2 * slots * rows * width * span, 8 * slots * rows * width),
         name="surfaces",
-    )(scalar(half), scalar(me), counts, part, *other, table)
+    )(scalar(half), scalar(me), counts, part, near, *other, table)
 
 
 def local(tiles, pairs, counts):
@@ -445,25 +474,25 @@
     down = jnp.asarray(np.tile(hann(height), (8, 1)))
     sideways = jnp.asarray(hann(width)[None, :])
 
-    sent = sent_columns(tiles, down, sideways, table_w, half, me, peers)
+    sent = near_columns(tiles, down, sideways, table_w, half, me, peers)
     arrived = [across(sent[k], k) for k in range(2)]
     *sent, held = lax.optimization_barrier((*sent, half))
-    kept = kept_columns(tiles, down, sideways, table_w, held, me, peers)
+    kept, *sent = rest_columns(tiles, down, sideways, table_w, held, me, peers)
     *sent, kept, pairs = lax.optimization_barrier((*sent, kept, pairs))
-    arrived += [across(sent[k], k) for k in range(2, peers)]
+    arrived += [across(sent[k - 2], k) for k in range(2, peers)]
     mine = along(kept)
 
     table_h = height_table(height)
     theirs = across(pairs, 0)
     place = (scalar(half), scalar(me))
     spectra, edge = own_spectra(place, mine, table_h)
-    *back, spectra, edge = partner_slots(place, theirs, arrived, table_h, spectra, edge)
-    came = [across(back[j], 2 * j) for j in range(peers // 2)]
-    own = along(own_slots(place, pairs, table_h, spectra, edge, peers))
-    part = own_surfaces(half, own, table_w)
-    came[-1], part = lax.optimization_barrier((came[-1], part))
-    swapped = [swap(value[1]) for value in came]
-    return surfaces_of(half, me, counts, part, came, swapped, table_w)
+    near, spectra, edge, phases = partner_slots(place, theirs, arrived, table_h, spectra, edge)
+    near = across(near, 0)
+    own, *far = own_slots(place, pairs, table_h, spectra, edge, phases, peers)
+    far = [across(far[k - 2], k) for k in range(2, peers)]
+    part = own_surfaces(half, along(own), table_w)
+    *far, part = lax.optimization_barrier((*far, part))
+    return surfaces_of(half, me, counts, part, near, [swap(near[1]), *far], table_w)
 
 
 def solution(mesh):

time: 67.3 us -> 64.7 us (0.961)
  waiting for transfers between devices: 17.1 us -> 10.9 us
  starting transfers between devices: 22.5 us -> 24.9 us
  local copies, waits for them, and re-layouts: 7.3 us -> 9.35 us
  Pallas kernels: 19.2 us -> 18.4 us
    ppermute x7 -> x8, waiting for transfers between devices: 16.5 us -> 7.65 us  [across(): return lax.ppermute(value, axes, moves)]
    all_to_all x2, waiting for transfers between devices: 0.01 us -> 3.26 us  [along(): return lax.all_to_all(blocks, 'rows', split_axis=0, concat_axis=0)]
    unnamed x22, local copies, waits for them, and re-layouts: 6.63 us -> 9.34 us
    ppermute x7 -> x8, starting transfers between devices: 15.5 us -> 17.9 us  [across(): return lax.ppermute(value, axes, moves)]
    pallas_call x2, Pallas kernels: 7.24 us -> 6.52 us  [the longest x1 4.12 us: near_columns(): pl.pallas_call(body, grid_spec=pltpu.PrefetchScalarGridSpec(num_scalar_pr...]
    ppermute x2 -> x1, waiting for transfers between devices: 0.68 us -> 0.01 us  [swap(): return lax.ppermute(value, 'rows', [(r, r ^ 1) for r in range(peers)])]
    pallas_call x1, Pallas kernels: 3.65 us -> 2.98 us  [partner_slots(): pl.pallas_call(body, in_specs=[pl.BlockSpec(memory_space=pltpu.SMEM)] * 3...]
  transfers between devices with their start and end apart: 11 -> 11, of which waited for: 4 -> 4; matrix products, arithmetic and copies ran while one was open for 1% -> 0% of each run, Pallas kernels for 13% -> 14%
where the time goes in v8:
time: 64.7 us; the launch traced here: 64.3 us
  starting transfers between devices  24.9 us (38%)
  Pallas kernels  18.4 us (28%)
  waiting for transfers between devices  10.9 us (17%)
  local copies, waits for them, and re-layouts  9.35 us (14%)
  between operations  0.79 us (1%)
    ppermute x8, starting transfers between devices, across(): return lax.ppermute(value, axes, moves)  17.9 us
    unnamed x22, local copies, waits for them, and re-layouts  9.34 us
    ppermute x8, waiting for transfers between devices, across(): return lax.ppermute(value, axes, moves)  7.65 us
    all_to_all x2, starting transfers between devices, along(): return lax.all_to_all(blocks, 'rows', split_axis=0, concat_axis=0)  6.94 us
    pallas_call x1, Pallas kernels, near_columns(): pl.pallas_call(body, grid_spec=pltpu.PrefetchScalarGridSpec(num_scalar_pr...  4.12 us
    pallas_call x1, Pallas kernels, own_slots(): pl.pallas_call(body, in_specs=[pl.BlockSpec(memory_space=pltpu.SMEM)] * 3...  3.56 us
    all_to_all x2, waiting for transfers between devices, along(): return lax.all_to_all(blocks, 'rows', split_axis=0, concat_axis=0)  3.26 us
    pallas_call x1, Pallas kernels, partner_slots(): pl.pallas_call(body, in_specs=[pl.BlockSpec(memory_space=pltpu.SMEM)] * 3...  2.98 us
  transfers between devices with their start and end apart: 11, of which 4 were waited for; matrix products, arithmetic and copies ran while one was open for 0% of the time, Pallas kernels for 14%

profile of v8, /device:TPU:0, one launch (start us, length us, event | category | flops | bytes accessed | tf_op | source)
XLA Modules:
  0.0 64.3 jit_solution(17565446181835442709)
XLA Ops:
  0.0 4.1 %near_columns.1 = (bf16[2,128,256]{2,1,0:T(8,128)(2,1)}, bf16[2,128,256]{2,1,0:T(8,128)(2,1)}) custom-call(s32[1]{0:T(128)} %bitcast.half_ref, s32[1]{0:T(128)} %bitcast.1.me_ref, f32[2,256,1024]{2,1,0:T(8,128)} %tile_ref.1, f32[8,1024]{1,0:T(8,128)} %constant.36.clone.down_ref, f32[1,1024]{1,0:T(1,128)} %constant.37.clone.across_ref, ...), custom_call_target="tpu_custom_call" | custom-call | flops 268435456 | bytes 2621440 | tf_op jit(solution)/shard_map/near_columns/pallas_call | solution.py:119
  4.1 4.1 %collective-permute-start.1 = (bf16[2,128,256]{2,1,0:T(8,128)(2,1)}, bf16[2,128,256]{2,1,0:T(8,128)(2,1)S(1)}, u32[]{:S(2)}, u32[]{:S(2)}) collective-permute-start(bf16[2,128,256]{2,1,0:T(8,128)(2,1)} %get-tuple-element.27), channel_id=1, source_target_pairs={{0,8},{1,9},{2,10},{3,11},{4,12},{5,13},{6,14},{7,15},{8,0},{9,1},... | collective-permute-start | bytes 393224 | tf_op jit(solution)/shard_map/ppermute | solution.py:465
  8.3 1.6 %copy-done.3 = f32[2,256,1024]{2,1,0:T(8,128)S(1)} copy-done((f32[2,256,1024]{2,1,0:T(8,128)S(1)}, f32[2,256,1024]{2,1,0:T(8,128)}, u32[]{:S(2)}) %copy-start.3) | copy-done | bytes 2097176
  9.9 2.4 %rest_columns.1 = (bf16[4,2,128,256]{3,2,1,0:T(8,128)(2,1)}, bf16[2,128,256]{2,1,0:T(8,128)(2,1)S(1)}, bf16[2,128,256]{2,1,0:T(8,128)(2,1)S(1)}) custom-call(s32[1]{0:T(128)} %bitcast.2.half_ref, s32[1]{0:T(128)} %bitcast.1.me_ref, f32[2,256,1024]{2,1,0:T(8,128)S(1)} %copy-done.3, f32[8,1024]{1,0:T(8,128)S(1)} %copy-done.4, f32[1,1024]{1,0:T(1,128)S(1)} %copy-done.5, ...), custom_call_target="tpu_custom_call" | custom-call | flops 805306368 | bytes 4194304 | tf_op jit(solution)/shard_map/rest_columns/pallas_call | solution.py:165
  12.3 3.5 %all-to-all-start = ((bf16[4,2,128,256]{3,2,1,0:T(8,128)(2,1)}), bf16[4,2,128,256]{3,2,1,0:T(8,128)(2,1)S(1)}, u32[]{:S(2)}, u32[]{:S(2)}) async-start(bf16[4,2,128,256]{3,2,1,0:T(8,128)(2,1)} %get-tuple-element.36), calls=%async_computation | async-start | bytes 1048576 | tf_op jit(solution)/shard_map/all_to_all | solution.py:468
  15.8 3.5 %collective-permute-start.3 = (bf16[2,128,256]{2,1,0:T(8,128)(2,1)S(1)}, bf16[2,128,256]{2,1,0:T(8,128)(2,1)S(1)}, u32[]{:S(2)}, u32[]{:S(2)}) collective-permute-start(bf16[2,128,256]{2,1,0:T(8,128)(2,1)S(1)} %get-tuple-element.34), channel_id=1, source_target_pairs={{0,10},{1,11},{2,8},{3,9},{4,14},{5,15},{6,12},{7,13},{8,2},{9,3},... | collective-permute-start | bytes 393224 | tf_op jit(solution)/shard_map/ppermute | solution.py:465
  19.5 2.5 %collective-permute-start = (s32[1,2,2]{2,1,0:T(2,128)S(1)}, s32[1,2,2]{2,1,0:T(2,128)S(1)}, u32[]{:S(2)}, u32[]{:S(2)}) collective-permute-start(s32[1,2,2]{2,1,0:T(2,128)S(1)} %copy-done.6), channel_id=1, source_target_pairs={{0,8},{1,9},{2,10},{3,11},{4,12},{5,13},{6,14},{7,15},{8,0},{9,1},... | collective-permute-start | bytes 56 | tf_op jit(solution)/shard_map/ppermute | solution.py:465
  23.8 0.9 %copy-done.9 = f32[32,1024]{1,0:T(8,128)S(1)} copy-done((f32[32,1024]{1,0:T(8,128)S(1)}, f32[32,1024]{1,0:T(8,128)}, u32[]{:S(2)}) %copy-start.9) | copy-done | bytes 131096
  25.6 1.1 %height_table.1.table_ref.refs_4_ = bf16[1024,2048]{1,0:T(8,128)(2,1)S(1)} custom-call(f32[32,1024]{1,0:T(8,128)S(1)} %copy-done.7, f32[32,1024]{1,0:T(8,128)S(1)} %copy-done.8, f32[32,1024]{1,0:T(8,128)S(1)} %copy-done.9, f32[32,1024]{1,0:T(8,128)S(1)} %copy-done.10), custom_call_target="tpu_custom_call" | custom-call | flops 8589934592 | bytes 4194304 | tf_op jit(solution)/shard_map/height_table/pallas_call | solution.py:53
  26.7 1.9 %copy-done.1 = bf16[1024,2048]{1,0:T(8,128)(2,1)} copy-done((bf16[1024,2048]{1,0:T(8,128)(2,1)}, bf16[1024,2048]{1,0:T(8,128)(2,1)S(1)}, u32[]{:S(2)}) %copy-start.1) | copy-done | bytes 4194328
  28.7 2.2 %copy-done.2 = bf16[1024,2048]{1,0:T(8,128)(2,1)S(1)} copy-done((bf16[1024,2048]{1,0:T(8,128)(2,1)S(1)}, bf16[1024,2048]{1,0:T(8,128)(2,1)}, u32[]{:S(2)}) %copy-start.2) | copy-done | bytes 4194328
  30.9 1.2 %own_spectra.1 = (bf16[2,2,64,1024]{3,2,1,0:T(8,128)(2,1)S(1)}, bf16[2,2,16,1024]{3,2,1,0:T(8,128)(2,1)S(1)}) custom-call(s32[1]{0:T(128)} %bitcast.half_ref, s32[1]{0:T(128)} %bitcast.1.me_ref, bf16[4,2,128,256]{3,2,1,0:T(8,128)(2,1)S(1)} %all-to-all-done.pieces_ref, bf16[1024,2048]{1,0:T(8,128)(2,1)S(1)} %copy-done.2), custom_call_target="tpu_custom_call" | custom-call | flops 1073741824 | bytes 8388608 | tf_op jit(solution)/shard_map/own_spectra/pallas_call | solution.py:290
  32.2 3.0 %partner_slots.1 = (bf16[2,2,128,256]{3,2,1,0:T(8,128)(2,1)S(1)}, bf16[4,2,64,1024]{3,2,1,0:T(8,128)(2,1)S(1)}, bf16[4,2,16,1024]{3,2,1,0:T(8,128)(2,1)S(1)}, bf16[4,64,1024]{2,1,0:T(8,128)(2,1)S(1)}) custom-call(s32[1]{0:T(128)} %bitcast.half_ref, s32[1]{0:T(128)} %bitcast.1.me_ref, s32[1,2,2]{2,1,0:T(2,128)S(1)} %collective-permute-done.theirs_ref, ...), custom_call_target="tpu_custom_call" | custom-call | flops 2147483648 | bytes 8388608 | tf_op jit(solution)/shard_map/partner_slots/pallas_call | solution.py:326
  35.2 3.9 %collective-permute-start.7 = (bf16[2,2,128,256]{3,2,1,0:T(8,128)(2,1)S(1)}, bf16[2,2,128,256]{3,2,1,0:T(8,128)(2,1)S(1)}, u32[]{:S(2)}, u32[]{:S(2)}) collective-permute-start(bf16[2,2,128,256]{3,2,1,0:T(8,128)(2,1)S(1)} %get-tuple-element.46), channel_id=1, source_target_pairs={{0,8},{1,9},{2,10},{3,11},{4,12},{5,13},{6,14},{7,15},{8,0},{9,1},... | collective-permute-start | bytes 786440 | tf_op jit(solution)/shard_map/ppermute | solution.py:465
  39.1 3.6 %own_slots.1 = (bf16[4,2,128,256]{3,2,1,0:T(8,128)(2,1)}, bf16[2,128,256]{2,1,0:T(8,128)(2,1)}, bf16[2,128,256]{2,1,0:T(8,128)(2,1)S(1)}) custom-call(s32[1]{0:T(128)} %bitcast.half_ref, s32[1]{0:T(128)} %bitcast.1.me_ref, s32[1,2,2]{2,1,0:T(2,128)S(1)} %copy-done.6, bf16[1024,2048]{1,0:T(8,128)(2,1)S(1)} %copy-done.2, ...), custom_call_target="tpu_custom_call" | custom-call | flops 1073741824 | bytes 8388608 | tf_op jit(solution)/shard_map/own_slots/pallas_call | solution.py:358
  42.6 3.5 %all-to-all-start.1 = ((bf16[4,2,128,256]{3,2,1,0:T(8,128)(2,1)}), bf16[4,2,128,256]{3,2,1,0:T(8,128)(2,1)S(1)}, u32[]{:S(2)}, u32[]{:S(2)}) async-start(bf16[4,2,128,256]{3,2,1,0:T(8,128)(2,1)} %get-tuple-element.44), calls=%async_computation.1 | async-start | bytes 1048576 | tf_op jit(solution)/shard_map/all_to_all | solution.py:468
  46.1 1.4 %collective-permute-start.5 = (bf16[2,128,256]{2,1,0:T(8,128)(2,1)}, bf16[2,128,256]{2,1,0:T(8,128)(2,1)S(1)}, u32[]{:S(2)}, u32[]{:S(2)}) collective-permute-start(bf16[2,128,256]{2,1,0:T(8,128)(2,1)} %get-tuple-element.42), channel_id=1, source_target_pairs={{0,10},{1,11},{2,8},{3,9},{4,14},{5,15},{6,12},{7,13},{8,2},{9,3},... | collective-permute-start | bytes 393224 | tf_op jit(solution)/shard_map/ppermute | solution.py:465
  47.6 2.2 %collective-permute-start.6 = (bf16[2,128,256]{2,1,0:T(8,128)(2,1)S(1)}, bf16[2,128,256]{2,1,0:T(8,128)(2,1)S(1)}, u32[]{:S(2)}, u32[]{:S(2)}) collective-permute-start(bf16[2,128,256]{2,1,0:T(8,128)(2,1)S(1)} %get-tuple-element.43), channel_id=1, source_target_pairs={{0,11},{1,10},{2,9},{3,8},{4,15},{5,14},{6,13},{7,12},{8,3},{9,2},... | collective-permute-start | bytes 393224 | tf_op jit(solution)/shard_map/ppermute | solution.py:465
  49.8 1.3 %collective-permute-done.7.refs_0_ = bf16[2,2,128,256]{3,2,1,0:T(8,128)(2,1)S(1)} collective-permute-done((bf16[2,2,128,256]{3,2,1,0:T(8,128)(2,1)S(1)}, bf16[2,2,128,256]{3,2,1,0:T(8,128)(2,1)S(1)}, u32[]{:S(2)}, u32[]{:S(2)}) %collective-permute-start.7) | collective-permute-done | bytes 262176 | tf_op jit(solution)/shard_map/ppermute | solution.py:465
  51.8 3.3 %all-to-all-done.1.own_ref = bf16[4,2,128,256]{3,2,1,0:T(8,128)(2,1)S(1)} async-done(((bf16[4,2,128,256]{3,2,1,0:T(8,128)(2,1)}), bf16[4,2,128,256]{3,2,1,0:T(8,128)(2,1)S(1)}, u32[]{:S(2)}, u32[]{:S(2)}) %all-to-all-start.1) | async-done | bytes 524320 | tf_op jit(solution)/shard_map/all_to_all | solution.py:468
  55.0 1.0 %own_surfaces.1.part_ref = f32[2,256,1024]{2,1,0:T(8,128)S(1)} custom-call(s32[1]{0:T(128)} %bitcast.half_ref, bf16[4,2,128,256]{3,2,1,0:T(8,128)(2,1)S(1)} %all-to-all-done.1.own_ref, bf16[1024,1024]{1,0:T(8,128)(2,1)S(1)} %copy-done), custom_call_target="tpu_custom_call" | custom-call | flops 536870912 | bytes 2097152 | tf_op jit(solution)/shard_map/own_surfaces/pallas_call | solution.py:387
  56.0 3.6 %collective-permute-done.5.refs_2_ = bf16[2,128,256]{2,1,0:T(8,128)(2,1)S(1)} collective-permute-done((bf16[2,128,256]{2,1,0:T(8,128)(2,1)}, bf16[2,128,256]{2,1,0:T(8,128)(2,1)S(1)}, u32[]{:S(2)}, u32[]{:S(2)}) %collective-permute-start.5) | collective-permute-done | bytes 131104 | tf_op jit(solution)/shard_map/ppermute | solution.py:465
  59.7 2.7 %collective-permute-done.6.refs_3_ = bf16[2,128,256]{2,1,0:T(8,128)(2,1)S(1)} collective-permute-done((bf16[2,128,256]{2,1,0:T(8,128)(2,1)S(1)}, bf16[2,128,256]{2,1,0:T(8,128)(2,1)S(1)}, u32[]{:S(2)}, u32[]{:S(2)}) %collective-permute-start.6) | collective-permute-done | bytes 131104 | tf_op jit(solution)/shard_map/ppermute | solution.py:465
  62.4 2.0 %surfaces.1 = f32[2,256,1024]{2,1,0:T(8,128)} custom-call(s32[1]{0:T(128)} %bitcast.half_ref, s32[1]{0:T(128)} %bitcast.1.me_ref, s32[1]{0:T(128)S(6)} %copy.11.counts_ref, f32[2,256,1024]{2,1,0:T(8,128)S(1)} %own_surfaces.1.part_ref, bf16[2,2,128,256]{3,2,1,0:T(8,128)(2,1)S(1)} %collective-permute-done.7.refs_0_, ...), custom_call_target="tpu_custom_call" | custom-call | flops 536870912 | bytes 4194304 | tf_op jit(solution)/shard_map/surfaces/pallas_call | solution.py:427
  (29 shorter events, 3.0 us)
Async XLA Ops:
  0.0 8.3 %copy-start = (bf16[1024,1024]{1,0:T(8,128)(2,1)S(1)}, bf16[1024,1024]{1,0:T(8,128)(2,1)}, u32[]{:S(2)}) copy-start(bf16[1024,1024]{1,0:T(8,128)(2,1)} %constant.35.clone.table_hbm.table_ref.refs_4_) | copy-start | bytes 6291460
  0.0 8.3 %copy-start.4 = (f32[8,1024]{1,0:T(8,128)S(1)}, f32[8,1024]{1,0:T(8,128)}, u32[]{:S(2)}) copy-start(f32[8,1024]{1,0:T(8,128)} %constant.36.clone.down_ref) | copy-start | bytes 98308
  0.0 8.3 %copy-start.5 = (f32[1,1024]{1,0:T(1,128)S(1)}, f32[1,1024]{1,0:T(1,128)}, u32[]{:S(2)}) copy-start(f32[1,1024]{1,0:T(1,128)} %constant.37.clone.across_ref) | copy-start | bytes 12292
  4.1 28.0 %collective-permute-start.1 = (bf16[2,128,256]{2,1,0:T(8,128)(2,1)}, bf16[2,128,256]{2,1,0:T(8,128)(2,1)S(1)}, u32[]{:S(2)}, u32[]{:S(2)}) collective-permute-start(bf16[2,128,256]{2,1,0:T(8,128)(2,1)} %get-tuple-element.27), channel_id=1, source_target_pairs={{0,8},{1,9},{2,10},{3,11},{4,12},{5,13},{6,14},{7,15},{8,0},{9,1},... | collective-permute-start | bytes 393224 | tf_op jit(solution)/shard_map/ppermute | solution.py:465
  8.3 23.9 %collective-permute-start.2 = (bf16[2,128,256]{2,1,0:T(8,128)(2,1)}, bf16[2,128,256]{2,1,0:T(8,128)(2,1)S(1)}, u32[]{:S(2)}, u32[]{:S(2)}) collective-permute-start(bf16[2,128,256]{2,1,0:T(8,128)(2,1)} %get-tuple-element.28), channel_id=1, source_target_pairs={{0,9},{1,8},{2,11},{3,10},{4,13},{5,12},{6,15},{7,14},{8,1},{9,0},... | collective-permute-start | bytes 393224 | tf_op jit(solution)/shard_map/ppermute | solution.py:465
  8.3 1.6 %copy-start.3 = (f32[2,256,1024]{2,1,0:T(8,128)S(1)}, f32[2,256,1024]{2,1,0:T(8,128)}, u32[]{:S(2)}) copy-start(f32[2,256,1024]{2,1,0:T(8,128)} %tile_ref.1) | copy-start | bytes 6291460
  9.9 9.6 %copy-start.6 = (s32[1,2,2]{2,1,0:T(2,128)S(1)}, s32[1,2,2]{2,1,0:T(2,128)}, u32[]{:S(2)}) copy-start(s32[1,2,2]{2,1,0:T(2,128)} %pairs_ref) | copy-start | bytes 52
  12.3 16.4 %all-to-all-start = ((bf16[4,2,128,256]{3,2,1,0:T(8,128)(2,1)}), bf16[4,2,128,256]{3,2,1,0:T(8,128)(2,1)S(1)}, u32[]{:S(2)}, u32[]{:S(2)}) async-start(bf16[4,2,128,256]{3,2,1,0:T(8,128)(2,1)} %get-tuple-element.36), calls=%async_computation | async-start | bytes 1048576 | tf_op jit(solution)/shard_map/all_to_all | solution.py:468
  15.8 16.4 %collective-permute-start.3 = (bf16[2,128,256]{2,1,0:T(8,128)(2,1)S(1)}, bf16[2,128,256]{2,1,0:T(8,128)(2,1)S(1)}, u32[]{:S(2)}, u32[]{:S(2)}) collective-permute-start(bf16[2,128,256]{2,1,0:T(8,128)(2,1)S(1)} %get-tuple-element.34), channel_id=1, source_target_pairs={{0,10},{1,11},{2,8},{3,9},{4,14},{5,15},{6,12},{7,13},{8,2},{9,3},... | collective-permute-start | bytes 393224 | tf_op jit(solution)/shard_map/ppermute | solution.py:465
  19.2 12.9 %collective-permute-start.4 = (bf16[2,128,256]{2,1,0:T(8,128)(2,1)S(1)}, bf16[2,128,256]{2,1,0:T(8,128)(2,1)S(1)}, u32[]{:S(2)}, u32[]{:S(2)}) collective-permute-start(bf16[2,128,256]{2,1,0:T(8,128)(2,1)S(1)} %get-tuple-element.35), channel_id=1, source_target_pairs={{0,11},{1,10},{2,9},{3,8},{4,15},{5,14},{6,13},{7,12},{8,3},{9,2},... | collective-permute-start | bytes 393224 | tf_op jit(solution)/shard_map/ppermute | solution.py:465
  19.5 12.7 %collective-permute-start = (s32[1,2,2]{2,1,0:T(2,128)S(1)}, s32[1,2,2]{2,1,0:T(2,128)S(1)}, u32[]{:S(2)}, u32[]{:S(2)}) collective-permute-start(s32[1,2,2]{2,1,0:T(2,128)S(1)} %copy-done.6), channel_id=1, source_target_pairs={{0,8},{1,9},{2,10},{3,11},{4,12},{5,13},{6,14},{7,15},{8,0},{9,1},... | collective-permute-start | bytes 56 | tf_op jit(solution)/shard_map/ppermute | solution.py:465
  22.0 0.9 %copy-start.7 = (f32[32,1024]{1,0:T(8,128)S(1)}, f32[32,1024]{1,0:T(8,128)}, u32[]{:S(2)}) copy-start(f32[32,1024]{1,0:T(8,128)} %constant.38.clone.rc_ref) | copy-start | bytes 393220
  22.9 0.9 %copy-start.8 = (f32[32,1024]{1,0:T(8,128)S(1)}, f32[32,1024]{1,0:T(8,128)}, u32[]{:S(2)}) copy-start(f32[32,1024]{1,0:T(8,128)} %constant.39.clone.rs_ref) | copy-start | bytes 393220
  23.8 0.9 %copy-start.9 = (f32[32,1024]{1,0:T(8,128)S(1)}, f32[32,1024]{1,0:T(8,128)}, u32[]{:S(2)}) copy-start(f32[32,1024]{1,0:T(8,128)} %constant.40.clone.sc_ref) | copy-start | bytes 393220
  24.7 0.9 %copy-start.10 = (f32[32,1024]{1,0:T(8,128)S(1)}, f32[32,1024]{1,0:T(8,128)}, u32[]{:S(2)}) copy-start(f32[32,1024]{1,0:T(8,128)} %constant.41.clone.ss_ref) | copy-start | bytes 393220
  26.7 1.9 %copy-start.1 = (bf16[1024,2048]{1,0:T(8,128)(2,1)}, bf16[1024,2048]{1,0:T(8,128)(2,1)S(1)}, u32[]{:S(2)}) copy-start(bf16[1024,2048]{1,0:T(8,128)(2,1)S(1)} %height_table.1.table_ref.refs_4_) | copy-start | bytes 12582916
  28.7 2.2 %copy-start.2 = (bf16[1024,2048]{1,0:T(8,128)(2,1)S(1)}, bf16[1024,2048]{1,0:T(8,128)(2,1)}, u32[]{:S(2)}) copy-start(bf16[1024,2048]{1,0:T(8,128)(2,1)} %copy-done.1) | copy-start | bytes 12582916
  35.2 15.9 %collective-permute-start.7 = (bf16[2,2,128,256]{3,2,1,0:T(8,128)(2,1)S(1)}, bf16[2,2,128,256]{3,2,1,0:T(8,128)(2,1)S(1)}, u32[]{:S(2)}, u32[]{:S(2)}) collective-permute-start(bf16[2,2,128,256]{3,2,1,0:T(8,128)(2,1)S(1)} %get-tuple-element.46), channel_id=1, source_target_pairs={{0,8},{1,9},{2,10},{3,11},{4,12},{5,13},{6,14},{7,15},{8,0},{9,1},... | collective-permute-start | bytes 786440 | tf_op jit(solution)/shard_map/ppermute | solution.py:465
  42.6 12.4 %all-to-all-start.1 = ((bf16[4,2,128,256]{3,2,1,0:T(8,128)(2,1)}), bf16[4,2,128,256]{3,2,1,0:T(8,128)(2,1)S(1)}, u32[]{:S(2)}, u32[]{:S(2)}) async-start(bf16[4,2,128,256]{3,2,1,0:T(8,128)(2,1)} %get-tuple-element.44), calls=%async_computation.1 | async-start | bytes 1048576 | tf_op jit(solution)/shard_map/all_to_all | solution.py:468
  46.1 13.6 %collective-permute-start.5 = (bf16[2,128,256]{2,1,0:T(8,128)(2,1)}, bf16[2,128,256]{2,1,0:T(8,128)(2,1)S(1)}, u32[]{:S(2)}, u32[]{:S(2)}) collective-permute-start(bf16[2,128,256]{2,1,0:T(8,128)(2,1)} %get-tuple-element.42), channel_id=1, source_target_pairs={{0,10},{1,11},{2,8},{3,9},{4,14},{5,15},{6,12},{7,13},{8,2},{9,3},... | collective-permute-start | bytes 393224 | tf_op jit(solution)/shard_map/ppermute | solution.py:465
  47.6 14.8 %collective-permute-start.6 = (bf16[2,128,256]{2,1,0:T(8,128)(2,1)S(1)}, bf16[2,128,256]{2,1,0:T(8,128)(2,1)S(1)}, u32[]{:S(2)}, u32[]{:S(2)}) collective-permute-start(bf16[2,128,256]{2,1,0:T(8,128)(2,1)S(1)} %get-tuple-element.43), channel_id=1, source_target_pairs={{0,11},{1,10},{2,9},{3,8},{4,15},{5,14},{6,13},{7,12},{8,3},{9,2},... | collective-permute-start | bytes 393224 | tf_op jit(solution)/shard_map/ppermute | solution.py:465
  51.0 11.3 %collective-permute-start.8 = (bf16[2,128,256]{2,1,0:T(8,128)(2,1)S(1)}, bf16[2,128,256]{2,1,0:T(8,128)(2,1)S(1)}, u32[]{:S(2)}, u32[]{:S(2)}) collective-permute-start(bf16[2,128,256]{2,1,0:T(8,128)(2,1)S(1)} %slice_bitcast_fusion), channel_id=1, source_target_pairs={{0,1},{1,0},{2,3},{3,2},{4,5},{5,4},{6,7},{7,6},{8,9},{9,8},{10,11... | collective-permute-start | bytes 393224 | tf_op jit(solution)/shard_map/ppermute | solution.py:471

commit v9 on v8

--- a/solution.py
+++ b/solution.py
@@ -40,25 +40,25 @@
     rough = 2.0 * math.pi / height * (np.arange(coarse)[:, None] * fine * column % height)
     small = 2.0 * math.pi / height * (np.arange(fine)[:, None] * column % height)
     factor = 1.0 / math.sqrt(height)
-    tables = [np.cos(rough) * factor, np.sin(rough) * factor, np.cos(small), np.sin(small)]
-
-    def body(rc_ref, rs_ref, sc_ref, ss_ref, out_ref):
-        sc, ss = sc_ref[...], ss_ref[...]
-        for a in range(coarse):
-            rc, rs = rc_ref[a : a + 1, :], rs_ref[a : a + 1, :]
-            here = slice(a * fine, (a + 1) * fine)
+    short = [np.cos(small), np.sin(small), np.cos(rough) * factor, np.sin(rough) * factor]
+
+    def body(short_ref, out_ref):
+        sc, ss = short_ref[:fine], short_ref[fine : 2 * fine]
+        for a in range(2 * fine, 2 * fine + coarse):
+            rc, rs = short_ref[a : a + 1, :], short_ref[a + coarse : a + coarse + 1, :]
+            here = slice((a - 2 * fine) * fine, (a - 2 * fine + 1) * fine)
             out_ref[here, :height] = (rc * sc - rs * ss).astype(jnp.bfloat16)
             out_ref[here, height:] = (rs * sc + rc * ss).astype(jnp.bfloat16)
 
     return pl.pallas_call(
         body,
-        in_specs=[pl.BlockSpec(memory_space=pltpu.VMEM)] * 4,
+        in_specs=[pl.BlockSpec(memory_space=pltpu.VMEM)],
         out_specs=pl.BlockSpec(memory_space=pltpu.VMEM),
         out_shape=jax.ShapeDtypeStruct((height, 2 * height), jnp.bfloat16),
         compiler_params=params(),
         cost_estimate=cost(1 << 33, 4 * height * height),
         name="height_table",
-    )(*[jnp.asarray(table, jnp.float32) for table in tables])
+    )(jnp.asarray(np.concatenate(short), jnp.float32))
 
 
 def cost(flops, moved):

time: 64.7 us -> 64.7 us (level)
  waiting for transfers between devices: 10.9 us -> 13.5 us
  local copies, waits for them, and re-layouts: 9.35 us -> 6.77 us
    unnamed x22 -> x16, local copies, waits for them, and re-layouts: 9.34 us -> 6.77 us
    ppermute x8, waiting for transfers between devices: 7.65 us -> 10.2 us  [across(): return lax.ppermute(value, axes, moves)]
  transfers between devices with their start and end apart: 11 -> 11, of which waited for: 4 -> 5; matrix products, arithmetic and copies ran while one was open for 0% -> 0% of each run, Pallas kernels for 14% -> 14%
where the time goes in v9:
time: 64.7 us; the launch traced here: 64.3 us
  starting transfers between devices  25 us (39%)
  Pallas kernels  18.3 us (28%)
  waiting for transfers between devices  13.5 us (21%)
  local copies, waits for them, and re-layouts  6.77 us (10%)
  between operations  0.76 us (1%)
    ppermute x8, starting transfers between devices, across(): return lax.ppermute(value, axes, moves)  18 us
    ppermute x8, waiting for transfers between devices, across(): return lax.ppermute(value, axes, moves)  10.2 us
    all_to_all x2, starting transfers between devices, along(): return lax.all_to_all(blocks, 'rows', split_axis=0, concat_axis=0)  6.94 us
    unnamed x16, local copies, waits for them, and re-layouts  6.77 us
    pallas_call x1, Pallas kernels, near_columns(): pl.pallas_call(body, grid_spec=pltpu.PrefetchScalarGridSpec(num_scalar_pr...  4.11 us
    pallas_call x1, Pallas kernels, own_slots(): pl.pallas_call(body, in_specs=[pl.BlockSpec(memory_space=pltpu.SMEM)] * 3...  3.56 us
    all_to_all x2, waiting for transfers between devices, along(): return lax.all_to_all(blocks, 'rows', split_axis=0, concat_axis=0)  3.27 us
    pallas_call x1, Pallas kernels, partner_slots(): pl.pallas_call(body, in_specs=[pl.BlockSpec(memory_space=pltpu.SMEM)] * 3...  2.98 us
  transfers between devices with their start and end apart: 11, of which 5 were waited for; matrix products, arithmetic and copies ran while one was open for 0% of the time, Pallas kernels for 14%

profile of v9, /device:TPU:0, one launch (start us, length us, event | category | flops | bytes accessed | tf_op | source)
XLA Modules:
  0.0 64.3 jit_solution(4950685216631746375)
XLA Ops:
  0.0 4.1 %near_columns.1 = (bf16[2,128,256]{2,1,0:T(8,128)(2,1)}, bf16[2,128,256]{2,1,0:T(8,128)(2,1)}) custom-call(s32[1]{0:T(128)} %bitcast.half_ref, s32[1]{0:T(128)} %bitcast.1.me_ref, f32[2,256,1024]{2,1,0:T(8,128)} %tile_ref.1, f32[8,1024]{1,0:T(8,128)} %constant.30.clone.down_ref, f32[1,1024]{1,0:T(1,128)} %constant.31.clone.across_ref, ...), custom_call_target="tpu_custom_call" | custom-call | flops 268435456 | bytes 2621440 | tf_op jit(solution)/shard_map/near_columns/pallas_call | solution.py:119
  4.1 4.1 %collective-permute-start.1 = (bf16[2,128,256]{2,1,0:T(8,128)(2,1)}, bf16[2,128,256]{2,1,0:T(8,128)(2,1)S(1)}, u32[]{:S(2)}, u32[]{:S(2)}) collective-permute-start(bf16[2,128,256]{2,1,0:T(8,128)(2,1)} %get-tuple-element.27), channel_id=1, source_target_pairs={{0,8},{1,9},{2,10},{3,11},{4,12},{5,13},{6,14},{7,15},{8,0},{9,1},... | collective-permute-start | bytes 393224 | tf_op jit(solution)/shard_map/ppermute | solution.py:465
  8.3 1.6 %copy-done.3 = f32[2,256,1024]{2,1,0:T(8,128)S(1)} copy-done((f32[2,256,1024]{2,1,0:T(8,128)S(1)}, f32[2,256,1024]{2,1,0:T(8,128)}, u32[]{:S(2)}) %copy-start.3) | copy-done | bytes 2097176
  9.9 2.4 %rest_columns.1 = (bf16[4,2,128,256]{3,2,1,0:T(8,128)(2,1)}, bf16[2,128,256]{2,1,0:T(8,128)(2,1)S(1)}, bf16[2,128,256]{2,1,0:T(8,128)(2,1)S(1)}) custom-call(s32[1]{0:T(128)} %bitcast.2.half_ref, s32[1]{0:T(128)} %bitcast.1.me_ref, f32[2,256,1024]{2,1,0:T(8,128)S(1)} %copy-done.3, f32[8,1024]{1,0:T(8,128)S(1)} %copy-done.4, f32[1,1024]{1,0:T(1,128)S(1)} %copy-done.5, ...), custom_call_target="tpu_custom_call" | custom-call | flops 805306368 | bytes 4194304 | tf_op jit(solution)/shard_map/rest_columns/pallas_call | solution.py:165
  12.3 3.5 %all-to-all-start = ((bf16[4,2,128,256]{3,2,1,0:T(8,128)(2,1)}), bf16[4,2,128,256]{3,2,1,0:T(8,128)(2,1)S(1)}, u32[]{:S(2)}, u32[]{:S(2)}) async-start(bf16[4,2,128,256]{3,2,1,0:T(8,128)(2,1)} %get-tuple-element.36), calls=%async_computation | async-start | bytes 1048576 | tf_op jit(solution)/shard_map/all_to_all | solution.py:468
  15.7 3.5 %collective-permute-start.3 = (bf16[2,128,256]{2,1,0:T(8,128)(2,1)S(1)}, bf16[2,128,256]{2,1,0:T(8,128)(2,1)S(1)}, u32[]{:S(2)}, u32[]{:S(2)}) collective-permute-start(bf16[2,128,256]{2,1,0:T(8,128)(2,1)S(1)} %get-tuple-element.34), channel_id=1, source_target_pairs={{0,10},{1,11},{2,8},{3,9},{4,14},{5,15},{6,12},{7,13},{8,2},{9,3},... | collective-permute-start | bytes 393224 | tf_op jit(solution)/shard_map/ppermute | solution.py:465
  19.4 2.5 %collective-permute-start = (s32[1,2,2]{2,1,0:T(2,128)S(1)}, s32[1,2,2]{2,1,0:T(2,128)S(1)}, u32[]{:S(2)}, u32[]{:S(2)}) collective-permute-start(s32[1,2,2]{2,1,0:T(2,128)S(1)} %copy-done.6), channel_id=1, source_target_pairs={{0,8},{1,9},{2,10},{3,11},{4,12},{5,13},{6,14},{7,15},{8,0},{9,1},... | collective-permute-start | bytes 56 | tf_op jit(solution)/shard_map/ppermute | solution.py:465
  22.0 1.0 %copy-done.7 = f32[128,1024]{1,0:T(8,128)S(1)} copy-done((f32[128,1024]{1,0:T(8,128)S(1)}, f32[128,1024]{1,0:T(8,128)}, u32[]{:S(2)}) %copy-start.7) | copy-done | bytes 524312
  23.0 1.1 %height_table.1.table_ref.refs_4_ = bf16[1024,2048]{1,0:T(8,128)(2,1)S(1)} custom-call(f32[128,1024]{1,0:T(8,128)S(1)} %copy-done.7), custom_call_target="tpu_custom_call" | custom-call | flops 8589934592 | bytes 4194304 | tf_op jit(solution)/shard_map/height_table/pallas_call | solution.py:53
  24.1 1.9 %copy-done.1 = bf16[1024,2048]{1,0:T(8,128)(2,1)} copy-done((bf16[1024,2048]{1,0:T(8,128)(2,1)}, bf16[1024,2048]{1,0:T(8,128)(2,1)S(1)}, u32[]{:S(2)}) %copy-start.1) | copy-done | bytes 4194328
  26.1 2.2 %copy-done.2 = bf16[1024,2048]{1,0:T(8,128)(2,1)S(1)} copy-done((bf16[1024,2048]{1,0:T(8,128)(2,1)S(1)}, bf16[1024,2048]{1,0:T(8,128)(2,1)}, u32[]{:S(2)}) %copy-start.2) | copy-done | bytes 4194328
  28.3 1.2 %own_spectra.1 = (bf16[2,2,64,1024]{3,2,1,0:T(8,128)(2,1)S(1)}, bf16[2,2,16,1024]{3,2,1,0:T(8,128)(2,1)S(1)}) custom-call(s32[1]{0:T(128)} %bitcast.half_ref, s32[1]{0:T(128)} %bitcast.1.me_ref, bf16[4,2,128,256]{3,2,1,0:T(8,128)(2,1)S(1)} %all-to-all-done.pieces_ref, bf16[1024,2048]{1,0:T(8,128)(2,1)S(1)} %copy-done.2), custom_call_target="tpu_custom_call" | custom-call | flops 1073741824 | bytes 8388608 | tf_op jit(solution)/shard_map/own_spectra/pallas_call | solution.py:290
  29.5 2.6 %collective-permute-done.theirs_ref = s32[1,2,2]{2,1,0:T(2,128)S(1)} collective-permute-done((s32[1,2,2]{2,1,0:T(2,128)S(1)}, s32[1,2,2]{2,1,0:T(2,128)S(1)}, u32[]{:S(2)}, u32[]{:S(2)}) %collective-permute-start) | collective-permute-done | bytes 48 | tf_op jit(solution)/shard_map/ppermute | solution.py:465
  32.1 3.0 %partner_slots.1 = (bf16[2,2,128,256]{3,2,1,0:T(8,128)(2,1)S(1)}, bf16[4,2,64,1024]{3,2,1,0:T(8,128)(2,1)S(1)}, bf16[4,2,16,1024]{3,2,1,0:T(8,128)(2,1)S(1)}, bf16[4,64,1024]{2,1,0:T(8,128)(2,1)S(1)}) custom-call(s32[1]{0:T(128)} %bitcast.half_ref, s32[1]{0:T(128)} %bitcast.1.me_ref, s32[1,2,2]{2,1,0:T(2,128)S(1)} %collective-permute-done.theirs_ref, ...), custom_call_target="tpu_custom_call" | custom-call | flops 2147483648 | bytes 8388608 | tf_op jit(solution)/shard_map/partner_slots/pallas_call | solution.py:326
  35.1 4.0 %collective-permute-start.7 = (bf16[2,2,128,256]{3,2,1,0:T(8,128)(2,1)S(1)}, bf16[2,2,128,256]{3,2,1,0:T(8,128)(2,1)S(1)}, u32[]{:S(2)}, u32[]{:S(2)}) collective-permute-start(bf16[2,2,128,256]{3,2,1,0:T(8,128)(2,1)S(1)} %get-tuple-element.46), channel_id=1, source_target_pairs={{0,8},{1,9},{2,10},{3,11},{4,12},{5,13},{6,14},{7,15},{8,0},{9,1},... | collective-permute-start | bytes 786440 | tf_op jit(solution)/shard_map/ppermute | solution.py:465
  39.1 3.6 %own_slots.1 = (bf16[4,2,128,256]{3,2,1,0:T(8,128)(2,1)}, bf16[2,128,256]{2,1,0:T(8,128)(2,1)}, bf16[2,128,256]{2,1,0:T(8,128)(2,1)S(1)}) custom-call(s32[1]{0:T(128)} %bitcast.half_ref, s32[1]{0:T(128)} %bitcast.1.me_ref, s32[1,2,2]{2,1,0:T(2,128)S(1)} %copy-done.6, bf16[1024,2048]{1,0:T(8,128)(2,1)S(1)} %copy-done.2, ...), custom_call_target="tpu_custom_call" | custom-call | flops 1073741824 | bytes 8388608 | tf_op jit(solution)/shard_map/own_slots/pallas_call | solution.py:358
  42.6 3.5 %all-to-all-start.1 = ((bf16[4,2,128,256]{3,2,1,0:T(8,128)(2,1)}), bf16[4,2,128,256]{3,2,1,0:T(8,128)(2,1)S(1)}, u32[]{:S(2)}, u32[]{:S(2)}) async-start(bf16[4,2,128,256]{3,2,1,0:T(8,128)(2,1)} %get-tuple-element.44), calls=%async_computation.1 | async-start | bytes 1048576 | tf_op jit(solution)/shard_map/all_to_all | solution.py:468
  46.1 1.4 %collective-permute-start.5 = (bf16[2,128,256]{2,1,0:T(8,128)(2,1)}, bf16[2,128,256]{2,1,0:T(8,128)(2,1)S(1)}, u32[]{:S(2)}, u32[]{:S(2)}) collective-permute-start(bf16[2,128,256]{2,1,0:T(8,128)(2,1)} %get-tuple-element.42), channel_id=1, source_target_pairs={{0,10},{1,11},{2,8},{3,9},{4,14},{5,15},{6,12},{7,13},{8,2},{9,3},... | collective-permute-start | bytes 393224 | tf_op jit(solution)/shard_map/ppermute | solution.py:465
  47.5 2.2 %collective-permute-start.6 = (bf16[2,128,256]{2,1,0:T(8,128)(2,1)S(1)}, bf16[2,128,256]{2,1,0:T(8,128)(2,1)S(1)}, u32[]{:S(2)}, u32[]{:S(2)}) collective-permute-start(bf16[2,128,256]{2,1,0:T(8,128)(2,1)S(1)} %get-tuple-element.43), channel_id=1, source_target_pairs={{0,11},{1,10},{2,9},{3,8},{4,15},{5,14},{6,13},{7,12},{8,3},{9,2},... | collective-permute-start | bytes 393224 | tf_op jit(solution)/shard_map/ppermute | solution.py:465
  49.7 1.3 %collective-permute-done.7.refs_0_ = bf16[2,2,128,256]{3,2,1,0:T(8,128)(2,1)S(1)} collective-permute-done((bf16[2,2,128,256]{3,2,1,0:T(8,128)(2,1)S(1)}, bf16[2,2,128,256]{3,2,1,0:T(8,128)(2,1)S(1)}, u32[]{:S(2)}, u32[]{:S(2)}) %collective-permute-start.7) | collective-permute-done | bytes 262176 | tf_op jit(solution)/shard_map/ppermute | solution.py:465
  51.7 3.3 %all-to-all-done.1.own_ref = bf16[4,2,128,256]{3,2,1,0:T(8,128)(2,1)S(1)} async-done(((bf16[4,2,128,256]{3,2,1,0:T(8,128)(2,1)}), bf16[4,2,128,256]{3,2,1,0:T(8,128)(2,1)S(1)}, u32[]{:S(2)}, u32[]{:S(2)}) %all-to-all-start.1) | async-done | bytes 524320 | tf_op jit(solution)/shard_map/all_to_all | solution.py:468
  56.0 3.6 %collective-permute-done.5.refs_2_ = bf16[2,128,256]{2,1,0:T(8,128)(2,1)S(1)} collective-permute-done((bf16[2,128,256]{2,1,0:T(8,128)(2,1)}, bf16[2,128,256]{2,1,0:T(8,128)(2,1)S(1)}, u32[]{:S(2)}, u32[]{:S(2)}) %collective-permute-start.5) | collective-permute-done | bytes 131104 | tf_op jit(solution)/shard_map/ppermute | solution.py:465
  59.7 2.7 %collective-permute-done.6.refs_3_ = bf16[2,128,256]{2,1,0:T(8,128)(2,1)S(1)} collective-permute-done((bf16[2,128,256]{2,1,0:T(8,128)(2,1)S(1)}, bf16[2,128,256]{2,1,0:T(8,128)(2,1)S(1)}, u32[]{:S(2)}, u32[]{:S(2)}) %collective-permute-start.6) | collective-permute-done | bytes 131104 | tf_op jit(solution)/shard_map/ppermute | solution.py:465
  62.4 2.0 %surfaces.1 = f32[2,256,1024]{2,1,0:T(8,128)} custom-call(s32[1]{0:T(128)} %bitcast.half_ref, s32[1]{0:T(128)} %bitcast.1.me_ref, s32[1]{0:T(128)S(6)} %copy.8.counts_ref, f32[2,256,1024]{2,1,0:T(8,128)S(1)} %own_surfaces.1.part_ref, bf16[2,2,128,256]{3,2,1,0:T(8,128)(2,1)S(1)} %collective-permute-done.7.refs_0_, ...), custom_call_target="tpu_custom_call" | custom-call | flops 536870912 | bytes 4194304 | tf_op jit(solution)/shard_map/surfaces/pallas_call | solution.py:427
  (23 shorter events, 1.3 us)
Async XLA Ops:
  0.0 8.2 %copy-start = (bf16[1024,1024]{1,0:T(8,128)(2,1)S(1)}, bf16[1024,1024]{1,0:T(8,128)(2,1)}, u32[]{:S(2)}) copy-start(bf16[1024,1024]{1,0:T(8,128)(2,1)} %constant.29.clone.table_hbm.table_ref.refs_4_) | copy-start | bytes 6291460
  0.0 8.2 %copy-start.4 = (f32[8,1024]{1,0:T(8,128)S(1)}, f32[8,1024]{1,0:T(8,128)}, u32[]{:S(2)}) copy-start(f32[8,1024]{1,0:T(8,128)} %constant.30.clone.down_ref) | copy-start | bytes 98308
  0.0 8.2 %copy-start.5 = (f32[1,1024]{1,0:T(1,128)S(1)}, f32[1,1024]{1,0:T(1,128)}, u32[]{:S(2)}) copy-start(f32[1,1024]{1,0:T(1,128)} %constant.31.clone.across_ref) | copy-start | bytes 12292
  4.1 28.0 %collective-permute-start.1 = (bf16[2,128,256]{2,1,0:T(8,128)(2,1)}, bf16[2,128,256]{2,1,0:T(8,128)(2,1)S(1)}, u32[]{:S(2)}, u32[]{:S(2)}) collective-permute-start(bf16[2,128,256]{2,1,0:T(8,128)(2,1)} %get-tuple-element.27), channel_id=1, source_target_pairs={{0,8},{1,9},{2,10},{3,11},{4,12},{5,13},{6,14},{7,15},{8,0},{9,1},... | collective-permute-start | bytes 393224 | tf_op jit(solution)/shard_map/ppermute | solution.py:465
  8.2 23.9 %collective-permute-start.2 = (bf16[2,128,256]{2,1,0:T(8,128)(2,1)}, bf16[2,128,256]{2,1,0:T(8,128)(2,1)S(1)}, u32[]{:S(2)}, u32[]{:S(2)}) collective-permute-start(bf16[2,128,256]{2,1,0:T(8,128)(2,1)} %get-tuple-element.28), channel_id=1, source_target_pairs={{0,9},{1,8},{2,11},{3,10},{4,13},{5,12},{6,15},{7,14},{8,1},{9,0},... | collective-permute-start | bytes 393224 | tf_op jit(solution)/shard_map/ppermute | solution.py:465
  8.3 1.6 %copy-start.3 = (f32[2,256,1024]{2,1,0:T(8,128)S(1)}, f32[2,256,1024]{2,1,0:T(8,128)}, u32[]{:S(2)}) copy-start(f32[2,256,1024]{2,1,0:T(8,128)} %tile_ref.1) | copy-start | bytes 6291460
  9.9 9.6 %copy-start.6 = (s32[1,2,2]{2,1,0:T(2,128)S(1)}, s32[1,2,2]{2,1,0:T(2,128)}, u32[]{:S(2)}) copy-start(s32[1,2,2]{2,1,0:T(2,128)} %pairs_ref) | copy-start | bytes 52
  12.3 13.8 %all-to-all-start = ((bf16[4,2,128,256]{3,2,1,0:T(8,128)(2,1)}), bf16[4,2,128,256]{3,2,1,0:T(8,128)(2,1)S(1)}, u32[]{:S(2)}, u32[]{:S(2)}) async-start(bf16[4,2,128,256]{3,2,1,0:T(8,128)(2,1)} %get-tuple-element.36), calls=%async_computation | async-start | bytes 1048576 | tf_op jit(solution)/shard_map/all_to_all | solution.py:468
  15.7 16.3 %collective-permute-start.3 = (bf16[2,128,256]{2,1,0:T(8,128)(2,1)S(1)}, bf16[2,128,256]{2,1,0:T(8,128)(2,1)S(1)}, u32[]{:S(2)}, u32[]{:S(2)}) collective-permute-start(bf16[2,128,256]{2,1,0:T(8,128)(2,1)S(1)} %get-tuple-element.34), channel_id=1, source_target_pairs={{0,10},{1,11},{2,8},{3,9},{4,14},{5,15},{6,12},{7,13},{8,2},{9,3},... | collective-permute-start | bytes 393224 | tf_op jit(solution)/shard_map/ppermute | solution.py:465
  19.2 12.9 %collective-permute-start.4 = (bf16[2,128,256]{2,1,0:T(8,128)(2,1)S(1)}, bf16[2,128,256]{2,1,0:T(8,128)(2,1)S(1)}, u32[]{:S(2)}, u32[]{:S(2)}) collective-permute-start(bf16[2,128,256]{2,1,0:T(8,128)(2,1)S(1)} %get-tuple-element.35), channel_id=1, source_target_pairs={{0,11},{1,10},{2,9},{3,8},{4,15},{5,14},{6,13},{7,12},{8,3},{9,2},... | collective-permute-start | bytes 393224 | tf_op jit(solution)/shard_map/ppermute | solution.py:465
  19.4 12.6 %collective-permute-start = (s32[1,2,2]{2,1,0:T(2,128)S(1)}, s32[1,2,2]{2,1,0:T(2,128)S(1)}, u32[]{:S(2)}, u32[]{:S(2)}) collective-permute-start(s32[1,2,2]{2,1,0:T(2,128)S(1)} %copy-done.6), channel_id=1, source_target_pairs={{0,8},{1,9},{2,10},{3,11},{4,12},{5,13},{6,14},{7,15},{8,0},{9,1},... | collective-permute-start | bytes 56 | tf_op jit(solution)/shard_map/ppermute | solution.py:465
  22.0 1.0 %copy-start.7 = (f32[128,1024]{1,0:T(8,128)S(1)}, f32[128,1024]{1,0:T(8,128)}, u32[]{:S(2)}) copy-start(f32[128,1024]{1,0:T(8,128)} %constant.32.clone.short_ref) | copy-start | bytes 1572868
  24.1 1.9 %copy-start.1 = (bf16[1024,2048]{1,0:T(8,128)(2,1)}, bf16[1024,2048]{1,0:T(8,128)(2,1)S(1)}, u32[]{:S(2)}) copy-start(bf16[1024,2048]{1,0:T(8,128)(2,1)S(1)} %height_table.1.table_ref.refs_4_) | copy-start | bytes 12582916
  26.1 2.2 %copy-start.2 = (bf16[1024,2048]{1,0:T(8,128)(2,1)S(1)}, bf16[1024,2048]{1,0:T(8,128)(2,1)}, u32[]{:S(2)}) copy-start(bf16[1024,2048]{1,0:T(8,128)(2,1)} %copy-done.1) | copy-start | bytes 12582916
  35.1 15.9 %collective-permute-start.7 = (bf16[2,2,128,256]{3,2,1,0:T(8,128)(2,1)S(1)}, bf16[2,2,128,256]{3,2,1,0:T(8,128)(2,1)S(1)}, u32[]{:S(2)}, u32[]{:S(2)}) collective-permute-start(bf16[2,2,128,256]{3,2,1,0:T(8,128)(2,1)S(1)} %get-tuple-element.46), channel_id=1, source_target_pairs={{0,8},{1,9},{2,10},{3,11},{4,12},{5,13},{6,14},{7,15},{8,0},{9,1},... | collective-permute-start | bytes 786440 | tf_op jit(solution)/shard_map/ppermute | solution.py:465
  42.6 12.4 %all-to-all-start.1 = ((bf16[4,2,128,256]{3,2,1,0:T(8,128)(2,1)}), bf16[4,2,128,256]{3,2,1,0:T(8,128)(2,1)S(1)}, u32[]{:S(2)}, u32[]{:S(2)}) async-start(bf16[4,2,128,256]{3,2,1,0:T(8,128)(2,1)} %get-tuple-element.44), calls=%async_computation.1 | async-start | bytes 1048576 | tf_op jit(solution)/shard_map/all_to_all | solution.py:468
  46.1 13.6 %collective-permute-start.5 = (bf16[2,128,256]{2,1,0:T(8,128)(2,1)}, bf16[2,128,256]{2,1,0:T(8,128)(2,1)S(1)}, u32[]{:S(2)}, u32[]{:S(2)}) collective-permute-start(bf16[2,128,256]{2,1,0:T(8,128)(2,1)} %get-tuple-element.42), channel_id=1, source_target_pairs={{0,10},{1,11},{2,8},{3,9},{4,14},{5,15},{6,12},{7,13},{8,2},{9,3},... | collective-permute-start | bytes 393224 | tf_op jit(solution)/shard_map/ppermute | solution.py:465
  47.5 14.8 %collective-permute-start.6 = (bf16[2,128,256]{2,1,0:T(8,128)(2,1)S(1)}, bf16[2,128,256]{2,1,0:T(8,128)(2,1)S(1)}, u32[]{:S(2)}, u32[]{:S(2)}) collective-permute-start(bf16[2,128,256]{2,1,0:T(8,128)(2,1)S(1)} %get-tuple-element.43), channel_id=1, source_target_pairs={{0,11},{1,10},{2,9},{3,8},{4,15},{5,14},{6,13},{7,12},{8,3},{9,2},... | collective-permute-start | bytes 393224 | tf_op jit(solution)/shard_map/ppermute | solution.py:465
  51.0 11.4 %collective-permute-start.8 = (bf16[2,128,256]{2,1,0:T(8,128)(2,1)S(1)}, bf16[2,128,256]{2,1,0:T(8,128)(2,1)S(1)}, u32[]{:S(2)}, u32[]{:S(2)}) collective-permute-start(bf16[2,128,256]{2,1,0:T(8,128)(2,1)S(1)} %slice_bitcast_fusion), channel_id=1, source_target_pairs={{0,1},{1,0},{2,3},{3,2},{4,5},{5,4},{6,7},{7,6},{8,9},{9,8},{10,11... | collective-permute-start | bytes 393224 | tf_op jit(solution)/shard_map/ppermute | solution.py:471

commit v10 on v9

--- a/solution.py
+++ b/solution.py
@@ -33,7 +33,7 @@
     return table.reshape(width, width).astype(jnp.bfloat16)
 
 
-def height_table(height):
+def height_table(height, after):
     fine = 32
     coarse = height // fine
     column = np.arange(height)[None, :]
@@ -42,7 +42,8 @@
     factor = 1.0 / math.sqrt(height)
     short = [np.cos(small), np.sin(small), np.cos(rough) * factor, np.sin(rough) * factor]
 
-    def body(short_ref, out_ref):
+    def body(short_ref, *refs):
+        out_ref = refs[-1]
         sc, ss = short_ref[:fine], short_ref[fine : 2 * fine]
         for a in range(2 * fine, 2 * fine + coarse):
             rc, rs = short_ref[a : a + 1, :], short_ref[a + coarse : a + coarse + 1, :]
@@ -52,13 +53,14 @@
 
     return pl.pallas_call(
         body,
-        in_specs=[pl.BlockSpec(memory_space=pltpu.VMEM)],
+        in_specs=[pl.BlockSpec(memory_space=pltpu.VMEM)]
+        + [pl.BlockSpec(memory_space=pl.ANY)] * len(after),
         out_specs=pl.BlockSpec(memory_space=pltpu.VMEM),
         out_shape=jax.ShapeDtypeStruct((height, 2 * height), jnp.bfloat16),
         compiler_params=params(),
         cost_estimate=cost(1 << 33, 4 * height * height),
         name="height_table",
-    )(jnp.asarray(np.concatenate(short), jnp.float32))
+    )(jnp.asarray(np.concatenate(short), jnp.float32), *after)
 
 
 def cost(flops, moved):
@@ -142,62 +144,68 @@
     )(scalar(half), scalar(me), tiles, down, across, table)
 
 
-def rest_columns(tiles, down, across, table, half, me, peers):
+def rest_columns(tiles, down, across, table, half, me, first, peers):
     count, rows, width = tiles.shape
     span = table.shape[0] // 2
     block = span // peers
-
-    def body(half_ref, me_ref, tile_ref, down_ref, across_ref, table_ref, *refs):
+    distant = peers - 2
+
+    def body(half_ref, me_ref, first_ref, tile_ref, down_ref, across_ref, table_ref, *refs):
         out_ref, far, work = refs[0], refs[1:-1], refs[-1]
         half, me = half_ref[0], me_ref[0]
+        t = pl.program_id(0)
         shaded = shade(tile_ref[0], down_ref, across_ref)
         for j in range(1, peers // 2):
             start = pl.multiple_of((1 - half) * span + (me // 2 ^ j) * 2 * block, 2 * block)
             work[...] = times_table(table_ref[pl.ds(start, 2 * block), :], shaded)
             for k in range(2):
                 place = pl.multiple_of((me % 2 ^ k) * block, block)
-                far[2 * j - 2 + k][0] = work[pl.ds(place, block), :]
+                for i in range(count):
+
+                    @pl.when(t == i)
+                    def _():
+                        far[i * distant + 2 * j - 2 + k][...] = work[pl.ds(place, block), :]
+
         start = pl.multiple_of(half * span, span)
         y = times_table(table_ref[pl.ds(start, span), :], shaded)
         out_ref[:, 0] = y.reshape(peers, block, rows)
 
-    piece = pl.BlockSpec((1, block, rows), lambda t, half, me: (t, 0, 0))
     return pl.pallas_call(
         body,
         grid_spec=pltpu.PrefetchScalarGridSpec(
-            num_scalar_prefetch=2,
+            num_scalar_prefetch=3,
             grid=(count,),
             in_specs=[
-                pl.BlockSpec((1, rows, width), lambda t, half, me: (t, 0, 0)),
-                pl.BlockSpec((8, rows), lambda t, half, me: (0, me[0])),
-                pl.BlockSpec((1, width), lambda t, half, me: (0, 0)),
-                pl.BlockSpec((width, width), lambda t, half, me: (0, 0)),
+                pl.BlockSpec((1, rows, width), lambda t, half, me, a: ((a[0] + t) % count, 0, 0)),
+                pl.BlockSpec((8, rows), lambda t, half, me, a: (0, me[0])),
+                pl.BlockSpec((1, width), lambda t, half, me, a: (0, 0)),
+                pl.BlockSpec((width, width), lambda t, half, me, a: (0, 0)),
             ],
             out_specs=[
-                pl.BlockSpec((peers, 1, block, rows), lambda t, half, me: (0, t, 0, 0)),
-                *[piece] * (peers - 2),
+                pl.BlockSpec(
+                    (peers, 1, block, rows), lambda t, half, me, a: (0, (a[0] + t) % count, 0, 0)
+                ),
+                *[pl.BlockSpec((block, rows), lambda t, half, me, a: (0, 0))] * (count * distant),
             ],
             scratch_shapes=[pltpu.VMEM((2 * block, rows), jnp.bfloat16)],
         ),
         out_shape=[
             jax.ShapeDtypeStruct((peers, count, block, rows), jnp.bfloat16),
-            *[jax.ShapeDtypeStruct((count, block, rows), jnp.bfloat16)] * (peers - 2),
+            *[jax.ShapeDtypeStruct((block, rows), jnp.bfloat16)] * (count * distant),
         ],
         compiler_params=params(),
         cost_estimate=cost(3 * count * rows * width * span, 4 * tiles.size + 2 * width * width),
         name="rest_columns",
-    )(scalar(half), scalar(me), tiles, down, across, table)
+    )(scalar(half), scalar(me), scalar(first), tiles, down, across, table)
 
 
 def gather_rows(pieces, table_ref, me):
     total = None
     for k, piece in enumerate(pieces):
-        count, block, rows = piece.shape
+        rows = piece.shape[1]
         start = pl.multiple_of((me ^ k) * rows, rows)
         term = jnp.dot(
-            piece[...].reshape(count * block, rows),
-            table_ref[pl.ds(start, rows), :],
-            preferred_element_type=jnp.float32,
+            piece, table_ref[pl.ds(start, rows), :], preferred_element_type=jnp.float32
         )
         total = term if total is None else total + term
     return total
@@ -238,15 +246,15 @@
     )
 
 
-def correlate(s_ref, picks, spectra, edge, phases):
-    slots = len(picks)
-    height = spectra.shape[3]
+def correlate(s_ref, picks, phases):
+    height = phases.shape[2]
     lead = lax.broadcasted_iota(jnp.int32, (16, height), 0)
     packed = (lead == 0) & holds_packed(s_ref)
-    for p in range(slots):
-        a, c = picks[p]
-        q_real, q_imag = normalised(spectra[a, 0], spectra[a, 1], spectra[c, 0], spectra[c, 1])
-        e_real, e_imag = normalised(edge[a, 0], edge[a, 1], edge[c, 0], edge[c, 1])
+    for p, ((left, left_edge, a), (right, right_edge, c)) in enumerate(picks):
+        q_real, q_imag = normalised(left[a, 0], left[a, 1], right[c, 0], right[c, 1])
+        e_real, e_imag = normalised(
+            left_edge[a, 0], left_edge[a, 1], right_edge[c, 0], right_edge[c, 1]
+        )
         phases[2 * p] = q_real
         phases[2 * p + 1] = q_imag
         top_real = q_real[:16].astype(jnp.float32)
@@ -284,7 +292,7 @@
     height = table.shape[0]
 
     def body(half_ref, me_ref, pieces_ref, table_ref, spectra, edge):
-        inputs = [pieces_ref.at[k] for k in range(peers)]
+        inputs = [pieces_ref[k].reshape(count * double, rows) for k in range(peers)]
         store_spectra((half_ref, me_ref), gather_rows(inputs, table_ref, 0), spectra, edge, 0)
 
     return pl.pallas_call(
@@ -302,26 +310,22 @@
     )(*place, pieces, table)
 
 
-def partner_slots(place, theirs, pieces, table, spectra, edge):
-    peers = len(pieces)
-    count, double, rows = pieces[0].shape
+def first_slot(place, theirs, near, far, table, spectra, edge):
+    peers = len(near) + len(far)
+    count, double, rows = near[0].shape
     height = table.shape[0]
     block = double // 2
-    slots = theirs.shape[1]
 
     def body(half_ref, me_ref, theirs_ref, *refs):
         s_ref = (half_ref, me_ref)
         me = me_ref[0]
-        picks = [
-            [(theirs_ref[0, p, i] + count) % (2 * count) for i in range(2)] for p in range(slots)
-        ]
-        inputs, table_ref, own_ref, own_edge = refs[:peers], *refs[peers : peers + 3]
-        near, every, edges, phases = refs[peers + 3 :]
-        every[:count] = own_ref[...]
-        edges[:count] = own_edge[...]
-        store_spectra(s_ref, gather_rows(inputs, table_ref, me), every, edges, count)
-        correlate(s_ref, picks, every, edges, phases)
-        invert_columns(s_ref, me, phases, table_ref, {k: near.at[k] for k in range(2)})
+        left = theirs_ref[0, 0, 0]
+        pieces = [ref[left] for ref in refs[:2]] + [ref[...] for ref in refs[2:peers]]
+        table_ref, own, own_edge, out, lead, lead_edge, phases = refs[peers:]
+        store_spectra(s_ref, gather_rows(pieces, table_ref, me), lead, lead_edge, 0)
+        right = theirs_ref[0, 0, 1] - count
+        correlate(s_ref, [((lead, lead_edge, 0), (own, own_edge, right))], phases)
+        invert_columns(s_ref, me, phases, table_ref, {k: out.at[k] for k in range(2)})
 
     return pl.pallas_call(
         body,
@@ -329,35 +333,95 @@
         + [pl.BlockSpec(memory_space=pltpu.VMEM)] * (peers + 3),
         out_specs=[pl.BlockSpec(memory_space=pltpu.VMEM)] * 4,
         out_shape=[
-            jax.ShapeDtypeStruct((2, slots, double, rows), jnp.bfloat16),
+            jax.ShapeDtypeStruct((2, 1, double, rows), jnp.bfloat16),
+            jax.ShapeDtypeStruct((1, 2, block, height), jnp.bfloat16),
+            jax.ShapeDtypeStruct((1, 2, 16, height), jnp.bfloat16),
+            jax.ShapeDtypeStruct((2, block, height), jnp.bfloat16),
+        ],
+        compiler_params=params(),
+        cost_estimate=cost(8 * double * height * height, 8 * height * height),
+        name="first_slot",
+    )(*place, theirs, *near, *far, table, spectra, edge)
+
+
+def other_slots(place, theirs, near, far, table, spectra, edge, lead, lead_edge, phases):
+    peers = 2 + len(far[0])
+    count, double, rows = near[0].shape
+    height = table.shape[0]
+    block = double // 2
+    slots = theirs.shape[1]
+    rest = count - 1
+
+    def body(half_ref, me_ref, theirs_ref, *refs):
+        s_ref = (half_ref, me_ref)
+        me = me_ref[0]
+        first = theirs_ref[0, 0, 0]
+        near_refs = refs[:2]
+        far_refs = refs[2 : 2 + rest * (peers - 2)]
+        tail = refs[2 + rest * (peers - 2) :]
+        table_ref, own, own_edge, lead_ref, lead_edge_ref, done_ref = tail[:6]
+        out, every, edges, phases_ref = tail[6:]
+        every[:count] = own[...]
+        edges[:count] = own_edge[...]
+        every[count : count + 1] = lead_ref[...]
+        edges[count : count + 1] = lead_edge_ref[...]
+        for i in range(1, count):
+            pieces = [ref[(first + i) % count] for ref in near_refs]
+            pieces += [ref[...] for ref in far_refs[(i - 1) * (peers - 2) : i * (peers - 2)]]
+            store_spectra(s_ref, gather_rows(pieces, table_ref, me), every, edges, count + i)
+        picks = []
+        for p in range(1, slots):
+            a, c = theirs_ref[0, p, 0], theirs_ref[0, p, 1]
+            left = count + (a + count - first) % count
+            right = jnp.where(c < count, count + (c + count - first) % count, c - count)
+            picks.append(((every, edges, left), (every, edges, right)))
+        phases_ref[:2] = done_ref[...]
+        fresh = phases_ref.at[pl.ds(2, 2 * slots - 2)]
+        correlate(s_ref, picks, fresh)
+        invert_columns(s_ref, me, fresh, table_ref, {k: out.at[k] for k in range(2)})
+
+    flat = [piece for pieces in far for piece in pieces]
+    return pl.pallas_call(
+        body,
+        in_specs=[pl.BlockSpec(memory_space=pltpu.SMEM)] * 3
+        + [pl.BlockSpec(memory_space=pltpu.VMEM)] * (8 + len(flat)),
+        out_specs=[pl.BlockSpec(memory_space=pltpu.VMEM)] * 4,
+        out_shape=[
+            jax.ShapeDtypeStruct((2, slots - 1, double, rows), jnp.bfloat16),
             jax.ShapeDtypeStruct((2 * count, 2, block, height), jnp.bfloat16),
             jax.ShapeDtypeStruct((2 * count, 2, 16, height), jnp.bfloat16),
             jax.ShapeDtypeStruct((2 * slots, block, height), jnp.bfloat16),
         ],
         compiler_params=params(),
-        cost_estimate=cost(4 * (count + slots) * double * height * height, 8 * height * height),
-        name="partner_slots",
-    )(*place, theirs, *pieces, table, spectra, edge)
-
-
-def own_slots(place, pairs, table, spectra, edge, phases, peers):
+        cost_estimate=cost(8 * double * height * height, 8 * height * height),
+        name="other_slots",
+    )(*place, theirs, *near, *flat, table, spectra, edge, lead, lead_edge, phases)
+
+
+def own_slots(place, pairs, theirs, table, spectra, edge, phases, peers):
     block, height = spectra.shape[2:]
+    count = spectra.shape[0] // 2
     rows = height // peers
     slots = pairs.shape[1]
 
-    def body(half_ref, me_ref, pairs_ref, table_ref, every, edges, theirs, out_ref, *refs):
+    def body(half_ref, me_ref, pairs_ref, theirs_ref, table_ref, every, edges, done, out_ref, *refs):
         s_ref = (half_ref, me_ref)
         far, work = refs[:-1], refs[-1]
-        picks = [[pairs_ref[0, p, i] for i in range(2)] for p in range(slots)]
+        first = theirs_ref[0, 0, 0]
+        picks = []
+        for p in range(slots):
+            a, c = pairs_ref[0, p, 0], pairs_ref[0, p, 1]
+            right = jnp.where(c < count, c, count + (c - first) % count)
+            picks.append(((every, edges, a), (every, edges, right)))
         if far:
             outs = {k: far[k - 2] for k in range(2, peers)}
-            invert_columns(s_ref, me_ref[0], theirs, table_ref, outs)
-        correlate(s_ref, picks, every, edges, work)
+            invert_columns(s_ref, me_ref[0], done, table_ref, outs)
+        correlate(s_ref, picks, work)
         invert_columns(s_ref, 0, work, table_ref, {k: out_ref.at[k] for k in range(peers)})
 
     return pl.pallas_call(
         body,
-        in_specs=[pl.BlockSpec(memory_space=pltpu.SMEM)] * 3
+        in_specs=[pl.BlockSpec(memory_space=pltpu.SMEM)] * 4
         + [pl.BlockSpec(memory_space=pltpu.VMEM)] * 4,
         out_specs=[pl.BlockSpec(memory_space=pltpu.VMEM)] * (peers - 1),
         out_shape=[
@@ -368,7 +432,7 @@
         compiler_params=params(),
         cost_estimate=cost(8 * slots * block * height * height, 8 * height * height),
         name="own_slots",
-    )(*place, pairs, table, spectra, edge, phases)
+    )(*place, pairs, theirs, table, spectra, edge, phases)
 
 
 def own_surfaces(half, own, table):
@@ -402,28 +466,45 @@
     )(scalar(half), own, table)
 
 
-def surfaces_of(half, me, counts, part, near, other, table):
-    peers = 1 + len(other)
-    slots, double, rows = other[0].shape
-    width = table.shape[0]
+def surfaces_of(half, me, counts, part, lead, rest, far, table):
+    peers = 2 + len(far)
+    slots, rows, width = part.shape
+    double = lead[1].shape[1]
     span = peers * double
 
     def body(half_ref, me_ref, counts_ref, part_ref, *refs):
-        other_refs = refs[:peers]
-        table_ref, out_ref, work = refs[peers:]
-        for k in range(peers):
+        leads, rests, fars = refs[:2], refs[2:4], refs[4:-3]
+        table_ref, out_ref, work = refs[-3:]
+        slot = pl.program_id(0)
+
+        def put(k, piece):
             place = pl.multiple_of((me_ref[0] ^ k) * double, double)
-            piece = other_refs[k][0] if k else other_refs[k][0, 0]
             work[pl.ds(place, double), :] = piece
-        rest = lax.dot_general(
+
+        @pl.when(slot == 0)
+        def _():
+            put(0, leads[0][0, 0])
+            put(1, leads[1][0])
+
+        @pl.when(slot > 0)
+        def _():
+            put(0, rests[0][0, 0])
+            put(1, rests[1][0])
+
+        for k, ref in enumerate(fars):
+            put(k + 2, ref[0])
+        total = lax.dot_general(
             work[...], table_ref[...], (((0,), (0,)), ((), ())), preferred_element_type=jnp.float32
         )
-        live = pl.program_id(0) < counts_ref[0]
-        out_ref[0] = jnp.where(live, part_ref[0] + rest, 0.0)
-
-    pair = pl.BlockSpec((1, 1, double, rows), lambda p, half, me, counts: (0, p, 0, 0))
+        live = slot < counts_ref[0]
+        out_ref[0] = jnp.where(live, part_ref[0] + total, 0.0)
+
+    plane = pl.BlockSpec((1, rows, width), lambda p, half, me, counts: (p, 0, 0))
     piece = pl.BlockSpec((1, double, rows), lambda p, half, me, counts: (p, 0, 0))
-    plane = pl.BlockSpec((1, rows, width), lambda p, half, me, counts: (p, 0, 0))
+
+    def late(p):
+        return jnp.maximum(p - 1, 0)
+
     return pl.pallas_call(
         body,
         grid_spec=pltpu.PrefetchScalarGridSpec(
@@ -431,8 +512,11 @@
             grid=(slots,),
             in_specs=[
                 plane,
-                pair,
-                *[piece] * (peers - 1),
+                pl.BlockSpec((1, 1, double, rows), lambda p, half, me, counts: (0, 0, 0, 0)),
+                pl.BlockSpec((1, double, rows), lambda p, half, me, counts: (0, 0, 0)),
+                pl.BlockSpec((1, 1, double, rows), lambda p, half, me, counts: (0, late(p), 0, 0)),
+                pl.BlockSpec((1, double, rows), lambda p, half, me, counts: (late(p), 0, 0)),
+                *[piece] * (peers - 2),
                 pl.BlockSpec((span, width), lambda p, half, me, counts: (1 - half[0], 0)),
             ],
             out_specs=plane,
@@ -442,7 +526,7 @@
         compiler_params=params(),
         cost_estimate=cost(2 * slots * rows * width * span, 8 * slots * rows * width),
         name="surfaces",
-    )(scalar(half), scalar(me), counts, part, near, *other, table)
+    )(scalar(half), scalar(me), counts, part, *lead, *rest, *far, table)
 
 
 def local(tiles, pairs, counts):
@@ -475,24 +559,38 @@
     sideways = jnp.asarray(hann(width)[None, :])
 
     sent = near_columns(tiles, down, sideways, table_w, half, me, peers)
-    arrived = [across(sent[k], k) for k in range(2)]
+    near = [across(sent[k], k) for k in range(2)]
     *sent, held = lax.optimization_barrier((*sent, half))
-    kept, *sent = rest_columns(tiles, down, sideways, table_w, held, me, peers)
-    *sent, kept, pairs = lax.optimization_barrier((*sent, kept, pairs))
-    arrived += [across(sent[k - 2], k) for k in range(2, peers)]
+    kept, *sent = rest_columns(
+        tiles, down, sideways, table_w, held, me, pairs[0, 0, 0], peers
+    )
+    *sent, kept, told = lax.optimization_barrier((*sent, kept, pairs))
+    distant = peers - 2
+    far = [[across(sent[k - 2], k) for k in range(2, peers)]]
+    theirs = across(told, 0)
+    for i in range(1, count):
+        far.append([across(sent[i * distant + k - 2], k) for k in range(2, peers)])
     mine = along(kept)
 
-    table_h = height_table(height)
-    theirs = across(pairs, 0)
+    table_h = height_table(height, near)
     place = (scalar(half), scalar(me))
     spectra, edge = own_spectra(place, mine, table_h)
-    near, spectra, edge, phases = partner_slots(place, theirs, arrived, table_h, spectra, edge)
-    near = across(near, 0)
-    own, *far = own_slots(place, pairs, table_h, spectra, edge, phases, peers)
-    far = [across(far[k - 2], k) for k in range(2, peers)]
+    lead, lead_spectra, lead_edge, phases = first_slot(
+        place, theirs, near, far[0], table_h, spectra, edge
+    )
+    lead = across(lead, 0)
+    rest, spectra, edge, phases = other_slots(
+        place, theirs, near, far[1:], table_h, spectra, edge, lead_spectra, lead_edge, phases
+    )
+    rest = across(rest, 0)
+    lead, spectra, edge = lax.optimization_barrier((lead, spectra, edge))
+    own, *back = own_slots(place, pairs, theirs, table_h, spectra, edge, phases, peers)
+    back = [across(back[k - 2], k) for k in range(2, peers)]
     part = own_surfaces(half, along(own), table_w)
-    *far, part = lax.optimization_barrier((*far, part))
-    return surfaces_of(half, me, counts, part, near, [swap(near[1]), *far], table_w)
+    *back, part = lax.optimization_barrier((*back, part))
+    return surfaces_of(
+        half, me, counts, part, (lead, swap(lead[1])), (rest, swap(rest[1])), back, table_w
+    )
 
 
 def solution(mesh):

time: 64.7 us -> 75.5 us (1.17)
  Pallas kernels: 18.3 us -> 21.7 us
  starting transfers between devices: 25 us -> 28 us
  local copies, waits for them, and re-layouts: 6.77 us -> 9.5 us
  waiting for transfers between devices: 13.5 us -> 15.2 us
    ppermute x8 -> x11, starting transfers between devices: 18 us -> 20.5 us  [across(): return lax.ppermute(value, axes, moves)]
    pallas_call x3 -> x4, Pallas kernels: 7.64 us -> 9.35 us  [the longest x1 3.61 us: own_slots(): pl.pallas_call(body, in_specs=[pl.BlockSpec(memory_space=pltpu.SMEM)] * 4...]
    pallas_call x1, Pallas kernels: 2.41 us -> 3.95 us  [rest_columns(): pl.pallas_call(body, grid_spec=pltpu.PrefetchScalarGridSpec(num_scalar_pr...]
    squeeze x1 -> x2, local copies, waits for them, and re-layouts: 0.01 us -> 1.25 us  [the longest x1 0.62 us: local(): lead[1]]
    ppermute x8 -> x11, waiting for transfers between devices: 10.2 us -> 11.4 us  [across(): return lax.ppermute(value, axes, moves)]
    unnamed x16 -> x18, local copies, waits for them, and re-layouts: 6.77 us -> 7.67 us
  transfers between devices with their start and end apart: 11 -> 15, of which waited for: 5 -> 4; matrix products, arithmetic and copies ran while one was open for 0% -> 2% of each run, Pallas kernels for 14% -> 21%
where the time goes in v10:
time: 75.5 us; the launch traced here: 75.1 us
  starting transfers between devices  28 us (37%)
  Pallas kernels  21.7 us (29%)
  waiting for transfers between devices  15.2 us (20%)
  local copies, waits for them, and re-layouts  9.5 us (13%)
  between operations  0.76 us (1%)
    ppermute x11, starting transfers between devices, across(): return lax.ppermute(value, axes, moves)  20.5 us
    ppermute x11, waiting for transfers between devices, across(): return lax.ppermute(value, axes, moves)  11.4 us
    unnamed x18, local copies, waits for them, and re-layouts  7.67 us
    all_to_all x2, starting transfers between devices, along(): return lax.all_to_all(blocks, 'rows', split_axis=0, concat_axis=0)  6.94 us
    pallas_call x1, Pallas kernels, near_columns(): pl.pallas_call(body, grid_spec=pltpu.PrefetchScalarGridSpec(num_scalar_pr...  4.12 us
    pallas_call x1, Pallas kernels, rest_columns(): pl.pallas_call(body, grid_spec=pltpu.PrefetchScalarGridSpec(num_scalar_pr...  3.95 us
    all_to_all x2, waiting for transfers between devices, along(): return lax.all_to_all(blocks, 'rows', split_axis=0, concat_axis=0)  3.8 us
    pallas_call x1, Pallas kernels, own_slots(): pl.pallas_call(body, in_specs=[pl.BlockSpec(memory_space=pltpu.SMEM)] * 4...  3.61 us
  transfers between devices with their start and end apart: 15, of which 4 were waited for; matrix products, arithmetic and copies ran while one was open for 2% of the time, Pallas kernels for 21%

profile of v10, /device:TPU:0, one launch (start us, length us, event | category | flops | bytes accessed | tf_op | source)
XLA Modules:
  0.0 75.1 jit_solution(1387555478783776252)
XLA Ops:
  0.0 4.1 %near_columns.1 = (bf16[2,128,256]{2,1,0:T(8,128)(2,1)}, bf16[2,128,256]{2,1,0:T(8,128)(2,1)}) custom-call(s32[1]{0:T(128)} %bitcast.half_ref, s32[1]{0:T(128)} %bitcast.1.me_ref, f32[2,256,1024]{2,1,0:T(8,128)} %tile_ref.1, f32[8,1024]{1,0:T(8,128)} %constant.30.clone.down_ref, f32[1,1024]{1,0:T(1,128)} %constant.31.clone.across_ref, ...), custom_call_target="tpu_custom_call" | custom-call | flops 268435456 | bytes 2621440 | tf_op jit(solution)/shard_map/near_columns/pallas_call | solution.py:121
  4.1 4.1 %collective-permute-start.1 = (bf16[2,128,256]{2,1,0:T(8,128)(2,1)}, bf16[2,128,256]{2,1,0:T(8,128)(2,1)S(1)}, u32[]{:S(2)}, u32[]{:S(2)}) collective-permute-start(bf16[2,128,256]{2,1,0:T(8,128)(2,1)} %get-tuple-element.38), channel_id=1, source_target_pairs={{0,8},{1,9},{2,10},{3,11},{4,12},{5,13},{6,14},{7,15},{8,0},{9,1},... | collective-permute-start | bytes 393224 | tf_op jit(solution)/shard_map/ppermute | solution.py:549
  8.9 1.6 %copy-done.4 = f32[2,256,1024]{2,1,0:T(8,128)S(1)} copy-done((f32[2,256,1024]{2,1,0:T(8,128)S(1)}, f32[2,256,1024]{2,1,0:T(8,128)}, u32[]{:S(2)}) %copy-start.4) | copy-done | bytes 2097176
  10.4 3.9 %rest_columns.1 = (bf16[4,2,128,256]{3,2,1,0:T(8,128)(2,1)}, bf16[128,256]{1,0:T(8,128)(2,1)S(1)}, bf16[128,256]{1,0:T(8,128)(2,1)S(1)}, bf16[128,256]{1,0:T(8,128)(2,1)S(1)}, bf16[128,256]{1,0:T(8,128)(2,1)S(1)}) custom-call(s32[1]{0:T(128)} %bitcast.2.half_ref, s32[1]{0:T(128)} %bitcast.1.me_ref, s32[1]{0:T(128)} %bitcast.3.first_ref, ...), custom_call_target="tpu_custom_call" | custom-call | flops 805306368 | bytes 4194304 | tf_op jit(solution)/shard_map/rest_columns/pallas_call | solution.py:173
  14.4 3.5 %all-to-all-start = ((bf16[4,2,128,256]{3,2,1,0:T(8,128)(2,1)}), bf16[4,2,128,256]{3,2,1,0:T(8,128)(2,1)S(1)}, u32[]{:S(2)}, u32[]{:S(2)}) async-start(bf16[4,2,128,256]{3,2,1,0:T(8,128)(2,1)} %get-tuple-element.49), calls=%async_computation | async-start | bytes 1048576 | tf_op jit(solution)/shard_map/all_to_all | solution.py:552
  17.9 3.5 %collective-permute-start.3 = (bf16[128,256]{1,0:T(8,128)(2,1)S(1)}, bf16[128,256]{1,0:T(8,128)(2,1)S(1)}, u32[]{:S(2)}, u32[]{:S(2)}) collective-permute-start(bf16[128,256]{1,0:T(8,128)(2,1)S(1)} %get-tuple-element.47), channel_id=1, source_target_pairs={{0,10},{1,11},{2,8},{3,9},{4,14},{5,15},{6,12},{7,13},{8,2},{9,3},... | collective-permute-start | bytes 196616 | tf_op jit(solution)/shard_map/ppermute | solution.py:549
  21.6 2.5 %collective-permute-start = (s32[1,2,2]{2,1,0:T(2,128)S(1)}, s32[1,2,2]{2,1,0:T(2,128)S(1)}, u32[]{:S(2)}, u32[]{:S(2)}) collective-permute-start(s32[1,2,2]{2,1,0:T(2,128)S(1)} %copy-done.7), channel_id=1, source_target_pairs={{0,8},{1,9},{2,10},{3,11},{4,12},{5,13},{6,14},{7,15},{8,0},{9,1},... | collective-permute-start | bytes 56 | tf_op jit(solution)/shard_map/ppermute | solution.py:549
  24.1 1.4 %collective-permute-start.6 = (bf16[128,256]{1,0:T(8,128)(2,1)S(1)}, bf16[128,256]{1,0:T(8,128)(2,1)S(1)}, u32[]{:S(2)}, u32[]{:S(2)}) collective-permute-start(bf16[128,256]{1,0:T(8,128)(2,1)S(1)} %get-tuple-element.53), channel_id=1, source_target_pairs={{0,10},{1,11},{2,8},{3,9},{4,14},{5,15},{6,12},{7,13},{8,2},{9,3},... | collective-permute-start | bytes 196616 | tf_op jit(solution)/shard_map/ppermute | solution.py:549
  25.5 1.3 %collective-permute-start.7 = (bf16[128,256]{1,0:T(8,128)(2,1)S(1)}, bf16[128,256]{1,0:T(8,128)(2,1)S(1)}, u32[]{:S(2)}, u32[]{:S(2)}) collective-permute-start(bf16[128,256]{1,0:T(8,128)(2,1)S(1)} %get-tuple-element.54), channel_id=1, source_target_pairs={{0,11},{1,10},{2,9},{3,8},{4,15},{5,14},{6,13},{7,12},{8,3},{9,2},... | collective-permute-start | bytes 196616 | tf_op jit(solution)/shard_map/ppermute | solution.py:549
  27.9 1.1 %height_table.1.table_ref.refs_4_ = bf16[1024,2048]{1,0:T(8,128)(2,1)S(1)} custom-call(f32[128,1024]{1,0:T(8,128)S(1)} %copy-done.8, bf16[2,128,256]{2,1,0:T(8,128)(2,1)S(1)} %collective-permute-done.1.refs_0_, bf16[2,128,256]{2,1,0:T(8,128)(2,1)S(1)} %collective-permute-done.2.refs_1_), custom_call_target="tpu_custom_call" | custom-call | flops 8589934592 | bytes 4194304 | tf_op jit(solution)/shard_map/height_table/pallas_call | solution.py:54
  29.0 2.0 %copy-done = bf16[1024,2048]{1,0:T(8,128)(2,1)} copy-done((bf16[1024,2048]{1,0:T(8,128)(2,1)}, bf16[1024,2048]{1,0:T(8,128)(2,1)S(1)}, u32[]{:S(2)}) %copy-start) | copy-done | bytes 4194328
  31.0 2.2 %copy-done.1 = bf16[1024,2048]{1,0:T(8,128)(2,1)S(1)} copy-done((bf16[1024,2048]{1,0:T(8,128)(2,1)S(1)}, bf16[1024,2048]{1,0:T(8,128)(2,1)}, u32[]{:S(2)}) %copy-start.1) | copy-done | bytes 4194328
  33.1 1.3 %own_spectra.1 = (bf16[2,2,64,1024]{3,2,1,0:T(8,128)(2,1)S(1)}, bf16[2,2,16,1024]{3,2,1,0:T(8,128)(2,1)S(1)}) custom-call(s32[1]{0:T(128)} %bitcast.half_ref, s32[1]{0:T(128)} %bitcast.1.me_ref, bf16[4,2,128,256]{3,2,1,0:T(8,128)(2,1)S(1)} %all-to-all-done.pieces_ref, bf16[1024,2048]{1,0:T(8,128)(2,1)S(1)} %copy-done.1), custom_call_target="tpu_custom_call" | custom-call | flops 1073741824 | bytes 8388608 | tf_op jit(solution)/shard_map/own_spectra/pallas_call | solution.py:298
  35.3 2.0 %first_slot.1 = (bf16[2,1,128,256]{3,2,1,0:T(8,128)(2,1)S(1)}, bf16[1,2,64,1024]{3,2,1,0:T(8,128)(2,1)S(1)}, bf16[1,2,16,1024]{3,2,1,0:T(8,128)(2,1)S(1)}, bf16[2,64,1024]{2,1,0:T(8,128)(2,1)S(1)}) custom-call(s32[1]{0:T(128)} %bitcast.half_ref, s32[1]{0:T(128)} %bitcast.1.me_ref, s32[1,2,2]{2,1,0:T(2,128)S(1)} %collective-permute-done.theirs_ref, ...), custom_call_target="tpu_custom_call" | custom-call | flops 1073741824 | bytes 8388608 | tf_op jit(solution)/shard_map/first_slot/pallas_call | solution.py:330
  37.3 3.8 %collective-permute-start.5 = (bf16[2,1,128,256]{3,2,1,0:T(8,128)(2,1)S(1)}, bf16[2,1,128,256]{3,2,1,0:T(8,128)(2,1)S(1)}, u32[]{:S(2)}, u32[]{:S(2)}) collective-permute-start(bf16[2,1,128,256]{3,2,1,0:T(8,128)(2,1)S(1)} %get-tuple-element.52), channel_id=1, source_target_pairs={{0,8},{1,9},{2,10},{3,11},{4,12},{5,13},{6,14},{7,15},{8,0},{9,1},... | collective-permute-start | bytes 393224 | tf_op jit(solution)/shard_map/ppermute | solution.py:549
  41.1 2.7 %other_slots.1 = (bf16[2,1,128,256]{3,2,1,0:T(8,128)(2,1)}, bf16[4,2,64,1024]{3,2,1,0:T(8,128)(2,1)S(1)}, bf16[4,2,16,1024]{3,2,1,0:T(8,128)(2,1)S(1)}, bf16[4,64,1024]{2,1,0:T(8,128)(2,1)S(1)}) custom-call(s32[1]{0:T(128)} %bitcast.half_ref, s32[1]{0:T(128)} %bitcast.1.me_ref, s32[1,2,2]{2,1,0:T(2,128)S(1)} %collective-permute-done.theirs_ref, ...), custom_call_target="tpu_custom_call" | custom-call | flops 1073741824 | bytes 8388608 | tf_op jit(solution)/shard_map/other_slots/pallas_call | solution.py:384
  43.8 7.2 %collective-permute-done.5.refs_0_ = bf16[2,1,128,256]{3,2,1,0:T(8,128)(2,1)S(1)} collective-permute-done((bf16[2,1,128,256]{3,2,1,0:T(8,128)(2,1)S(1)}, bf16[2,1,128,256]{3,2,1,0:T(8,128)(2,1)S(1)}, u32[]{:S(2)}, u32[]{:S(2)}) %collective-permute-start.5) | collective-permute-done | bytes 131104 | tf_op jit(solution)/shard_map/ppermute | solution.py:549
  51.0 3.6 %own_slots.1 = (bf16[4,2,128,256]{3,2,1,0:T(8,128)(2,1)}, bf16[2,128,256]{2,1,0:T(8,128)(2,1)S(1)}, bf16[2,128,256]{2,1,0:T(8,128)(2,1)S(1)}) custom-call(s32[1]{0:T(128)} %bitcast.half_ref, s32[1]{0:T(128)} %bitcast.1.me_ref, s32[1,2,2]{2,1,0:T(2,128)S(1)} %copy-done.7, s32[1,2,2]{2,1,0:T(2,128)S(1)} %collective-permute-done.theirs_ref, ...), custom_call_target="tpu_custom_call" | custom-call | flops 1073741824 | bytes 8388608 | tf_op jit(solution)/shard_map/own_slots/pallas_call | solution.py:422
  54.6 3.5 %all-to-all-start.1 = ((bf16[4,2,128,256]{3,2,1,0:T(8,128)(2,1)}), bf16[4,2,128,256]{3,2,1,0:T(8,128)(2,1)S(1)}, u32[]{:S(2)}, u32[]{:S(2)}) async-start(bf16[4,2,128,256]{3,2,1,0:T(8,128)(2,1)} %get-tuple-element.65), calls=%async_computation.1 | async-start | bytes 1048576 | tf_op jit(solution)/shard_map/all_to_all | solution.py:552
  59.0 2.7 %collective-permute-start.9 = (bf16[2,128,256]{2,1,0:T(8,128)(2,1)S(1)}, bf16[2,128,256]{2,1,0:T(8,128)(2,1)S(1)}, u32[]{:S(2)}, u32[]{:S(2)}) collective-permute-start(bf16[2,128,256]{2,1,0:T(8,128)(2,1)S(1)} %get-tuple-element.64), channel_id=1, source_target_pairs={{0,11},{1,10},{2,9},{3,8},{4,15},{5,14},{6,13},{7,12},{8,3},{9,2},... | collective-permute-start | bytes 393224 | tf_op jit(solution)/shard_map/ppermute | solution.py:549
  64.1 3.8 %all-to-all-done.1.own_ref = bf16[4,2,128,256]{3,2,1,0:T(8,128)(2,1)S(1)} async-done(((bf16[4,2,128,256]{3,2,1,0:T(8,128)(2,1)}), bf16[4,2,128,256]{3,2,1,0:T(8,128)(2,1)S(1)}, u32[]{:S(2)}, u32[]{:S(2)}) %all-to-all-start.1) | async-done | bytes 524320 | tf_op jit(solution)/shard_map/all_to_all | solution.py:552
  68.9 1.6 %collective-permute-done.8.refs_4_ = bf16[2,128,256]{2,1,0:T(8,128)(2,1)S(1)} collective-permute-done((bf16[2,128,256]{2,1,0:T(8,128)(2,1)S(1)}, bf16[2,128,256]{2,1,0:T(8,128)(2,1)S(1)}, u32[]{:S(2)}, u32[]{:S(2)}) %collective-permute-start.8) | collective-permute-done | bytes 131104 | tf_op jit(solution)/shard_map/ppermute | solution.py:549
  70.5 2.6 %collective-permute-done.9.refs_5_ = bf16[2,128,256]{2,1,0:T(8,128)(2,1)S(1)} collective-permute-done((bf16[2,128,256]{2,1,0:T(8,128)(2,1)S(1)}, bf16[2,128,256]{2,1,0:T(8,128)(2,1)S(1)}, u32[]{:S(2)}, u32[]{:S(2)}) %collective-permute-start.9) | collective-permute-done | bytes 131104 | tf_op jit(solution)/shard_map/ppermute | solution.py:549
  73.1 2.0 %surfaces.1 = f32[2,256,1024]{2,1,0:T(8,128)} custom-call(s32[1]{0:T(128)} %bitcast.half_ref, s32[1]{0:T(128)} %bitcast.1.me_ref, s32[1]{0:T(128)S(6)} %copy.8.counts_ref, f32[2,256,1024]{2,1,0:T(8,128)S(1)} %own_surfaces.1.part_ref, bf16[2,1,128,256]{3,2,1,0:T(8,128)(2,1)S(1)} %collective-permute-done.5.refs_0_, ...), custom_call_target="tpu_custom_call" | custom-call | flops 536870912 | bytes 4194304 | tf_op jit(solution)/shard_map/surfaces/pallas_call | solution.py:508
  (36 shorter events, 6.5 us)
Async XLA Ops:
  0.0 8.3 %copy-start.7 = (s32[1,2,2]{2,1,0:T(2,128)S(1)}, s32[1,2,2]{2,1,0:T(2,128)}, u32[]{:S(2)}) copy-start(s32[1,2,2]{2,1,0:T(2,128)} %pairs_ref.1) | copy-start | bytes 52
  0.0 8.8 %copy-start.3 = (bf16[1024,1024]{1,0:T(8,128)(2,1)S(1)}, bf16[1024,1024]{1,0:T(8,128)(2,1)}, u32[]{:S(2)}) copy-start(bf16[1024,1024]{1,0:T(8,128)(2,1)} %constant.29.clone.table_hbm.table_ref.refs_6_) | copy-start | bytes 6291460
  0.0 8.8 %copy-start.5 = (f32[8,1024]{1,0:T(8,128)S(1)}, f32[8,1024]{1,0:T(8,128)}, u32[]{:S(2)}) copy-start(f32[8,1024]{1,0:T(8,128)} %constant.30.clone.down_ref) | copy-start | bytes 98308
  0.0 8.8 %copy-start.6 = (f32[1,1024]{1,0:T(1,128)S(1)}, f32[1,1024]{1,0:T(1,128)}, u32[]{:S(2)}) copy-start(f32[1,1024]{1,0:T(1,128)} %constant.31.clone.across_ref) | copy-start | bytes 12292
  4.1 20.0 %collective-permute-start.1 = (bf16[2,128,256]{2,1,0:T(8,128)(2,1)}, bf16[2,128,256]{2,1,0:T(8,128)(2,1)S(1)}, u32[]{:S(2)}, u32[]{:S(2)}) collective-permute-start(bf16[2,128,256]{2,1,0:T(8,128)(2,1)} %get-tuple-element.38), channel_id=1, source_target_pairs={{0,8},{1,9},{2,10},{3,11},{4,12},{5,13},{6,14},{7,15},{8,0},{9,1},... | collective-permute-start | bytes 393224 | tf_op jit(solution)/shard_map/ppermute | solution.py:549
  8.3 17.3 %collective-permute-start.2 = (bf16[2,128,256]{2,1,0:T(8,128)(2,1)}, bf16[2,128,256]{2,1,0:T(8,128)(2,1)S(1)}, u32[]{:S(2)}, u32[]{:S(2)}) collective-permute-start(bf16[2,128,256]{2,1,0:T(8,128)(2,1)} %get-tuple-element.39), channel_id=1, source_target_pairs={{0,9},{1,8},{2,11},{3,10},{4,13},{5,12},{6,15},{7,14},{8,1},{9,0},... | collective-permute-start | bytes 393224 | tf_op jit(solution)/shard_map/ppermute | solution.py:549
  8.8 1.6 %copy-start.4 = (f32[2,256,1024]{2,1,0:T(8,128)S(1)}, f32[2,256,1024]{2,1,0:T(8,128)}, u32[]{:S(2)}) copy-start(f32[2,256,1024]{2,1,0:T(8,128)} %tile_ref.1) | copy-start | bytes 6291460
  14.4 16.6 %all-to-all-start = ((bf16[4,2,128,256]{3,2,1,0:T(8,128)(2,1)}), bf16[4,2,128,256]{3,2,1,0:T(8,128)(2,1)S(1)}, u32[]{:S(2)}, u32[]{:S(2)}) async-start(bf16[4,2,128,256]{3,2,1,0:T(8,128)(2,1)} %get-tuple-element.49), calls=%async_computation | async-start | bytes 1048576 | tf_op jit(solution)/shard_map/all_to_all | solution.py:552
  17.9 16.6 %collective-permute-start.3 = (bf16[128,256]{1,0:T(8,128)(2,1)S(1)}, bf16[128,256]{1,0:T(8,128)(2,1)S(1)}, u32[]{:S(2)}, u32[]{:S(2)}) collective-permute-start(bf16[128,256]{1,0:T(8,128)(2,1)S(1)} %get-tuple-element.47), channel_id=1, source_target_pairs={{0,10},{1,11},{2,8},{3,9},{4,14},{5,15},{6,12},{7,13},{8,2},{9,3},... | collective-permute-start | bytes 196616 | tf_op jit(solution)/shard_map/ppermute | solution.py:549
  21.4 13.1 %collective-permute-start.4 = (bf16[128,256]{1,0:T(8,128)(2,1)S(1)}, bf16[128,256]{1,0:T(8,128)(2,1)S(1)}, u32[]{:S(2)}, u32[]{:S(2)}) collective-permute-start(bf16[128,256]{1,0:T(8,128)(2,1)S(1)} %get-tuple-element.48), channel_id=1, source_target_pairs={{0,11},{1,10},{2,9},{3,8},{4,15},{5,14},{6,13},{7,12},{8,3},{9,2},... | collective-permute-start | bytes 196616 | tf_op jit(solution)/shard_map/ppermute | solution.py:549
  21.6 12.9 %collective-permute-start = (s32[1,2,2]{2,1,0:T(2,128)S(1)}, s32[1,2,2]{2,1,0:T(2,128)S(1)}, u32[]{:S(2)}, u32[]{:S(2)}) collective-permute-start(s32[1,2,2]{2,1,0:T(2,128)S(1)} %copy-done.7), channel_id=1, source_target_pairs={{0,8},{1,9},{2,10},{3,11},{4,12},{5,13},{6,14},{7,15},{8,0},{9,1},... | collective-permute-start | bytes 56 | tf_op jit(solution)/shard_map/ppermute | solution.py:549
  24.1 17.0 %collective-permute-start.6 = (bf16[128,256]{1,0:T(8,128)(2,1)S(1)}, bf16[128,256]{1,0:T(8,128)(2,1)S(1)}, u32[]{:S(2)}, u32[]{:S(2)}) collective-permute-start(bf16[128,256]{1,0:T(8,128)(2,1)S(1)} %get-tuple-element.53), channel_id=1, source_target_pairs={{0,10},{1,11},{2,8},{3,9},{4,14},{5,15},{6,12},{7,13},{8,2},{9,3},... | collective-permute-start | bytes 196616 | tf_op jit(solution)/shard_map/ppermute | solution.py:549
  25.5 15.5 %collective-permute-start.7 = (bf16[128,256]{1,0:T(8,128)(2,1)S(1)}, bf16[128,256]{1,0:T(8,128)(2,1)S(1)}, u32[]{:S(2)}, u32[]{:S(2)}) collective-permute-start(bf16[128,256]{1,0:T(8,128)(2,1)S(1)} %get-tuple-element.54), channel_id=1, source_target_pairs={{0,11},{1,10},{2,9},{3,8},{4,15},{5,14},{6,13},{7,12},{8,3},{9,2},... | collective-permute-start | bytes 196616 | tf_op jit(solution)/shard_map/ppermute | solution.py:549
  26.8 1.0 %copy-start.8 = (f32[128,1024]{1,0:T(8,128)S(1)}, f32[128,1024]{1,0:T(8,128)}, u32[]{:S(2)}) copy-start(f32[128,1024]{1,0:T(8,128)} %constant.32.clone.short_ref) | copy-start | bytes 1572868
  29.0 2.0 %copy-start = (bf16[1024,2048]{1,0:T(8,128)(2,1)}, bf16[1024,2048]{1,0:T(8,128)(2,1)S(1)}, u32[]{:S(2)}) copy-start(bf16[1024,2048]{1,0:T(8,128)(2,1)S(1)} %height_table.1.table_ref.refs_4_) | copy-start | bytes 12582916
  30.9 2.2 %copy-start.1 = (bf16[1024,2048]{1,0:T(8,128)(2,1)S(1)}, bf16[1024,2048]{1,0:T(8,128)(2,1)}, u32[]{:S(2)}) copy-start(bf16[1024,2048]{1,0:T(8,128)(2,1)} %copy-done) | copy-start | bytes 12582916
  33.1 2.2 %copy-start.2 = (bf16[1024,2048]{1,0:T(8,128)(2,1)S(1)}, bf16[1024,2048]{1,0:T(8,128)(2,1)}, u32[]{:S(2)}) copy-start(bf16[1024,2048]{1,0:T(8,128)(2,1)} %copy-done) | copy-start | bytes 12582916
  37.3 13.7 %collective-permute-start.5 = (bf16[2,1,128,256]{3,2,1,0:T(8,128)(2,1)S(1)}, bf16[2,1,128,256]{3,2,1,0:T(8,128)(2,1)S(1)}, u32[]{:S(2)}, u32[]{:S(2)}) collective-permute-start(bf16[2,1,128,256]{3,2,1,0:T(8,128)(2,1)S(1)} %get-tuple-element.52), channel_id=1, source_target_pairs={{0,8},{1,9},{2,10},{3,11},{4,12},{5,13},{6,14},{7,15},{8,0},{9,1},... | collective-permute-start | bytes 393224 | tf_op jit(solution)/shard_map/ppermute | solution.py:549
  43.8 18.0 %collective-permute-start.11 = (bf16[2,1,128,256]{3,2,1,0:T(8,128)(2,1)}, bf16[2,1,128,256]{3,2,1,0:T(8,128)(2,1)S(1)}, u32[]{:S(2)}, u32[]{:S(2)}) collective-permute-start(bf16[2,1,128,256]{3,2,1,0:T(8,128)(2,1)} %get-tuple-element.68), channel_id=1, source_target_pairs={{0,8},{1,9},{2,10},{3,11},{4,12},{5,13},{6,14},{7,15},{8,0},{9,1},... | collective-permute-start | bytes 393224 | tf_op jit(solution)/shard_map/ppermute | solution.py:549
  54.6 13.3 %all-to-all-start.1 = ((bf16[4,2,128,256]{3,2,1,0:T(8,128)(2,1)}), bf16[4,2,128,256]{3,2,1,0:T(8,128)(2,1)S(1)}, u32[]{:S(2)}, u32[]{:S(2)}) async-start(bf16[4,2,128,256]{3,2,1,0:T(8,128)(2,1)} %get-tuple-element.65), calls=%async_computation.1 | async-start | bytes 1048576 | tf_op jit(solution)/shard_map/all_to_all | solution.py:552
  58.1 12.5 %collective-permute-start.8 = (bf16[2,128,256]{2,1,0:T(8,128)(2,1)S(1)}, bf16[2,128,256]{2,1,0:T(8,128)(2,1)S(1)}, u32[]{:S(2)}, u32[]{:S(2)}) collective-permute-start(bf16[2,128,256]{2,1,0:T(8,128)(2,1)S(1)} %get-tuple-element.63), channel_id=1, source_target_pairs={{0,10},{1,11},{2,8},{3,9},{4,14},{5,15},{6,12},{7,13},{8,2},{9,3},... | collective-permute-start | bytes 393224 | tf_op jit(solution)/shard_map/ppermute | solution.py:549
  59.0 14.1 %collective-permute-start.9 = (bf16[2,128,256]{2,1,0:T(8,128)(2,1)S(1)}, bf16[2,128,256]{2,1,0:T(8,128)(2,1)S(1)}, u32[]{:S(2)}, u32[]{:S(2)}) collective-permute-start(bf16[2,128,256]{2,1,0:T(8,128)(2,1)S(1)} %get-tuple-element.64), channel_id=1, source_target_pairs={{0,11},{1,10},{2,9},{3,8},{4,15},{5,14},{6,13},{7,12},{8,3},{9,2},... | collective-permute-start | bytes 393224 | tf_op jit(solution)/shard_map/ppermute | solution.py:549
  62.3 10.8 %collective-permute-start.12 = (bf16[1,128,256]{2,1,0:T(8,128)(2,1)}, bf16[1,128,256]{2,1,0:T(8,128)(2,1)S(1)}, u32[]{:S(2)}, u32[]{:S(2)}) collective-permute-start(bf16[1,128,256]{2,1,0:T(8,128)(2,1)} %slice_bitcast_fusion), channel_id=1, source_target_pairs={{0,1},{1,0},{2,3},{3,2},{4,5},{5,4},{6,7},{7,6},{8,9},{9,8},{10,11... | collective-permute-start | bytes 196616 | tf_op jit(solution)/shard_map/ppermute | solution.py:555
  63.3 9.8 %collective-permute-start.10 = (bf16[1,128,256]{2,1,0:T(8,128)(2,1)}, bf16[1,128,256]{2,1,0:T(8,128)(2,1)S(1)}, u32[]{:S(2)}, u32[]{:S(2)}) collective-permute-start(bf16[1,128,256]{2,1,0:T(8,128)(2,1)} %slice_bitcast_fusion.1), channel_id=1, source_target_pairs={{0,1},{1,0},{2,3},{3,2},{4,5},{5,4},{6,7},{7,6},{8,9},{9,8},{10,11... | collective-permute-start | bytes 196616 | tf_op jit(solution)/shard_map/ppermute | solution.py:555

commit v11 on v10

--- a/solution.py
+++ b/solution.py
@@ -144,14 +144,17 @@
     )(scalar(half), scalar(me), tiles, down, across, table)
 
 
-def rest_columns(tiles, down, across, table, half, me, first, peers):
+def rest_columns(tiles, down, across, table, half, me, pairs, peers):
     count, rows, width = tiles.shape
     span = table.shape[0] // 2
     block = span // peers
     distant = peers - 2
 
-    def body(half_ref, me_ref, first_ref, tile_ref, down_ref, across_ref, table_ref, *refs):
-        out_ref, far, work = refs[0], refs[1:-1], refs[-1]
+    def body(half_ref, me_ref, pairs_ref, tile_ref, down_ref, across_ref, table_ref, *refs):
+        out_ref, far, (work, stage, done) = refs[0], refs[1:-3], refs[-3:]
+        copies = [
+            pltpu.make_async_copy(stage.at[i], far[i], done.at[i]) for i in range(count * distant)
+        ]
         half, me = half_ref[0], me_ref[0]
         t = pl.program_id(0)
         shaded = shade(tile_ref[0], down_ref, across_ref)
@@ -164,11 +167,18 @@
 
                     @pl.when(t == i)
                     def _():
-                        far[i * distant + 2 * j - 2 + k][...] = work[pl.ds(place, block), :]
+                        to = i * distant + 2 * j - 2 + k
+                        stage[to] = work[pl.ds(place, block), :]
+                        copies[to].start()
 
         start = pl.multiple_of(half * span, span)
         y = times_table(table_ref[pl.ds(start, span), :], shaded)
         out_ref[:, 0] = y.reshape(peers, block, rows)
+
+        @pl.when(t == count - 1)
+        def _():
+            for copy in copies:
+                copy.wait()
 
     return pl.pallas_call(
         body,
@@ -176,18 +186,22 @@
             num_scalar_prefetch=3,
             grid=(count,),
             in_specs=[
-                pl.BlockSpec((1, rows, width), lambda t, half, me, a: ((a[0] + t) % count, 0, 0)),
+                pl.BlockSpec((1, rows, width), lambda t, half, me, a: ((a[0, 0, 0] + t) % count, 0, 0)),
                 pl.BlockSpec((8, rows), lambda t, half, me, a: (0, me[0])),
                 pl.BlockSpec((1, width), lambda t, half, me, a: (0, 0)),
                 pl.BlockSpec((width, width), lambda t, half, me, a: (0, 0)),
             ],
             out_specs=[
                 pl.BlockSpec(
-                    (peers, 1, block, rows), lambda t, half, me, a: (0, (a[0] + t) % count, 0, 0)
+                    (peers, 1, block, rows), lambda t, half, me, a: (0, (a[0, 0, 0] + t) % count, 0, 0)
                 ),
-                *[pl.BlockSpec((block, rows), lambda t, half, me, a: (0, 0))] * (count * distant),
+                *[pl.BlockSpec(memory_space=pltpu.HBM)] * (count * distant),
             ],
-            scratch_shapes=[pltpu.VMEM((2 * block, rows), jnp.bfloat16)],
+            scratch_shapes=[
+                pltpu.VMEM((2 * block, rows), jnp.bfloat16),
+                pltpu.VMEM((count * distant, block, rows), jnp.bfloat16),
+                pltpu.SemaphoreType.DMA((count * distant,)),
+            ],
         ),
         out_shape=[
             jax.ShapeDtypeStruct((peers, count, block, rows), jnp.bfloat16),
@@ -196,7 +210,7 @@
         compiler_params=params(),
         cost_estimate=cost(3 * count * rows * width * span, 4 * tiles.size + 2 * width * width),
         name="rest_columns",
-    )(scalar(half), scalar(me), scalar(first), tiles, down, across, table)
+    )(scalar(half), scalar(me), pairs, tiles, down, across, table)
 
 
 def gather_rows(pieces, table_ref, me):
@@ -360,7 +374,8 @@
         far_refs = refs[2 : 2 + rest * (peers - 2)]
         tail = refs[2 + rest * (peers - 2) :]
         table_ref, own, own_edge, lead_ref, lead_edge_ref, done_ref = tail[:6]
-        out, every, edges, phases_ref = tail[6:]
+        out, every, edges = tail[6:9]
+        distant, phases_ref = tail[9:-1], tail[-1]
         every[:count] = own[...]
         edges[:count] = own_edge[...]
         every[count : count + 1] = lead_ref[...]
@@ -379,60 +394,57 @@
         fresh = phases_ref.at[pl.ds(2, 2 * slots - 2)]
         correlate(s_ref, picks, fresh)
         invert_columns(s_ref, me, fresh, table_ref, {k: out.at[k] for k in range(2)})
+        if distant:
+            outs = {k: distant[k - 2] for k in range(2, peers)}
+            invert_columns(s_ref, me, phases_ref, table_ref, outs)
 
     flat = [piece for pieces in far for piece in pieces]
     return pl.pallas_call(
         body,
         in_specs=[pl.BlockSpec(memory_space=pltpu.SMEM)] * 3
         + [pl.BlockSpec(memory_space=pltpu.VMEM)] * (8 + len(flat)),
-        out_specs=[pl.BlockSpec(memory_space=pltpu.VMEM)] * 4,
+        out_specs=[pl.BlockSpec(memory_space=pltpu.VMEM)] * (1 + peers),
         out_shape=[
             jax.ShapeDtypeStruct((2, slots - 1, double, rows), jnp.bfloat16),
             jax.ShapeDtypeStruct((2 * count, 2, block, height), jnp.bfloat16),
             jax.ShapeDtypeStruct((2 * count, 2, 16, height), jnp.bfloat16),
-            jax.ShapeDtypeStruct((2 * slots, block, height), jnp.bfloat16),
+            *[jax.ShapeDtypeStruct((slots, double, rows), jnp.bfloat16)] * (peers - 2),
         ],
+        scratch_shapes=[pltpu.VMEM((2 * slots, block, height), jnp.bfloat16)],
         compiler_params=params(),
         cost_estimate=cost(8 * double * height * height, 8 * height * height),
         name="other_slots",
     )(*place, theirs, *near, *flat, table, spectra, edge, lead, lead_edge, phases)
 
 
-def own_slots(place, pairs, theirs, table, spectra, edge, phases, peers):
+def own_slots(place, pairs, theirs, table, spectra, edge, peers):
     block, height = spectra.shape[2:]
     count = spectra.shape[0] // 2
     rows = height // peers
     slots = pairs.shape[1]
 
-    def body(half_ref, me_ref, pairs_ref, theirs_ref, table_ref, every, edges, done, out_ref, *refs):
+    def body(half_ref, me_ref, pairs_ref, theirs_ref, table_ref, every, edges, out_ref, work):
         s_ref = (half_ref, me_ref)
-        far, work = refs[:-1], refs[-1]
         first = theirs_ref[0, 0, 0]
         picks = []
         for p in range(slots):
             a, c = pairs_ref[0, p, 0], pairs_ref[0, p, 1]
             right = jnp.where(c < count, c, count + (c - first) % count)
             picks.append(((every, edges, a), (every, edges, right)))
-        if far:
-            outs = {k: far[k - 2] for k in range(2, peers)}
-            invert_columns(s_ref, me_ref[0], done, table_ref, outs)
         correlate(s_ref, picks, work)
         invert_columns(s_ref, 0, work, table_ref, {k: out_ref.at[k] for k in range(peers)})
 
     return pl.pallas_call(
         body,
         in_specs=[pl.BlockSpec(memory_space=pltpu.SMEM)] * 4
-        + [pl.BlockSpec(memory_space=pltpu.VMEM)] * 4,
-        out_specs=[pl.BlockSpec(memory_space=pltpu.VMEM)] * (peers - 1),
-        out_shape=[
-            jax.ShapeDtypeStruct((peers, slots, 2 * block, rows), jnp.bfloat16),
-            *[jax.ShapeDtypeStruct((slots, 2 * block, rows), jnp.bfloat16)] * (peers - 2),
-        ],
+        + [pl.BlockSpec(memory_space=pltpu.VMEM)] * 3,
+        out_specs=pl.BlockSpec(memory_space=pltpu.VMEM),
+        out_shape=jax.ShapeDtypeStruct((peers, slots, 2 * block, rows), jnp.bfloat16),
         scratch_shapes=[pltpu.VMEM((2 * slots, block, height), jnp.bfloat16)],
         compiler_params=params(),
         cost_estimate=cost(8 * slots * block * height * height, 8 * height * height),
         name="own_slots",
-    )(*place, pairs, theirs, table, spectra, edge, phases)
+    )(*place, pairs, theirs, table, spectra, edge)
 
 
 def own_surfaces(half, own, table):
@@ -562,7 +574,7 @@
     near = [across(sent[k], k) for k in range(2)]
     *sent, held = lax.optimization_barrier((*sent, half))
     kept, *sent = rest_columns(
-        tiles, down, sideways, table_w, held, me, pairs[0, 0, 0], peers
+        tiles, down, sideways, table_w, held, me, pairs, peers
     )
     *sent, kept, told = lax.optimization_barrier((*sent, kept, pairs))
     distant = peers - 2
@@ -579,13 +591,13 @@
         place, theirs, near, far[0], table_h, spectra, edge
     )
     lead = across(lead, 0)
-    rest, spectra, edge, phases = other_slots(
+    rest, spectra, edge, *back = other_slots(
         place, theirs, near, far[1:], table_h, spectra, edge, lead_spectra, lead_edge, phases
     )
     rest = across(rest, 0)
+    back = [across(back[k - 2], k) for k in range(2, peers)]
     lead, spectra, edge = lax.optimization_barrier((lead, spectra, edge))
-    own, *back = own_slots(place, pairs, theirs, table_h, spectra, edge, phases, peers)
-    back = [across(back[k - 2], k) for k in range(2, peers)]
+    own = own_slots(place, pairs, theirs, table_h, spectra, edge, peers)
     part = own_surfaces(half, along(own), table_w)
     *back, part = lax.optimization_barrier((*back, part))
     return surfaces_of(

time: 75.5 us -> 75.2 us (level)
    all_to_all x2, waiting for transfers between devices: 3.8 us -> 6.12 us  [along(): return lax.all_to_all(blocks, 'rows', split_axis=0, concat_axis=0)]
    ppermute x11, waiting for transfers between devices: 11.4 us -> 9.56 us  [across(): return lax.ppermute(value, axes, moves)]
  transfers between devices with their start and end apart: 15 -> 15, of which waited for: 4 -> 3; matrix products, arithmetic and copies ran while one was open for 2% -> 2% of each run, Pallas kernels for 21% -> 21%
where the time goes in v11:
time: 75.2 us; the launch traced here: 74.8 us
  starting transfers between devices  27.6 us (37%)
  Pallas kernels  21.7 us (29%)
  waiting for transfers between devices  15.7 us (21%)
  local copies, waits for them, and re-layouts  8.92 us (12%)
  between operations  0.82 us (1%)
    ppermute x11, starting transfers between devices, across(): return lax.ppermute(value, axes, moves)  20.2 us
    ppermute x11, waiting for transfers between devices, across(): return lax.ppermute(value, axes, moves)  9.56 us
    unnamed x18, local copies, waits for them, and re-layouts  7.66 us
    all_to_all x2, starting transfers between devices, along(): return lax.all_to_all(blocks, 'rows', split_axis=0, concat_axis=0)  6.96 us
    all_to_all x2, waiting for transfers between devices, along(): return lax.all_to_all(blocks, 'rows', split_axis=0, concat_axis=0)  6.12 us
    pallas_call x1, Pallas kernels, rest_columns(): pl.pallas_call(body, grid_spec=pltpu.PrefetchScalarGridSpec(num_scalar_pr...  4.24 us
    pallas_call x1, Pallas kernels, near_columns(): pl.pallas_call(body, grid_spec=pltpu.PrefetchScalarGridSpec(num_scalar_pr...  4.12 us
    pallas_call x1, Pallas kernels, own_slots(): pl.pallas_call(body, in_specs=[pl.BlockSpec(memory_space=pltpu.SMEM)] * 4...  3.05 us
  transfers between devices with their start and end apart: 15, of which 3 were waited for; matrix products, arithmetic and copies ran while one was open for 2% of the time, Pallas kernels for 21%

profile of v11, /device:TPU:0, one launch (start us, length us, event | category | flops | bytes accessed | tf_op | source)
XLA Modules:
  0.0 74.8 jit_solution(2279788574079593727)
XLA Ops:
  0.0 4.1 %near_columns.1 = (bf16[2,128,256]{2,1,0:T(8,128)(2,1)}, bf16[2,128,256]{2,1,0:T(8,128)(2,1)}) custom-call(s32[1]{0:T(128)} %bitcast.half_ref, s32[1]{0:T(128)} %bitcast.1.me_ref, f32[2,256,1024]{2,1,0:T(8,128)} %tile_ref.1, f32[8,1024]{1,0:T(8,128)} %constant.30.clone.down_ref, f32[1,1024]{1,0:T(1,128)} %constant.31.clone.across_ref, ...), custom_call_target="tpu_custom_call" | custom-call | flops 268435456 | bytes 2621440 | tf_op jit(solution)/shard_map/near_columns/pallas_call | solution.py:121
  4.1 4.1 %collective-permute-start.1 = (bf16[2,128,256]{2,1,0:T(8,128)(2,1)}, bf16[2,128,256]{2,1,0:T(8,128)(2,1)S(1)}, u32[]{:S(2)}, u32[]{:S(2)}) collective-permute-start(bf16[2,128,256]{2,1,0:T(8,128)(2,1)} %get-tuple-element.36), channel_id=1, source_target_pairs={{0,8},{1,9},{2,10},{3,11},{4,12},{5,13},{6,14},{7,15},{8,0},{9,1},... | collective-permute-start | bytes 393224 | tf_op jit(solution)/shard_map/ppermute | solution.py:561
  8.3 1.6 %copy-done.4 = f32[2,256,1024]{2,1,0:T(8,128)S(1)} copy-done((f32[2,256,1024]{2,1,0:T(8,128)S(1)}, f32[2,256,1024]{2,1,0:T(8,128)}, u32[]{:S(2)}) %copy-start.4) | copy-done | bytes 2097176
  9.9 4.2 %rest_columns.1 = (bf16[4,2,128,256]{3,2,1,0:T(8,128)(2,1)}, bf16[128,256]{1,0:T(8,128)(2,1)S(1)}, bf16[128,256]{1,0:T(8,128)(2,1)S(1)}, bf16[128,256]{1,0:T(8,128)(2,1)S(1)}, bf16[128,256]{1,0:T(8,128)(2,1)S(1)}) custom-call(s32[1]{0:T(128)} %bitcast.2.half_ref, s32[1]{0:T(128)} %bitcast.1.me_ref, s32[1,2,2]{2,1,0:T(2,128)S(1)} %copy-done.7, ...), custom_call_target="tpu_custom_call" | custom-call | flops 805306368 | bytes 4194304 | tf_op jit(solution)/shard_map/rest_columns/pallas_call | solution.py:183
  14.1 3.5 %all-to-all-start = ((bf16[4,2,128,256]{3,2,1,0:T(8,128)(2,1)}), bf16[4,2,128,256]{3,2,1,0:T(8,128)(2,1)S(1)}, u32[]{:S(2)}, u32[]{:S(2)}) async-start(bf16[4,2,128,256]{3,2,1,0:T(8,128)(2,1)} %get-tuple-element.47), calls=%async_computation | async-start | bytes 1048576 | tf_op jit(solution)/shard_map/all_to_all | solution.py:564
  17.6 3.5 %collective-permute-start.5 = (bf16[128,256]{1,0:T(8,128)(2,1)S(1)}, bf16[128,256]{1,0:T(8,128)(2,1)S(1)}, u32[]{:S(2)}, u32[]{:S(2)}) collective-permute-start(bf16[128,256]{1,0:T(8,128)(2,1)S(1)} %get-tuple-element.50), channel_id=1, source_target_pairs={{0,10},{1,11},{2,8},{3,9},{4,14},{5,15},{6,12},{7,13},{8,2},{9,3},... | collective-permute-start | bytes 196616 | tf_op jit(solution)/shard_map/ppermute | solution.py:561
  21.3 2.5 %collective-permute-start = (s32[1,2,2]{2,1,0:T(2,128)S(1)}, s32[1,2,2]{2,1,0:T(2,128)S(1)}, u32[]{:S(2)}, u32[]{:S(2)}) collective-permute-start(s32[1,2,2]{2,1,0:T(2,128)S(1)} %copy-done.7), channel_id=1, source_target_pairs={{0,8},{1,9},{2,10},{3,11},{4,12},{5,13},{6,14},{7,15},{8,0},{9,1},... | collective-permute-start | bytes 56 | tf_op jit(solution)/shard_map/ppermute | solution.py:561
  23.9 1.4 %collective-permute-start.3 = (bf16[128,256]{1,0:T(8,128)(2,1)S(1)}, bf16[128,256]{1,0:T(8,128)(2,1)S(1)}, u32[]{:S(2)}, u32[]{:S(2)}) collective-permute-start(bf16[128,256]{1,0:T(8,128)(2,1)S(1)} %get-tuple-element.45), channel_id=1, source_target_pairs={{0,10},{1,11},{2,8},{3,9},{4,14},{5,15},{6,12},{7,13},{8,2},{9,3},... | collective-permute-start | bytes 196616 | tf_op jit(solution)/shard_map/ppermute | solution.py:561
  25.3 1.3 %collective-permute-start.4 = (bf16[128,256]{1,0:T(8,128)(2,1)S(1)}, bf16[128,256]{1,0:T(8,128)(2,1)S(1)}, u32[]{:S(2)}, u32[]{:S(2)}) collective-permute-start(bf16[128,256]{1,0:T(8,128)(2,1)S(1)} %get-tuple-element.46), channel_id=1, source_target_pairs={{0,11},{1,10},{2,9},{3,8},{4,15},{5,14},{6,13},{7,12},{8,3},{9,2},... | collective-permute-start | bytes 196616 | tf_op jit(solution)/shard_map/ppermute | solution.py:561
  26.6 1.0 %copy-done.8 = f32[128,1024]{1,0:T(8,128)S(1)} copy-done((f32[128,1024]{1,0:T(8,128)S(1)}, f32[128,1024]{1,0:T(8,128)}, u32[]{:S(2)}) %copy-start.8) | copy-done | bytes 524312
  27.6 1.1 %height_table.1.table_ref.refs_4_ = bf16[1024,2048]{1,0:T(8,128)(2,1)S(1)} custom-call(f32[128,1024]{1,0:T(8,128)S(1)} %copy-done.8, bf16[2,128,256]{2,1,0:T(8,128)(2,1)S(1)} %collective-permute-done.1.refs_0_, bf16[2,128,256]{2,1,0:T(8,128)(2,1)S(1)} %collective-permute-done.2.refs_1_), custom_call_target="tpu_custom_call" | custom-call | flops 8589934592 | bytes 4194304 | tf_op jit(solution)/shard_map/height_table/pallas_call | solution.py:54
  28.7 1.9 %copy-done = bf16[1024,2048]{1,0:T(8,128)(2,1)} copy-done((bf16[1024,2048]{1,0:T(8,128)(2,1)}, bf16[1024,2048]{1,0:T(8,128)(2,1)S(1)}, u32[]{:S(2)}) %copy-start) | copy-done | bytes 4194328
  30.7 2.2 %copy-done.1 = bf16[1024,2048]{1,0:T(8,128)(2,1)S(1)} copy-done((bf16[1024,2048]{1,0:T(8,128)(2,1)S(1)}, bf16[1024,2048]{1,0:T(8,128)(2,1)}, u32[]{:S(2)}) %copy-start.1) | copy-done | bytes 4194328
  32.9 1.3 %own_spectra.1 = (bf16[2,2,64,1024]{3,2,1,0:T(8,128)(2,1)S(1)}, bf16[2,2,16,1024]{3,2,1,0:T(8,128)(2,1)S(1)}) custom-call(s32[1]{0:T(128)} %bitcast.half_ref, s32[1]{0:T(128)} %bitcast.1.me_ref, bf16[4,2,128,256]{3,2,1,0:T(8,128)(2,1)S(1)} %all-to-all-done.pieces_ref, bf16[1024,2048]{1,0:T(8,128)(2,1)S(1)} %copy-done.1), custom_call_target="tpu_custom_call" | custom-call | flops 1073741824 | bytes 8388608 | tf_op jit(solution)/shard_map/own_spectra/pallas_call | solution.py:312
  35.1 2.0 %first_slot.1 = (bf16[2,1,128,256]{3,2,1,0:T(8,128)(2,1)S(1)}, bf16[1,2,64,1024]{3,2,1,0:T(8,128)(2,1)S(1)}, bf16[1,2,16,1024]{3,2,1,0:T(8,128)(2,1)S(1)}, bf16[2,64,1024]{2,1,0:T(8,128)(2,1)S(1)}) custom-call(s32[1]{0:T(128)} %bitcast.half_ref, s32[1]{0:T(128)} %bitcast.1.me_ref, s32[1,2,2]{2,1,0:T(2,128)S(1)} %collective-permute-done.theirs_ref, ...), custom_call_target="tpu_custom_call" | custom-call | flops 1073741824 | bytes 8388608 | tf_op jit(solution)/shard_map/first_slot/pallas_call | solution.py:344
  37.0 3.8 %collective-permute-start.9 = (bf16[2,1,128,256]{3,2,1,0:T(8,128)(2,1)S(1)}, bf16[2,1,128,256]{3,2,1,0:T(8,128)(2,1)S(1)}, u32[]{:S(2)}, u32[]{:S(2)}) collective-permute-start(bf16[2,1,128,256]{3,2,1,0:T(8,128)(2,1)S(1)} %get-tuple-element.57), channel_id=1, source_target_pairs={{0,8},{1,9},{2,10},{3,11},{4,12},{5,13},{6,14},{7,15},{8,0},{9,1},... | collective-permute-start | bytes 393224 | tf_op jit(solution)/shard_map/ppermute | solution.py:561
  40.8 3.0 %other_slots.1 = (bf16[2,1,128,256]{3,2,1,0:T(8,128)(2,1)}, bf16[4,2,64,1024]{3,2,1,0:T(8,128)(2,1)S(1)}, bf16[4,2,16,1024]{3,2,1,0:T(8,128)(2,1)S(1)}, bf16[2,1...) custom-call(s32[1]{0:T(128)} %bitcast.half_ref, s32[1]{0:T(128)} %bitcast.1.me_ref, ...), custom_call_target="tpu_custom_call" | custom-call | flops 1073741824 | bytes 8388608 | tf_op jit(solution)/shard_map/other_slots/pallas_call | solution.py:402
  44.4 2.1 %collective-permute-start.8 = (bf16[2,128,256]{2,1,0:T(8,128)(2,1)S(1)}, bf16[2,128,256]{2,1,0:T(8,128)(2,1)S(1)}, u32[]{:S(2)}, u32[]{:S(2)}) collective-permute-start(bf16[2,128,256]{2,1,0:T(8,128)(2,1)S(1)} %get-tuple-element.56), channel_id=1, source_target_pairs={{0,11},{1,10},{2,9},{3,8},{4,15},{5,14},{6,13},{7,12},{8,3},{9,2},... | collective-permute-start | bytes 393224 | tf_op jit(solution)/shard_map/ppermute | solution.py:561
  47.1 9.2 %collective-permute-done.9.refs_0_ = bf16[2,1,128,256]{3,2,1,0:T(8,128)(2,1)S(1)} collective-permute-done((bf16[2,1,128,256]{3,2,1,0:T(8,128)(2,1)S(1)}, bf16[2,1,128,256]{3,2,1,0:T(8,128)(2,1)S(1)}, u32[]{:S(2)}, u32[]{:S(2)}) %collective-permute-start.9) | collective-permute-done | bytes 131104 | tf_op jit(solution)/shard_map/ppermute | solution.py:561
  56.3 3.1 %own_slots.1 = bf16[4,2,128,256]{3,2,1,0:T(8,128)(2,1)} custom-call(s32[1]{0:T(128)} %bitcast.half_ref, s32[1]{0:T(128)} %bitcast.1.me_ref, s32[1,2,2]{2,1,0:T(2,128)S(1)} %copy-done.7, s32[1,2,2]{2,1,0:T(2,128)S(1)} %collective-permute-done.theirs_ref, bf16[1024,2048]{1,0:T(8,128)(2,1)S(1)} %copy-done.2, ...), custom_call_target="tpu_custom_call" | custom-call | flops 1073741824 | bytes 8388608 | tf_op jit(solution)/shard_map/own_slots/pallas_call | solution.py:437
  59.4 3.5 %all-to-all-start.1 = ((bf16[4,2,128,256]{3,2,1,0:T(8,128)(2,1)}), bf16[4,2,128,256]{3,2,1,0:T(8,128)(2,1)S(1)}, u32[]{:S(2)}, u32[]{:S(2)}) async-start(bf16[4,2,128,256]{3,2,1,0:T(8,128)(2,1)} %own_slots.1), calls=%async_computation.1 | async-start | bytes 1048576 | tf_op jit(solution)/shard_map/all_to_all | solution.py:564
  65.6 6.1 %all-to-all-done.1.own_ref = bf16[4,2,128,256]{3,2,1,0:T(8,128)(2,1)S(1)} async-done(((bf16[4,2,128,256]{3,2,1,0:T(8,128)(2,1)}), bf16[4,2,128,256]{3,2,1,0:T(8,128)(2,1)S(1)}, u32[]{:S(2)}, u32[]{:S(2)}) %all-to-all-start.1) | async-done | bytes 524320 | tf_op jit(solution)/shard_map/all_to_all | solution.py:564
  71.7 1.0 %own_surfaces.1.part_ref = f32[2,256,1024]{2,1,0:T(8,128)S(1)} custom-call(s32[1]{0:T(128)} %bitcast.half_ref, bf16[4,2,128,256]{3,2,1,0:T(8,128)(2,1)S(1)} %all-to-all-done.1.own_ref, bf16[1024,1024]{1,0:T(8,128)(2,1)S(1)} %copy-done.3), custom_call_target="tpu_custom_call" | custom-call | flops 536870912 | bytes 2097152 | tf_op jit(solution)/shard_map/own_surfaces/pallas_call | solution.py:463
  72.7 2.0 %surfaces.1 = f32[2,256,1024]{2,1,0:T(8,128)} custom-call(s32[1]{0:T(128)} %bitcast.half_ref, s32[1]{0:T(128)} %bitcast.1.me_ref, s32[1]{0:T(128)S(6)} %copy.8.counts_ref, f32[2,256,1024]{2,1,0:T(8,128)S(1)} %own_surfaces.1.part_ref, bf16[2,1,128,256]{3,2,1,0:T(8,128)(2,1)S(1)} %collective-permute-done.9.refs_0_, ...), custom_call_target="tpu_custom_call" | custom-call | flops 536870912 | bytes 4194304 | tf_op jit(solution)/shard_map/surfaces/pallas_call | solution.py:520
  (35 shorter events, 4.3 us)
Async XLA Ops:
  0.0 8.3 %copy-start.3 = (bf16[1024,1024]{1,0:T(8,128)(2,1)S(1)}, bf16[1024,1024]{1,0:T(8,128)(2,1)}, u32[]{:S(2)}) copy-start(bf16[1024,1024]{1,0:T(8,128)(2,1)} %constant.29.clone.table_hbm.table_ref.refs_6_) | copy-start | bytes 6291460
  0.0 8.3 %copy-start.5 = (f32[8,1024]{1,0:T(8,128)S(1)}, f32[8,1024]{1,0:T(8,128)}, u32[]{:S(2)}) copy-start(f32[8,1024]{1,0:T(8,128)} %constant.30.clone.down_ref) | copy-start | bytes 98308
  0.0 8.3 %copy-start.6 = (f32[1,1024]{1,0:T(1,128)S(1)}, f32[1,1024]{1,0:T(1,128)}, u32[]{:S(2)}) copy-start(f32[1,1024]{1,0:T(1,128)} %constant.31.clone.across_ref) | copy-start | bytes 12292
  0.0 8.3 %copy-start.7 = (s32[1,2,2]{2,1,0:T(2,128)S(1)}, s32[1,2,2]{2,1,0:T(2,128)}, u32[]{:S(2)}) copy-start(s32[1,2,2]{2,1,0:T(2,128)} %pairs_ref.3) | copy-start | bytes 52
  4.1 19.7 %collective-permute-start.1 = (bf16[2,128,256]{2,1,0:T(8,128)(2,1)}, bf16[2,128,256]{2,1,0:T(8,128)(2,1)S(1)}, u32[]{:S(2)}, u32[]{:S(2)}) collective-permute-start(bf16[2,128,256]{2,1,0:T(8,128)(2,1)} %get-tuple-element.36), channel_id=1, source_target_pairs={{0,8},{1,9},{2,10},{3,11},{4,12},{5,13},{6,14},{7,15},{8,0},{9,1},... | collective-permute-start | bytes 393224 | tf_op jit(solution)/shard_map/ppermute | solution.py:561
  8.3 17.0 %collective-permute-start.2 = (bf16[2,128,256]{2,1,0:T(8,128)(2,1)}, bf16[2,128,256]{2,1,0:T(8,128)(2,1)S(1)}, u32[]{:S(2)}, u32[]{:S(2)}) collective-permute-start(bf16[2,128,256]{2,1,0:T(8,128)(2,1)} %get-tuple-element.37), channel_id=1, source_target_pairs={{0,9},{1,8},{2,11},{3,10},{4,13},{5,12},{6,15},{7,14},{8,1},{9,0},... | collective-permute-start | bytes 393224 | tf_op jit(solution)/shard_map/ppermute | solution.py:561
  8.3 1.6 %copy-start.4 = (f32[2,256,1024]{2,1,0:T(8,128)S(1)}, f32[2,256,1024]{2,1,0:T(8,128)}, u32[]{:S(2)}) copy-start(f32[2,256,1024]{2,1,0:T(8,128)} %tile_ref.1) | copy-start | bytes 6291460
  14.1 16.6 %all-to-all-start = ((bf16[4,2,128,256]{3,2,1,0:T(8,128)(2,1)}), bf16[4,2,128,256]{3,2,1,0:T(8,128)(2,1)S(1)}, u32[]{:S(2)}, u32[]{:S(2)}) async-start(bf16[4,2,128,256]{3,2,1,0:T(8,128)(2,1)} %get-tuple-element.47), calls=%async_computation | async-start | bytes 1048576 | tf_op jit(solution)/shard_map/all_to_all | solution.py:564
  17.6 16.5 %collective-permute-start.5 = (bf16[128,256]{1,0:T(8,128)(2,1)S(1)}, bf16[128,256]{1,0:T(8,128)(2,1)S(1)}, u32[]{:S(2)}, u32[]{:S(2)}) collective-permute-start(bf16[128,256]{1,0:T(8,128)(2,1)S(1)} %get-tuple-element.50), channel_id=1, source_target_pairs={{0,10},{1,11},{2,8},{3,9},{4,14},{5,15},{6,12},{7,13},{8,2},{9,3},... | collective-permute-start | bytes 196616 | tf_op jit(solution)/shard_map/ppermute | solution.py:561
  21.1 13.1 %collective-permute-start.6 = (bf16[128,256]{1,0:T(8,128)(2,1)S(1)}, bf16[128,256]{1,0:T(8,128)(2,1)S(1)}, u32[]{:S(2)}, u32[]{:S(2)}) collective-permute-start(bf16[128,256]{1,0:T(8,128)(2,1)S(1)} %get-tuple-element.51), channel_id=1, source_target_pairs={{0,11},{1,10},{2,9},{3,8},{4,15},{5,14},{6,13},{7,12},{8,3},{9,2},... | collective-permute-start | bytes 196616 | tf_op jit(solution)/shard_map/ppermute | solution.py:561
  21.3 12.8 %collective-permute-start = (s32[1,2,2]{2,1,0:T(2,128)S(1)}, s32[1,2,2]{2,1,0:T(2,128)S(1)}, u32[]{:S(2)}, u32[]{:S(2)}) collective-permute-start(s32[1,2,2]{2,1,0:T(2,128)S(1)} %copy-done.7), channel_id=1, source_target_pairs={{0,8},{1,9},{2,10},{3,11},{4,12},{5,13},{6,14},{7,15},{8,0},{9,1},... | collective-permute-start | bytes 56 | tf_op jit(solution)/shard_map/ppermute | solution.py:561
  23.9 17.0 %collective-permute-start.3 = (bf16[128,256]{1,0:T(8,128)(2,1)S(1)}, bf16[128,256]{1,0:T(8,128)(2,1)S(1)}, u32[]{:S(2)}, u32[]{:S(2)}) collective-permute-start(bf16[128,256]{1,0:T(8,128)(2,1)S(1)} %get-tuple-element.45), channel_id=1, source_target_pairs={{0,10},{1,11},{2,8},{3,9},{4,14},{5,15},{6,12},{7,13},{8,2},{9,3},... | collective-permute-start | bytes 196616 | tf_op jit(solution)/shard_map/ppermute | solution.py:561
  25.3 15.5 %collective-permute-start.4 = (bf16[128,256]{1,0:T(8,128)(2,1)S(1)}, bf16[128,256]{1,0:T(8,128)(2,1)S(1)}, u32[]{:S(2)}, u32[]{:S(2)}) collective-permute-start(bf16[128,256]{1,0:T(8,128)(2,1)S(1)} %get-tuple-element.46), channel_id=1, source_target_pairs={{0,11},{1,10},{2,9},{3,8},{4,15},{5,14},{6,13},{7,12},{8,3},{9,2},... | collective-permute-start | bytes 196616 | tf_op jit(solution)/shard_map/ppermute | solution.py:561
  26.6 1.0 %copy-start.8 = (f32[128,1024]{1,0:T(8,128)S(1)}, f32[128,1024]{1,0:T(8,128)}, u32[]{:S(2)}) copy-start(f32[128,1024]{1,0:T(8,128)} %constant.32.clone.short_ref) | copy-start | bytes 1572868
  28.7 2.0 %copy-start = (bf16[1024,2048]{1,0:T(8,128)(2,1)}, bf16[1024,2048]{1,0:T(8,128)(2,1)S(1)}, u32[]{:S(2)}) copy-start(bf16[1024,2048]{1,0:T(8,128)(2,1)S(1)} %height_table.1.table_ref.refs_4_) | copy-start | bytes 12582916
  30.7 2.2 %copy-start.1 = (bf16[1024,2048]{1,0:T(8,128)(2,1)S(1)}, bf16[1024,2048]{1,0:T(8,128)(2,1)}, u32[]{:S(2)}) copy-start(bf16[1024,2048]{1,0:T(8,128)(2,1)} %copy-done) | copy-start | bytes 12582916
  32.9 2.2 %copy-start.2 = (bf16[1024,2048]{1,0:T(8,128)(2,1)S(1)}, bf16[1024,2048]{1,0:T(8,128)(2,1)}, u32[]{:S(2)}) copy-start(bf16[1024,2048]{1,0:T(8,128)(2,1)} %copy-done) | copy-start | bytes 12582916
  37.0 19.3 %collective-permute-start.9 = (bf16[2,1,128,256]{3,2,1,0:T(8,128)(2,1)S(1)}, bf16[2,1,128,256]{3,2,1,0:T(8,128)(2,1)S(1)}, u32[]{:S(2)}, u32[]{:S(2)}) collective-permute-start(bf16[2,1,128,256]{3,2,1,0:T(8,128)(2,1)S(1)} %get-tuple-element.57), channel_id=1, source_target_pairs={{0,8},{1,9},{2,10},{3,11},{4,12},{5,13},{6,14},{7,15},{8,0},{9,1},... | collective-permute-start | bytes 393224 | tf_op jit(solution)/shard_map/ppermute | solution.py:561
  43.8 28.9 %collective-permute-start.7 = (bf16[2,128,256]{2,1,0:T(8,128)(2,1)S(1)}, bf16[2,128,256]{2,1,0:T(8,128)(2,1)S(1)}, u32[]{:S(2)}, u32[]{:S(2)}) collective-permute-start(bf16[2,128,256]{2,1,0:T(8,128)(2,1)S(1)} %get-tuple-element.55), channel_id=1, source_target_pairs={{0,10},{1,11},{2,8},{3,9},{4,14},{5,15},{6,12},{7,13},{8,2},{9,3},... | collective-permute-start | bytes 393224 | tf_op jit(solution)/shard_map/ppermute | solution.py:561
  44.4 28.3 %collective-permute-start.8 = (bf16[2,128,256]{2,1,0:T(8,128)(2,1)S(1)}, bf16[2,128,256]{2,1,0:T(8,128)(2,1)S(1)}, u32[]{:S(2)}, u32[]{:S(2)}) collective-permute-start(bf16[2,128,256]{2,1,0:T(8,128)(2,1)S(1)} %get-tuple-element.56), channel_id=1, source_target_pairs={{0,11},{1,10},{2,9},{3,8},{4,15},{5,14},{6,13},{7,12},{8,3},{9,2},... | collective-permute-start | bytes 393224 | tf_op jit(solution)/shard_map/ppermute | solution.py:561
  46.5 17.7 %collective-permute-start.11 = (bf16[2,1,128,256]{3,2,1,0:T(8,128)(2,1)}, bf16[2,1,128,256]{3,2,1,0:T(8,128)(2,1)S(1)}, u32[]{:S(2)}, u32[]{:S(2)}) collective-permute-start(bf16[2,1,128,256]{3,2,1,0:T(8,128)(2,1)} %get-tuple-element.64), channel_id=1, source_target_pairs={{0,8},{1,9},{2,10},{3,11},{4,12},{5,13},{6,14},{7,15},{8,0},{9,1},... | collective-permute-start | bytes 393224 | tf_op jit(solution)/shard_map/ppermute | solution.py:561
  59.4 12.3 %all-to-all-start.1 = ((bf16[4,2,128,256]{3,2,1,0:T(8,128)(2,1)}), bf16[4,2,128,256]{3,2,1,0:T(8,128)(2,1)S(1)}, u32[]{:S(2)}, u32[]{:S(2)}) async-start(bf16[4,2,128,256]{3,2,1,0:T(8,128)(2,1)} %own_slots.1), calls=%async_computation.1 | async-start | bytes 1048576 | tf_op jit(solution)/shard_map/all_to_all | solution.py:564
  63.5 9.2 %collective-permute-start.10 = (bf16[1,128,256]{2,1,0:T(8,128)(2,1)}, bf16[1,128,256]{2,1,0:T(8,128)(2,1)S(1)}, u32[]{:S(2)}, u32[]{:S(2)}) collective-permute-start(bf16[1,128,256]{2,1,0:T(8,128)(2,1)} %slice_bitcast_fusion.1), channel_id=1, source_target_pairs={{0,1},{1,0},{2,3},{3,2},{4,5},{5,4},{6,7},{7,6},{8,9},{9,8},{10,11... | collective-permute-start | bytes 196616 | tf_op jit(solution)/shard_map/ppermute | solution.py:567
  64.9 7.8 %collective-permute-start.12 = (bf16[1,128,256]{2,1,0:T(8,128)(2,1)}, bf16[1,128,256]{2,1,0:T(8,128)(2,1)S(1)}, u32[]{:S(2)}, u32[]{:S(2)}) collective-permute-start(bf16[1,128,256]{2,1,0:T(8,128)(2,1)} %slice_bitcast_fusion), channel_id=1, source_target_pairs={{0,1},{1,0},{2,3},{3,2},{4,5},{5,4},{6,7},{7,6},{8,9},{9,8},{10,11... | collective-permute-start | bytes 196616 | tf_op jit(solution)/shard_map/ppermute | solution.py:567

commit v12 on v11

--- a/solution.py
+++ b/solution.py
@@ -33,34 +33,47 @@
     return table.reshape(width, width).astype(jnp.bfloat16)
 
 
-def height_table(height, after):
-    fine = 32
-    coarse = height // fine
+FINE = 32
+
+
+def short_tables(height):
     column = np.arange(height)[None, :]
-    rough = 2.0 * math.pi / height * (np.arange(coarse)[:, None] * fine * column % height)
-    small = 2.0 * math.pi / height * (np.arange(fine)[:, None] * column % height)
+    rough = 2.0 * math.pi / height * (np.arange(height // FINE)[:, None] * FINE * column % height)
+    small = 2.0 * math.pi / height * (np.arange(FINE)[:, None] * column % height)
+    short = [np.cos(small), np.sin(small), np.cos(rough), np.sin(rough)]
+    return jnp.asarray(np.concatenate(short), jnp.float32)
+
+
+def scaled_tables(height, after):
     factor = 1.0 / math.sqrt(height)
-    short = [np.cos(small), np.sin(small), np.cos(rough) * factor, np.sin(rough) * factor]
 
     def body(short_ref, *refs):
-        out_ref = refs[-1]
-        sc, ss = short_ref[:fine], short_ref[fine : 2 * fine]
-        for a in range(2 * fine, 2 * fine + coarse):
-            rc, rs = short_ref[a : a + 1, :], short_ref[a + coarse : a + coarse + 1, :]
-            here = slice((a - 2 * fine) * fine, (a - 2 * fine + 1) * fine)
-            out_ref[here, :height] = (rc * sc - rs * ss).astype(jnp.bfloat16)
-            out_ref[here, height:] = (rs * sc + rc * ss).astype(jnp.bfloat16)
-
+        refs[-1][: 2 * FINE] = short_ref[: 2 * FINE]
+        refs[-1][2 * FINE :] = short_ref[2 * FINE :] * factor
+
+    short = short_tables(height)
     return pl.pallas_call(
         body,
         in_specs=[pl.BlockSpec(memory_space=pltpu.VMEM)]
         + [pl.BlockSpec(memory_space=pl.ANY)] * len(after),
         out_specs=pl.BlockSpec(memory_space=pltpu.VMEM),
-        out_shape=jax.ShapeDtypeStruct((height, 2 * height), jnp.bfloat16),
-        compiler_params=params(),
-        cost_estimate=cost(1 << 33, 4 * height * height),
-        name="height_table",
-    )(jnp.asarray(np.concatenate(short), jnp.float32), *after)
+        out_shape=jax.ShapeDtypeStruct(short.shape, short.dtype),
+        compiler_params=params(),
+        cost_estimate=cost(1 << 33, 8 * short.size),
+        name="scaled_tables",
+    )(short, *after)
+
+
+def make_table(short_ref, out_ref, first, rows):
+    height = short_ref.shape[1]
+    coarse = height // FINE
+    sc, ss = short_ref[:FINE], short_ref[FINE : 2 * FINE]
+    for j in range(first // FINE, (first + rows) // FINE):
+        a = 2 * FINE + j
+        rc, rs = short_ref[a : a + 1, :], short_ref[a + coarse : a + coarse + 1, :]
+        here = slice(j * FINE, (j + 1) * FINE)
+        out_ref[here, :height] = (rc * sc - rs * ss).astype(jnp.bfloat16)
+        out_ref[here, height:] = (rs * sc + rc * ss).astype(jnp.bfloat16)
 
 
 def cost(flops, moved):
@@ -151,10 +164,7 @@
     distant = peers - 2
 
     def body(half_ref, me_ref, pairs_ref, tile_ref, down_ref, across_ref, table_ref, *refs):
-        out_ref, far, (work, stage, done) = refs[0], refs[1:-3], refs[-3:]
-        copies = [
-            pltpu.make_async_copy(stage.at[i], far[i], done.at[i]) for i in range(count * distant)
-        ]
+        out_ref, far, work = refs[0], refs[1:-1], refs[-1]
         half, me = half_ref[0], me_ref[0]
         t = pl.program_id(0)
         shaded = shade(tile_ref[0], down_ref, across_ref)
@@ -167,18 +177,11 @@
 
                     @pl.when(t == i)
                     def _():
-                        to = i * distant + 2 * j - 2 + k
-                        stage[to] = work[pl.ds(place, block), :]
-                        copies[to].start()
+                        far[i * distant + 2 * j - 2 + k][...] = work[pl.ds(place, block), :]
 
         start = pl.multiple_of(half * span, span)
         y = times_table(table_ref[pl.ds(start, span), :], shaded)
         out_ref[:, 0] = y.reshape(peers, block, rows)
-
-        @pl.when(t == count - 1)
-        def _():
-            for copy in copies:
-                copy.wait()
 
     return pl.pallas_call(
         body,
@@ -195,13 +198,9 @@
                 pl.BlockSpec(
                     (peers, 1, block, rows), lambda t, half, me, a: (0, (a[0, 0, 0] + t) % count, 0, 0)
                 ),
-                *[pl.BlockSpec(memory_space=pltpu.HBM)] * (count * distant),
+                *[pl.BlockSpec((block, rows), lambda t, half, me, a: (0, 0))] * (count * distant),
             ],
-            scratch_shapes=[
-                pltpu.VMEM((2 * block, rows), jnp.bfloat16),
-                pltpu.VMEM((count * distant, block, rows), jnp.bfloat16),
-                pltpu.SemaphoreType.DMA((count * distant,)),
-            ],
+            scratch_shapes=[pltpu.VMEM((2 * block, rows), jnp.bfloat16)],
         ),
         out_shape=[
             jax.ShapeDtypeStruct((peers, count, block, rows), jnp.bfloat16),
@@ -301,27 +300,37 @@
             out[p, block:] = ((s_part[re] + c_part[im]) * twice).astype(jnp.bfloat16)
 
 
-def own_spectra(place, pieces, table):
+def own_spectra(place, pieces, short):
     peers, count, double, rows = pieces.shape
-    height = table.shape[0]
-
-    def body(half_ref, me_ref, pieces_ref, table_ref, spectra, edge):
-        inputs = [pieces_ref[k].reshape(count * double, rows) for k in range(peers)]
-        store_spectra((half_ref, me_ref), gather_rows(inputs, table_ref, 0), spectra, edge, 0)
+    height = peers * rows
+
+    def body(half_ref, me_ref, pieces_ref, short_ref, *refs):
+        spectra, edge, table_ref = refs[-3:]
+        total = None
+        for k in range(peers):
+            make_table(short_ref, table_ref, k * rows, rows)
+            term = jnp.dot(
+                pieces_ref[k].reshape(count * double, rows),
+                table_ref[k * rows : (k + 1) * rows],
+                preferred_element_type=jnp.float32,
+            )
+            total = term if total is None else total + term
+        store_spectra((half_ref, me_ref), total, spectra, edge, 0)
 
     return pl.pallas_call(
         body,
         in_specs=[pl.BlockSpec(memory_space=pltpu.SMEM)] * 2
         + [pl.BlockSpec(memory_space=pltpu.VMEM)] * 2,
-        out_specs=[pl.BlockSpec(memory_space=pltpu.VMEM)] * 2,
+        out_specs=[pl.BlockSpec(memory_space=pltpu.VMEM)] * 3,
         out_shape=[
             jax.ShapeDtypeStruct((count, 2, double // 2, height), jnp.bfloat16),
             jax.ShapeDtypeStruct((count, 2, 16, height), jnp.bfloat16),
+            jax.ShapeDtypeStruct((height, 2 * height), jnp.bfloat16),
         ],
         compiler_params=params(),
         cost_estimate=cost(4 * count * double * height * height, 8 * height * height),
         name="own_spectra",
-    )(*place, pieces, table)
+    )(*place, pieces, short)
 
 
 def first_slot(place, theirs, near, far, table, spectra, edge):
@@ -584,9 +593,8 @@
         far.append([across(sent[i * distant + k - 2], k) for k in range(2, peers)])
     mine = along(kept)
 
-    table_h = height_table(height, near)
     place = (scalar(half), scalar(me))
-    spectra, edge = own_spectra(place, mine, table_h)
+    spectra, edge, table_h = own_spectra(place, mine, scaled_tables(height, near))
     lead, lead_spectra, lead_edge, phases = first_slot(
         place, theirs, near, far[0], table_h, spectra, edge
     )
@@ -595,8 +603,8 @@
         place, theirs, near, far[1:], table_h, spectra, edge, lead_spectra, lead_edge, phases
     )
     rest = across(rest, 0)
+    lead, *back = lax.optimization_barrier((lead, *back))
     back = [across(back[k - 2], k) for k in range(2, peers)]
-    lead, spectra, edge = lax.optimization_barrier((lead, spectra, edge))
     own = own_slots(place, pairs, theirs, table_h, spectra, edge, peers)
     part = own_surfaces(half, along(own), table_w)
     *back, part = lax.optimization_barrier((*back, part))

time: 75.2 us -> 67.1 us (0.89)
  waiting for transfers between devices: 15.7 us -> 9.73 us
  local copies, waits for them, and re-layouts: 8.92 us -> 5.73 us
  starting transfers between devices: 27.6 us -> 29.3 us
    ppermute x11, waiting for transfers between devices: 9.56 us -> 5.56 us  [across(): return lax.ppermute(value, axes, moves)]
    unnamed x18 -> x16, local copies, waits for them, and re-layouts: 7.66 us -> 4.48 us
    all_to_all x2, waiting for transfers between devices: 6.12 us -> 4.16 us  [along(): return lax.all_to_all(blocks, 'rows', split_axis=0, concat_axis=0)]
    ppermute x11, starting transfers between devices: 20.2 us -> 21.8 us  [across(): return lax.ppermute(value, axes, moves)]
    pallas_call x1, Pallas kernels: 1.11 us -> 0.04 us  [scaled_tables(): pl.pallas_call(body, in_specs=[pl.BlockSpec(memory_space=pltpu.VMEM)] + [...]
  transfers between devices with their start and end apart: 15 -> 15, of which waited for: 3 -> 5; matrix products, arithmetic and copies ran while one was open for 2% -> 2% of each run, Pallas kernels for 21% -> 23%
where the time goes in v12:
time: 67.1 us; the launch traced here: 66.8 us
  starting transfers between devices  29.3 us (44%)
  Pallas kernels  21.2 us (32%)
  waiting for transfers between devices  9.73 us (15%)
  local copies, waits for them, and re-layouts  5.73 us (9%)
  between operations  0.78 us (1%)
    ppermute x11, starting transfers between devices, across(): return lax.ppermute(value, axes, moves)  21.8 us
    all_to_all x2, starting transfers between devices, along(): return lax.all_to_all(blocks, 'rows', split_axis=0, concat_axis=0)  6.94 us
    ppermute x11, waiting for transfers between devices, across(): return lax.ppermute(value, axes, moves)  5.56 us
    unnamed x16, local copies, waits for them, and re-layouts  4.48 us
    all_to_all x2, waiting for transfers between devices, along(): return lax.all_to_all(blocks, 'rows', split_axis=0, concat_axis=0)  4.16 us
    pallas_call x1, Pallas kernels, near_columns(): pl.pallas_call(body, grid_spec=pltpu.PrefetchScalarGridSpec(num_scalar_pr...  4.11 us
    pallas_call x1, Pallas kernels, rest_columns(): pl.pallas_call(body, grid_spec=pltpu.PrefetchScalarGridSpec(num_scalar_pr...  3.86 us
    pallas_call x1, Pallas kernels, own_slots(): pl.pallas_call(body, in_specs=[pl.BlockSpec(memory_space=pltpu.SMEM)] * 4...  3.05 us
  transfers between devices with their start and end apart: 15, of which 5 were waited for; matrix products, arithmetic and copies ran while one was open for 2% of the time, Pallas kernels for 23%

profile of v12, /device:TPU:0, one launch (start us, length us, event | category | flops | bytes accessed | tf_op | source)
XLA Modules:
  0.0 66.8 jit_solution(6064499917340757445)
XLA Ops:
  0.0 4.1 %near_columns.1 = (bf16[2,128,256]{2,1,0:T(8,128)(2,1)}, bf16[2,128,256]{2,1,0:T(8,128)(2,1)}) custom-call(s32[1]{0:T(128)} %bitcast.half_ref, s32[1]{0:T(128)} %bitcast.1.me_ref, f32[2,256,1024]{2,1,0:T(8,128)} %tile_ref.1, f32[8,1024]{1,0:T(8,128)} %constant.30.clone.down_ref, f32[1,1024]{1,0:T(1,128)} %constant.31.clone.across_ref, ...), custom_call_target="tpu_custom_call" | custom-call | flops 268435456 | bytes 2621440 | tf_op jit(solution)/shard_map/near_columns/pallas_call | solution.py:134
  4.1 4.1 %collective-permute-start.1 = (bf16[2,128,256]{2,1,0:T(8,128)(2,1)}, bf16[2,128,256]{2,1,0:T(8,128)(2,1)S(1)}, u32[]{:S(2)}, u32[]{:S(2)}) collective-permute-start(bf16[2,128,256]{2,1,0:T(8,128)(2,1)} %get-tuple-element.37), channel_id=1, source_target_pairs={{0,8},{1,9},{2,10},{3,11},{4,12},{5,13},{6,14},{7,15},{8,0},{9,1},... | collective-permute-start | bytes 393224 | tf_op jit(solution)/shard_map/ppermute | solution.py:570
  8.3 1.6 %copy-done.1 = f32[2,256,1024]{2,1,0:T(8,128)S(1)} copy-done((f32[2,256,1024]{2,1,0:T(8,128)S(1)}, f32[2,256,1024]{2,1,0:T(8,128)}, u32[]{:S(2)}) %copy-start.1) | copy-done | bytes 2097176
  9.9 3.9 %rest_columns.1 = (bf16[4,2,128,256]{3,2,1,0:T(8,128)(2,1)}, bf16[128,256]{1,0:T(8,128)(2,1)S(1)}, bf16[128,256]{1,0:T(8,128)(2,1)S(1)}, bf16[128,256]{1,0:T(8,128)(2,1)S(1)}, bf16[128,256]{1,0:T(8,128)(2,1)S(1)}) custom-call(s32[1]{0:T(128)} %bitcast.2.half_ref, s32[1]{0:T(128)} %bitcast.1.me_ref, s32[1,2,2]{2,1,0:T(2,128)S(1)} %copy-done.4, ...), custom_call_target="tpu_custom_call" | custom-call | flops 805306368 | bytes 4194304 | tf_op jit(solution)/shard_map/rest_columns/pallas_call | solution.py:186
  13.7 3.5 %all-to-all-start = ((bf16[4,2,128,256]{3,2,1,0:T(8,128)(2,1)}), bf16[4,2,128,256]{3,2,1,0:T(8,128)(2,1)S(1)}, u32[]{:S(2)}, u32[]{:S(2)}) async-start(bf16[4,2,128,256]{3,2,1,0:T(8,128)(2,1)} %get-tuple-element.48), calls=%async_computation | async-start | bytes 1048576 | tf_op jit(solution)/shard_map/all_to_all | solution.py:573
  17.2 3.5 %collective-permute-start.3 = (bf16[128,256]{1,0:T(8,128)(2,1)S(1)}, bf16[128,256]{1,0:T(8,128)(2,1)S(1)}, u32[]{:S(2)}, u32[]{:S(2)}) collective-permute-start(bf16[128,256]{1,0:T(8,128)(2,1)S(1)} %get-tuple-element.46), channel_id=1, source_target_pairs={{0,10},{1,11},{2,8},{3,9},{4,14},{5,15},{6,12},{7,13},{8,2},{9,3},... | collective-permute-start | bytes 196616 | tf_op jit(solution)/shard_map/ppermute | solution.py:570
  20.9 2.5 %collective-permute-start = (s32[1,2,2]{2,1,0:T(2,128)S(1)}, s32[1,2,2]{2,1,0:T(2,128)S(1)}, u32[]{:S(2)}, u32[]{:S(2)}) collective-permute-start(s32[1,2,2]{2,1,0:T(2,128)S(1)} %copy-done.4), channel_id=1, source_target_pairs={{0,8},{1,9},{2,10},{3,11},{4,12},{5,13},{6,14},{7,15},{8,0},{9,1},... | collective-permute-start | bytes 56 | tf_op jit(solution)/shard_map/ppermute | solution.py:570
  23.4 1.4 %collective-permute-start.6 = (bf16[128,256]{1,0:T(8,128)(2,1)S(1)}, bf16[128,256]{1,0:T(8,128)(2,1)S(1)}, u32[]{:S(2)}, u32[]{:S(2)}) collective-permute-start(bf16[128,256]{1,0:T(8,128)(2,1)S(1)} %get-tuple-element.53), channel_id=1, source_target_pairs={{0,10},{1,11},{2,8},{3,9},{4,14},{5,15},{6,12},{7,13},{8,2},{9,3},... | collective-permute-start | bytes 196616 | tf_op jit(solution)/shard_map/ppermute | solution.py:570
  24.9 1.3 %collective-permute-start.7 = (bf16[128,256]{1,0:T(8,128)(2,1)S(1)}, bf16[128,256]{1,0:T(8,128)(2,1)S(1)}, u32[]{:S(2)}, u32[]{:S(2)}) collective-permute-start(bf16[128,256]{1,0:T(8,128)(2,1)S(1)} %get-tuple-element.54), channel_id=1, source_target_pairs={{0,11},{1,10},{2,9},{3,8},{4,15},{5,14},{6,13},{7,12},{8,3},{9,2},... | collective-permute-start | bytes 196616 | tf_op jit(solution)/shard_map/ppermute | solution.py:570
  26.2 1.0 %copy-done.5 = f32[128,1024]{1,0:T(8,128)S(1)} copy-done((f32[128,1024]{1,0:T(8,128)S(1)}, f32[128,1024]{1,0:T(8,128)}, u32[]{:S(2)}) %copy-start.5) | copy-done | bytes 524312
  28.0 0.9 %all-to-all-done.pieces_ref = bf16[4,2,128,256]{3,2,1,0:T(8,128)(2,1)S(1)} async-done(((bf16[4,2,128,256]{3,2,1,0:T(8,128)(2,1)}), bf16[4,2,128,256]{3,2,1,0:T(8,128)(2,1)S(1)}, u32[]{:S(2)}, u32[]{:S(2)}) %all-to-all-start) | async-done | bytes 524320 | tf_op jit(solution)/shard_map/all_to_all | solution.py:573
  28.9 1.0 %copy-done.7 = f32[128,1024]{1,0:T(8,128)S(1)} copy-done((f32[128,1024]{1,0:T(8,128)S(1)}, f32[128,1024]{1,0:T(8,128)}, u32[]{:S(2)}) %copy-start.7) | copy-done | bytes 524312
  30.0 1.6 %own_spectra.1 = (bf16[2,2,64,1024]{3,2,1,0:T(8,128)(2,1)S(1)}, bf16[2,2,16,1024]{3,2,1,0:T(8,128)(2,1)S(1)}, bf16[1024,2048]{1,0:T(8,128)(2,1)S(1)}) custom-call(s32[1]{0:T(128)} %bitcast.half_ref, s32[1]{0:T(128)} %bitcast.1.me_ref, bf16[4,2,128,256]{3,2,1,0:T(8,128)(2,1)S(1)} %all-to-all-done.pieces_ref, f32[128,1024]{1,0:T(8,128)S(1)} %copy-done.7), custom_call_target="tpu_custom_call" | custom-call | flops 1073741824 | bytes 8388608 | tf_op jit(solution)/shard_map/own_spectra/pallas_call | solution.py:320
  31.6 2.6 %first_slot.1 = (bf16[2,1,128,256]{3,2,1,0:T(8,128)(2,1)}, bf16[1,2,64,1024]{3,2,1,0:T(8,128)(2,1)S(1)}, bf16[1,2,16,1024]{3,2,1,0:T(8,128)(2,1)S(1)}, bf16[2,64,1024]{2,1,0:T(8,128)(2,1)S(1)}) custom-call(s32[1]{0:T(128)} %bitcast.half_ref, s32[1]{0:T(128)} %bitcast.1.me_ref, s32[1,2,2]{2,1,0:T(2,128)S(1)} %collective-permute-done.theirs_ref, ...), custom_call_target="tpu_custom_call" | custom-call | flops 1073741824 | bytes 8388608 | tf_op jit(solution)/shard_map/first_slot/pallas_call | solution.py:353
  34.2 5.1 %collective-permute-start.5 = (bf16[2,1,128,256]{3,2,1,0:T(8,128)(2,1)}, bf16[2,1,128,256]{3,2,1,0:T(8,128)(2,1)S(1)}, u32[]{:S(2)}, u32[]{:S(2)}) collective-permute-start(bf16[2,1,128,256]{3,2,1,0:T(8,128)(2,1)} %get-tuple-element.52), channel_id=1, source_target_pairs={{0,8},{1,9},{2,10},{3,11},{4,12},{5,13},{6,14},{7,15},{8,0},{9,1},... | collective-permute-start | bytes 393224 | tf_op jit(solution)/shard_map/ppermute | solution.py:570
  39.3 3.0 %other_slots.1 = (bf16[2,1,128,256]{3,2,1,0:T(8,128)(2,1)}, bf16[4,2,64,1024]{3,2,1,0:T(8,128)(2,1)S(1)}, bf16[4,2,16,1024]{3,2,1,0:T(8,128)(2,1)S(1)}, bf16[2,1...) custom-call(s32[1]{0:T(128)} %bitcast.half_ref, s32[1]{0:T(128)} %bitcast.1.me_ref, ...), custom_call_target="tpu_custom_call" | custom-call | flops 1073741824 | bytes 8388608 | tf_op jit(solution)/shard_map/other_slots/pallas_call | solution.py:411
  42.3 3.0 %own_slots.1 = bf16[4,2,128,256]{3,2,1,0:T(8,128)(2,1)} custom-call(s32[1]{0:T(128)} %bitcast.half_ref, s32[1]{0:T(128)} %bitcast.1.me_ref, s32[1,2,2]{2,1,0:T(2,128)S(1)} %copy-done.4, s32[1,2,2]{2,1,0:T(2,128)S(1)} %collective-permute-done.theirs_ref, bf16[1024,2048]{1,0:T(8,128)(2,1)S(1)} %get-tuple-element.49.refs_4_.table_ref, ...), custom_call_target="tpu_custom_call" | custom-call | flops 1073741824 | bytes 8388608 | tf_op jit(solution)/shard_map/own_slots/pallas_call | solution.py:446
  45.3 3.5 %all-to-all-start.1 = ((bf16[4,2,128,256]{3,2,1,0:T(8,128)(2,1)}), bf16[4,2,128,256]{3,2,1,0:T(8,128)(2,1)S(1)}, u32[]{:S(2)}, u32[]{:S(2)}) async-start(bf16[4,2,128,256]{3,2,1,0:T(8,128)(2,1)} %own_slots.1), calls=%async_computation.1 | async-start | bytes 1048576 | tf_op jit(solution)/shard_map/all_to_all | solution.py:573
  49.4 3.7 %collective-permute-start.8 = (bf16[2,128,256]{2,1,0:T(8,128)(2,1)S(1)}, bf16[2,128,256]{2,1,0:T(8,128)(2,1)S(1)}, u32[]{:S(2)}, u32[]{:S(2)}) collective-permute-start(bf16[2,128,256]{2,1,0:T(8,128)(2,1)S(1)} %get-tuple-element.60), channel_id=1, source_target_pairs={{0,10},{1,11},{2,8},{3,9},{4,14},{5,15},{6,12},{7,13},{8,2},{9,3},... | collective-permute-start | bytes 393224 | tf_op jit(solution)/shard_map/ppermute | solution.py:570
  55.5 3.3 %all-to-all-done.1.own_ref = bf16[4,2,128,256]{3,2,1,0:T(8,128)(2,1)S(1)} async-done(((bf16[4,2,128,256]{3,2,1,0:T(8,128)(2,1)}), bf16[4,2,128,256]{3,2,1,0:T(8,128)(2,1)S(1)}, u32[]{:S(2)}, u32[]{:S(2)}) %all-to-all-start.1) | async-done | bytes 524320 | tf_op jit(solution)/shard_map/all_to_all | solution.py:573
  58.8 1.0 %own_surfaces.1.part_ref = f32[2,256,1024]{2,1,0:T(8,128)S(1)} custom-call(s32[1]{0:T(128)} %bitcast.half_ref, bf16[4,2,128,256]{3,2,1,0:T(8,128)(2,1)S(1)} %all-to-all-done.1.own_ref, bf16[1024,1024]{1,0:T(8,128)(2,1)S(1)} %copy-done), custom_call_target="tpu_custom_call" | custom-call | flops 536870912 | bytes 2097152 | tf_op jit(solution)/shard_map/own_surfaces/pallas_call | solution.py:472
  59.8 3.3 %collective-permute-done.8.refs_4_ = bf16[2,128,256]{2,1,0:T(8,128)(2,1)S(1)} collective-permute-done((bf16[2,128,256]{2,1,0:T(8,128)(2,1)S(1)}, bf16[2,128,256]{2,1,0:T(8,128)(2,1)S(1)}, u32[]{:S(2)}, u32[]{:S(2)}) %collective-permute-start.8) | collective-permute-done | bytes 131104 | tf_op jit(solution)/shard_map/ppermute | solution.py:570
  63.2 1.6 %collective-permute-done.9.refs_5_ = bf16[2,128,256]{2,1,0:T(8,128)(2,1)S(1)} collective-permute-done((bf16[2,128,256]{2,1,0:T(8,128)(2,1)S(1)}, bf16[2,128,256]{2,1,0:T(8,128)(2,1)S(1)}, u32[]{:S(2)}, u32[]{:S(2)}) %collective-permute-start.9) | collective-permute-done | bytes 131104 | tf_op jit(solution)/shard_map/ppermute | solution.py:570
  64.7 2.0 %surfaces.1 = f32[2,256,1024]{2,1,0:T(8,128)} custom-call(s32[1]{0:T(128)} %bitcast.half_ref, s32[1]{0:T(128)} %bitcast.1.me_ref, s32[1]{0:T(128)S(6)} %copy.8.counts_ref, f32[2,256,1024]{2,1,0:T(8,128)S(1)} %own_surfaces.1.part_ref, bf16[2,1,128,256]{3,2,1,0:T(8,128)(2,1)S(1)} %collective-permute-done.5.refs_0_, ...), custom_call_target="tpu_custom_call" | custom-call | flops 536870912 | bytes 4194304 | tf_op jit(solution)/shard_map/surfaces/pallas_call | solution.py:529
  (33 shorter events, 3.5 us)
Async XLA Ops:
  0.0 8.2 %copy-start = (bf16[1024,1024]{1,0:T(8,128)(2,1)S(1)}, bf16[1024,1024]{1,0:T(8,128)(2,1)}, u32[]{:S(2)}) copy-start(bf16[1024,1024]{1,0:T(8,128)(2,1)} %constant.29.clone.table_hbm.table_ref.refs_6_) | copy-start | bytes 6291460
  0.0 8.2 %copy-start.2 = (f32[8,1024]{1,0:T(8,128)S(1)}, f32[8,1024]{1,0:T(8,128)}, u32[]{:S(2)}) copy-start(f32[8,1024]{1,0:T(8,128)} %constant.30.clone.down_ref) | copy-start | bytes 98308
  0.0 8.3 %copy-start.3 = (f32[1,1024]{1,0:T(1,128)S(1)}, f32[1,1024]{1,0:T(1,128)}, u32[]{:S(2)}) copy-start(f32[1,1024]{1,0:T(1,128)} %constant.31.clone.across_ref) | copy-start | bytes 12292
  0.0 8.3 %copy-start.4 = (s32[1,2,2]{2,1,0:T(2,128)S(1)}, s32[1,2,2]{2,1,0:T(2,128)}, u32[]{:S(2)}) copy-start(s32[1,2,2]{2,1,0:T(2,128)} %pairs_ref.3) | copy-start | bytes 52
  4.1 19.3 %collective-permute-start.1 = (bf16[2,128,256]{2,1,0:T(8,128)(2,1)}, bf16[2,128,256]{2,1,0:T(8,128)(2,1)S(1)}, u32[]{:S(2)}, u32[]{:S(2)}) collective-permute-start(bf16[2,128,256]{2,1,0:T(8,128)(2,1)} %get-tuple-element.37), channel_id=1, source_target_pairs={{0,8},{1,9},{2,10},{3,11},{4,12},{5,13},{6,14},{7,15},{8,0},{9,1},... | collective-permute-start | bytes 393224 | tf_op jit(solution)/shard_map/ppermute | solution.py:570
  8.2 16.6 %collective-permute-start.2 = (bf16[2,128,256]{2,1,0:T(8,128)(2,1)}, bf16[2,128,256]{2,1,0:T(8,128)(2,1)S(1)}, u32[]{:S(2)}, u32[]{:S(2)}) collective-permute-start(bf16[2,128,256]{2,1,0:T(8,128)(2,1)} %get-tuple-element.38), channel_id=1, source_target_pairs={{0,9},{1,8},{2,11},{3,10},{4,13},{5,12},{6,15},{7,14},{8,1},{9,0},... | collective-permute-start | bytes 393224 | tf_op jit(solution)/shard_map/ppermute | solution.py:570
  8.3 1.6 %copy-start.1 = (f32[2,256,1024]{2,1,0:T(8,128)S(1)}, f32[2,256,1024]{2,1,0:T(8,128)}, u32[]{:S(2)}) copy-start(f32[2,256,1024]{2,1,0:T(8,128)} %tile_ref.1) | copy-start | bytes 6291460
  13.7 15.2 %all-to-all-start = ((bf16[4,2,128,256]{3,2,1,0:T(8,128)(2,1)}), bf16[4,2,128,256]{3,2,1,0:T(8,128)(2,1)S(1)}, u32[]{:S(2)}, u32[]{:S(2)}) async-start(bf16[4,2,128,256]{3,2,1,0:T(8,128)(2,1)} %get-tuple-element.48), calls=%async_computation | async-start | bytes 1048576 | tf_op jit(solution)/shard_map/all_to_all | solution.py:573
  17.2 14.4 %collective-permute-start.3 = (bf16[128,256]{1,0:T(8,128)(2,1)S(1)}, bf16[128,256]{1,0:T(8,128)(2,1)S(1)}, u32[]{:S(2)}, u32[]{:S(2)}) collective-permute-start(bf16[128,256]{1,0:T(8,128)(2,1)S(1)} %get-tuple-element.46), channel_id=1, source_target_pairs={{0,10},{1,11},{2,8},{3,9},{4,14},{5,15},{6,12},{7,13},{8,2},{9,3},... | collective-permute-start | bytes 196616 | tf_op jit(solution)/shard_map/ppermute | solution.py:570
  20.7 10.9 %collective-permute-start.4 = (bf16[128,256]{1,0:T(8,128)(2,1)S(1)}, bf16[128,256]{1,0:T(8,128)(2,1)S(1)}, u32[]{:S(2)}, u32[]{:S(2)}) collective-permute-start(bf16[128,256]{1,0:T(8,128)(2,1)S(1)} %get-tuple-element.47), channel_id=1, source_target_pairs={{0,11},{1,10},{2,9},{3,8},{4,15},{5,14},{6,13},{7,12},{8,3},{9,2},... | collective-permute-start | bytes 196616 | tf_op jit(solution)/shard_map/ppermute | solution.py:570
  20.9 10.7 %collective-permute-start = (s32[1,2,2]{2,1,0:T(2,128)S(1)}, s32[1,2,2]{2,1,0:T(2,128)S(1)}, u32[]{:S(2)}, u32[]{:S(2)}) collective-permute-start(s32[1,2,2]{2,1,0:T(2,128)S(1)} %copy-done.4), channel_id=1, source_target_pairs={{0,8},{1,9},{2,10},{3,11},{4,12},{5,13},{6,14},{7,15},{8,0},{9,1},... | collective-permute-start | bytes 56 | tf_op jit(solution)/shard_map/ppermute | solution.py:570
  23.4 15.8 %collective-permute-start.6 = (bf16[128,256]{1,0:T(8,128)(2,1)S(1)}, bf16[128,256]{1,0:T(8,128)(2,1)S(1)}, u32[]{:S(2)}, u32[]{:S(2)}) collective-permute-start(bf16[128,256]{1,0:T(8,128)(2,1)S(1)} %get-tuple-element.53), channel_id=1, source_target_pairs={{0,10},{1,11},{2,8},{3,9},{4,14},{5,15},{6,12},{7,13},{8,2},{9,3},... | collective-permute-start | bytes 196616 | tf_op jit(solution)/shard_map/ppermute | solution.py:570
  24.9 14.4 %collective-permute-start.7 = (bf16[128,256]{1,0:T(8,128)(2,1)S(1)}, bf16[128,256]{1,0:T(8,128)(2,1)S(1)}, u32[]{:S(2)}, u32[]{:S(2)}) collective-permute-start(bf16[128,256]{1,0:T(8,128)(2,1)S(1)} %get-tuple-element.54), channel_id=1, source_target_pairs={{0,11},{1,10},{2,9},{3,8},{4,15},{5,14},{6,13},{7,12},{8,3},{9,2},... | collective-permute-start | bytes 196616 | tf_op jit(solution)/shard_map/ppermute | solution.py:570
  26.2 1.0 %copy-start.5 = (f32[128,1024]{1,0:T(8,128)S(1)}, f32[128,1024]{1,0:T(8,128)}, u32[]{:S(2)}) copy-start(f32[128,1024]{1,0:T(8,128)} %constant.32.clone.short_ref) | copy-start | bytes 1572868
  27.2 0.8 %copy-start.6 = (f32[128,1024]{1,0:T(8,128)}, f32[128,1024]{1,0:T(8,128)S(1)}, u32[]{:S(2)}) copy-start(f32[128,1024]{1,0:T(8,128)S(1)} %scaled_tables.1.short_ref) | copy-start | bytes 1572868
  28.9 1.0 %copy-start.7 = (f32[128,1024]{1,0:T(8,128)S(1)}, f32[128,1024]{1,0:T(8,128)}, u32[]{:S(2)}) copy-start(f32[128,1024]{1,0:T(8,128)} %copy-done.6) | copy-start | bytes 1572868
  34.2 15.2 %collective-permute-start.5 = (bf16[2,1,128,256]{3,2,1,0:T(8,128)(2,1)}, bf16[2,1,128,256]{3,2,1,0:T(8,128)(2,1)S(1)}, u32[]{:S(2)}, u32[]{:S(2)}) collective-permute-start(bf16[2,1,128,256]{3,2,1,0:T(8,128)(2,1)} %get-tuple-element.52), channel_id=1, source_target_pairs={{0,8},{1,9},{2,10},{3,11},{4,12},{5,13},{6,14},{7,15},{8,0},{9,1},... | collective-permute-start | bytes 393224 | tf_op jit(solution)/shard_map/ppermute | solution.py:570
  42.2 10.9 %collective-permute-start.11 = (bf16[2,1,128,256]{3,2,1,0:T(8,128)(2,1)}, bf16[2,1,128,256]{3,2,1,0:T(8,128)(2,1)S(1)}, u32[]{:S(2)}, u32[]{:S(2)}) collective-permute-start(bf16[2,1,128,256]{3,2,1,0:T(8,128)(2,1)} %get-tuple-element.66), channel_id=1, source_target_pairs={{0,8},{1,9},{2,10},{3,11},{4,12},{5,13},{6,14},{7,15},{8,0},{9,1},... | collective-permute-start | bytes 393224 | tf_op jit(solution)/shard_map/ppermute | solution.py:570
  45.3 13.5 %all-to-all-start.1 = ((bf16[4,2,128,256]{3,2,1,0:T(8,128)(2,1)}), bf16[4,2,128,256]{3,2,1,0:T(8,128)(2,1)S(1)}, u32[]{:S(2)}, u32[]{:S(2)}) async-start(bf16[4,2,128,256]{3,2,1,0:T(8,128)(2,1)} %own_slots.1), calls=%async_computation.1 | async-start | bytes 1048576 | tf_op jit(solution)/shard_map/all_to_all | solution.py:573
  49.4 13.7 %collective-permute-start.8 = (bf16[2,128,256]{2,1,0:T(8,128)(2,1)S(1)}, bf16[2,128,256]{2,1,0:T(8,128)(2,1)S(1)}, u32[]{:S(2)}, u32[]{:S(2)}) collective-permute-start(bf16[2,128,256]{2,1,0:T(8,128)(2,1)S(1)} %get-tuple-element.60), channel_id=1, source_target_pairs={{0,10},{1,11},{2,8},{3,9},{4,14},{5,15},{6,12},{7,13},{8,2},{9,3},... | collective-permute-start | bytes 393224 | tf_op jit(solution)/shard_map/ppermute | solution.py:570
  53.1 11.6 %collective-permute-start.9 = (bf16[2,128,256]{2,1,0:T(8,128)(2,1)S(1)}, bf16[2,128,256]{2,1,0:T(8,128)(2,1)S(1)}, u32[]{:S(2)}, u32[]{:S(2)}) collective-permute-start(bf16[2,128,256]{2,1,0:T(8,128)(2,1)S(1)} %get-tuple-element.61), channel_id=1, source_target_pairs={{0,11},{1,10},{2,9},{3,8},{4,15},{5,14},{6,13},{7,12},{8,3},{9,2},... | collective-permute-start | bytes 393224 | tf_op jit(solution)/shard_map/ppermute | solution.py:570
  53.8 11.0 %collective-permute-start.12 = (bf16[1,128,256]{2,1,0:T(8,128)(2,1)}, bf16[1,128,256]{2,1,0:T(8,128)(2,1)S(1)}, u32[]{:S(2)}, u32[]{:S(2)}) collective-permute-start(bf16[1,128,256]{2,1,0:T(8,128)(2,1)} %slice_bitcast_fusion), channel_id=1, source_target_pairs={{0,1},{1,0},{2,3},{3,2},{4,5},{5,4},{6,7},{7,6},{8,9},{9,8},{10,11... | collective-permute-start | bytes 196616 | tf_op jit(solution)/shard_map/ppermute | solution.py:576
  54.6 10.1 %collective-permute-start.10 = (bf16[1,128,256]{2,1,0:T(8,128)(2,1)}, bf16[1,128,256]{2,1,0:T(8,128)(2,1)S(1)}, u32[]{:S(2)}, u32[]{:S(2)}) collective-permute-start(bf16[1,128,256]{2,1,0:T(8,128)(2,1)} %slice_bitcast_fusion.1), channel_id=1, source_target_pairs={{0,1},{1,0},{2,3},{3,2},{4,5},{5,4},{6,7},{7,6},{8,9},{9,8},{10,11... | collective-permute-start | bytes 196616 | tf_op jit(solution)/shard_map/ppermute | solution.py:576

commit v13 on v9

--- a/solution.py
+++ b/solution.py
@@ -85,9 +85,9 @@
     span = table.shape[0] // 2
     block = span // peers
 
-    def body(half_ref, me_ref, tile_hbm, down_ref, across_ref, table_hbm, *refs):
+    def body(half_ref, me_ref, tile_hbm, down_hbm, across_hbm, table_hbm, *refs):
         outs = refs[:2]
-        tile_ref, table_ref, work, done = refs[2:]
+        tile_ref, table_ref, work, down_ref, across_ref, done = refs[2:]
         t = pl.program_id(0)
         me = me_ref[0]
         start = pl.multiple_of((1 - half_ref[0]) * span + me // 2 * 2 * block, 2 * block)
@@ -98,11 +98,21 @@
             pltpu.make_async_copy(tile_hbm.at[i], tile_ref.at[i], done.at[i]) for i in range(count)
         ]
 
+        lane = pl.multiple_of(me * rows, rows)
+        extra = [
+            pltpu.make_async_copy(down_hbm.at[:, pl.ds(lane, rows)], down_ref, done.at[count + 1]),
+            pltpu.make_async_copy(across_hbm, across_ref, done.at[count + 2]),
+        ]
+
         @pl.when(t == 0)
         def _():
+            for copy in extra:
+                copy.start()
             fetch.start()
             for load in loads:
                 load.start()
+            for copy in extra:
+                copy.wait()
             fetch.wait()
 
         for i in range(count):
@@ -123,8 +133,8 @@
             grid=(count,),
             in_specs=[
                 pl.BlockSpec(memory_space=pltpu.HBM),
-                pl.BlockSpec((8, rows), lambda t, half, me: (0, me[0])),
-                pl.BlockSpec((1, width), lambda t, half, me: (0, 0)),
+                pl.BlockSpec(memory_space=pltpu.HBM),
+                pl.BlockSpec(memory_space=pltpu.HBM),
                 pl.BlockSpec(memory_space=pltpu.HBM),
             ],
             out_specs=[pl.BlockSpec((1, block, rows), lambda t, half, me: (t, 0, 0))] * 2,
@@ -132,7 +142,9 @@
                 pltpu.VMEM((count, rows, width), tiles.dtype),
                 pltpu.VMEM((2 * block, width), table.dtype),
                 pltpu.VMEM((2 * block, rows), jnp.bfloat16),
-                pltpu.SemaphoreType.DMA((count + 1,)),
+                pltpu.VMEM((8, rows), jnp.float32),
+                pltpu.VMEM((1, width), jnp.float32),
+                pltpu.SemaphoreType.DMA((count + 3,)),
             ],
         ),
         out_shape=[jax.ShapeDtypeStruct((count, block, rows), jnp.bfloat16)] * 2,
@@ -189,9 +201,8 @@
     )(scalar(half), scalar(me), tiles, down, across, table)
 
 
-def gather_rows(pieces, table_ref, me):
-    total = None
-    for k, piece in enumerate(pieces):
+def gather_rows(pieces, table_ref, me, first=0, total=None):
+    for k, piece in enumerate(pieces, first):
         count, block, rows = piece.shape
         start = pl.multiple_of((me ^ k) * rows, rows)
         term = jnp.dot(
@@ -279,31 +290,33 @@
             out[p, block:] = ((s_part[re] + c_part[im]) * twice).astype(jnp.bfloat16)
 
 
-def own_spectra(place, pieces, table):
+def own_spectra(place, pieces, near, table):
     peers, count, double, rows = pieces.shape
     height = table.shape[0]
 
-    def body(half_ref, me_ref, pieces_ref, table_ref, spectra, edge):
+    def body(half_ref, me_ref, pieces_ref, near_a, near_b, table_ref, spectra, edge, share):
         inputs = [pieces_ref.at[k] for k in range(peers)]
         store_spectra((half_ref, me_ref), gather_rows(inputs, table_ref, 0), spectra, edge, 0)
+        share[...] = gather_rows([near_a, near_b], table_ref, me_ref[0])
 
     return pl.pallas_call(
         body,
         in_specs=[pl.BlockSpec(memory_space=pltpu.SMEM)] * 2
-        + [pl.BlockSpec(memory_space=pltpu.VMEM)] * 2,
-        out_specs=[pl.BlockSpec(memory_space=pltpu.VMEM)] * 2,
+        + [pl.BlockSpec(memory_space=pltpu.VMEM)] * 4,
+        out_specs=[pl.BlockSpec(memory_space=pltpu.VMEM)] * 3,
         out_shape=[
             jax.ShapeDtypeStruct((count, 2, double // 2, height), jnp.bfloat16),
             jax.ShapeDtypeStruct((count, 2, 16, height), jnp.bfloat16),
+            jax.ShapeDtypeStruct((count * double, 2 * height), jnp.float32),
         ],
         compiler_params=params(),
-        cost_estimate=cost(4 * count * double * height * height, 8 * height * height),
+        cost_estimate=cost(6 * count * double * height * height, 8 * height * height),
         name="own_spectra",
-    )(*place, pieces, table)
-
-
-def partner_slots(place, theirs, pieces, table, spectra, edge):
-    peers = len(pieces)
+    )(*place, pieces, *near, table)
+
+
+def partner_slots(place, theirs, pieces, share, table, spectra, edge):
+    distant = len(pieces)
     count, double, rows = pieces[0].shape
     height = table.shape[0]
     block = double // 2
@@ -315,18 +328,19 @@
         picks = [
             [(theirs_ref[0, p, i] + count) % (2 * count) for i in range(2)] for p in range(slots)
         ]
-        inputs, table_ref, own_ref, own_edge = refs[:peers], *refs[peers : peers + 3]
-        near, every, edges, phases = refs[peers + 3 :]
+        inputs = refs[:distant]
+        share_ref, table_ref, own_ref, own_edge, near, every, edges, phases = refs[distant:]
         every[:count] = own_ref[...]
         edges[:count] = own_edge[...]
-        store_spectra(s_ref, gather_rows(inputs, table_ref, me), every, edges, count)
+        total = gather_rows(inputs, table_ref, me, 2, share_ref[...])
+        store_spectra(s_ref, total, every, edges, count)
         correlate(s_ref, picks, every, edges, phases)
         invert_columns(s_ref, me, phases, table_ref, {k: near.at[k] for k in range(2)})
 
     return pl.pallas_call(
         body,
         in_specs=[pl.BlockSpec(memory_space=pltpu.SMEM)] * 3
-        + [pl.BlockSpec(memory_space=pltpu.VMEM)] * (peers + 3),
+        + [pl.BlockSpec(memory_space=pltpu.VMEM)] * (distant + 4),
         out_specs=[pl.BlockSpec(memory_space=pltpu.VMEM)] * 4,
         out_shape=[
             jax.ShapeDtypeStruct((2, slots, double, rows), jnp.bfloat16),
@@ -337,7 +351,7 @@
         compiler_params=params(),
         cost_estimate=cost(4 * (count + slots) * double * height * height, 8 * height * height),
         name="partner_slots",
-    )(*place, theirs, *pieces, table, spectra, edge)
+    )(*place, theirs, *pieces, share, table, spectra, edge)
 
 
 def own_slots(place, pairs, table, spectra, edge, phases, peers):
@@ -485,8 +499,10 @@
     table_h = height_table(height)
     theirs = across(pairs, 0)
     place = (scalar(half), scalar(me))
-    spectra, edge = own_spectra(place, mine, table_h)
-    near, spectra, edge, phases = partner_slots(place, theirs, arrived, table_h, spectra, edge)
+    spectra, edge, share = own_spectra(place, mine, arrived[:2], table_h)
+    near, spectra, edge, phases = partner_slots(
+        place, theirs, arrived[2:], share, table_h, spectra, edge
+    )
     near = across(near, 0)
     own, *far = own_slots(place, pairs, table_h, spectra, edge, phases, peers)
     far = [across(far[k - 2], k) for k in range(2, peers)]

time: 64.7 us -> 63.7 us (0.985)
  waiting for transfers between devices: 13.5 us -> 12.4 us
    all_to_all x2, waiting for transfers between devices: 3.27 us -> 0.01 us  [along(): return lax.all_to_all(blocks, 'rows', split_axis=0, concat_axis=0)]
    ppermute x8, waiting for transfers between devices: 10.2 us -> 12.4 us  [across(): return lax.ppermute(value, axes, moves)]
    pallas_call x1, Pallas kernels: 4.11 us -> 3.44 us  [near_columns(): pl.pallas_call(body, grid_spec=pltpu.PrefetchScalarGridSpec(num_scalar_pr...]
  transfers between devices with their start and end apart: 11 -> 11, of which waited for: 5 -> 4; matrix products, arithmetic and copies ran while one was open for 0% -> 0% of each run, Pallas kernels for 14% -> 16%
where the time goes in v13:
time: 63.7 us; the launch traced here: 63.3 us
  starting transfers between devices  25.5 us (40%)
  Pallas kernels  17.8 us (28%)
  waiting for transfers between devices  12.4 us (19%)
  local copies, waits for them, and re-layouts  6.77 us (11%)
  between operations  0.77 us (1%)
    ppermute x8, starting transfers between devices, across(): return lax.ppermute(value, axes, moves)  18.5 us
    ppermute x8, waiting for transfers between devices, across(): return lax.ppermute(value, axes, moves)  12.4 us
    all_to_all x2, starting transfers between devices, along(): return lax.all_to_all(blocks, 'rows', split_axis=0, concat_axis=0)  6.94 us
    unnamed x16, local copies, waits for them, and re-layouts  6.76 us
    pallas_call x1, Pallas kernels, own_slots(): pl.pallas_call(body, in_specs=[pl.BlockSpec(memory_space=pltpu.SMEM)] * 3...  3.56 us
    pallas_call x1, Pallas kernels, near_columns(): pl.pallas_call(body, grid_spec=pltpu.PrefetchScalarGridSpec(num_scalar_pr...  3.44 us
    pallas_call x1, Pallas kernels, partner_slots(): pl.pallas_call(body, in_specs=[pl.BlockSpec(memory_space=pltpu.SMEM)] * 3...  2.53 us
    pallas_call x1, Pallas kernels, rest_columns(): pl.pallas_call(body, grid_spec=pltpu.PrefetchScalarGridSpec(num_scalar_pr...  2.4 us
  transfers between devices with their start and end apart: 11, of which 4 were waited for; matrix products, arithmetic and copies ran while one was open for 0% of the time, Pallas kernels for 16%

profile of v13, /device:TPU:0, one launch (start us, length us, event | category | flops | bytes accessed | tf_op | source)
XLA Modules:
  0.0 63.3 jit_solution(17243532836661410354)
XLA Ops:
  0.0 3.4 %near_columns.1 = (bf16[2,128,256]{2,1,0:T(8,128)(2,1)}, bf16[2,128,256]{2,1,0:T(8,128)(2,1)}) custom-call(s32[1]{0:T(128)} %bitcast.half_ref, s32[1]{0:T(128)} %bitcast.1.me_ref, f32[2,256,1024]{2,1,0:T(8,128)} %tile_ref.1, f32[8,1024]{1,0:T(8,128)} %constant.30.clone.down_hbm.down_ref, f32[1,1024]{1,0:T(1,128)} %constant.31.clone.across_hbm.across_ref, ...), custom_call_target="tpu_custom_call" | custom-call | flops 268435456 | bytes 2621440 | tf_op jit(solution)/shard_map/near_columns/pallas_call | solution.py:129
  3.5 4.1 %collective-permute-start.3 = (bf16[2,128,256]{2,1,0:T(8,128)(2,1)}, bf16[2,128,256]{2,1,0:T(8,128)(2,1)S(1)}, u32[]{:S(2)}, u32[]{:S(2)}) collective-permute-start(bf16[2,128,256]{2,1,0:T(8,128)(2,1)} %get-tuple-element.28), channel_id=1, source_target_pairs={{0,8},{1,9},{2,10},{3,11},{4,12},{5,13},{6,14},{7,15},{8,0},{9,1},... | collective-permute-start | bytes 393224 | tf_op jit(solution)/shard_map/ppermute | solution.py:479
  7.6 1.6 %copy-done.1 = f32[2,256,1024]{2,1,0:T(8,128)S(1)} copy-done((f32[2,256,1024]{2,1,0:T(8,128)S(1)}, f32[2,256,1024]{2,1,0:T(8,128)}, u32[]{:S(2)}) %copy-start.1) | copy-done | bytes 2097176
  9.2 2.4 %rest_columns.1 = (bf16[4,2,128,256]{3,2,1,0:T(8,128)(2,1)}, bf16[2,128,256]{2,1,0:T(8,128)(2,1)S(1)}, bf16[2,128,256]{2,1,0:T(8,128)(2,1)S(1)}) custom-call(s32[1]{0:T(128)} %bitcast.2.half_ref, s32[1]{0:T(128)} %bitcast.1.me_ref, f32[2,256,1024]{2,1,0:T(8,128)S(1)} %copy-done.1, f32[8,1024]{1,0:T(8,128)S(1)} %copy-done.4, f32[1,1024]{1,0:T(1,128)S(1)} %copy-done.5, ...), custom_call_target="tpu_custom_call" | custom-call | flops 805306368 | bytes 4194304 | tf_op jit(solution)/shard_map/rest_columns/pallas_call | solution.py:177
  11.6 3.5 %all-to-all-start = ((bf16[4,2,128,256]{3,2,1,0:T(8,128)(2,1)}), bf16[4,2,128,256]{3,2,1,0:T(8,128)(2,1)S(1)}, u32[]{:S(2)}, u32[]{:S(2)}) async-start(bf16[4,2,128,256]{3,2,1,0:T(8,128)(2,1)} %get-tuple-element.37), calls=%async_computation | async-start | bytes 1048576 | tf_op jit(solution)/shard_map/all_to_all | solution.py:482
  15.1 3.5 %collective-permute-start.1 = (bf16[2,128,256]{2,1,0:T(8,128)(2,1)S(1)}, bf16[2,128,256]{2,1,0:T(8,128)(2,1)S(1)}, u32[]{:S(2)}, u32[]{:S(2)}) collective-permute-start(bf16[2,128,256]{2,1,0:T(8,128)(2,1)S(1)} %get-tuple-element.35), channel_id=1, source_target_pairs={{0,10},{1,11},{2,8},{3,9},{4,14},{5,15},{6,12},{7,13},{8,2},{9,3},... | collective-permute-start | bytes 393224 | tf_op jit(solution)/shard_map/ppermute | solution.py:479
  18.8 2.5 %collective-permute-start = (s32[1,2,2]{2,1,0:T(2,128)S(1)}, s32[1,2,2]{2,1,0:T(2,128)S(1)}, u32[]{:S(2)}, u32[]{:S(2)}) collective-permute-start(s32[1,2,2]{2,1,0:T(2,128)S(1)} %copy-done.6), channel_id=1, source_target_pairs={{0,8},{1,9},{2,10},{3,11},{4,12},{5,13},{6,14},{7,15},{8,0},{9,1},... | collective-permute-start | bytes 56 | tf_op jit(solution)/shard_map/ppermute | solution.py:479
  21.3 1.0 %copy-done.7 = f32[128,1024]{1,0:T(8,128)S(1)} copy-done((f32[128,1024]{1,0:T(8,128)S(1)}, f32[128,1024]{1,0:T(8,128)}, u32[]{:S(2)}) %copy-start.7) | copy-done | bytes 524312
  22.4 1.1 %height_table.1.table_ref.refs_3_ = bf16[1024,2048]{1,0:T(8,128)(2,1)S(1)} custom-call(f32[128,1024]{1,0:T(8,128)S(1)} %copy-done.7), custom_call_target="tpu_custom_call" | custom-call | flops 8589934592 | bytes 4194304 | tf_op jit(solution)/shard_map/height_table/pallas_call | solution.py:53
  23.5 1.9 %copy-done.2 = bf16[1024,2048]{1,0:T(8,128)(2,1)} copy-done((bf16[1024,2048]{1,0:T(8,128)(2,1)}, bf16[1024,2048]{1,0:T(8,128)(2,1)S(1)}, u32[]{:S(2)}) %copy-start.2) | copy-done | bytes 4194328
  25.4 2.2 %copy-done.3 = bf16[1024,2048]{1,0:T(8,128)(2,1)S(1)} copy-done((bf16[1024,2048]{1,0:T(8,128)(2,1)S(1)}, bf16[1024,2048]{1,0:T(8,128)(2,1)}, u32[]{:S(2)}) %copy-start.3) | copy-done | bytes 4194328
  27.6 1.8 %own_spectra.1 = (bf16[2,2,64,1024]{3,2,1,0:T(8,128)(2,1)S(1)}, bf16[2,2,16,1024]{3,2,1,0:T(8,128)(2,1)S(1)}, f32[256,2048]{1,0:T(8,128)S(1)}) custom-call(s32[1]{0:T(128)} %bitcast.half_ref, s32[1]{0:T(128)} %bitcast.1.me_ref, bf16[4,2,128,256]{3,2,1,0:T(8,128)(2,1)S(1)} %all-to-all-done.pieces_ref, bf16[2,128,256]{2,1,0:T(8,128)(2,1)S(1)} %collective-permute-done.3.near_a, ...), custom_call_target="tpu_custom_call" | custom-call | flops 1610612736 | bytes 8388608 | tf_op jit(solution)/shard_map/own_spectra/pallas_call | solution.py:302
  29.4 2.0 %collective-permute-done.theirs_ref = s32[1,2,2]{2,1,0:T(2,128)S(1)} collective-permute-done((s32[1,2,2]{2,1,0:T(2,128)S(1)}, s32[1,2,2]{2,1,0:T(2,128)S(1)}, u32[]{:S(2)}, u32[]{:S(2)}) %collective-permute-start) | collective-permute-done | bytes 48 | tf_op jit(solution)/shard_map/ppermute | solution.py:479
  31.4 2.5 %partner_slots.1 = (bf16[2,2,128,256]{3,2,1,0:T(8,128)(2,1)S(1)}, bf16[4,2,64,1024]{3,2,1,0:T(8,128)(2,1)S(1)}, bf16[4,2,16,1024]{3,2,1,0:T(8,128)(2,1)S(1)}, bf16[4,64,1024]{2,1,0:T(8,128)(2,1)S(1)}) custom-call(s32[1]{0:T(128)} %bitcast.half_ref, s32[1]{0:T(128)} %bitcast.1.me_ref, s32[1,2,2]{2,1,0:T(2,128)S(1)} %collective-permute-done.theirs_ref, ...), custom_call_target="tpu_custom_call" | custom-call | flops 2147483648 | bytes 8388608 | tf_op jit(solution)/shard_map/partner_slots/pallas_call | solution.py:340
  33.9 4.5 %collective-permute-start.7 = (bf16[2,2,128,256]{3,2,1,0:T(8,128)(2,1)S(1)}, bf16[2,2,128,256]{3,2,1,0:T(8,128)(2,1)S(1)}, u32[]{:S(2)}, u32[]{:S(2)}) collective-permute-start(bf16[2,2,128,256]{3,2,1,0:T(8,128)(2,1)S(1)} %get-tuple-element.48), channel_id=1, source_target_pairs={{0,8},{1,9},{2,10},{3,11},{4,12},{5,13},{6,14},{7,15},{8,0},{9,1},... | collective-permute-start | bytes 786440 | tf_op jit(solution)/shard_map/ppermute | solution.py:479
  38.5 3.6 %own_slots.1 = (bf16[4,2,128,256]{3,2,1,0:T(8,128)(2,1)}, bf16[2,128,256]{2,1,0:T(8,128)(2,1)}, bf16[2,128,256]{2,1,0:T(8,128)(2,1)S(1)}) custom-call(s32[1]{0:T(128)} %bitcast.half_ref, s32[1]{0:T(128)} %bitcast.1.me_ref, s32[1,2,2]{2,1,0:T(2,128)S(1)} %copy-done.6, bf16[1024,2048]{1,0:T(8,128)(2,1)S(1)} %copy-done.3, ...), custom_call_target="tpu_custom_call" | custom-call | flops 1073741824 | bytes 8388608 | tf_op jit(solution)/shard_map/own_slots/pallas_call | solution.py:372
  42.0 3.5 %all-to-all-start.1 = ((bf16[4,2,128,256]{3,2,1,0:T(8,128)(2,1)}), bf16[4,2,128,256]{3,2,1,0:T(8,128)(2,1)S(1)}, u32[]{:S(2)}, u32[]{:S(2)}) async-start(bf16[4,2,128,256]{3,2,1,0:T(8,128)(2,1)} %get-tuple-element.46), calls=%async_computation.1 | async-start | bytes 1048576 | tf_op jit(solution)/shard_map/all_to_all | solution.py:482
  45.5 1.4 %collective-permute-start.5 = (bf16[2,128,256]{2,1,0:T(8,128)(2,1)}, bf16[2,128,256]{2,1,0:T(8,128)(2,1)S(1)}, u32[]{:S(2)}, u32[]{:S(2)}) collective-permute-start(bf16[2,128,256]{2,1,0:T(8,128)(2,1)} %get-tuple-element.44), channel_id=1, source_target_pairs={{0,10},{1,11},{2,8},{3,9},{4,14},{5,15},{6,12},{7,13},{8,2},{9,3},... | collective-permute-start | bytes 393224 | tf_op jit(solution)/shard_map/ppermute | solution.py:479
  47.0 2.2 %collective-permute-start.6 = (bf16[2,128,256]{2,1,0:T(8,128)(2,1)S(1)}, bf16[2,128,256]{2,1,0:T(8,128)(2,1)S(1)}, u32[]{:S(2)}, u32[]{:S(2)}) collective-permute-start(bf16[2,128,256]{2,1,0:T(8,128)(2,1)S(1)} %get-tuple-element.45), channel_id=1, source_target_pairs={{0,11},{1,10},{2,9},{3,8},{4,15},{5,14},{6,13},{7,12},{8,3},{9,2},... | collective-permute-start | bytes 393224 | tf_op jit(solution)/shard_map/ppermute | solution.py:479
  49.2 6.9 %collective-permute-done.7.refs_0_ = bf16[2,2,128,256]{3,2,1,0:T(8,128)(2,1)S(1)} collective-permute-done((bf16[2,2,128,256]{3,2,1,0:T(8,128)(2,1)S(1)}, bf16[2,2,128,256]{3,2,1,0:T(8,128)(2,1)S(1)}, u32[]{:S(2)}, u32[]{:S(2)}) %collective-permute-start.7) | collective-permute-done | bytes 262176 | tf_op jit(solution)/shard_map/ppermute | solution.py:479
  56.8 1.0 %own_surfaces.1.part_ref = f32[2,256,1024]{2,1,0:T(8,128)S(1)} custom-call(s32[1]{0:T(128)} %bitcast.half_ref, bf16[4,2,128,256]{3,2,1,0:T(8,128)(2,1)S(1)} %all-to-all-done.1.own_ref, bf16[1024,1024]{1,0:T(8,128)(2,1)S(1)} %copy-done), custom_call_target="tpu_custom_call" | custom-call | flops 536870912 | bytes 2097152 | tf_op jit(solution)/shard_map/own_surfaces/pallas_call | solution.py:401
  57.8 0.8 %collective-permute-done.5.refs_2_ = bf16[2,128,256]{2,1,0:T(8,128)(2,1)S(1)} collective-permute-done((bf16[2,128,256]{2,1,0:T(8,128)(2,1)}, bf16[2,128,256]{2,1,0:T(8,128)(2,1)S(1)}, u32[]{:S(2)}, u32[]{:S(2)}) %collective-permute-start.5) | collective-permute-done | bytes 131104 | tf_op jit(solution)/shard_map/ppermute | solution.py:479
  58.6 2.8 %collective-permute-done.6.refs_3_ = bf16[2,128,256]{2,1,0:T(8,128)(2,1)S(1)} collective-permute-done((bf16[2,128,256]{2,1,0:T(8,128)(2,1)S(1)}, bf16[2,128,256]{2,1,0:T(8,128)(2,1)S(1)}, u32[]{:S(2)}, u32[]{:S(2)}) %collective-permute-start.6) | collective-permute-done | bytes 131104 | tf_op jit(solution)/shard_map/ppermute | solution.py:479
  61.4 2.0 %surfaces.1 = f32[2,256,1024]{2,1,0:T(8,128)} custom-call(s32[1]{0:T(128)} %bitcast.half_ref, s32[1]{0:T(128)} %bitcast.1.me_ref, s32[1]{0:T(128)S(6)} %copy.8.counts_ref, f32[2,256,1024]{2,1,0:T(8,128)S(1)} %own_surfaces.1.part_ref, bf16[2,2,128,256]{3,2,1,0:T(8,128)(2,1)S(1)} %collective-permute-done.7.refs_0_, ...), custom_call_target="tpu_custom_call" | custom-call | flops 536870912 | bytes 4194304 | tf_op jit(solution)/shard_map/surfaces/pallas_call | solution.py:441
  (23 shorter events, 0.3 us)
Async XLA Ops:
  0.0 7.6 %copy-start = (bf16[1024,1024]{1,0:T(8,128)(2,1)S(1)}, bf16[1024,1024]{1,0:T(8,128)(2,1)}, u32[]{:S(2)}) copy-start(bf16[1024,1024]{1,0:T(8,128)(2,1)} %constant.29.clone.table_hbm.table_ref.refs_4_) | copy-start | bytes 6291460
  0.0 7.6 %copy-start.4 = (f32[8,1024]{1,0:T(8,128)S(1)}, f32[8,1024]{1,0:T(8,128)}, u32[]{:S(2)}) copy-start(f32[8,1024]{1,0:T(8,128)} %constant.30.clone.down_hbm.down_ref) | copy-start | bytes 98308
  0.0 7.6 %copy-start.5 = (f32[1,1024]{1,0:T(1,128)S(1)}, f32[1,1024]{1,0:T(1,128)}, u32[]{:S(2)}) copy-start(f32[1,1024]{1,0:T(1,128)} %constant.31.clone.across_hbm.across_ref) | copy-start | bytes 12292
  3.5 22.0 %collective-permute-start.3 = (bf16[2,128,256]{2,1,0:T(8,128)(2,1)}, bf16[2,128,256]{2,1,0:T(8,128)(2,1)S(1)}, u32[]{:S(2)}, u32[]{:S(2)}) collective-permute-start(bf16[2,128,256]{2,1,0:T(8,128)(2,1)} %get-tuple-element.28), channel_id=1, source_target_pairs={{0,8},{1,9},{2,10},{3,11},{4,12},{5,13},{6,14},{7,15},{8,0},{9,1},... | collective-permute-start | bytes 393224 | tf_op jit(solution)/shard_map/ppermute | solution.py:479
  7.6 17.8 %collective-permute-start.4 = (bf16[2,128,256]{2,1,0:T(8,128)(2,1)}, bf16[2,128,256]{2,1,0:T(8,128)(2,1)S(1)}, u32[]{:S(2)}, u32[]{:S(2)}) collective-permute-start(bf16[2,128,256]{2,1,0:T(8,128)(2,1)} %get-tuple-element.29), channel_id=1, source_target_pairs={{0,9},{1,8},{2,11},{3,10},{4,13},{5,12},{6,15},{7,14},{8,1},{9,0},... | collective-permute-start | bytes 393224 | tf_op jit(solution)/shard_map/ppermute | solution.py:479
  7.6 1.6 %copy-start.1 = (f32[2,256,1024]{2,1,0:T(8,128)S(1)}, f32[2,256,1024]{2,1,0:T(8,128)}, u32[]{:S(2)}) copy-start(f32[2,256,1024]{2,1,0:T(8,128)} %tile_ref.1) | copy-start | bytes 6291460
  9.2 9.6 %copy-start.6 = (s32[1,2,2]{2,1,0:T(2,128)S(1)}, s32[1,2,2]{2,1,0:T(2,128)}, u32[]{:S(2)}) copy-start(s32[1,2,2]{2,1,0:T(2,128)} %pairs_ref) | copy-start | bytes 52
  11.6 13.8 %all-to-all-start = ((bf16[4,2,128,256]{3,2,1,0:T(8,128)(2,1)}), bf16[4,2,128,256]{3,2,1,0:T(8,128)(2,1)S(1)}, u32[]{:S(2)}, u32[]{:S(2)}) async-start(bf16[4,2,128,256]{3,2,1,0:T(8,128)(2,1)} %get-tuple-element.37), calls=%async_computation | async-start | bytes 1048576 | tf_op jit(solution)/shard_map/all_to_all | solution.py:482
  15.1 16.3 %collective-permute-start.1 = (bf16[2,128,256]{2,1,0:T(8,128)(2,1)S(1)}, bf16[2,128,256]{2,1,0:T(8,128)(2,1)S(1)}, u32[]{:S(2)}, u32[]{:S(2)}) collective-permute-start(bf16[2,128,256]{2,1,0:T(8,128)(2,1)S(1)} %get-tuple-element.35), channel_id=1, source_target_pairs={{0,10},{1,11},{2,8},{3,9},{4,14},{5,15},{6,12},{7,13},{8,2},{9,3},... | collective-permute-start | bytes 393224 | tf_op jit(solution)/shard_map/ppermute | solution.py:479
  18.6 12.8 %collective-permute-start.2 = (bf16[2,128,256]{2,1,0:T(8,128)(2,1)S(1)}, bf16[2,128,256]{2,1,0:T(8,128)(2,1)S(1)}, u32[]{:S(2)}, u32[]{:S(2)}) collective-permute-start(bf16[2,128,256]{2,1,0:T(8,128)(2,1)S(1)} %get-tuple-element.36), channel_id=1, source_target_pairs={{0,11},{1,10},{2,9},{3,8},{4,15},{5,14},{6,13},{7,12},{8,3},{9,2},... | collective-permute-start | bytes 393224 | tf_op jit(solution)/shard_map/ppermute | solution.py:479
  18.8 12.6 %collective-permute-start = (s32[1,2,2]{2,1,0:T(2,128)S(1)}, s32[1,2,2]{2,1,0:T(2,128)S(1)}, u32[]{:S(2)}, u32[]{:S(2)}) collective-permute-start(s32[1,2,2]{2,1,0:T(2,128)S(1)} %copy-done.6), channel_id=1, source_target_pairs={{0,8},{1,9},{2,10},{3,11},{4,12},{5,13},{6,14},{7,15},{8,0},{9,1},... | collective-permute-start | bytes 56 | tf_op jit(solution)/shard_map/ppermute | solution.py:479
  21.3 1.0 %copy-start.7 = (f32[128,1024]{1,0:T(8,128)S(1)}, f32[128,1024]{1,0:T(8,128)}, u32[]{:S(2)}) copy-start(f32[128,1024]{1,0:T(8,128)} %constant.32.clone.short_ref) | copy-start | bytes 1572868
  23.5 1.9 %copy-start.2 = (bf16[1024,2048]{1,0:T(8,128)(2,1)}, bf16[1024,2048]{1,0:T(8,128)(2,1)S(1)}, u32[]{:S(2)}) copy-start(bf16[1024,2048]{1,0:T(8,128)(2,1)S(1)} %height_table.1.table_ref.refs_3_) | copy-start | bytes 12582916
  25.4 2.2 %copy-start.3 = (bf16[1024,2048]{1,0:T(8,128)(2,1)S(1)}, bf16[1024,2048]{1,0:T(8,128)(2,1)}, u32[]{:S(2)}) copy-start(bf16[1024,2048]{1,0:T(8,128)(2,1)} %copy-done.2) | copy-start | bytes 12582916
  33.9 22.1 %collective-permute-start.7 = (bf16[2,2,128,256]{3,2,1,0:T(8,128)(2,1)S(1)}, bf16[2,2,128,256]{3,2,1,0:T(8,128)(2,1)S(1)}, u32[]{:S(2)}, u32[]{:S(2)}) collective-permute-start(bf16[2,2,128,256]{3,2,1,0:T(8,128)(2,1)S(1)} %get-tuple-element.48), channel_id=1, source_target_pairs={{0,8},{1,9},{2,10},{3,11},{4,12},{5,13},{6,14},{7,15},{8,0},{9,1},... | collective-permute-start | bytes 786440 | tf_op jit(solution)/shard_map/ppermute | solution.py:479
  42.0 14.8 %all-to-all-start.1 = ((bf16[4,2,128,256]{3,2,1,0:T(8,128)(2,1)}), bf16[4,2,128,256]{3,2,1,0:T(8,128)(2,1)S(1)}, u32[]{:S(2)}, u32[]{:S(2)}) async-start(bf16[4,2,128,256]{3,2,1,0:T(8,128)(2,1)} %get-tuple-element.46), calls=%async_computation.1 | async-start | bytes 1048576 | tf_op jit(solution)/shard_map/all_to_all | solution.py:482
  45.5 13.1 %collective-permute-start.5 = (bf16[2,128,256]{2,1,0:T(8,128)(2,1)}, bf16[2,128,256]{2,1,0:T(8,128)(2,1)S(1)}, u32[]{:S(2)}, u32[]{:S(2)}) collective-permute-start(bf16[2,128,256]{2,1,0:T(8,128)(2,1)} %get-tuple-element.44), channel_id=1, source_target_pairs={{0,10},{1,11},{2,8},{3,9},{4,14},{5,15},{6,12},{7,13},{8,2},{9,3},... | collective-permute-start | bytes 393224 | tf_op jit(solution)/shard_map/ppermute | solution.py:479
  47.0 14.4 %collective-permute-start.6 = (bf16[2,128,256]{2,1,0:T(8,128)(2,1)S(1)}, bf16[2,128,256]{2,1,0:T(8,128)(2,1)S(1)}, u32[]{:S(2)}, u32[]{:S(2)}) collective-permute-start(bf16[2,128,256]{2,1,0:T(8,128)(2,1)S(1)} %get-tuple-element.45), channel_id=1, source_target_pairs={{0,11},{1,10},{2,9},{3,8},{4,15},{5,14},{6,13},{7,12},{8,3},{9,2},... | collective-permute-start | bytes 393224 | tf_op jit(solution)/shard_map/ppermute | solution.py:479
  56.1 5.3 %collective-permute-start.8 = (bf16[2,128,256]{2,1,0:T(8,128)(2,1)S(1)}, bf16[2,128,256]{2,1,0:T(8,128)(2,1)S(1)}, u32[]{:S(2)}, u32[]{:S(2)}) collective-permute-start(bf16[2,128,256]{2,1,0:T(8,128)(2,1)S(1)} %slice_bitcast_fusion), channel_id=1, source_target_pairs={{0,1},{1,0},{2,3},{3,2},{4,5},{5,4},{6,7},{7,6},{8,9},{9,8},{10,11... | collective-permute-start | bytes 393224 | tf_op jit(solution)/shard_map/ppermute | solution.py:485

commit v14 on v13

--- a/solution.py
+++ b/solution.py
@@ -33,32 +33,47 @@
     return table.reshape(width, width).astype(jnp.bfloat16)
 
 
-def height_table(height):
-    fine = 32
-    coarse = height // fine
+FINE = 32
+
+
+def short_tables(height):
     column = np.arange(height)[None, :]
-    rough = 2.0 * math.pi / height * (np.arange(coarse)[:, None] * fine * column % height)
-    small = 2.0 * math.pi / height * (np.arange(fine)[:, None] * column % height)
+    rough = 2.0 * math.pi / height * (np.arange(height // FINE)[:, None] * FINE * column % height)
+    small = 2.0 * math.pi / height * (np.arange(FINE)[:, None] * column % height)
+    short = [np.cos(small), np.sin(small), np.cos(rough), np.sin(rough)]
+    return jnp.asarray(np.concatenate(short), jnp.float32)
+
+
+def scaled_tables(height, after):
     factor = 1.0 / math.sqrt(height)
-    short = [np.cos(small), np.sin(small), np.cos(rough) * factor, np.sin(rough) * factor]
-
-    def body(short_ref, out_ref):
-        sc, ss = short_ref[:fine], short_ref[fine : 2 * fine]
-        for a in range(2 * fine, 2 * fine + coarse):
-            rc, rs = short_ref[a : a + 1, :], short_ref[a + coarse : a + coarse + 1, :]
-            here = slice((a - 2 * fine) * fine, (a - 2 * fine + 1) * fine)
-            out_ref[here, :height] = (rc * sc - rs * ss).astype(jnp.bfloat16)
-            out_ref[here, height:] = (rs * sc + rc * ss).astype(jnp.bfloat16)
-
-    return pl.pallas_call(
-        body,
-        in_specs=[pl.BlockSpec(memory_space=pltpu.VMEM)],
+
+    def body(short_ref, *refs):
+        refs[-1][: 2 * FINE] = short_ref[: 2 * FINE]
+        refs[-1][2 * FINE :] = short_ref[2 * FINE :] * factor
+
+    short = short_tables(height)
+    return pl.pallas_call(
+        body,
+        in_specs=[pl.BlockSpec(memory_space=pltpu.VMEM)]
+        + [pl.BlockSpec(memory_space=pl.ANY)] * len(after),
         out_specs=pl.BlockSpec(memory_space=pltpu.VMEM),
-        out_shape=jax.ShapeDtypeStruct((height, 2 * height), jnp.bfloat16),
-        compiler_params=params(),
-        cost_estimate=cost(1 << 33, 4 * height * height),
-        name="height_table",
-    )(jnp.asarray(np.concatenate(short), jnp.float32))
+        out_shape=jax.ShapeDtypeStruct(short.shape, short.dtype),
+        compiler_params=params(),
+        cost_estimate=cost(1 << 33, 8 * short.size),
+        name="scaled_tables",
+    )(short, *after)
+
+
+def make_table(short_ref, out_ref, first, rows):
+    height = short_ref.shape[1]
+    coarse = height // FINE
+    sc, ss = short_ref[:FINE], short_ref[FINE : 2 * FINE]
+    for j in range(first // FINE, (first + rows) // FINE):
+        a = 2 * FINE + j
+        rc, rs = short_ref[a : a + 1, :], short_ref[a + coarse : a + coarse + 1, :]
+        here = slice(j * FINE, (j + 1) * FINE)
+        out_ref[here, :height] = (rc * sc - rs * ss).astype(jnp.bfloat16)
+        out_ref[here, height:] = (rs * sc + rc * ss).astype(jnp.bfloat16)
 
 
 def cost(flops, moved):
@@ -290,29 +305,38 @@
             out[p, block:] = ((s_part[re] + c_part[im]) * twice).astype(jnp.bfloat16)
 
 
-def own_spectra(place, pieces, near, table):
+def own_spectra(place, pieces, near, short):
     peers, count, double, rows = pieces.shape
-    height = table.shape[0]
-
-    def body(half_ref, me_ref, pieces_ref, near_a, near_b, table_ref, spectra, edge, share):
-        inputs = [pieces_ref.at[k] for k in range(peers)]
-        store_spectra((half_ref, me_ref), gather_rows(inputs, table_ref, 0), spectra, edge, 0)
+    height = peers * rows
+
+    def body(half_ref, me_ref, pieces_ref, near_a, near_b, short_ref, spectra, edge, share, table_ref):
+        total = None
+        for k in range(peers):
+            make_table(short_ref, table_ref, k * rows, rows)
+            term = jnp.dot(
+                pieces_ref[k].reshape(count * double, rows),
+                table_ref[k * rows : (k + 1) * rows],
+                preferred_element_type=jnp.float32,
+            )
+            total = term if total is None else total + term
+        store_spectra((half_ref, me_ref), total, spectra, edge, 0)
         share[...] = gather_rows([near_a, near_b], table_ref, me_ref[0])
 
     return pl.pallas_call(
         body,
         in_specs=[pl.BlockSpec(memory_space=pltpu.SMEM)] * 2
         + [pl.BlockSpec(memory_space=pltpu.VMEM)] * 4,
-        out_specs=[pl.BlockSpec(memory_space=pltpu.VMEM)] * 3,
+        out_specs=[pl.BlockSpec(memory_space=pltpu.VMEM)] * 4,
         out_shape=[
             jax.ShapeDtypeStruct((count, 2, double // 2, height), jnp.bfloat16),
             jax.ShapeDtypeStruct((count, 2, 16, height), jnp.bfloat16),
             jax.ShapeDtypeStruct((count * double, 2 * height), jnp.float32),
+            jax.ShapeDtypeStruct((height, 2 * height), jnp.bfloat16),
         ],
         compiler_params=params(),
         cost_estimate=cost(6 * count * double * height * height, 8 * height * height),
         name="own_spectra",
-    )(*place, pieces, *near, table)
+    )(*place, pieces, *near, short)
 
 
 def partner_slots(place, theirs, pieces, share, table, spectra, edge):
@@ -496,10 +520,11 @@
     arrived += [across(sent[k - 2], k) for k in range(2, peers)]
     mine = along(kept)
 
-    table_h = height_table(height)
     theirs = across(pairs, 0)
     place = (scalar(half), scalar(me))
-    spectra, edge, share = own_spectra(place, mine, arrived[:2], table_h)
+    spectra, edge, share, table_h = own_spectra(
+        place, mine, arrived[:2], scaled_tables(height, [])
+    )
     near, spectra, edge, phases = partner_slots(
         place, theirs, arrived[2:], share, table_h, spectra, edge
     )

time: 63.7 us -> 63.1 us (level)
  waiting for transfers between devices: 12.4 us -> 15.7 us
  local copies, waits for them, and re-layouts: 6.77 us -> 4.49 us
  Pallas kernels: 17.8 us -> 17.1 us
  starting transfers between devices: 25.5 us -> 24.8 us
    all_to_all x2, waiting for transfers between devices: 0.01 us -> 5.2 us  [along(): return lax.all_to_all(blocks, 'rows', split_axis=0, concat_axis=0)]
    unnamed x16, local copies, waits for them, and re-layouts: 6.76 us -> 4.48 us
    ppermute x8, waiting for transfers between devices: 12.4 us -> 10.5 us  [across(): return lax.ppermute(value, axes, moves)]
    pallas_call x1, Pallas kernels: 1.11 us -> 0.04 us  [scaled_tables(): pl.pallas_call(body, in_specs=[pl.BlockSpec(memory_space=pltpu.VMEM)] + [...]
    ppermute x8, starting transfers between devices: 18.5 us -> 17.7 us  [across(): return lax.ppermute(value, axes, moves)]
  transfers between devices with their start and end apart: 11 -> 11, of which waited for: 4 -> 6; matrix products, arithmetic and copies ran while one was open for 0% -> 0% of each run, Pallas kernels for 16% -> 15%
where the time goes in v14:
time: 63.1 us; the launch traced here: 62.7 us
  starting transfers between devices  24.8 us (39%)
  Pallas kernels  17.1 us (27%)
  waiting for transfers between devices  15.7 us (25%)
  local copies, waits for them, and re-layouts  4.49 us (7%)
  between operations  0.75 us (1%)
    ppermute x8, starting transfers between devices, across(): return lax.ppermute(value, axes, moves)  17.7 us
    ppermute x8, waiting for transfers between devices, across(): return lax.ppermute(value, axes, moves)  10.5 us
    all_to_all x2, starting transfers between devices, along(): return lax.all_to_all(blocks, 'rows', split_axis=0, concat_axis=0)  6.94 us
    all_to_all x2, waiting for transfers between devices, along(): return lax.all_to_all(blocks, 'rows', split_axis=0, concat_axis=0)  5.2 us
    unnamed x16, local copies, waits for them, and re-layouts  4.48 us
    pallas_call x1, Pallas kernels, own_slots(): pl.pallas_call(body, in_specs=[pl.BlockSpec(memory_space=pltpu.SMEM)] * 3...  3.58 us
    pallas_call x1, Pallas kernels, near_columns(): pl.pallas_call(body, grid_spec=pltpu.PrefetchScalarGridSpec(num_scalar_pr...  3.43 us
    pallas_call x1, Pallas kernels, partner_slots(): pl.pallas_call(body, in_specs=[pl.BlockSpec(memory_space=pltpu.SMEM)] * 3...  2.52 us
  transfers between devices with their start and end apart: 11, of which 6 were waited for; matrix products, arithmetic and copies ran while one was open for 0% of the time, Pallas kernels for 15%

profile of v14, /device:TPU:0, one launch (start us, length us, event | category | flops | bytes accessed | tf_op | source)
XLA Modules:
  0.0 62.7 jit_solution(761996457047299015)
XLA Ops:
  0.0 3.4 %near_columns.1 = (bf16[2,128,256]{2,1,0:T(8,128)(2,1)}, bf16[2,128,256]{2,1,0:T(8,128)(2,1)}) custom-call(s32[1]{0:T(128)} %bitcast.half_ref, s32[1]{0:T(128)} %bitcast.1.me_ref, f32[2,256,1024]{2,1,0:T(8,128)} %tile_ref.1, f32[8,1024]{1,0:T(8,128)} %constant.30.clone.down_hbm.down_ref, f32[1,1024]{1,0:T(1,128)} %constant.31.clone.across_hbm.across_ref, ...), custom_call_target="tpu_custom_call" | custom-call | flops 268435456 | bytes 2621440 | tf_op jit(solution)/shard_map/near_columns/pallas_call | solution.py:144
  3.4 4.1 %collective-permute-start = (bf16[2,128,256]{2,1,0:T(8,128)(2,1)}, bf16[2,128,256]{2,1,0:T(8,128)(2,1)S(1)}, u32[]{:S(2)}, u32[]{:S(2)}) collective-permute-start(bf16[2,128,256]{2,1,0:T(8,128)(2,1)} %get-tuple-element.29), channel_id=1, source_target_pairs={{0,8},{1,9},{2,10},{3,11},{4,12},{5,13},{6,14},{7,15},{8,0},{9,1},... | collective-permute-start | bytes 393224 | tf_op jit(solution)/shard_map/ppermute | solution.py:503
  7.6 1.6 %copy-done.1 = f32[2,256,1024]{2,1,0:T(8,128)S(1)} copy-done((f32[2,256,1024]{2,1,0:T(8,128)S(1)}, f32[2,256,1024]{2,1,0:T(8,128)}, u32[]{:S(2)}) %copy-start.1) | copy-done | bytes 2097176
  9.2 2.4 %rest_columns.1 = (bf16[4,2,128,256]{3,2,1,0:T(8,128)(2,1)}, bf16[2,128,256]{2,1,0:T(8,128)(2,1)S(1)}, bf16[2,128,256]{2,1,0:T(8,128)(2,1)S(1)}) custom-call(s32[1]{0:T(128)} %bitcast.2.half_ref, s32[1]{0:T(128)} %bitcast.1.me_ref, f32[2,256,1024]{2,1,0:T(8,128)S(1)} %copy-done.1, f32[8,1024]{1,0:T(8,128)S(1)} %copy-done.2, f32[1,1024]{1,0:T(1,128)S(1)} %copy-done.3, ...), custom_call_target="tpu_custom_call" | custom-call | flops 805306368 | bytes 4194304 | tf_op jit(solution)/shard_map/rest_columns/pallas_call | solution.py:192
  11.6 3.5 %all-to-all-start = ((bf16[4,2,128,256]{3,2,1,0:T(8,128)(2,1)}), bf16[4,2,128,256]{3,2,1,0:T(8,128)(2,1)S(1)}, u32[]{:S(2)}, u32[]{:S(2)}) async-start(bf16[4,2,128,256]{3,2,1,0:T(8,128)(2,1)} %get-tuple-element.36), calls=%async_computation | async-start | bytes 1048576 | tf_op jit(solution)/shard_map/all_to_all | solution.py:506
  15.1 3.5 %collective-permute-start.3 = (bf16[2,128,256]{2,1,0:T(8,128)(2,1)S(1)}, bf16[2,128,256]{2,1,0:T(8,128)(2,1)S(1)}, u32[]{:S(2)}, u32[]{:S(2)}) collective-permute-start(bf16[2,128,256]{2,1,0:T(8,128)(2,1)S(1)} %get-tuple-element.38), channel_id=1, source_target_pairs={{0,10},{1,11},{2,8},{3,9},{4,14},{5,15},{6,12},{7,13},{8,2},{9,3},... | collective-permute-start | bytes 393224 | tf_op jit(solution)/shard_map/ppermute | solution.py:503
  18.8 2.5 %collective-permute-start.2 = (s32[1,2,2]{2,1,0:T(2,128)S(1)}, s32[1,2,2]{2,1,0:T(2,128)S(1)}, u32[]{:S(2)}, u32[]{:S(2)}) collective-permute-start(s32[1,2,2]{2,1,0:T(2,128)S(1)} %copy-done.4), channel_id=1, source_target_pairs={{0,8},{1,9},{2,10},{3,11},{4,12},{5,13},{6,14},{7,15},{8,0},{9,1},... | collective-permute-start | bytes 56 | tf_op jit(solution)/shard_map/ppermute | solution.py:503
  21.3 1.0 %copy-done.5 = f32[128,1024]{1,0:T(8,128)S(1)} copy-done((f32[128,1024]{1,0:T(8,128)S(1)}, f32[128,1024]{1,0:T(8,128)}, u32[]{:S(2)}) %copy-start.5) | copy-done | bytes 524312
  23.2 1.7 %all-to-all-done.pieces_ref = bf16[4,2,128,256]{3,2,1,0:T(8,128)(2,1)S(1)} async-done(((bf16[4,2,128,256]{3,2,1,0:T(8,128)(2,1)}), bf16[4,2,128,256]{3,2,1,0:T(8,128)(2,1)S(1)}, u32[]{:S(2)}, u32[]{:S(2)}) %all-to-all-start) | async-done | bytes 524320 | tf_op jit(solution)/shard_map/all_to_all | solution.py:506
  24.9 1.0 %copy-done.7 = f32[128,1024]{1,0:T(8,128)S(1)} copy-done((f32[128,1024]{1,0:T(8,128)S(1)}, f32[128,1024]{1,0:T(8,128)}, u32[]{:S(2)}) %copy-start.7) | copy-done | bytes 524312
  25.9 2.2 %own_spectra.1 = (bf16[2,2,64,1024]{3,2,1,0:T(8,128)(2,1)S(1)}, bf16[2,2,16,1024]{3,2,1,0:T(8,128)(2,1)S(1)}, f32[256,2048]{1,0:T(8,128)S(1)}, bf16[1024,2048]{1,0:T(8,128)(2,1)S(1)}) custom-call(s32[1]{0:T(128)} %bitcast.half_ref, s32[1]{0:T(128)} %bitcast.1.me_ref, bf16[4,2,128,256]{3,2,1,0:T(8,128)(2,1)S(1)} %all-to-all-done.pieces_ref, ...), custom_call_target="tpu_custom_call" | custom-call | flops 1610612736 | bytes 8388608 | tf_op jit(solution)/shard_map/own_spectra/pallas_call | solution.py:325
  28.1 3.3 %collective-permute-done.2.theirs_ref = s32[1,2,2]{2,1,0:T(2,128)S(1)} collective-permute-done((s32[1,2,2]{2,1,0:T(2,128)S(1)}, s32[1,2,2]{2,1,0:T(2,128)S(1)}, u32[]{:S(2)}, u32[]{:S(2)}) %collective-permute-start.2) | collective-permute-done | bytes 48 | tf_op jit(solution)/shard_map/ppermute | solution.py:503
  31.4 2.5 %partner_slots.1 = (bf16[2,2,128,256]{3,2,1,0:T(8,128)(2,1)S(1)}, bf16[4,2,64,1024]{3,2,1,0:T(8,128)(2,1)S(1)}, bf16[4,2,16,1024]{3,2,1,0:T(8,128)(2,1)S(1)}, bf16[4,64,1024]{2,1,0:T(8,128)(2,1)S(1)}) custom-call(s32[1]{0:T(128)} %bitcast.half_ref, s32[1]{0:T(128)} %bitcast.1.me_ref, s32[1,2,2]{2,1,0:T(2,128)S(1)} %collective-permute-done.2.theirs_ref, ...), custom_call_target="tpu_custom_call" | custom-call | flops 2147483648 | bytes 8388608 | tf_op jit(solution)/shard_map/partner_slots/pallas_call | solution.py:364
  33.9 3.8 %collective-permute-start.7 = (bf16[2,2,128,256]{3,2,1,0:T(8,128)(2,1)S(1)}, bf16[2,2,128,256]{3,2,1,0:T(8,128)(2,1)S(1)}, u32[]{:S(2)}, u32[]{:S(2)}) collective-permute-start(bf16[2,2,128,256]{3,2,1,0:T(8,128)(2,1)S(1)} %get-tuple-element.50), channel_id=1, source_target_pairs={{0,8},{1,9},{2,10},{3,11},{4,12},{5,13},{6,14},{7,15},{8,0},{9,1},... | collective-permute-start | bytes 786440 | tf_op jit(solution)/shard_map/ppermute | solution.py:503
  37.7 3.6 %own_slots.1 = (bf16[4,2,128,256]{3,2,1,0:T(8,128)(2,1)}, bf16[2,128,256]{2,1,0:T(8,128)(2,1)}, bf16[2,128,256]{2,1,0:T(8,128)(2,1)S(1)}) custom-call(s32[1]{0:T(128)} %bitcast.half_ref, s32[1]{0:T(128)} %bitcast.1.me_ref, s32[1,2,2]{2,1,0:T(2,128)S(1)} %copy-done.4, bf16[1024,2048]{1,0:T(8,128)(2,1)S(1)} %get-tuple-element.37.refs_3_.table_ref, ...), custom_call_target="tpu_custom_call" | custom-call | flops 1073741824 | bytes 8388608 | tf_op jit(solution)/shard_map/own_slots/pallas_call | solution.py:396
  41.3 3.5 %all-to-all-start.1 = ((bf16[4,2,128,256]{3,2,1,0:T(8,128)(2,1)}), bf16[4,2,128,256]{3,2,1,0:T(8,128)(2,1)S(1)}, u32[]{:S(2)}, u32[]{:S(2)}) async-start(bf16[4,2,128,256]{3,2,1,0:T(8,128)(2,1)} %get-tuple-element.48), calls=%async_computation.1 | async-start | bytes 1048576 | tf_op jit(solution)/shard_map/all_to_all | solution.py:506
  44.7 1.4 %collective-permute-start.5 = (bf16[2,128,256]{2,1,0:T(8,128)(2,1)}, bf16[2,128,256]{2,1,0:T(8,128)(2,1)S(1)}, u32[]{:S(2)}, u32[]{:S(2)}) collective-permute-start(bf16[2,128,256]{2,1,0:T(8,128)(2,1)} %get-tuple-element.46), channel_id=1, source_target_pairs={{0,10},{1,11},{2,8},{3,9},{4,14},{5,15},{6,12},{7,13},{8,2},{9,3},... | collective-permute-start | bytes 393224 | tf_op jit(solution)/shard_map/ppermute | solution.py:503
  46.2 2.2 %collective-permute-start.6 = (bf16[2,128,256]{2,1,0:T(8,128)(2,1)S(1)}, bf16[2,128,256]{2,1,0:T(8,128)(2,1)S(1)}, u32[]{:S(2)}, u32[]{:S(2)}) collective-permute-start(bf16[2,128,256]{2,1,0:T(8,128)(2,1)S(1)} %get-tuple-element.47), channel_id=1, source_target_pairs={{0,11},{1,10},{2,9},{3,8},{4,15},{5,14},{6,13},{7,12},{8,3},{9,2},... | collective-permute-start | bytes 393224 | tf_op jit(solution)/shard_map/ppermute | solution.py:503
  48.4 1.2 %collective-permute-done.7.refs_0_ = bf16[2,2,128,256]{3,2,1,0:T(8,128)(2,1)S(1)} collective-permute-done((bf16[2,2,128,256]{3,2,1,0:T(8,128)(2,1)S(1)}, bf16[2,2,128,256]{3,2,1,0:T(8,128)(2,1)S(1)}, u32[]{:S(2)}, u32[]{:S(2)}) %collective-permute-start.7) | collective-permute-done | bytes 262176 | tf_op jit(solution)/shard_map/ppermute | solution.py:503
  50.4 3.5 %all-to-all-done.1.own_ref = bf16[4,2,128,256]{3,2,1,0:T(8,128)(2,1)S(1)} async-done(((bf16[4,2,128,256]{3,2,1,0:T(8,128)(2,1)}), bf16[4,2,128,256]{3,2,1,0:T(8,128)(2,1)S(1)}, u32[]{:S(2)}, u32[]{:S(2)}) %all-to-all-start.1) | async-done | bytes 524320 | tf_op jit(solution)/shard_map/all_to_all | solution.py:506
  53.9 1.0 %own_surfaces.1.part_ref = f32[2,256,1024]{2,1,0:T(8,128)S(1)} custom-call(s32[1]{0:T(128)} %bitcast.half_ref, bf16[4,2,128,256]{3,2,1,0:T(8,128)(2,1)S(1)} %all-to-all-done.1.own_ref, bf16[1024,1024]{1,0:T(8,128)(2,1)S(1)} %copy-done), custom_call_target="tpu_custom_call" | custom-call | flops 536870912 | bytes 2097152 | tf_op jit(solution)/shard_map/own_surfaces/pallas_call | solution.py:425
  54.9 3.6 %collective-permute-done.5.refs_2_ = bf16[2,128,256]{2,1,0:T(8,128)(2,1)S(1)} collective-permute-done((bf16[2,128,256]{2,1,0:T(8,128)(2,1)}, bf16[2,128,256]{2,1,0:T(8,128)(2,1)S(1)}, u32[]{:S(2)}, u32[]{:S(2)}) %collective-permute-start.5) | collective-permute-done | bytes 131104 | tf_op jit(solution)/shard_map/ppermute | solution.py:503
  58.5 2.2 %collective-permute-done.6.refs_3_ = bf16[2,128,256]{2,1,0:T(8,128)(2,1)S(1)} collective-permute-done((bf16[2,128,256]{2,1,0:T(8,128)(2,1)S(1)}, bf16[2,128,256]{2,1,0:T(8,128)(2,1)S(1)}, u32[]{:S(2)}, u32[]{:S(2)}) %collective-permute-start.6) | collective-permute-done | bytes 131104 | tf_op jit(solution)/shard_map/ppermute | solution.py:503
  60.8 2.0 %surfaces.1 = f32[2,256,1024]{2,1,0:T(8,128)} custom-call(s32[1]{0:T(128)} %bitcast.half_ref, s32[1]{0:T(128)} %bitcast.1.me_ref, s32[1]{0:T(128)S(6)} %copy.8.counts_ref, f32[2,256,1024]{2,1,0:T(8,128)S(1)} %own_surfaces.1.part_ref, bf16[2,2,128,256]{3,2,1,0:T(8,128)(2,1)S(1)} %collective-permute-done.7.refs_0_, ...), custom_call_target="tpu_custom_call" | custom-call | flops 536870912 | bytes 4194304 | tf_op jit(solution)/shard_map/surfaces/pallas_call | solution.py:465
  (23 shorter events, 1.2 us)
Async XLA Ops:
  0.0 7.6 %copy-start = (bf16[1024,1024]{1,0:T(8,128)(2,1)S(1)}, bf16[1024,1024]{1,0:T(8,128)(2,1)}, u32[]{:S(2)}) copy-start(bf16[1024,1024]{1,0:T(8,128)(2,1)} %constant.29.clone.table_hbm.table_ref.refs_4_) | copy-start | bytes 6291460
  0.0 7.6 %copy-start.2 = (f32[8,1024]{1,0:T(8,128)S(1)}, f32[8,1024]{1,0:T(8,128)}, u32[]{:S(2)}) copy-start(f32[8,1024]{1,0:T(8,128)} %constant.30.clone.down_hbm.down_ref) | copy-start | bytes 98308
  0.0 7.6 %copy-start.3 = (f32[1,1024]{1,0:T(1,128)S(1)}, f32[1,1024]{1,0:T(1,128)}, u32[]{:S(2)}) copy-start(f32[1,1024]{1,0:T(1,128)} %constant.31.clone.across_hbm.across_ref) | copy-start | bytes 12292
  3.4 19.7 %collective-permute-start = (bf16[2,128,256]{2,1,0:T(8,128)(2,1)}, bf16[2,128,256]{2,1,0:T(8,128)(2,1)S(1)}, u32[]{:S(2)}, u32[]{:S(2)}) collective-permute-start(bf16[2,128,256]{2,1,0:T(8,128)(2,1)} %get-tuple-element.29), channel_id=1, source_target_pairs={{0,8},{1,9},{2,10},{3,11},{4,12},{5,13},{6,14},{7,15},{8,0},{9,1},... | collective-permute-start | bytes 393224 | tf_op jit(solution)/shard_map/ppermute | solution.py:503
  7.6 15.6 %collective-permute-start.1 = (bf16[2,128,256]{2,1,0:T(8,128)(2,1)}, bf16[2,128,256]{2,1,0:T(8,128)(2,1)S(1)}, u32[]{:S(2)}, u32[]{:S(2)}) collective-permute-start(bf16[2,128,256]{2,1,0:T(8,128)(2,1)} %get-tuple-element.30), channel_id=1, source_target_pairs={{0,9},{1,8},{2,11},{3,10},{4,13},{5,12},{6,15},{7,14},{8,1},{9,0},... | collective-permute-start | bytes 393224 | tf_op jit(solution)/shard_map/ppermute | solution.py:503
  7.6 1.6 %copy-start.1 = (f32[2,256,1024]{2,1,0:T(8,128)S(1)}, f32[2,256,1024]{2,1,0:T(8,128)}, u32[]{:S(2)}) copy-start(f32[2,256,1024]{2,1,0:T(8,128)} %tile_ref.1) | copy-start | bytes 6291460
  9.2 9.6 %copy-start.4 = (s32[1,2,2]{2,1,0:T(2,128)S(1)}, s32[1,2,2]{2,1,0:T(2,128)}, u32[]{:S(2)}) copy-start(s32[1,2,2]{2,1,0:T(2,128)} %pairs_ref) | copy-start | bytes 52
  11.6 13.3 %all-to-all-start = ((bf16[4,2,128,256]{3,2,1,0:T(8,128)(2,1)}), bf16[4,2,128,256]{3,2,1,0:T(8,128)(2,1)S(1)}, u32[]{:S(2)}, u32[]{:S(2)}) async-start(bf16[4,2,128,256]{3,2,1,0:T(8,128)(2,1)} %get-tuple-element.36), calls=%async_computation | async-start | bytes 1048576 | tf_op jit(solution)/shard_map/all_to_all | solution.py:506
  15.1 16.3 %collective-permute-start.3 = (bf16[2,128,256]{2,1,0:T(8,128)(2,1)S(1)}, bf16[2,128,256]{2,1,0:T(8,128)(2,1)S(1)}, u32[]{:S(2)}, u32[]{:S(2)}) collective-permute-start(bf16[2,128,256]{2,1,0:T(8,128)(2,1)S(1)} %get-tuple-element.38), channel_id=1, source_target_pairs={{0,10},{1,11},{2,8},{3,9},{4,14},{5,15},{6,12},{7,13},{8,2},{9,3},... | collective-permute-start | bytes 393224 | tf_op jit(solution)/shard_map/ppermute | solution.py:503
  18.6 12.8 %collective-permute-start.4 = (bf16[2,128,256]{2,1,0:T(8,128)(2,1)S(1)}, bf16[2,128,256]{2,1,0:T(8,128)(2,1)S(1)}, u32[]{:S(2)}, u32[]{:S(2)}) collective-permute-start(bf16[2,128,256]{2,1,0:T(8,128)(2,1)S(1)} %get-tuple-element.39), channel_id=1, source_target_pairs={{0,11},{1,10},{2,9},{3,8},{4,15},{5,14},{6,13},{7,12},{8,3},{9,2},... | collective-permute-start | bytes 393224 | tf_op jit(solution)/shard_map/ppermute | solution.py:503
  18.8 12.6 %collective-permute-start.2 = (s32[1,2,2]{2,1,0:T(2,128)S(1)}, s32[1,2,2]{2,1,0:T(2,128)S(1)}, u32[]{:S(2)}, u32[]{:S(2)}) collective-permute-start(s32[1,2,2]{2,1,0:T(2,128)S(1)} %copy-done.4), channel_id=1, source_target_pairs={{0,8},{1,9},{2,10},{3,11},{4,12},{5,13},{6,14},{7,15},{8,0},{9,1},... | collective-permute-start | bytes 56 | tf_op jit(solution)/shard_map/ppermute | solution.py:503
  21.3 1.0 %copy-start.5 = (f32[128,1024]{1,0:T(8,128)S(1)}, f32[128,1024]{1,0:T(8,128)}, u32[]{:S(2)}) copy-start(f32[128,1024]{1,0:T(8,128)} %constant.32.clone.short_ref) | copy-start | bytes 1572868
  22.4 0.8 %copy-start.6 = (f32[128,1024]{1,0:T(8,128)}, f32[128,1024]{1,0:T(8,128)S(1)}, u32[]{:S(2)}) copy-start(f32[128,1024]{1,0:T(8,128)S(1)} %scaled_tables.1.short_ref) | copy-start | bytes 1572868
  24.8 1.0 %copy-start.7 = (f32[128,1024]{1,0:T(8,128)S(1)}, f32[128,1024]{1,0:T(8,128)}, u32[]{:S(2)}) copy-start(f32[128,1024]{1,0:T(8,128)} %copy-done.6) | copy-start | bytes 1572868
  33.9 15.7 %collective-permute-start.7 = (bf16[2,2,128,256]{3,2,1,0:T(8,128)(2,1)S(1)}, bf16[2,2,128,256]{3,2,1,0:T(8,128)(2,1)S(1)}, u32[]{:S(2)}, u32[]{:S(2)}) collective-permute-start(bf16[2,2,128,256]{3,2,1,0:T(8,128)(2,1)S(1)} %get-tuple-element.50), channel_id=1, source_target_pairs={{0,8},{1,9},{2,10},{3,11},{4,12},{5,13},{6,14},{7,15},{8,0},{9,1},... | collective-permute-start | bytes 786440 | tf_op jit(solution)/shard_map/ppermute | solution.py:503
  41.3 12.6 %all-to-all-start.1 = ((bf16[4,2,128,256]{3,2,1,0:T(8,128)(2,1)}), bf16[4,2,128,256]{3,2,1,0:T(8,128)(2,1)S(1)}, u32[]{:S(2)}, u32[]{:S(2)}) async-start(bf16[4,2,128,256]{3,2,1,0:T(8,128)(2,1)} %get-tuple-element.48), calls=%async_computation.1 | async-start | bytes 1048576 | tf_op jit(solution)/shard_map/all_to_all | solution.py:506
  44.7 13.8 %collective-permute-start.5 = (bf16[2,128,256]{2,1,0:T(8,128)(2,1)}, bf16[2,128,256]{2,1,0:T(8,128)(2,1)S(1)}, u32[]{:S(2)}, u32[]{:S(2)}) collective-permute-start(bf16[2,128,256]{2,1,0:T(8,128)(2,1)} %get-tuple-element.46), channel_id=1, source_target_pairs={{0,10},{1,11},{2,8},{3,9},{4,14},{5,15},{6,12},{7,13},{8,2},{9,3},... | collective-permute-start | bytes 393224 | tf_op jit(solution)/shard_map/ppermute | solution.py:503
  46.2 14.6 %collective-permute-start.6 = (bf16[2,128,256]{2,1,0:T(8,128)(2,1)S(1)}, bf16[2,128,256]{2,1,0:T(8,128)(2,1)S(1)}, u32[]{:S(2)}, u32[]{:S(2)}) collective-permute-start(bf16[2,128,256]{2,1,0:T(8,128)(2,1)S(1)} %get-tuple-element.47), channel_id=1, source_target_pairs={{0,11},{1,10},{2,9},{3,8},{4,15},{5,14},{6,13},{7,12},{8,3},{9,2},... | collective-permute-start | bytes 393224 | tf_op jit(solution)/shard_map/ppermute | solution.py:503
  49.6 11.2 %collective-permute-start.8 = (bf16[2,128,256]{2,1,0:T(8,128)(2,1)S(1)}, bf16[2,128,256]{2,1,0:T(8,128)(2,1)S(1)}, u32[]{:S(2)}, u32[]{:S(2)}) collective-permute-start(bf16[2,128,256]{2,1,0:T(8,128)(2,1)S(1)} %slice_bitcast_fusion), channel_id=1, source_target_pairs={{0,1},{1,0},{2,3},{3,2},{4,5},{5,4},{6,7},{7,6},{8,9},{9,8},{10,11... | collective-permute-start | bytes 393224 | tf_op jit(solution)/shard_map/ppermute | solution.py:509

commit v15 on v14

--- a/solution.py
+++ b/solution.py
@@ -9,7 +9,7 @@
 
 FLOOR = 0.05
 VMEM_LIMIT = 24 * 1024 * 1024
-FIRST_LIMIT = 60 * 1024 * 1024
+FIRST_LIMIT = 58 * 1024 * 1024
 
 
 def hann(length):

time: 63.1 us -> 61.9 us (0.981)
  local copies, waits for them, and re-layouts: 4.49 us -> 2.91 us
  waiting for transfers between devices: 15.7 us -> 17.1 us
  starting transfers between devices: 24.8 us -> 23.6 us
    ppermute x8, waiting for transfers between devices: 10.5 us -> 13.3 us  [across(): return lax.ppermute(value, axes, moves)]
    unnamed x16, local copies, waits for them, and re-layouts: 4.48 us -> 2.9 us
    all_to_all x2, waiting for transfers between devices: 5.2 us -> 3.85 us  [along(): return lax.all_to_all(blocks, 'rows', split_axis=0, concat_axis=0)]
    ppermute x8, starting transfers between devices: 17.7 us -> 16.6 us  [across(): return lax.ppermute(value, axes, moves)]
where the time goes in v15:
time: 61.9 us; the launch traced here: 61.6 us
  starting transfers between devices  23.6 us (38%)
  Pallas kernels  17.1 us (28%)
  waiting for transfers between devices  17.1 us (28%)
  local copies, waits for them, and re-layouts  2.91 us (5%)
  between operations  0.76 us (1%)
    ppermute x8, starting transfers between devices, across(): return lax.ppermute(value, axes, moves)  16.6 us
    ppermute x8, waiting for transfers between devices, across(): return lax.ppermute(value, axes, moves)  13.3 us
    all_to_all x2, starting transfers between devices, along(): return lax.all_to_all(blocks, 'rows', split_axis=0, concat_axis=0)  6.94 us
    all_to_all x2, waiting for transfers between devices, along(): return lax.all_to_all(blocks, 'rows', split_axis=0, concat_axis=0)  3.85 us
    pallas_call x1, Pallas kernels, own_slots(): pl.pallas_call(body, in_specs=[pl.BlockSpec(memory_space=pltpu.SMEM)] * 3...  3.58 us
    pallas_call x1, Pallas kernels, near_columns(): pl.pallas_call(body, grid_spec=pltpu.PrefetchScalarGridSpec(num_scalar_pr...  3.44 us
    unnamed x16, local copies, waits for them, and re-layouts  2.9 us
    pallas_call x1, Pallas kernels, partner_slots(): pl.pallas_call(body, in_specs=[pl.BlockSpec(memory_space=pltpu.SMEM)] * 3...  2.53 us
  transfers between devices with their start and end apart: 11, of which 6 were waited for; matrix products, arithmetic and copies ran while one was open for 0% of the time, Pallas kernels for 15%

profile of v15, /device:TPU:0, one launch (start us, length us, event | category | flops | bytes accessed | tf_op | source)
XLA Modules:
  0.0 61.6 jit_solution(1992859505002692094)
XLA Ops:
  0.0 3.4 %near_columns.1 = (bf16[2,128,256]{2,1,0:T(8,128)(2,1)}, bf16[2,128,256]{2,1,0:T(8,128)(2,1)}) custom-call(s32[1]{0:T(128)} %bitcast.half_ref, s32[1]{0:T(128)} %bitcast.1.me_ref, f32[2,256,1024]{2,1,0:T(8,128)} %tile_ref.1, f32[8,1024]{1,0:T(8,128)} %constant.30.clone.down_hbm.down_ref, f32[1,1024]{1,0:T(1,128)} %constant.31.clone.across_hbm.across_ref, ...), custom_call_target="tpu_custom_call" | custom-call | flops 268435456 | bytes 2621440 | tf_op jit(solution)/shard_map/near_columns/pallas_call | solution.py:144
  3.5 4.1 %collective-permute-start = (bf16[2,128,256]{2,1,0:T(8,128)(2,1)}, bf16[2,128,256]{2,1,0:T(8,128)(2,1)S(1)}, u32[]{:S(2)}, u32[]{:S(2)}) collective-permute-start(bf16[2,128,256]{2,1,0:T(8,128)(2,1)} %get-tuple-element.29), channel_id=1, source_target_pairs={{0,8},{1,9},{2,10},{3,11},{4,12},{5,13},{6,14},{7,15},{8,0},{9,1},... | collective-permute-start | bytes 393224 | tf_op jit(solution)/shard_map/ppermute | solution.py:503
  7.6 2.4 %rest_columns.1 = (bf16[4,2,128,256]{3,2,1,0:T(8,128)(2,1)}, bf16[2,128,256]{2,1,0:T(8,128)(2,1)S(1)}, bf16[2,128,256]{2,1,0:T(8,128)(2,1)S(1)}) custom-call(s32[1]{0:T(128)} %bitcast.2.half_ref, s32[1]{0:T(128)} %bitcast.1.me_ref, f32[2,256,1024]{2,1,0:T(8,128)S(1)} %copy-done.1, f32[8,1024]{1,0:T(8,128)S(1)} %copy-done.2, f32[1,1024]{1,0:T(1,128)S(1)} %copy-done.3, ...), custom_call_target="tpu_custom_call" | custom-call | flops 805306368 | bytes 4194304 | tf_op jit(solution)/shard_map/rest_columns/pallas_call | solution.py:192
  10.1 3.5 %all-to-all-start = ((bf16[4,2,128,256]{3,2,1,0:T(8,128)(2,1)}), bf16[4,2,128,256]{3,2,1,0:T(8,128)(2,1)S(1)}, u32[]{:S(2)}, u32[]{:S(2)}) async-start(bf16[4,2,128,256]{3,2,1,0:T(8,128)(2,1)} %get-tuple-element.36), calls=%async_computation | async-start | bytes 1048576 | tf_op jit(solution)/shard_map/all_to_all | solution.py:506
  13.5 3.5 %collective-permute-start.3 = (bf16[2,128,256]{2,1,0:T(8,128)(2,1)S(1)}, bf16[2,128,256]{2,1,0:T(8,128)(2,1)S(1)}, u32[]{:S(2)}, u32[]{:S(2)}) collective-permute-start(bf16[2,128,256]{2,1,0:T(8,128)(2,1)S(1)} %get-tuple-element.38), channel_id=1, source_target_pairs={{0,10},{1,11},{2,8},{3,9},{4,14},{5,15},{6,12},{7,13},{8,2},{9,3},... | collective-permute-start | bytes 393224 | tf_op jit(solution)/shard_map/ppermute | solution.py:503
  17.2 2.5 %collective-permute-start.2 = (s32[1,2,2]{2,1,0:T(2,128)S(1)}, s32[1,2,2]{2,1,0:T(2,128)S(1)}, u32[]{:S(2)}, u32[]{:S(2)}) collective-permute-start(s32[1,2,2]{2,1,0:T(2,128)S(1)} %copy-done.4), channel_id=1, source_target_pairs={{0,8},{1,9},{2,10},{3,11},{4,12},{5,13},{6,14},{7,15},{8,0},{9,1},... | collective-permute-start | bytes 56 | tf_op jit(solution)/shard_map/ppermute | solution.py:503
  19.8 1.0 %copy-done.5 = f32[128,1024]{1,0:T(8,128)S(1)} copy-done((f32[128,1024]{1,0:T(8,128)S(1)}, f32[128,1024]{1,0:T(8,128)}, u32[]{:S(2)}) %copy-start.5) | copy-done | bytes 524312
  20.9 0.8 %copy-done.6 = f32[128,1024]{1,0:T(8,128)} copy-done((f32[128,1024]{1,0:T(8,128)}, f32[128,1024]{1,0:T(8,128)S(1)}, u32[]{:S(2)}) %copy-start.6) | copy-done | bytes 524312
  21.7 0.7 %all-to-all-done.pieces_ref = bf16[4,2,128,256]{3,2,1,0:T(8,128)(2,1)S(1)} async-done(((bf16[4,2,128,256]{3,2,1,0:T(8,128)(2,1)}), bf16[4,2,128,256]{3,2,1,0:T(8,128)(2,1)S(1)}, u32[]{:S(2)}, u32[]{:S(2)}) %all-to-all-start) | async-done | bytes 524320 | tf_op jit(solution)/shard_map/all_to_all | solution.py:506
  22.3 1.0 %copy-done.7 = f32[128,1024]{1,0:T(8,128)S(1)} copy-done((f32[128,1024]{1,0:T(8,128)S(1)}, f32[128,1024]{1,0:T(8,128)}, u32[]{:S(2)}) %copy-start.7) | copy-done | bytes 524312
  23.4 2.2 %own_spectra.1 = (bf16[2,2,64,1024]{3,2,1,0:T(8,128)(2,1)S(1)}, bf16[2,2,16,1024]{3,2,1,0:T(8,128)(2,1)S(1)}, f32[256,2048]{1,0:T(8,128)S(1)}, bf16[1024,2048]{1,0:T(8,128)(2,1)S(1)}) custom-call(s32[1]{0:T(128)} %bitcast.half_ref, s32[1]{0:T(128)} %bitcast.1.me_ref, bf16[4,2,128,256]{3,2,1,0:T(8,128)(2,1)S(1)} %all-to-all-done.pieces_ref, ...), custom_call_target="tpu_custom_call" | custom-call | flops 1610612736 | bytes 8388608 | tf_op jit(solution)/shard_map/own_spectra/pallas_call | solution.py:325
  25.6 5.4 %collective-permute-done.2.theirs_ref = s32[1,2,2]{2,1,0:T(2,128)S(1)} collective-permute-done((s32[1,2,2]{2,1,0:T(2,128)S(1)}, s32[1,2,2]{2,1,0:T(2,128)S(1)}, u32[]{:S(2)}, u32[]{:S(2)}) %collective-permute-start.2) | collective-permute-done | bytes 48 | tf_op jit(solution)/shard_map/ppermute | solution.py:503
  31.0 2.5 %partner_slots.1 = (bf16[2,2,128,256]{3,2,1,0:T(8,128)(2,1)S(1)}, bf16[4,2,64,1024]{3,2,1,0:T(8,128)(2,1)S(1)}, bf16[4,2,16,1024]{3,2,1,0:T(8,128)(2,1)S(1)}, bf16[4,64,1024]{2,1,0:T(8,128)(2,1)S(1)}) custom-call(s32[1]{0:T(128)} %bitcast.half_ref, s32[1]{0:T(128)} %bitcast.1.me_ref, s32[1,2,2]{2,1,0:T(2,128)S(1)} %collective-permute-done.2.theirs_ref, ...), custom_call_target="tpu_custom_call" | custom-call | flops 2147483648 | bytes 8388608 | tf_op jit(solution)/shard_map/partner_slots/pallas_call | solution.py:364
  33.5 2.6 %collective-permute-start.7 = (bf16[2,2,128,256]{3,2,1,0:T(8,128)(2,1)S(1)}, bf16[2,2,128,256]{3,2,1,0:T(8,128)(2,1)S(1)}, u32[]{:S(2)}, u32[]{:S(2)}) collective-permute-start(bf16[2,2,128,256]{3,2,1,0:T(8,128)(2,1)S(1)} %get-tuple-element.50), channel_id=1, source_target_pairs={{0,8},{1,9},{2,10},{3,11},{4,12},{5,13},{6,14},{7,15},{8,0},{9,1},... | collective-permute-start | bytes 786440 | tf_op jit(solution)/shard_map/ppermute | solution.py:503
  36.2 3.6 %own_slots.1 = (bf16[4,2,128,256]{3,2,1,0:T(8,128)(2,1)}, bf16[2,128,256]{2,1,0:T(8,128)(2,1)}, bf16[2,128,256]{2,1,0:T(8,128)(2,1)S(1)}) custom-call(s32[1]{0:T(128)} %bitcast.half_ref, s32[1]{0:T(128)} %bitcast.1.me_ref, s32[1,2,2]{2,1,0:T(2,128)S(1)} %copy-done.4, bf16[1024,2048]{1,0:T(8,128)(2,1)S(1)} %get-tuple-element.37.refs_3_.table_ref, ...), custom_call_target="tpu_custom_call" | custom-call | flops 1073741824 | bytes 8388608 | tf_op jit(solution)/shard_map/own_slots/pallas_call | solution.py:396
  39.7 3.5 %all-to-all-start.1 = ((bf16[4,2,128,256]{3,2,1,0:T(8,128)(2,1)}), bf16[4,2,128,256]{3,2,1,0:T(8,128)(2,1)S(1)}, u32[]{:S(2)}, u32[]{:S(2)}) async-start(bf16[4,2,128,256]{3,2,1,0:T(8,128)(2,1)} %get-tuple-element.48), calls=%async_computation.1 | async-start | bytes 1048576 | tf_op jit(solution)/shard_map/all_to_all | solution.py:506
  43.2 1.8 %collective-permute-start.5 = (bf16[2,128,256]{2,1,0:T(8,128)(2,1)}, bf16[2,128,256]{2,1,0:T(8,128)(2,1)S(1)}, u32[]{:S(2)}, u32[]{:S(2)}) collective-permute-start(bf16[2,128,256]{2,1,0:T(8,128)(2,1)} %get-tuple-element.46), channel_id=1, source_target_pairs={{0,10},{1,11},{2,8},{3,9},{4,14},{5,15},{6,12},{7,13},{8,2},{9,3},... | collective-permute-start | bytes 393224 | tf_op jit(solution)/shard_map/ppermute | solution.py:503
  45.0 1.9 %collective-permute-start.6 = (bf16[2,128,256]{2,1,0:T(8,128)(2,1)S(1)}, bf16[2,128,256]{2,1,0:T(8,128)(2,1)S(1)}, u32[]{:S(2)}, u32[]{:S(2)}) collective-permute-start(bf16[2,128,256]{2,1,0:T(8,128)(2,1)S(1)} %get-tuple-element.47), channel_id=1, source_target_pairs={{0,11},{1,10},{2,9},{3,8},{4,15},{5,14},{6,13},{7,12},{8,3},{9,2},... | collective-permute-start | bytes 393224 | tf_op jit(solution)/shard_map/ppermute | solution.py:503
  46.9 2.4 %collective-permute-done.7.refs_0_ = bf16[2,2,128,256]{3,2,1,0:T(8,128)(2,1)S(1)} collective-permute-done((bf16[2,2,128,256]{3,2,1,0:T(8,128)(2,1)S(1)}, bf16[2,2,128,256]{3,2,1,0:T(8,128)(2,1)S(1)}, u32[]{:S(2)}, u32[]{:S(2)}) %collective-permute-start.7) | collective-permute-done | bytes 262176 | tf_op jit(solution)/shard_map/ppermute | solution.py:503
  50.0 3.2 %all-to-all-done.1.own_ref = bf16[4,2,128,256]{3,2,1,0:T(8,128)(2,1)S(1)} async-done(((bf16[4,2,128,256]{3,2,1,0:T(8,128)(2,1)}), bf16[4,2,128,256]{3,2,1,0:T(8,128)(2,1)S(1)}, u32[]{:S(2)}, u32[]{:S(2)}) %all-to-all-start.1) | async-done | bytes 524320 | tf_op jit(solution)/shard_map/all_to_all | solution.py:506
  53.2 1.0 %own_surfaces.1.part_ref = f32[2,256,1024]{2,1,0:T(8,128)S(1)} custom-call(s32[1]{0:T(128)} %bitcast.half_ref, bf16[4,2,128,256]{3,2,1,0:T(8,128)(2,1)S(1)} %all-to-all-done.1.own_ref, bf16[1024,1024]{1,0:T(8,128)(2,1)S(1)} %copy-done), custom_call_target="tpu_custom_call" | custom-call | flops 536870912 | bytes 2097152 | tf_op jit(solution)/shard_map/own_surfaces/pallas_call | solution.py:425
  54.2 3.9 %collective-permute-done.5.refs_2_ = bf16[2,128,256]{2,1,0:T(8,128)(2,1)S(1)} collective-permute-done((bf16[2,128,256]{2,1,0:T(8,128)(2,1)}, bf16[2,128,256]{2,1,0:T(8,128)(2,1)S(1)}, u32[]{:S(2)}, u32[]{:S(2)}) %collective-permute-start.5) | collective-permute-done | bytes 131104 | tf_op jit(solution)/shard_map/ppermute | solution.py:503
  58.1 1.5 %collective-permute-done.6.refs_3_ = bf16[2,128,256]{2,1,0:T(8,128)(2,1)S(1)} collective-permute-done((bf16[2,128,256]{2,1,0:T(8,128)(2,1)S(1)}, bf16[2,128,256]{2,1,0:T(8,128)(2,1)S(1)}, u32[]{:S(2)}, u32[]{:S(2)}) %collective-permute-start.6) | collective-permute-done | bytes 131104 | tf_op jit(solution)/shard_map/ppermute | solution.py:503
  59.6 2.0 %surfaces.1 = f32[2,256,1024]{2,1,0:T(8,128)} custom-call(s32[1]{0:T(128)} %bitcast.half_ref, s32[1]{0:T(128)} %bitcast.1.me_ref, s32[1]{0:T(128)S(6)} %copy.8.counts_ref, f32[2,256,1024]{2,1,0:T(8,128)S(1)} %own_surfaces.1.part_ref, bf16[2,2,128,256]{3,2,1,0:T(8,128)(2,1)S(1)} %collective-permute-done.7.refs_0_, ...), custom_call_target="tpu_custom_call" | custom-call | flops 536870912 | bytes 4194304 | tf_op jit(solution)/shard_map/surfaces/pallas_call | solution.py:465
  (23 shorter events, 0.4 us)
Async XLA Ops:
  0.0 7.6 %copy-start = (bf16[1024,1024]{1,0:T(8,128)(2,1)S(1)}, bf16[1024,1024]{1,0:T(8,128)(2,1)}, u32[]{:S(2)}) copy-start(bf16[1024,1024]{1,0:T(8,128)(2,1)} %constant.29.clone.table_hbm.table_ref.refs_4_) | copy-start | bytes 6291460
  0.0 7.6 %copy-start.1 = (f32[2,256,1024]{2,1,0:T(8,128)S(1)}, f32[2,256,1024]{2,1,0:T(8,128)}, u32[]{:S(2)}) copy-start(f32[2,256,1024]{2,1,0:T(8,128)} %tile_ref.1) | copy-start | bytes 6291460
  0.0 7.6 %copy-start.2 = (f32[8,1024]{1,0:T(8,128)S(1)}, f32[8,1024]{1,0:T(8,128)}, u32[]{:S(2)}) copy-start(f32[8,1024]{1,0:T(8,128)} %constant.30.clone.down_hbm.down_ref) | copy-start | bytes 98308
  0.0 7.6 %copy-start.3 = (f32[1,1024]{1,0:T(1,128)S(1)}, f32[1,1024]{1,0:T(1,128)}, u32[]{:S(2)}) copy-start(f32[1,1024]{1,0:T(1,128)} %constant.31.clone.across_hbm.across_ref) | copy-start | bytes 12292
  3.5 18.2 %collective-permute-start = (bf16[2,128,256]{2,1,0:T(8,128)(2,1)}, bf16[2,128,256]{2,1,0:T(8,128)(2,1)S(1)}, u32[]{:S(2)}, u32[]{:S(2)}) collective-permute-start(bf16[2,128,256]{2,1,0:T(8,128)(2,1)} %get-tuple-element.29), channel_id=1, source_target_pairs={{0,8},{1,9},{2,10},{3,11},{4,12},{5,13},{6,14},{7,15},{8,0},{9,1},... | collective-permute-start | bytes 393224 | tf_op jit(solution)/shard_map/ppermute | solution.py:503
  7.6 14.1 %collective-permute-start.1 = (bf16[2,128,256]{2,1,0:T(8,128)(2,1)}, bf16[2,128,256]{2,1,0:T(8,128)(2,1)S(1)}, u32[]{:S(2)}, u32[]{:S(2)}) collective-permute-start(bf16[2,128,256]{2,1,0:T(8,128)(2,1)} %get-tuple-element.30), channel_id=1, source_target_pairs={{0,9},{1,8},{2,11},{3,10},{4,13},{5,12},{6,15},{7,14},{8,1},{9,0},... | collective-permute-start | bytes 393224 | tf_op jit(solution)/shard_map/ppermute | solution.py:503
  7.6 9.6 %copy-start.4 = (s32[1,2,2]{2,1,0:T(2,128)S(1)}, s32[1,2,2]{2,1,0:T(2,128)}, u32[]{:S(2)}) copy-start(s32[1,2,2]{2,1,0:T(2,128)} %pairs_ref) | copy-start | bytes 52
  10.1 12.3 %all-to-all-start = ((bf16[4,2,128,256]{3,2,1,0:T(8,128)(2,1)}), bf16[4,2,128,256]{3,2,1,0:T(8,128)(2,1)S(1)}, u32[]{:S(2)}, u32[]{:S(2)}) async-start(bf16[4,2,128,256]{3,2,1,0:T(8,128)(2,1)} %get-tuple-element.36), calls=%async_computation | async-start | bytes 1048576 | tf_op jit(solution)/shard_map/all_to_all | solution.py:506
  13.5 17.5 %collective-permute-start.3 = (bf16[2,128,256]{2,1,0:T(8,128)(2,1)S(1)}, bf16[2,128,256]{2,1,0:T(8,128)(2,1)S(1)}, u32[]{:S(2)}, u32[]{:S(2)}) collective-permute-start(bf16[2,128,256]{2,1,0:T(8,128)(2,1)S(1)} %get-tuple-element.38), channel_id=1, source_target_pairs={{0,10},{1,11},{2,8},{3,9},{4,14},{5,15},{6,12},{7,13},{8,2},{9,3},... | collective-permute-start | bytes 393224 | tf_op jit(solution)/shard_map/ppermute | solution.py:503
  17.0 14.0 %collective-permute-start.4 = (bf16[2,128,256]{2,1,0:T(8,128)(2,1)S(1)}, bf16[2,128,256]{2,1,0:T(8,128)(2,1)S(1)}, u32[]{:S(2)}, u32[]{:S(2)}) collective-permute-start(bf16[2,128,256]{2,1,0:T(8,128)(2,1)S(1)} %get-tuple-element.39), channel_id=1, source_target_pairs={{0,11},{1,10},{2,9},{3,8},{4,15},{5,14},{6,13},{7,12},{8,3},{9,2},... | collective-permute-start | bytes 393224 | tf_op jit(solution)/shard_map/ppermute | solution.py:503
  17.2 13.8 %collective-permute-start.2 = (s32[1,2,2]{2,1,0:T(2,128)S(1)}, s32[1,2,2]{2,1,0:T(2,128)S(1)}, u32[]{:S(2)}, u32[]{:S(2)}) collective-permute-start(s32[1,2,2]{2,1,0:T(2,128)S(1)} %copy-done.4), channel_id=1, source_target_pairs={{0,8},{1,9},{2,10},{3,11},{4,12},{5,13},{6,14},{7,15},{8,0},{9,1},... | collective-permute-start | bytes 56 | tf_op jit(solution)/shard_map/ppermute | solution.py:503
  19.8 1.0 %copy-start.5 = (f32[128,1024]{1,0:T(8,128)S(1)}, f32[128,1024]{1,0:T(8,128)}, u32[]{:S(2)}) copy-start(f32[128,1024]{1,0:T(8,128)} %constant.32.clone.short_ref) | copy-start | bytes 1572868
  20.9 0.8 %copy-start.6 = (f32[128,1024]{1,0:T(8,128)}, f32[128,1024]{1,0:T(8,128)S(1)}, u32[]{:S(2)}) copy-start(f32[128,1024]{1,0:T(8,128)S(1)} %scaled_tables.1.short_ref) | copy-start | bytes 1572868
  22.3 1.0 %copy-start.7 = (f32[128,1024]{1,0:T(8,128)S(1)}, f32[128,1024]{1,0:T(8,128)}, u32[]{:S(2)}) copy-start(f32[128,1024]{1,0:T(8,128)} %copy-done.6) | copy-start | bytes 1572868
  33.5 15.8 %collective-permute-start.7 = (bf16[2,2,128,256]{3,2,1,0:T(8,128)(2,1)S(1)}, bf16[2,2,128,256]{3,2,1,0:T(8,128)(2,1)S(1)}, u32[]{:S(2)}, u32[]{:S(2)}) collective-permute-start(bf16[2,2,128,256]{3,2,1,0:T(8,128)(2,1)S(1)} %get-tuple-element.50), channel_id=1, source_target_pairs={{0,8},{1,9},{2,10},{3,11},{4,12},{5,13},{6,14},{7,15},{8,0},{9,1},... | collective-permute-start | bytes 786440 | tf_op jit(solution)/shard_map/ppermute | solution.py:503
  39.7 13.5 %all-to-all-start.1 = ((bf16[4,2,128,256]{3,2,1,0:T(8,128)(2,1)}), bf16[4,2,128,256]{3,2,1,0:T(8,128)(2,1)S(1)}, u32[]{:S(2)}, u32[]{:S(2)}) async-start(bf16[4,2,128,256]{3,2,1,0:T(8,128)(2,1)} %get-tuple-element.48), calls=%async_computation.1 | async-start | bytes 1048576 | tf_op jit(solution)/shard_map/all_to_all | solution.py:506
  43.2 14.9 %collective-permute-start.5 = (bf16[2,128,256]{2,1,0:T(8,128)(2,1)}, bf16[2,128,256]{2,1,0:T(8,128)(2,1)S(1)}, u32[]{:S(2)}, u32[]{:S(2)}) collective-permute-start(bf16[2,128,256]{2,1,0:T(8,128)(2,1)} %get-tuple-element.46), channel_id=1, source_target_pairs={{0,10},{1,11},{2,8},{3,9},{4,14},{5,15},{6,12},{7,13},{8,2},{9,3},... | collective-permute-start | bytes 393224 | tf_op jit(solution)/shard_map/ppermute | solution.py:503
  45.0 14.6 %collective-permute-start.6 = (bf16[2,128,256]{2,1,0:T(8,128)(2,1)S(1)}, bf16[2,128,256]{2,1,0:T(8,128)(2,1)S(1)}, u32[]{:S(2)}, u32[]{:S(2)}) collective-permute-start(bf16[2,128,256]{2,1,0:T(8,128)(2,1)S(1)} %get-tuple-element.47), channel_id=1, source_target_pairs={{0,11},{1,10},{2,9},{3,8},{4,15},{5,14},{6,13},{7,12},{8,3},{9,2},... | collective-permute-start | bytes 393224 | tf_op jit(solution)/shard_map/ppermute | solution.py:503
  49.3 10.3 %collective-permute-start.8 = (bf16[2,128,256]{2,1,0:T(8,128)(2,1)S(1)}, bf16[2,128,256]{2,1,0:T(8,128)(2,1)S(1)}, u32[]{:S(2)}, u32[]{:S(2)}) collective-permute-start(bf16[2,128,256]{2,1,0:T(8,128)(2,1)S(1)} %slice_bitcast_fusion), channel_id=1, source_target_pairs={{0,1},{1,0},{2,3},{3,2},{4,5},{5,4},{6,7},{7,6},{8,9},{9,8},{10,11... | collective-permute-start | bytes 393224 | tf_op jit(solution)/shard_map/ppermute | solution.py:509

commit v16 on v15

--- a/solution.py
+++ b/solution.py
@@ -177,7 +177,7 @@
     def body(half_ref, me_ref, tile_ref, down_ref, across_ref, table_ref, *refs):
         out_ref, far, work = refs[0], refs[1:-1], refs[-1]
         half, me = half_ref[0], me_ref[0]
-        shaded = shade(tile_ref[0], down_ref, across_ref)
+        shaded = shade(tile_ref[pl.program_id(0)], down_ref, across_ref)
         for j in range(1, peers // 2):
             start = pl.multiple_of((1 - half) * span + (me // 2 ^ j) * 2 * block, 2 * block)
             work[...] = times_table(table_ref[pl.ds(start, 2 * block), :], shaded)
@@ -195,10 +195,10 @@
             num_scalar_prefetch=2,
             grid=(count,),
             in_specs=[
-                pl.BlockSpec((1, rows, width), lambda t, half, me: (t, 0, 0)),
+                pl.BlockSpec(memory_space=pltpu.VMEM),
                 pl.BlockSpec((8, rows), lambda t, half, me: (0, me[0])),
                 pl.BlockSpec((1, width), lambda t, half, me: (0, 0)),
-                pl.BlockSpec((width, width), lambda t, half, me: (0, 0)),
+                pl.BlockSpec(memory_space=pltpu.VMEM),
             ],
             out_specs=[
                 pl.BlockSpec((peers, 1, block, rows), lambda t, half, me: (0, t, 0, 0)),
@@ -453,11 +453,15 @@
             place = pl.multiple_of((me_ref[0] ^ k) * double, double)
             piece = other_refs[k][0] if k else other_refs[k][0, 0]
             work[pl.ds(place, double), :] = piece
+        start = pl.multiple_of((1 - half_ref[0]) * span, span)
         rest = lax.dot_general(
-            work[...], table_ref[...], (((0,), (0,)), ((), ())), preferred_element_type=jnp.float32
+            work[...],
+            table_ref[pl.ds(start, span), :],
+            (((0,), (0,)), ((), ())),
+            preferred_element_type=jnp.float32,
         )
         live = pl.program_id(0) < counts_ref[0]
-        out_ref[0] = jnp.where(live, part_ref[0] + rest, 0.0)
+        out_ref[0] = jnp.where(live, part_ref[pl.program_id(0)] + rest, 0.0)
 
     pair = pl.BlockSpec((1, 1, double, rows), lambda p, half, me, counts: (0, p, 0, 0))
     piece = pl.BlockSpec((1, double, rows), lambda p, half, me, counts: (p, 0, 0))
@@ -468,10 +472,10 @@
             num_scalar_prefetch=3,
             grid=(slots,),
             in_specs=[
-                plane,
+                pl.BlockSpec(memory_space=pltpu.VMEM),
                 pair,
                 *[piece] * (peers - 1),
-                pl.BlockSpec((span, width), lambda p, half, me, counts: (1 - half[0], 0)),
+                pl.BlockSpec(memory_space=pltpu.VMEM),
             ],
             out_specs=plane,
             scratch_shapes=[pltpu.VMEM((span, rows), jnp.bfloat16)],

time: 61.9 us -> 61.9 us (level)
  no operation moved by 1% of the time
where the time goes in v16:
time: 61.9 us; the launch traced here: 61.6 us
  starting transfers between devices  23.7 us (38%)
  Pallas kernels  17.1 us (28%)
  waiting for transfers between devices  17.1 us (28%)
  local copies, waits for them, and re-layouts  2.91 us (5%)
  between operations  0.76 us (1%)
    ppermute x8, starting transfers between devices, across(): return lax.ppermute(value, axes, moves)  16.6 us
    ppermute x8, waiting for transfers between devices, across(): return lax.ppermute(value, axes, moves)  13.3 us
    all_to_all x2, starting transfers between devices, along(): return lax.all_to_all(blocks, 'rows', split_axis=0, concat_axis=0)  6.94 us
    all_to_all x2, waiting for transfers between devices, along(): return lax.all_to_all(blocks, 'rows', split_axis=0, concat_axis=0)  3.84 us
    pallas_call x1, Pallas kernels, own_slots(): pl.pallas_call(body, in_specs=[pl.BlockSpec(memory_space=pltpu.SMEM)] * 3...  3.58 us
    pallas_call x1, Pallas kernels, near_columns(): pl.pallas_call(body, grid_spec=pltpu.PrefetchScalarGridSpec(num_scalar_pr...  3.44 us
    unnamed x16, local copies, waits for them, and re-layouts  2.9 us
    pallas_call x1, Pallas kernels, partner_slots(): pl.pallas_call(body, in_specs=[pl.BlockSpec(memory_space=pltpu.SMEM)] * 3...  2.53 us
  transfers between devices with their start and end apart: 11, of which 6 were waited for; matrix products, arithmetic and copies ran while one was open for 0% of the time, Pallas kernels for 15%

profile of v16, /device:TPU:0, one launch (start us, length us, event | category | flops | bytes accessed | tf_op | source)
XLA Modules:
  0.0 61.6 jit_solution(3480252076475490431)
XLA Ops:
  0.0 3.4 %near_columns.1 = (bf16[2,128,256]{2,1,0:T(8,128)(2,1)}, bf16[2,128,256]{2,1,0:T(8,128)(2,1)}) custom-call(s32[1]{0:T(128)} %bitcast.half_ref, s32[1]{0:T(128)} %bitcast.1.me_ref, f32[2,256,1024]{2,1,0:T(8,128)} %tile_ref.1, f32[8,1024]{1,0:T(8,128)} %constant.30.clone.down_hbm.down_ref, f32[1,1024]{1,0:T(1,128)} %constant.31.clone.across_hbm.across_ref, ...), custom_call_target="tpu_custom_call" | custom-call | flops 268435456 | bytes 2621440 | tf_op jit(solution)/shard_map/near_columns/pallas_call | solution.py:144
  3.5 4.1 %collective-permute-start = (bf16[2,128,256]{2,1,0:T(8,128)(2,1)}, bf16[2,128,256]{2,1,0:T(8,128)(2,1)S(1)}, u32[]{:S(2)}, u32[]{:S(2)}) collective-permute-start(bf16[2,128,256]{2,1,0:T(8,128)(2,1)} %get-tuple-element.29), channel_id=1, source_target_pairs={{0,8},{1,9},{2,10},{3,11},{4,12},{5,13},{6,14},{7,15},{8,0},{9,1},... | collective-permute-start | bytes 393224 | tf_op jit(solution)/shard_map/ppermute | solution.py:507
  7.6 2.4 %rest_columns.1 = (bf16[4,2,128,256]{3,2,1,0:T(8,128)(2,1)}, bf16[2,128,256]{2,1,0:T(8,128)(2,1)S(1)}, bf16[2,128,256]{2,1,0:T(8,128)(2,1)S(1)}) custom-call(s32[1]{0:T(128)} %bitcast.2.half_ref, s32[1]{0:T(128)} %bitcast.1.me_ref, f32[2,256,1024]{2,1,0:T(8,128)S(1)} %copy-done.1, f32[8,1024]{1,0:T(8,128)S(1)} %copy-done.2, f32[1,1024]{1,0:T(1,128)S(1)} %copy-done.3, ...), custom_call_target="tpu_custom_call" | custom-call | flops 805306368 | bytes 4194304 | tf_op jit(solution)/shard_map/rest_columns/pallas_call | solution.py:192
  10.1 3.5 %all-to-all-start = ((bf16[4,2,128,256]{3,2,1,0:T(8,128)(2,1)}), bf16[4,2,128,256]{3,2,1,0:T(8,128)(2,1)S(1)}, u32[]{:S(2)}, u32[]{:S(2)}) async-start(bf16[4,2,128,256]{3,2,1,0:T(8,128)(2,1)} %get-tuple-element.36), calls=%async_computation | async-start | bytes 1048576 | tf_op jit(solution)/shard_map/all_to_all | solution.py:510
  13.5 3.5 %collective-permute-start.3 = (bf16[2,128,256]{2,1,0:T(8,128)(2,1)S(1)}, bf16[2,128,256]{2,1,0:T(8,128)(2,1)S(1)}, u32[]{:S(2)}, u32[]{:S(2)}) collective-permute-start(bf16[2,128,256]{2,1,0:T(8,128)(2,1)S(1)} %get-tuple-element.38), channel_id=1, source_target_pairs={{0,10},{1,11},{2,8},{3,9},{4,14},{5,15},{6,12},{7,13},{8,2},{9,3},... | collective-permute-start | bytes 393224 | tf_op jit(solution)/shard_map/ppermute | solution.py:507
  17.2 2.5 %collective-permute-start.2 = (s32[1,2,2]{2,1,0:T(2,128)S(1)}, s32[1,2,2]{2,1,0:T(2,128)S(1)}, u32[]{:S(2)}, u32[]{:S(2)}) collective-permute-start(s32[1,2,2]{2,1,0:T(2,128)S(1)} %copy-done.4), channel_id=1, source_target_pairs={{0,8},{1,9},{2,10},{3,11},{4,12},{5,13},{6,14},{7,15},{8,0},{9,1},... | collective-permute-start | bytes 56 | tf_op jit(solution)/shard_map/ppermute | solution.py:507
  19.8 1.0 %copy-done.5 = f32[128,1024]{1,0:T(8,128)S(1)} copy-done((f32[128,1024]{1,0:T(8,128)S(1)}, f32[128,1024]{1,0:T(8,128)}, u32[]{:S(2)}) %copy-start.5) | copy-done | bytes 524312
  20.9 0.8 %copy-done.6 = f32[128,1024]{1,0:T(8,128)} copy-done((f32[128,1024]{1,0:T(8,128)}, f32[128,1024]{1,0:T(8,128)S(1)}, u32[]{:S(2)}) %copy-start.6) | copy-done | bytes 524312
  21.7 0.7 %all-to-all-done.pieces_ref = bf16[4,2,128,256]{3,2,1,0:T(8,128)(2,1)S(1)} async-done(((bf16[4,2,128,256]{3,2,1,0:T(8,128)(2,1)}), bf16[4,2,128,256]{3,2,1,0:T(8,128)(2,1)S(1)}, u32[]{:S(2)}, u32[]{:S(2)}) %all-to-all-start) | async-done | bytes 524320 | tf_op jit(solution)/shard_map/all_to_all | solution.py:510
  22.3 1.0 %copy-done.7 = f32[128,1024]{1,0:T(8,128)S(1)} copy-done((f32[128,1024]{1,0:T(8,128)S(1)}, f32[128,1024]{1,0:T(8,128)}, u32[]{:S(2)}) %copy-start.7) | copy-done | bytes 524312
  23.4 2.2 %own_spectra.1 = (bf16[2,2,64,1024]{3,2,1,0:T(8,128)(2,1)S(1)}, bf16[2,2,16,1024]{3,2,1,0:T(8,128)(2,1)S(1)}, f32[256,2048]{1,0:T(8,128)S(1)}, bf16[1024,2048]{1,0:T(8,128)(2,1)S(1)}) custom-call(s32[1]{0:T(128)} %bitcast.half_ref, s32[1]{0:T(128)} %bitcast.1.me_ref, bf16[4,2,128,256]{3,2,1,0:T(8,128)(2,1)S(1)} %all-to-all-done.pieces_ref, ...), custom_call_target="tpu_custom_call" | custom-call | flops 1610612736 | bytes 8388608 | tf_op jit(solution)/shard_map/own_spectra/pallas_call | solution.py:325
  25.5 5.4 %collective-permute-done.2.theirs_ref = s32[1,2,2]{2,1,0:T(2,128)S(1)} collective-permute-done((s32[1,2,2]{2,1,0:T(2,128)S(1)}, s32[1,2,2]{2,1,0:T(2,128)S(1)}, u32[]{:S(2)}, u32[]{:S(2)}) %collective-permute-start.2) | collective-permute-done | bytes 48 | tf_op jit(solution)/shard_map/ppermute | solution.py:507
  31.0 2.5 %partner_slots.1 = (bf16[2,2,128,256]{3,2,1,0:T(8,128)(2,1)S(1)}, bf16[4,2,64,1024]{3,2,1,0:T(8,128)(2,1)S(1)}, bf16[4,2,16,1024]{3,2,1,0:T(8,128)(2,1)S(1)}, bf16[4,64,1024]{2,1,0:T(8,128)(2,1)S(1)}) custom-call(s32[1]{0:T(128)} %bitcast.half_ref, s32[1]{0:T(128)} %bitcast.1.me_ref, s32[1,2,2]{2,1,0:T(2,128)S(1)} %collective-permute-done.2.theirs_ref, ...), custom_call_target="tpu_custom_call" | custom-call | flops 2147483648 | bytes 8388608 | tf_op jit(solution)/shard_map/partner_slots/pallas_call | solution.py:364
  33.5 2.6 %collective-permute-start.7 = (bf16[2,2,128,256]{3,2,1,0:T(8,128)(2,1)S(1)}, bf16[2,2,128,256]{3,2,1,0:T(8,128)(2,1)S(1)}, u32[]{:S(2)}, u32[]{:S(2)}) collective-permute-start(bf16[2,2,128,256]{3,2,1,0:T(8,128)(2,1)S(1)} %get-tuple-element.50), channel_id=1, source_target_pairs={{0,8},{1,9},{2,10},{3,11},{4,12},{5,13},{6,14},{7,15},{8,0},{9,1},... | collective-permute-start | bytes 786440 | tf_op jit(solution)/shard_map/ppermute | solution.py:507
  36.2 3.6 %own_slots.1 = (bf16[4,2,128,256]{3,2,1,0:T(8,128)(2,1)}, bf16[2,128,256]{2,1,0:T(8,128)(2,1)}, bf16[2,128,256]{2,1,0:T(8,128)(2,1)S(1)}) custom-call(s32[1]{0:T(128)} %bitcast.half_ref, s32[1]{0:T(128)} %bitcast.1.me_ref, s32[1,2,2]{2,1,0:T(2,128)S(1)} %copy-done.4, bf16[1024,2048]{1,0:T(8,128)(2,1)S(1)} %get-tuple-element.37.refs_3_.table_ref, ...), custom_call_target="tpu_custom_call" | custom-call | flops 1073741824 | bytes 8388608 | tf_op jit(solution)/shard_map/own_slots/pallas_call | solution.py:396
  39.7 3.5 %all-to-all-start.1 = ((bf16[4,2,128,256]{3,2,1,0:T(8,128)(2,1)}), bf16[4,2,128,256]{3,2,1,0:T(8,128)(2,1)S(1)}, u32[]{:S(2)}, u32[]{:S(2)}) async-start(bf16[4,2,128,256]{3,2,1,0:T(8,128)(2,1)} %get-tuple-element.48), calls=%async_computation.1 | async-start | bytes 1048576 | tf_op jit(solution)/shard_map/all_to_all | solution.py:510
  43.2 1.8 %collective-permute-start.5 = (bf16[2,128,256]{2,1,0:T(8,128)(2,1)}, bf16[2,128,256]{2,1,0:T(8,128)(2,1)S(1)}, u32[]{:S(2)}, u32[]{:S(2)}) collective-permute-start(bf16[2,128,256]{2,1,0:T(8,128)(2,1)} %get-tuple-element.46), channel_id=1, source_target_pairs={{0,10},{1,11},{2,8},{3,9},{4,14},{5,15},{6,12},{7,13},{8,2},{9,3},... | collective-permute-start | bytes 393224 | tf_op jit(solution)/shard_map/ppermute | solution.py:507
  45.0 1.9 %collective-permute-start.6 = (bf16[2,128,256]{2,1,0:T(8,128)(2,1)S(1)}, bf16[2,128,256]{2,1,0:T(8,128)(2,1)S(1)}, u32[]{:S(2)}, u32[]{:S(2)}) collective-permute-start(bf16[2,128,256]{2,1,0:T(8,128)(2,1)S(1)} %get-tuple-element.47), channel_id=1, source_target_pairs={{0,11},{1,10},{2,9},{3,8},{4,15},{5,14},{6,13},{7,12},{8,3},{9,2},... | collective-permute-start | bytes 393224 | tf_op jit(solution)/shard_map/ppermute | solution.py:507
  46.9 2.4 %collective-permute-done.7.refs_0_ = bf16[2,2,128,256]{3,2,1,0:T(8,128)(2,1)S(1)} collective-permute-done((bf16[2,2,128,256]{3,2,1,0:T(8,128)(2,1)S(1)}, bf16[2,2,128,256]{3,2,1,0:T(8,128)(2,1)S(1)}, u32[]{:S(2)}, u32[]{:S(2)}) %collective-permute-start.7) | collective-permute-done | bytes 262176 | tf_op jit(solution)/shard_map/ppermute | solution.py:507
  50.0 3.2 %all-to-all-done.1.own_ref = bf16[4,2,128,256]{3,2,1,0:T(8,128)(2,1)S(1)} async-done(((bf16[4,2,128,256]{3,2,1,0:T(8,128)(2,1)}), bf16[4,2,128,256]{3,2,1,0:T(8,128)(2,1)S(1)}, u32[]{:S(2)}, u32[]{:S(2)}) %all-to-all-start.1) | async-done | bytes 524320 | tf_op jit(solution)/shard_map/all_to_all | solution.py:510
  53.2 1.0 %own_surfaces.1.part_ref = f32[2,256,1024]{2,1,0:T(8,128)S(1)} custom-call(s32[1]{0:T(128)} %bitcast.half_ref, bf16[4,2,128,256]{3,2,1,0:T(8,128)(2,1)S(1)} %all-to-all-done.1.own_ref, bf16[1024,1024]{1,0:T(8,128)(2,1)S(1)} %copy-done), custom_call_target="tpu_custom_call" | custom-call | flops 536870912 | bytes 2097152 | tf_op jit(solution)/shard_map/own_surfaces/pallas_call | solution.py:425
  54.2 3.9 %collective-permute-done.5.refs_2_ = bf16[2,128,256]{2,1,0:T(8,128)(2,1)S(1)} collective-permute-done((bf16[2,128,256]{2,1,0:T(8,128)(2,1)}, bf16[2,128,256]{2,1,0:T(8,128)(2,1)S(1)}, u32[]{:S(2)}, u32[]{:S(2)}) %collective-permute-start.5) | collective-permute-done | bytes 131104 | tf_op jit(solution)/shard_map/ppermute | solution.py:507
  58.1 1.5 %collective-permute-done.6.refs_3_ = bf16[2,128,256]{2,1,0:T(8,128)(2,1)S(1)} collective-permute-done((bf16[2,128,256]{2,1,0:T(8,128)(2,1)S(1)}, bf16[2,128,256]{2,1,0:T(8,128)(2,1)S(1)}, u32[]{:S(2)}, u32[]{:S(2)}) %collective-permute-start.6) | collective-permute-done | bytes 131104 | tf_op jit(solution)/shard_map/ppermute | solution.py:507
  59.6 2.0 %surfaces.1 = f32[2,256,1024]{2,1,0:T(8,128)} custom-call(s32[1]{0:T(128)} %bitcast.half_ref, s32[1]{0:T(128)} %bitcast.1.me_ref, s32[1]{0:T(128)S(6)} %copy.8.counts_ref, f32[2,256,1024]{2,1,0:T(8,128)S(1)} %own_surfaces.1.part_ref, bf16[2,2,128,256]{3,2,1,0:T(8,128)(2,1)S(1)} %collective-permute-done.7.refs_0_, ...), custom_call_target="tpu_custom_call" | custom-call | flops 536870912 | bytes 4194304 | tf_op jit(solution)/shard_map/surfaces/pallas_call | solution.py:469
  (23 shorter events, 0.4 us)
Async XLA Ops:
  0.0 7.6 %copy-start = (bf16[1024,1024]{1,0:T(8,128)(2,1)S(1)}, bf16[1024,1024]{1,0:T(8,128)(2,1)}, u32[]{:S(2)}) copy-start(bf16[1024,1024]{1,0:T(8,128)(2,1)} %constant.29.clone.table_hbm.table_ref.refs_4_) | copy-start | bytes 6291460
  0.0 7.6 %copy-start.1 = (f32[2,256,1024]{2,1,0:T(8,128)S(1)}, f32[2,256,1024]{2,1,0:T(8,128)}, u32[]{:S(2)}) copy-start(f32[2,256,1024]{2,1,0:T(8,128)} %tile_ref.1) | copy-start | bytes 6291460
  0.0 7.6 %copy-start.2 = (f32[8,1024]{1,0:T(8,128)S(1)}, f32[8,1024]{1,0:T(8,128)}, u32[]{:S(2)}) copy-start(f32[8,1024]{1,0:T(8,128)} %constant.30.clone.down_hbm.down_ref) | copy-start | bytes 98308
  0.0 7.6 %copy-start.3 = (f32[1,1024]{1,0:T(1,128)S(1)}, f32[1,1024]{1,0:T(1,128)}, u32[]{:S(2)}) copy-start(f32[1,1024]{1,0:T(1,128)} %constant.31.clone.across_hbm.across_ref) | copy-start | bytes 12292
  3.5 18.2 %collective-permute-start = (bf16[2,128,256]{2,1,0:T(8,128)(2,1)}, bf16[2,128,256]{2,1,0:T(8,128)(2,1)S(1)}, u32[]{:S(2)}, u32[]{:S(2)}) collective-permute-start(bf16[2,128,256]{2,1,0:T(8,128)(2,1)} %get-tuple-element.29), channel_id=1, source_target_pairs={{0,8},{1,9},{2,10},{3,11},{4,12},{5,13},{6,14},{7,15},{8,0},{9,1},... | collective-permute-start | bytes 393224 | tf_op jit(solution)/shard_map/ppermute | solution.py:507
  7.6 14.1 %collective-permute-start.1 = (bf16[2,128,256]{2,1,0:T(8,128)(2,1)}, bf16[2,128,256]{2,1,0:T(8,128)(2,1)S(1)}, u32[]{:S(2)}, u32[]{:S(2)}) collective-permute-start(bf16[2,128,256]{2,1,0:T(8,128)(2,1)} %get-tuple-element.30), channel_id=1, source_target_pairs={{0,9},{1,8},{2,11},{3,10},{4,13},{5,12},{6,15},{7,14},{8,1},{9,0},... | collective-permute-start | bytes 393224 | tf_op jit(solution)/shard_map/ppermute | solution.py:507
  7.6 9.6 %copy-start.4 = (s32[1,2,2]{2,1,0:T(2,128)S(1)}, s32[1,2,2]{2,1,0:T(2,128)}, u32[]{:S(2)}) copy-start(s32[1,2,2]{2,1,0:T(2,128)} %pairs_ref) | copy-start | bytes 52
  10.1 12.3 %all-to-all-start = ((bf16[4,2,128,256]{3,2,1,0:T(8,128)(2,1)}), bf16[4,2,128,256]{3,2,1,0:T(8,128)(2,1)S(1)}, u32[]{:S(2)}, u32[]{:S(2)}) async-start(bf16[4,2,128,256]{3,2,1,0:T(8,128)(2,1)} %get-tuple-element.36), calls=%async_computation | async-start | bytes 1048576 | tf_op jit(solution)/shard_map/all_to_all | solution.py:510
  13.5 17.5 %collective-permute-start.3 = (bf16[2,128,256]{2,1,0:T(8,128)(2,1)S(1)}, bf16[2,128,256]{2,1,0:T(8,128)(2,1)S(1)}, u32[]{:S(2)}, u32[]{:S(2)}) collective-permute-start(bf16[2,128,256]{2,1,0:T(8,128)(2,1)S(1)} %get-tuple-element.38), channel_id=1, source_target_pairs={{0,10},{1,11},{2,8},{3,9},{4,14},{5,15},{6,12},{7,13},{8,2},{9,3},... | collective-permute-start | bytes 393224 | tf_op jit(solution)/shard_map/ppermute | solution.py:507
  17.0 14.0 %collective-permute-start.4 = (bf16[2,128,256]{2,1,0:T(8,128)(2,1)S(1)}, bf16[2,128,256]{2,1,0:T(8,128)(2,1)S(1)}, u32[]{:S(2)}, u32[]{:S(2)}) collective-permute-start(bf16[2,128,256]{2,1,0:T(8,128)(2,1)S(1)} %get-tuple-element.39), channel_id=1, source_target_pairs={{0,11},{1,10},{2,9},{3,8},{4,15},{5,14},{6,13},{7,12},{8,3},{9,2},... | collective-permute-start | bytes 393224 | tf_op jit(solution)/shard_map/ppermute | solution.py:507
  17.2 13.8 %collective-permute-start.2 = (s32[1,2,2]{2,1,0:T(2,128)S(1)}, s32[1,2,2]{2,1,0:T(2,128)S(1)}, u32[]{:S(2)}, u32[]{:S(2)}) collective-permute-start(s32[1,2,2]{2,1,0:T(2,128)S(1)} %copy-done.4), channel_id=1, source_target_pairs={{0,8},{1,9},{2,10},{3,11},{4,12},{5,13},{6,14},{7,15},{8,0},{9,1},... | collective-permute-start | bytes 56 | tf_op jit(solution)/shard_map/ppermute | solution.py:507
  19.8 1.0 %copy-start.5 = (f32[128,1024]{1,0:T(8,128)S(1)}, f32[128,1024]{1,0:T(8,128)}, u32[]{:S(2)}) copy-start(f32[128,1024]{1,0:T(8,128)} %constant.32.clone.short_ref) | copy-start | bytes 1572868
  20.9 0.8 %copy-start.6 = (f32[128,1024]{1,0:T(8,128)}, f32[128,1024]{1,0:T(8,128)S(1)}, u32[]{:S(2)}) copy-start(f32[128,1024]{1,0:T(8,128)S(1)} %scaled_tables.1.short_ref) | copy-start | bytes 1572868
  22.3 1.0 %copy-start.7 = (f32[128,1024]{1,0:T(8,128)S(1)}, f32[128,1024]{1,0:T(8,128)}, u32[]{:S(2)}) copy-start(f32[128,1024]{1,0:T(8,128)} %copy-done.6) | copy-start | bytes 1572868
  33.5 15.8 %collective-permute-start.7 = (bf16[2,2,128,256]{3,2,1,0:T(8,128)(2,1)S(1)}, bf16[2,2,128,256]{3,2,1,0:T(8,128)(2,1)S(1)}, u32[]{:S(2)}, u32[]{:S(2)}) collective-permute-start(bf16[2,2,128,256]{3,2,1,0:T(8,128)(2,1)S(1)} %get-tuple-element.50), channel_id=1, source_target_pairs={{0,8},{1,9},{2,10},{3,11},{4,12},{5,13},{6,14},{7,15},{8,0},{9,1},... | collective-permute-start | bytes 786440 | tf_op jit(solution)/shard_map/ppermute | solution.py:507
  39.7 13.5 %all-to-all-start.1 = ((bf16[4,2,128,256]{3,2,1,0:T(8,128)(2,1)}), bf16[4,2,128,256]{3,2,1,0:T(8,128)(2,1)S(1)}, u32[]{:S(2)}, u32[]{:S(2)}) async-start(bf16[4,2,128,256]{3,2,1,0:T(8,128)(2,1)} %get-tuple-element.48), calls=%async_computation.1 | async-start | bytes 1048576 | tf_op jit(solution)/shard_map/all_to_all | solution.py:510
  43.2 14.9 %collective-permute-start.5 = (bf16[2,128,256]{2,1,0:T(8,128)(2,1)}, bf16[2,128,256]{2,1,0:T(8,128)(2,1)S(1)}, u32[]{:S(2)}, u32[]{:S(2)}) collective-permute-start(bf16[2,128,256]{2,1,0:T(8,128)(2,1)} %get-tuple-element.46), channel_id=1, source_target_pairs={{0,10},{1,11},{2,8},{3,9},{4,14},{5,15},{6,12},{7,13},{8,2},{9,3},... | collective-permute-start | bytes 393224 | tf_op jit(solution)/shard_map/ppermute | solution.py:507
  45.0 14.6 %collective-permute-start.6 = (bf16[2,128,256]{2,1,0:T(8,128)(2,1)S(1)}, bf16[2,128,256]{2,1,0:T(8,128)(2,1)S(1)}, u32[]{:S(2)}, u32[]{:S(2)}) collective-permute-start(bf16[2,128,256]{2,1,0:T(8,128)(2,1)S(1)} %get-tuple-element.47), channel_id=1, source_target_pairs={{0,11},{1,10},{2,9},{3,8},{4,15},{5,14},{6,13},{7,12},{8,3},{9,2},... | collective-permute-start | bytes 393224 | tf_op jit(solution)/shard_map/ppermute | solution.py:507
  49.3 10.3 %collective-permute-start.8 = (bf16[2,128,256]{2,1,0:T(8,128)(2,1)S(1)}, bf16[2,128,256]{2,1,0:T(8,128)(2,1)S(1)}, u32[]{:S(2)}, u32[]{:S(2)}) collective-permute-start(bf16[2,128,256]{2,1,0:T(8,128)(2,1)S(1)} %slice_bitcast_fusion), channel_id=1, source_target_pairs={{0,1},{1,0},{2,3},{3,2},{4,5},{5,4},{6,7},{7,6},{8,9},{9,8},{10,11... | collective-permute-start | bytes 393224 | tf_op jit(solution)/shard_map/ppermute | solution.py:513

commit v17 on v16

--- a/solution.py
+++ b/solution.py
@@ -521,14 +521,13 @@
     *sent, held = lax.optimization_barrier((*sent, half))
     kept, *sent = rest_columns(tiles, down, sideways, table_w, held, me, peers)
     *sent, kept, pairs = lax.optimization_barrier((*sent, kept, pairs))
+    mine = along(kept)
+    *sent, short = lax.optimization_barrier((*sent, scaled_tables(height, [])))
     arrived += [across(sent[k - 2], k) for k in range(2, peers)]
-    mine = along(kept)
 
     theirs = across(pairs, 0)
     place = (scalar(half), scalar(me))
-    spectra, edge, share, table_h = own_spectra(
-        place, mine, arrived[:2], scaled_tables(height, [])
-    )
+    spectra, edge, share, table_h = own_spectra(place, mine, arrived[:2], short)
     near, spectra, edge, phases = partner_slots(
         place, theirs, arrived[2:], share, table_h, spectra, edge
     )

time: 61.9 us -> 64.5 us (1.042)
  waiting for transfers between devices: 17.1 us -> 19 us
  local copies, waits for them, and re-layouts: 2.91 us -> 4.47 us
  starting transfers between devices: 23.7 us -> 22.8 us
    ppermute x8, waiting for transfers between devices: 13.3 us -> 15.5 us  [across(): return lax.ppermute(value, axes, moves)]
    unnamed x16 -> x20, local copies, waits for them, and re-layouts: 2.9 us -> 4.46 us
    ppermute x8, starting transfers between devices: 16.6 us -> 15.8 us  [across(): return lax.ppermute(value, axes, moves)]
  transfers between devices with their start and end apart: 11 -> 11, of which waited for: 6 -> 6; matrix products, arithmetic and copies ran while one was open for 0% -> 0% of each run, Pallas kernels for 15% -> 14%
where the time goes in v17:
time: 64.5 us; the launch traced here: 64.1 us
  starting transfers between devices  22.8 us (35%)
  waiting for transfers between devices  19 us (29%)
  Pallas kernels  17.1 us (27%)
  local copies, waits for them, and re-layouts  4.47 us (7%)
  between operations  0.76 us (1%)
    ppermute x8, starting transfers between devices, across(): return lax.ppermute(value, axes, moves)  15.8 us
    ppermute x8, waiting for transfers between devices, across(): return lax.ppermute(value, axes, moves)  15.5 us
    all_to_all x2, starting transfers between devices, along(): return lax.all_to_all(blocks, 'rows', split_axis=0, concat_axis=0)  6.94 us
    unnamed x20, local copies, waits for them, and re-layouts  4.46 us
    pallas_call x1, Pallas kernels, own_slots(): pl.pallas_call(body, in_specs=[pl.BlockSpec(memory_space=pltpu.SMEM)] * 3...  3.58 us
    all_to_all x2, waiting for transfers between devices, along(): return lax.all_to_all(blocks, 'rows', split_axis=0, concat_axis=0)  3.48 us
    pallas_call x1, Pallas kernels, near_columns(): pl.pallas_call(body, grid_spec=pltpu.PrefetchScalarGridSpec(num_scalar_pr...  3.46 us
    pallas_call x1, Pallas kernels, partner_slots(): pl.pallas_call(body, in_specs=[pl.BlockSpec(memory_space=pltpu.SMEM)] * 3...  2.52 us
  transfers between devices with their start and end apart: 11, of which 6 were waited for; matrix products, arithmetic and copies ran while one was open for 0% of the time, Pallas kernels for 14%

profile of v17, /device:TPU:0, one launch (start us, length us, event | category | flops | bytes accessed | tf_op | source)
XLA Modules:
  0.0 64.1 jit_solution(3017839003479457979)
XLA Ops:
  0.0 3.5 %near_columns.1 = (bf16[2,128,256]{2,1,0:T(8,128)(2,1)}, bf16[2,128,256]{2,1,0:T(8,128)(2,1)}) custom-call(s32[1]{0:T(128)} %bitcast.half_ref, s32[1]{0:T(128)} %bitcast.1.me_ref, f32[2,256,1024]{2,1,0:T(8,128)} %tile_ref.1, f32[8,1024]{1,0:T(8,128)} %constant.30.clone.down_hbm.down_ref, f32[1,1024]{1,0:T(1,128)} %constant.31.clone.across_hbm.across_ref, ...), custom_call_target="tpu_custom_call" | custom-call | flops 268435456 | bytes 2621440 | tf_op jit(solution)/shard_map/near_columns/pallas_call | solution.py:144
  3.5 4.1 %collective-permute-start = (bf16[2,128,256]{2,1,0:T(8,128)(2,1)}, bf16[2,128,256]{2,1,0:T(8,128)(2,1)S(1)}, u32[]{:S(2)}, u32[]{:S(2)}) collective-permute-start(bf16[2,128,256]{2,1,0:T(8,128)(2,1)} %get-tuple-element.32), channel_id=1, source_target_pairs={{0,8},{1,9},{2,10},{3,11},{4,12},{5,13},{6,14},{7,15},{8,0},{9,1},... | collective-permute-start | bytes 393224 | tf_op jit(solution)/shard_map/ppermute | solution.py:507
  7.6 2.4 %rest_columns.1 = (bf16[4,2,128,256]{3,2,1,0:T(8,128)(2,1)}, bf16[2,128,256]{2,1,0:T(8,128)(2,1)S(1)}, bf16[2,128,256]{2,1,0:T(8,128)(2,1)S(1)}) custom-call(s32[1]{0:T(128)} %bitcast.2.half_ref, s32[1]{0:T(128)} %bitcast.1.me_ref, f32[2,256,1024]{2,1,0:T(8,128)S(1)} %copy-done.1, f32[8,1024]{1,0:T(8,128)S(1)} %copy-done.2, f32[1,1024]{1,0:T(1,128)S(1)} %copy-done.3, ...), custom_call_target="tpu_custom_call" | custom-call | flops 805306368 | bytes 4194304 | tf_op jit(solution)/shard_map/rest_columns/pallas_call | solution.py:192
  10.1 3.5 %all-to-all-start = ((bf16[4,2,128,256]{3,2,1,0:T(8,128)(2,1)}), bf16[4,2,128,256]{3,2,1,0:T(8,128)(2,1)S(1)}, u32[]{:S(2)}, u32[]{:S(2)}) async-start(bf16[4,2,128,256]{3,2,1,0:T(8,128)(2,1)} %get-tuple-element.39), calls=%async_computation | async-start | bytes 1048576 | tf_op jit(solution)/shard_map/all_to_all | solution.py:510
  13.5 1.0 %copy-done.7 = f32[128,1024]{1,0:T(8,128)S(1)} copy-done((f32[128,1024]{1,0:T(8,128)S(1)}, f32[128,1024]{1,0:T(8,128)}, u32[]{:S(2)}) %copy-start.7) | copy-done | bytes 524312
  15.4 3.5 %collective-permute-start.3 = (bf16[2,128,256]{2,1,0:T(8,128)(2,1)S(1)}, bf16[2,128,256]{2,1,0:T(8,128)(2,1)S(1)}, u32[]{:S(2)}, u32[]{:S(2)}) collective-permute-start(bf16[2,128,256]{2,1,0:T(8,128)(2,1)S(1)} %get-tuple-element.44), channel_id=1, source_target_pairs={{0,10},{1,11},{2,8},{3,9},{4,14},{5,15},{6,12},{7,13},{8,2},{9,3},... | collective-permute-start | bytes 393224 | tf_op jit(solution)/shard_map/ppermute | solution.py:507
  19.0 2.6 %collective-permute-start.2 = (s32[1,2,2]{2,1,0:T(2,128)S(1)}, s32[1,2,2]{2,1,0:T(2,128)S(1)}, u32[]{:S(2)}, u32[]{:S(2)}) collective-permute-start(s32[1,2,2]{2,1,0:T(2,128)S(1)} %copy-done.4), channel_id=1, source_target_pairs={{0,8},{1,9},{2,10},{3,11},{4,12},{5,13},{6,14},{7,15},{8,0},{9,1},... | collective-permute-start | bytes 56 | tf_op jit(solution)/shard_map/ppermute | solution.py:507
  21.6 1.4 %all-to-all-done.pieces_ref = bf16[4,2,128,256]{3,2,1,0:T(8,128)(2,1)S(1)} async-done(((bf16[4,2,128,256]{3,2,1,0:T(8,128)(2,1)}), bf16[4,2,128,256]{3,2,1,0:T(8,128)(2,1)S(1)}, u32[]{:S(2)}, u32[]{:S(2)}) %all-to-all-start) | async-done | bytes 524320 | tf_op jit(solution)/shard_map/all_to_all | solution.py:510
  23.0 1.0 %copy-done.9 = f32[128,1024]{1,0:T(8,128)S(1)} copy-done((f32[128,1024]{1,0:T(8,128)S(1)}, f32[128,1024]{1,0:T(8,128)}, u32[]{:S(2)}) %copy-start.9) | copy-done | bytes 524312
  24.1 2.2 %own_spectra.1 = (bf16[2,2,64,1024]{3,2,1,0:T(8,128)(2,1)S(1)}, bf16[2,2,16,1024]{3,2,1,0:T(8,128)(2,1)S(1)}, f32[256,2048]{1,0:T(8,128)S(1)}, bf16[1024,2048]{1,0:T(8,128)(2,1)S(1)}) custom-call(s32[1]{0:T(128)} %bitcast.half_ref, s32[1]{0:T(128)} %bitcast.1.me_ref, bf16[4,2,128,256]{3,2,1,0:T(8,128)(2,1)S(1)} %all-to-all-done.pieces_ref, ...), custom_call_target="tpu_custom_call" | custom-call | flops 1610612736 | bytes 8388608 | tf_op jit(solution)/shard_map/own_spectra/pallas_call | solution.py:325
  26.3 5.5 %collective-permute-done.2.theirs_ref = s32[1,2,2]{2,1,0:T(2,128)S(1)} collective-permute-done((s32[1,2,2]{2,1,0:T(2,128)S(1)}, s32[1,2,2]{2,1,0:T(2,128)S(1)}, u32[]{:S(2)}, u32[]{:S(2)}) %collective-permute-start.2) | collective-permute-done | bytes 48 | tf_op jit(solution)/shard_map/ppermute | solution.py:507
  32.4 0.9 %copy-done.6 = bf16[2,128,256]{2,1,0:T(8,128)(2,1)S(1)} copy-done((bf16[2,128,256]{2,1,0:T(8,128)(2,1)S(1)}, bf16[2,128,256]{2,1,0:T(8,128)(2,1)}, u32[]{:S(2)}) %copy-start.6) | copy-done | bytes 131096
  33.3 2.5 %partner_slots.1 = (bf16[2,2,128,256]{3,2,1,0:T(8,128)(2,1)S(1)}, bf16[4,2,64,1024]{3,2,1,0:T(8,128)(2,1)S(1)}, bf16[4,2,16,1024]{3,2,1,0:T(8,128)(2,1)S(1)}, bf16[4,64,1024]{2,1,0:T(8,128)(2,1)S(1)}) custom-call(s32[1]{0:T(128)} %bitcast.half_ref, s32[1]{0:T(128)} %bitcast.1.me_ref, s32[1,2,2]{2,1,0:T(2,128)S(1)} %collective-permute-done.2.theirs_ref, ...), custom_call_target="tpu_custom_call" | custom-call | flops 2147483648 | bytes 8388608 | tf_op jit(solution)/shard_map/partner_slots/pallas_call | solution.py:364
  35.9 1.8 %collective-permute-start.7 = (bf16[2,2,128,256]{3,2,1,0:T(8,128)(2,1)S(1)}, bf16[2,2,128,256]{3,2,1,0:T(8,128)(2,1)S(1)}, u32[]{:S(2)}, u32[]{:S(2)}) collective-permute-start(bf16[2,2,128,256]{3,2,1,0:T(8,128)(2,1)S(1)} %get-tuple-element.56), channel_id=1, source_target_pairs={{0,8},{1,9},{2,10},{3,11},{4,12},{5,13},{6,14},{7,15},{8,0},{9,1},... | collective-permute-start | bytes 786440 | tf_op jit(solution)/shard_map/ppermute | solution.py:507
  37.7 3.6 %own_slots.1 = (bf16[4,2,128,256]{3,2,1,0:T(8,128)(2,1)}, bf16[2,128,256]{2,1,0:T(8,128)(2,1)}, bf16[2,128,256]{2,1,0:T(8,128)(2,1)S(1)}) custom-call(s32[1]{0:T(128)} %bitcast.half_ref, s32[1]{0:T(128)} %bitcast.1.me_ref, s32[1,2,2]{2,1,0:T(2,128)S(1)} %copy-done.4, bf16[1024,2048]{1,0:T(8,128)(2,1)S(1)} %get-tuple-element.43.refs_3_.table_ref, ...), custom_call_target="tpu_custom_call" | custom-call | flops 1073741824 | bytes 8388608 | tf_op jit(solution)/shard_map/own_slots/pallas_call | solution.py:396
  41.3 3.5 %all-to-all-start.1 = ((bf16[4,2,128,256]{3,2,1,0:T(8,128)(2,1)}), bf16[4,2,128,256]{3,2,1,0:T(8,128)(2,1)S(1)}, u32[]{:S(2)}, u32[]{:S(2)}) async-start(bf16[4,2,128,256]{3,2,1,0:T(8,128)(2,1)} %get-tuple-element.54), calls=%async_computation.1 | async-start | bytes 1048576 | tf_op jit(solution)/shard_map/all_to_all | solution.py:510
  44.8 2.6 %collective-permute-start.5 = (bf16[2,128,256]{2,1,0:T(8,128)(2,1)}, bf16[2,128,256]{2,1,0:T(8,128)(2,1)S(1)}, u32[]{:S(2)}, u32[]{:S(2)}) collective-permute-start(bf16[2,128,256]{2,1,0:T(8,128)(2,1)} %get-tuple-element.52), channel_id=1, source_target_pairs={{0,10},{1,11},{2,8},{3,9},{4,14},{5,15},{6,12},{7,13},{8,2},{9,3},... | collective-permute-start | bytes 393224 | tf_op jit(solution)/shard_map/ppermute | solution.py:507
  47.3 1.1 %collective-permute-start.6 = (bf16[2,128,256]{2,1,0:T(8,128)(2,1)S(1)}, bf16[2,128,256]{2,1,0:T(8,128)(2,1)S(1)}, u32[]{:S(2)}, u32[]{:S(2)}) collective-permute-start(bf16[2,128,256]{2,1,0:T(8,128)(2,1)S(1)} %get-tuple-element.53), channel_id=1, source_target_pairs={{0,11},{1,10},{2,9},{3,8},{4,15},{5,14},{6,13},{7,12},{8,3},{9,2},... | collective-permute-start | bytes 393224 | tf_op jit(solution)/shard_map/ppermute | solution.py:507
  48.4 2.8 %collective-permute-done.7.refs_0_ = bf16[2,2,128,256]{3,2,1,0:T(8,128)(2,1)S(1)} collective-permute-done((bf16[2,2,128,256]{3,2,1,0:T(8,128)(2,1)S(1)}, bf16[2,2,128,256]{3,2,1,0:T(8,128)(2,1)S(1)}, u32[]{:S(2)}, u32[]{:S(2)}) %collective-permute-start.7) | collective-permute-done | bytes 262176 | tf_op jit(solution)/shard_map/ppermute | solution.py:507
  51.9 2.1 %all-to-all-done.1.own_ref = bf16[4,2,128,256]{3,2,1,0:T(8,128)(2,1)S(1)} async-done(((bf16[4,2,128,256]{3,2,1,0:T(8,128)(2,1)}), bf16[4,2,128,256]{3,2,1,0:T(8,128)(2,1)S(1)}, u32[]{:S(2)}, u32[]{:S(2)}) %all-to-all-start.1) | async-done | bytes 524320 | tf_op jit(solution)/shard_map/all_to_all | solution.py:510
  54.0 1.0 %own_surfaces.1.part_ref = f32[2,256,1024]{2,1,0:T(8,128)S(1)} custom-call(s32[1]{0:T(128)} %bitcast.half_ref, bf16[4,2,128,256]{3,2,1,0:T(8,128)(2,1)S(1)} %all-to-all-done.1.own_ref, bf16[1024,1024]{1,0:T(8,128)(2,1)S(1)} %copy-done), custom_call_target="tpu_custom_call" | custom-call | flops 536870912 | bytes 2097152 | tf_op jit(solution)/shard_map/own_surfaces/pallas_call | solution.py:425
  55.0 5.2 %collective-permute-done.5.refs_2_ = bf16[2,128,256]{2,1,0:T(8,128)(2,1)S(1)} collective-permute-done((bf16[2,128,256]{2,1,0:T(8,128)(2,1)}, bf16[2,128,256]{2,1,0:T(8,128)(2,1)S(1)}, u32[]{:S(2)}, u32[]{:S(2)}) %collective-permute-start.5) | collective-permute-done | bytes 131104 | tf_op jit(solution)/shard_map/ppermute | solution.py:507
  60.2 2.0 %collective-permute-done.6.refs_3_ = bf16[2,128,256]{2,1,0:T(8,128)(2,1)S(1)} collective-permute-done((bf16[2,128,256]{2,1,0:T(8,128)(2,1)S(1)}, bf16[2,128,256]{2,1,0:T(8,128)(2,1)S(1)}, u32[]{:S(2)}, u32[]{:S(2)}) %collective-permute-start.6) | collective-permute-done | bytes 131104 | tf_op jit(solution)/shard_map/ppermute | solution.py:507
  62.2 2.0 %surfaces.1 = f32[2,256,1024]{2,1,0:T(8,128)} custom-call(s32[1]{0:T(128)} %bitcast.half_ref, s32[1]{0:T(128)} %bitcast.1.me_ref, s32[1]{0:T(128)S(6)} %copy.8.counts_ref, f32[2,256,1024]{2,1,0:T(8,128)S(1)} %own_surfaces.1.part_ref, bf16[2,2,128,256]{3,2,1,0:T(8,128)(2,1)S(1)} %collective-permute-done.7.refs_0_, ...), custom_call_target="tpu_custom_call" | custom-call | flops 536870912 | bytes 4194304 | tf_op jit(solution)/shard_map/surfaces/pallas_call | solution.py:469
  (27 shorter events, 1.7 us)
Async XLA Ops:
  0.0 7.6 %copy-start = (bf16[1024,1024]{1,0:T(8,128)(2,1)S(1)}, bf16[1024,1024]{1,0:T(8,128)(2,1)}, u32[]{:S(2)}) copy-start(bf16[1024,1024]{1,0:T(8,128)(2,1)} %constant.29.clone.table_hbm.table_ref.refs_4_) | copy-start | bytes 6291460
  0.0 7.6 %copy-start.1 = (f32[2,256,1024]{2,1,0:T(8,128)S(1)}, f32[2,256,1024]{2,1,0:T(8,128)}, u32[]{:S(2)}) copy-start(f32[2,256,1024]{2,1,0:T(8,128)} %tile_ref.1) | copy-start | bytes 6291460
  0.0 7.6 %copy-start.2 = (f32[8,1024]{1,0:T(8,128)S(1)}, f32[8,1024]{1,0:T(8,128)}, u32[]{:S(2)}) copy-start(f32[8,1024]{1,0:T(8,128)} %constant.30.clone.down_hbm.down_ref) | copy-start | bytes 98308
  0.0 7.6 %copy-start.3 = (f32[1,1024]{1,0:T(1,128)S(1)}, f32[1,1024]{1,0:T(1,128)}, u32[]{:S(2)}) copy-start(f32[1,1024]{1,0:T(1,128)} %constant.31.clone.across_hbm.across_ref) | copy-start | bytes 12292
  3.5 18.1 %collective-permute-start = (bf16[2,128,256]{2,1,0:T(8,128)(2,1)}, bf16[2,128,256]{2,1,0:T(8,128)(2,1)S(1)}, u32[]{:S(2)}, u32[]{:S(2)}) collective-permute-start(bf16[2,128,256]{2,1,0:T(8,128)(2,1)} %get-tuple-element.32), channel_id=1, source_target_pairs={{0,8},{1,9},{2,10},{3,11},{4,12},{5,13},{6,14},{7,15},{8,0},{9,1},... | collective-permute-start | bytes 393224 | tf_op jit(solution)/shard_map/ppermute | solution.py:507
  7.6 14.0 %collective-permute-start.1 = (bf16[2,128,256]{2,1,0:T(8,128)(2,1)}, bf16[2,128,256]{2,1,0:T(8,128)(2,1)S(1)}, u32[]{:S(2)}, u32[]{:S(2)}) collective-permute-start(bf16[2,128,256]{2,1,0:T(8,128)(2,1)} %get-tuple-element.33), channel_id=1, source_target_pairs={{0,9},{1,8},{2,11},{3,10},{4,13},{5,12},{6,15},{7,14},{8,1},{9,0},... | collective-permute-start | bytes 393224 | tf_op jit(solution)/shard_map/ppermute | solution.py:507
  10.1 13.0 %all-to-all-start = ((bf16[4,2,128,256]{3,2,1,0:T(8,128)(2,1)}), bf16[4,2,128,256]{3,2,1,0:T(8,128)(2,1)S(1)}, u32[]{:S(2)}, u32[]{:S(2)}) async-start(bf16[4,2,128,256]{3,2,1,0:T(8,128)(2,1)} %get-tuple-element.39), calls=%async_computation | async-start | bytes 1048576 | tf_op jit(solution)/shard_map/all_to_all | solution.py:510
  13.5 1.0 %copy-start.7 = (f32[128,1024]{1,0:T(8,128)S(1)}, f32[128,1024]{1,0:T(8,128)}, u32[]{:S(2)}) copy-start(f32[128,1024]{1,0:T(8,128)} %constant.32.clone.short_ref) | copy-start | bytes 1572868
  14.6 4.5 %copy-start.4 = (s32[1,2,2]{2,1,0:T(2,128)S(1)}, s32[1,2,2]{2,1,0:T(2,128)}, u32[]{:S(2)}) copy-start(s32[1,2,2]{2,1,0:T(2,128)} %pairs_ref) | copy-start | bytes 52
  14.6 0.8 %copy-start.8 = (f32[128,1024]{1,0:T(8,128)}, f32[128,1024]{1,0:T(8,128)S(1)}, u32[]{:S(2)}) copy-start(f32[128,1024]{1,0:T(8,128)S(1)} %scaled_tables.1.short_ref) | copy-start | bytes 1572868
  15.4 16.3 %collective-permute-start.3 = (bf16[2,128,256]{2,1,0:T(8,128)(2,1)S(1)}, bf16[2,128,256]{2,1,0:T(8,128)(2,1)S(1)}, u32[]{:S(2)}, u32[]{:S(2)}) collective-permute-start(bf16[2,128,256]{2,1,0:T(8,128)(2,1)S(1)} %get-tuple-element.44), channel_id=1, source_target_pairs={{0,10},{1,11},{2,8},{3,9},{4,14},{5,15},{6,12},{7,13},{8,2},{9,3},... | collective-permute-start | bytes 393224 | tf_op jit(solution)/shard_map/ppermute | solution.py:507
  18.9 12.9 %collective-permute-start.4 = (bf16[2,128,256]{2,1,0:T(8,128)(2,1)S(1)}, bf16[2,128,256]{2,1,0:T(8,128)(2,1)S(1)}, u32[]{:S(2)}, u32[]{:S(2)}) collective-permute-start(bf16[2,128,256]{2,1,0:T(8,128)(2,1)S(1)} %get-tuple-element.45), channel_id=1, source_target_pairs={{0,11},{1,10},{2,9},{3,8},{4,15},{5,14},{6,13},{7,12},{8,3},{9,2},... | collective-permute-start | bytes 393224 | tf_op jit(solution)/shard_map/ppermute | solution.py:507
  19.0 12.7 %collective-permute-start.2 = (s32[1,2,2]{2,1,0:T(2,128)S(1)}, s32[1,2,2]{2,1,0:T(2,128)S(1)}, u32[]{:S(2)}, u32[]{:S(2)}) collective-permute-start(s32[1,2,2]{2,1,0:T(2,128)S(1)} %copy-done.4), channel_id=1, source_target_pairs={{0,8},{1,9},{2,10},{3,11},{4,12},{5,13},{6,14},{7,15},{8,0},{9,1},... | collective-permute-start | bytes 56 | tf_op jit(solution)/shard_map/ppermute | solution.py:507
  23.0 1.0 %copy-start.9 = (f32[128,1024]{1,0:T(8,128)S(1)}, f32[128,1024]{1,0:T(8,128)}, u32[]{:S(2)}) copy-start(f32[128,1024]{1,0:T(8,128)} %copy-done.8) | copy-start | bytes 1572868
  31.8 0.7 %copy-start.5 = (bf16[2,128,256]{2,1,0:T(8,128)(2,1)}, bf16[2,128,256]{2,1,0:T(8,128)(2,1)S(1)}, u32[]{:S(2)}) copy-start(bf16[2,128,256]{2,1,0:T(8,128)(2,1)S(1)} %collective-permute-done.4.refs_1_) | copy-start | bytes 393220
  32.4 0.9 %copy-start.6 = (bf16[2,128,256]{2,1,0:T(8,128)(2,1)S(1)}, bf16[2,128,256]{2,1,0:T(8,128)(2,1)}, u32[]{:S(2)}) copy-start(bf16[2,128,256]{2,1,0:T(8,128)(2,1)} %copy-done.5) | copy-start | bytes 393220
  35.9 15.3 %collective-permute-start.7 = (bf16[2,2,128,256]{3,2,1,0:T(8,128)(2,1)S(1)}, bf16[2,2,128,256]{3,2,1,0:T(8,128)(2,1)S(1)}, u32[]{:S(2)}, u32[]{:S(2)}) collective-permute-start(bf16[2,2,128,256]{3,2,1,0:T(8,128)(2,1)S(1)} %get-tuple-element.56), channel_id=1, source_target_pairs={{0,8},{1,9},{2,10},{3,11},{4,12},{5,13},{6,14},{7,15},{8,0},{9,1},... | collective-permute-start | bytes 786440 | tf_op jit(solution)/shard_map/ppermute | solution.py:507
  41.3 12.7 %all-to-all-start.1 = ((bf16[4,2,128,256]{3,2,1,0:T(8,128)(2,1)}), bf16[4,2,128,256]{3,2,1,0:T(8,128)(2,1)S(1)}, u32[]{:S(2)}, u32[]{:S(2)}) async-start(bf16[4,2,128,256]{3,2,1,0:T(8,128)(2,1)} %get-tuple-element.54), calls=%async_computation.1 | async-start | bytes 1048576 | tf_op jit(solution)/shard_map/all_to_all | solution.py:510
  44.8 15.4 %collective-permute-start.5 = (bf16[2,128,256]{2,1,0:T(8,128)(2,1)}, bf16[2,128,256]{2,1,0:T(8,128)(2,1)S(1)}, u32[]{:S(2)}, u32[]{:S(2)}) collective-permute-start(bf16[2,128,256]{2,1,0:T(8,128)(2,1)} %get-tuple-element.52), channel_id=1, source_target_pairs={{0,10},{1,11},{2,8},{3,9},{4,14},{5,15},{6,12},{7,13},{8,2},{9,3},... | collective-permute-start | bytes 393224 | tf_op jit(solution)/shard_map/ppermute | solution.py:507
  47.3 14.8 %collective-permute-start.6 = (bf16[2,128,256]{2,1,0:T(8,128)(2,1)S(1)}, bf16[2,128,256]{2,1,0:T(8,128)(2,1)S(1)}, u32[]{:S(2)}, u32[]{:S(2)}) collective-permute-start(bf16[2,128,256]{2,1,0:T(8,128)(2,1)S(1)} %get-tuple-element.53), channel_id=1, source_target_pairs={{0,11},{1,10},{2,9},{3,8},{4,15},{5,14},{6,13},{7,12},{8,3},{9,2},... | collective-permute-start | bytes 393224 | tf_op jit(solution)/shard_map/ppermute | solution.py:507
  51.2 11.0 %collective-permute-start.8 = (bf16[2,128,256]{2,1,0:T(8,128)(2,1)S(1)}, bf16[2,128,256]{2,1,0:T(8,128)(2,1)S(1)}, u32[]{:S(2)}, u32[]{:S(2)}) collective-permute-start(bf16[2,128,256]{2,1,0:T(8,128)(2,1)S(1)} %slice_bitcast_fusion), channel_id=1, source_target_pairs={{0,1},{1,0},{2,3},{3,2},{4,5},{5,4},{6,7},{7,6},{8,9},{9,8},{10,11... | collective-permute-start | bytes 393224 | tf_op jit(solution)/shard_map/ppermute | solution.py:513

commit v18 on v16

--- a/solution.py
+++ b/solution.py
@@ -285,7 +285,7 @@
 def invert_columns(s_ref, me, phases, table_ref, outs):
     _, block, height = phases.shape
     slots = phases.shape[0] // 2
-    rows = next(iter(outs.values())).shape[2]
+    rows = next(iter(outs.values()))[0].shape[1]
     row = lax.broadcasted_iota(jnp.int32, (block, rows), 0)
     twice = jnp.where((row == 0) & holds_packed(s_ref), 1.0, 2.0)
     flat = phases[...].reshape(2 * slots * block, height)
@@ -301,8 +301,8 @@
         for p in range(slots):
             re = slice(2 * p * block, (2 * p + 1) * block)
             im = slice((2 * p + 1) * block, (2 * p + 2) * block)
-            out[p, :block] = ((c_part[re] - s_part[im]) * twice).astype(jnp.bfloat16)
-            out[p, block:] = ((s_part[re] + c_part[im]) * twice).astype(jnp.bfloat16)
+            out[p][:block] = ((c_part[re] - s_part[im]) * twice).astype(jnp.bfloat16)
+            out[p][block:] = ((s_part[re] + c_part[im]) * twice).astype(jnp.bfloat16)
 
 
 def own_spectra(place, pieces, near, short):
@@ -359,7 +359,7 @@
         total = gather_rows(inputs, table_ref, me, 2, share_ref[...])
         store_spectra(s_ref, total, every, edges, count)
         correlate(s_ref, picks, every, edges, phases)
-        invert_columns(s_ref, me, phases, table_ref, {k: near.at[k] for k in range(2)})
+        invert_columns(s_ref, me, phases, table_ref, {k: [near.at[k, p] for p in range(slots)] for k in range(2)})
 
     return pl.pallas_call(
         body,
@@ -388,19 +388,22 @@
         far, work = refs[:-1], refs[-1]
         picks = [[pairs_ref[0, p, i] for i in range(2)] for p in range(slots)]
         if far:
-            outs = {k: far[k - 2] for k in range(2, peers)}
+            outs = {
+                k: [far[(k - 2) * slots + p].at[0] for p in range(slots)] for k in range(2, peers)
+            }
             invert_columns(s_ref, me_ref[0], theirs, table_ref, outs)
         correlate(s_ref, picks, every, edges, work)
-        invert_columns(s_ref, 0, work, table_ref, {k: out_ref.at[k] for k in range(peers)})
+        outs = {k: [out_ref.at[k, p] for p in range(slots)] for k in range(peers)}
+        invert_columns(s_ref, 0, work, table_ref, outs)
 
     return pl.pallas_call(
         body,
         in_specs=[pl.BlockSpec(memory_space=pltpu.SMEM)] * 3
         + [pl.BlockSpec(memory_space=pltpu.VMEM)] * 4,
-        out_specs=[pl.BlockSpec(memory_space=pltpu.VMEM)] * (peers - 1),
+        out_specs=[pl.BlockSpec(memory_space=pltpu.VMEM)] * (1 + (peers - 2) * slots),
         out_shape=[
             jax.ShapeDtypeStruct((peers, slots, 2 * block, rows), jnp.bfloat16),
-            *[jax.ShapeDtypeStruct((slots, 2 * block, rows), jnp.bfloat16)] * (peers - 2),
+            *[jax.ShapeDtypeStruct((1, 2 * block, rows), jnp.bfloat16)] * ((peers - 2) * slots),
         ],
         scratch_shapes=[pltpu.VMEM((2 * slots, block, height), jnp.bfloat16)],
         compiler_params=params(),
@@ -440,18 +443,17 @@
     )(scalar(half), own, table)
 
 
-def surfaces_of(half, me, counts, part, near, other, table):
-    peers = 1 + len(other)
-    slots, double, rows = other[0].shape
+def surface_of(slot, half, me, counts, part, near, swapped, far, table, before):
+    peers = 2 + len(far)
+    slots, double, rows = swapped.shape
     width = table.shape[0]
     span = peers * double
 
-    def body(half_ref, me_ref, counts_ref, part_ref, *refs):
-        other_refs = refs[:peers]
-        table_ref, out_ref, work = refs[peers:]
-        for k in range(peers):
+    def body(half_ref, me_ref, counts_ref, part_ref, near_ref, swapped_ref, *refs):
+        far_refs, table_ref, out_ref, work = refs[: peers - 2], refs[peers - 2], refs[-2], refs[-1]
+        pieces = [near_ref[0, 0], swapped_ref[0]] + [ref[0] for ref in far_refs]
+        for k, piece in enumerate(pieces):
             place = pl.multiple_of((me_ref[0] ^ k) * double, double)
-            piece = other_refs[k][0] if k else other_refs[k][0, 0]
             work[pl.ds(place, double), :] = piece
         start = pl.multiple_of((1 - half_ref[0]) * span, span)
         rest = lax.dot_general(
@@ -460,31 +462,31 @@
             (((0,), (0,)), ((), ())),
             preferred_element_type=jnp.float32,
         )
-        live = pl.program_id(0) < counts_ref[0]
-        out_ref[0] = jnp.where(live, part_ref[pl.program_id(0)] + rest, 0.0)
-
-    pair = pl.BlockSpec((1, 1, double, rows), lambda p, half, me, counts: (0, p, 0, 0))
-    piece = pl.BlockSpec((1, double, rows), lambda p, half, me, counts: (p, 0, 0))
-    plane = pl.BlockSpec((1, rows, width), lambda p, half, me, counts: (p, 0, 0))
+        out_ref[0] = jnp.where(slot < counts_ref[0], part_ref[slot] + rest, 0.0)
+
     return pl.pallas_call(
         body,
         grid_spec=pltpu.PrefetchScalarGridSpec(
             num_scalar_prefetch=3,
-            grid=(slots,),
+            grid=(1,),
             in_specs=[
                 pl.BlockSpec(memory_space=pltpu.VMEM),
-                pair,
-                *[piece] * (peers - 1),
+                pl.BlockSpec((1, 1, double, rows), lambda i, half, me, counts: (0, slot, 0, 0)),
+                pl.BlockSpec((1, double, rows), lambda i, half, me, counts: (slot, 0, 0)),
+                *[pl.BlockSpec((1, double, rows), lambda i, half, me, counts: (0, 0, 0))]
+                * (peers - 2),
                 pl.BlockSpec(memory_space=pltpu.VMEM),
+                *[pl.BlockSpec(memory_space=pl.ANY)] * len(before),
             ],
-            out_specs=plane,
+            out_specs=pl.BlockSpec((1, rows, width), lambda i, half, me, counts: (slot, 0, 0)),
             scratch_shapes=[pltpu.VMEM((span, rows), jnp.bfloat16)],
         ),
         out_shape=jax.ShapeDtypeStruct((slots, rows, width), jnp.float32),
-        compiler_params=params(),
-        cost_estimate=cost(2 * slots * rows * width * span, 8 * slots * rows * width),
-        name="surfaces",
-    )(scalar(half), scalar(me), counts, part, near, *other, table)
+        input_output_aliases={7 + peers - 2: 0} if before else {},
+        compiler_params=params(),
+        cost_estimate=cost(2 * rows * width * span, 8 * rows * width),
+        name="surface",
+    )(scalar(half), scalar(me), counts, part, near, swapped, *far, table, *before)
 
 
 def local(tiles, pairs, counts):
@@ -534,10 +536,19 @@
     )
     near = across(near, 0)
     own, *far = own_slots(place, pairs, table_h, spectra, edge, phases, peers)
-    far = [across(far[k - 2], k) for k in range(2, peers)]
+    slots = pairs.shape[1]
+    far = [
+        [across(far[(k - 2) * slots + p], k) for k in range(2, peers)] for p in range(slots)
+    ]
     part = own_surfaces(half, along(own), table_w)
-    *far, part = lax.optimization_barrier((*far, part))
-    return surfaces_of(half, me, counts, part, near, [swap(near[1]), *far], table_w)
+    *far[0], part = lax.optimization_barrier((*far[0], part))
+    swapped = swap(near[1])
+    before = []
+    for p in range(slots):
+        before = [
+            surface_of(p, half, me, counts, part, near, swapped, far[p], table_w, before)
+        ]
+    return before[0]
 
 
 def solution(mesh):

time: 61.9 us -> 66.9 us (1.081)
  starting transfers between devices: 23.7 us -> 27.4 us
  Pallas kernels: 17.1 us -> 18.1 us
    ppermute x8 -> x10, starting transfers between devices: 16.6 us -> 20.4 us  [across(): return lax.ppermute(value, axes, moves)]
    all_to_all x2, waiting for transfers between devices: 3.84 us -> 0.69 us  [along(): return lax.all_to_all(blocks, 'rows', split_axis=0, concat_axis=0)]
    ppermute x8 -> x10, waiting for transfers between devices: 13.3 us -> 16 us  [across(): return lax.ppermute(value, axes, moves)]
    pallas_call x1 -> x2, Pallas kernels: 1.95 us -> 2.91 us  [surface_of(): pl.pallas_call(body, grid_spec=pltpu.PrefetchScalarGridSpec(num_scalar_pr...]
  transfers between devices with their start and end apart: 11 -> 13, of which waited for: 6 -> 6; matrix products, arithmetic and copies ran while one was open for 0% -> 1% of each run, Pallas kernels for 15% -> 16%
where the time goes in v18:
time: 66.9 us; the launch traced here: 66.5 us
  starting transfers between devices  27.4 us (41%)
  Pallas kernels  18.1 us (27%)
  waiting for transfers between devices  16.7 us (25%)
  local copies, waits for them, and re-layouts  3.57 us (5%)
  between operations  0.77 us (1%)
    ppermute x10, starting transfers between devices, across(): return lax.ppermute(value, axes, moves)  20.4 us
    ppermute x10, waiting for transfers between devices, across(): return lax.ppermute(value, axes, moves)  16 us
    all_to_all x2, starting transfers between devices, along(): return lax.all_to_all(blocks, 'rows', split_axis=0, concat_axis=0)  6.94 us
    pallas_call x1, Pallas kernels, own_slots(): pl.pallas_call(body, in_specs=[pl.BlockSpec(memory_space=pltpu.SMEM)] * 3...  3.58 us
    pallas_call x1, Pallas kernels, near_columns(): pl.pallas_call(body, grid_spec=pltpu.PrefetchScalarGridSpec(num_scalar_pr...  3.46 us
    pallas_call x2, Pallas kernels, surface_of(): pl.pallas_call(body, grid_spec=pltpu.PrefetchScalarGridSpec(num_scalar_pr...  2.91 us
    unnamed x16, local copies, waits for them, and re-layouts  2.91 us
    pallas_call x1, Pallas kernels, partner_slots(): pl.pallas_call(body, in_specs=[pl.BlockSpec(memory_space=pltpu.SMEM)] * 3...  2.53 us
  transfers between devices with their start and end apart: 13, of which 6 were waited for; matrix products, arithmetic and copies ran while one was open for 1% of the time, Pallas kernels for 16%

profile of v18, /device:TPU:0, one launch (start us, length us, event | category | flops | bytes accessed | tf_op | source)
XLA Modules:
  0.0 66.5 jit_solution(260984604485029954)
XLA Ops:
  0.0 3.5 %near_columns.1 = (bf16[2,128,256]{2,1,0:T(8,128)(2,1)}, bf16[2,128,256]{2,1,0:T(8,128)(2,1)}) custom-call(s32[1]{0:T(128)} %bitcast.half_ref, s32[1]{0:T(128)} %bitcast.1.me_ref, f32[2,256,1024]{2,1,0:T(8,128)} %tile_ref.1, f32[8,1024]{1,0:T(8,128)} %constant.30.clone.down_hbm.down_ref, f32[1,1024]{1,0:T(1,128)} %constant.31.clone.across_hbm.across_ref, ...), custom_call_target="tpu_custom_call" | custom-call | flops 268435456 | bytes 2621440 | tf_op jit(solution)/shard_map/near_columns/pallas_call | solution.py:144
  3.5 4.1 %collective-permute-start = (bf16[2,128,256]{2,1,0:T(8,128)(2,1)}, bf16[2,128,256]{2,1,0:T(8,128)(2,1)S(1)}, u32[]{:S(2)}, u32[]{:S(2)}) collective-permute-start(bf16[2,128,256]{2,1,0:T(8,128)(2,1)} %get-tuple-element.31), channel_id=1, source_target_pairs={{0,8},{1,9},{2,10},{3,11},{4,12},{5,13},{6,14},{7,15},{8,0},{9,1},... | collective-permute-start | bytes 393224 | tf_op jit(solution)/shard_map/ppermute | solution.py:509
  7.6 2.4 %rest_columns.1 = (bf16[4,2,128,256]{3,2,1,0:T(8,128)(2,1)}, bf16[2,128,256]{2,1,0:T(8,128)(2,1)S(1)}, bf16[2,128,256]{2,1,0:T(8,128)(2,1)S(1)}) custom-call(s32[1]{0:T(128)} %bitcast.2.half_ref, s32[1]{0:T(128)} %bitcast.1.me_ref, f32[2,256,1024]{2,1,0:T(8,128)S(1)} %copy-done.1, f32[8,1024]{1,0:T(8,128)S(1)} %copy-done.2, f32[1,1024]{1,0:T(1,128)S(1)} %copy-done.3, ...), custom_call_target="tpu_custom_call" | custom-call | flops 805306368 | bytes 4194304 | tf_op jit(solution)/shard_map/rest_columns/pallas_call | solution.py:192
  10.1 3.5 %all-to-all-start = ((bf16[4,2,128,256]{3,2,1,0:T(8,128)(2,1)}), bf16[4,2,128,256]{3,2,1,0:T(8,128)(2,1)S(1)}, u32[]{:S(2)}, u32[]{:S(2)}) async-start(bf16[4,2,128,256]{3,2,1,0:T(8,128)(2,1)} %get-tuple-element.38), calls=%async_computation | async-start | bytes 1048576 | tf_op jit(solution)/shard_map/all_to_all | solution.py:512
  13.6 3.5 %collective-permute-start.3 = (bf16[2,128,256]{2,1,0:T(8,128)(2,1)S(1)}, bf16[2,128,256]{2,1,0:T(8,128)(2,1)S(1)}, u32[]{:S(2)}, u32[]{:S(2)}) collective-permute-start(bf16[2,128,256]{2,1,0:T(8,128)(2,1)S(1)} %get-tuple-element.40), channel_id=1, source_target_pairs={{0,10},{1,11},{2,8},{3,9},{4,14},{5,15},{6,12},{7,13},{8,2},{9,3},... | collective-permute-start | bytes 393224 | tf_op jit(solution)/shard_map/ppermute | solution.py:509
  17.3 2.5 %collective-permute-start.2 = (s32[1,2,2]{2,1,0:T(2,128)S(1)}, s32[1,2,2]{2,1,0:T(2,128)S(1)}, u32[]{:S(2)}, u32[]{:S(2)}) collective-permute-start(s32[1,2,2]{2,1,0:T(2,128)S(1)} %copy-done.4), channel_id=1, source_target_pairs={{0,8},{1,9},{2,10},{3,11},{4,12},{5,13},{6,14},{7,15},{8,0},{9,1},... | collective-permute-start | bytes 56 | tf_op jit(solution)/shard_map/ppermute | solution.py:509
  19.8 1.0 %copy-done.5 = f32[128,1024]{1,0:T(8,128)S(1)} copy-done((f32[128,1024]{1,0:T(8,128)S(1)}, f32[128,1024]{1,0:T(8,128)}, u32[]{:S(2)}) %copy-start.5) | copy-done | bytes 524312
  20.9 0.8 %copy-done.6 = f32[128,1024]{1,0:T(8,128)} copy-done((f32[128,1024]{1,0:T(8,128)}, f32[128,1024]{1,0:T(8,128)S(1)}, u32[]{:S(2)}) %copy-start.6) | copy-done | bytes 524312
  22.4 1.0 %copy-done.7 = f32[128,1024]{1,0:T(8,128)S(1)} copy-done((f32[128,1024]{1,0:T(8,128)S(1)}, f32[128,1024]{1,0:T(8,128)}, u32[]{:S(2)}) %copy-start.7) | copy-done | bytes 524312
  23.4 2.2 %own_spectra.1 = (bf16[2,2,64,1024]{3,2,1,0:T(8,128)(2,1)S(1)}, bf16[2,2,16,1024]{3,2,1,0:T(8,128)(2,1)S(1)}, f32[256,2048]{1,0:T(8,128)S(1)}, bf16[1024,2048]{1,0:T(8,128)(2,1)S(1)}) custom-call(s32[1]{0:T(128)} %bitcast.half_ref, s32[1]{0:T(128)} %bitcast.1.me_ref, bf16[4,2,128,256]{3,2,1,0:T(8,128)(2,1)S(1)} %all-to-all-done.pieces_ref, ...), custom_call_target="tpu_custom_call" | custom-call | flops 1610612736 | bytes 8388608 | tf_op jit(solution)/shard_map/own_spectra/pallas_call | solution.py:325
  25.6 5.4 %collective-permute-done.2.theirs_ref = s32[1,2,2]{2,1,0:T(2,128)S(1)} collective-permute-done((s32[1,2,2]{2,1,0:T(2,128)S(1)}, s32[1,2,2]{2,1,0:T(2,128)S(1)}, u32[]{:S(2)}, u32[]{:S(2)}) %collective-permute-start.2) | collective-permute-done | bytes 48 | tf_op jit(solution)/shard_map/ppermute | solution.py:509
  31.0 2.5 %partner_slots.1 = (bf16[2,2,128,256]{3,2,1,0:T(8,128)(2,1)S(1)}, bf16[4,2,64,1024]{3,2,1,0:T(8,128)(2,1)S(1)}, bf16[4,2,16,1024]{3,2,1,0:T(8,128)(2,1)S(1)}, bf16[4,64,1024]{2,1,0:T(8,128)(2,1)S(1)}) custom-call(s32[1]{0:T(128)} %bitcast.half_ref, s32[1]{0:T(128)} %bitcast.1.me_ref, s32[1,2,2]{2,1,0:T(2,128)S(1)} %collective-permute-done.2.theirs_ref, ...), custom_call_target="tpu_custom_call" | custom-call | flops 2147483648 | bytes 8388608 | tf_op jit(solution)/shard_map/partner_slots/pallas_call | solution.py:364
  33.5 2.6 %collective-permute-start.7 = (bf16[2,2,128,256]{3,2,1,0:T(8,128)(2,1)S(1)}, bf16[2,2,128,256]{3,2,1,0:T(8,128)(2,1)S(1)}, u32[]{:S(2)}, u32[]{:S(2)}) collective-permute-start(bf16[2,2,128,256]{3,2,1,0:T(8,128)(2,1)S(1)} %get-tuple-element.52), channel_id=1, source_target_pairs={{0,8},{1,9},{2,10},{3,11},{4,12},{5,13},{6,14},{7,15},{8,0},{9,1},... | collective-permute-start | bytes 786440 | tf_op jit(solution)/shard_map/ppermute | solution.py:509
  36.2 3.6 %own_slots.1 = (bf16[4,2,128,256]{3,2,1,0:T(8,128)(2,1)}, bf16[1,128,256]{2,1,0:T(8,128)(2,1)S(1)}, bf16[1,128,256]{2,1,0:T(8,128)(2,1)S(1)}, bf16[1,128,256]{2,1,0:T(8,128)(2,1)S(1)}, bf16[1,128,256]{2,1,0:T(8,128)(2,1)S(1)}) custom-call(s32[1]{0:T(128)} %bitcast.half_ref, s32[1]{0:T(128)} %bitcast.1.me_ref, s32[1,2,2]{2,1,0:T(2,128)S(1)} %copy-done.4, ...), custom_call_target="tpu_custom_call" | custom-call | flops 1073741824 | bytes 8388608 | tf_op jit(solution)/shard_map/own_slots/pallas_call | solution.py:399
  39.8 3.5 %all-to-all-start.1 = ((bf16[4,2,128,256]{3,2,1,0:T(8,128)(2,1)}), bf16[4,2,128,256]{3,2,1,0:T(8,128)(2,1)S(1)}, u32[]{:S(2)}, u32[]{:S(2)}) async-start(bf16[4,2,128,256]{3,2,1,0:T(8,128)(2,1)} %get-tuple-element.50), calls=%async_computation.1 | async-start | bytes 1048576 | tf_op jit(solution)/shard_map/all_to_all | solution.py:512
  43.2 5.9 %collective-permute-done.7.near_ref = bf16[2,2,128,256]{3,2,1,0:T(8,128)(2,1)S(1)} collective-permute-done((bf16[2,2,128,256]{3,2,1,0:T(8,128)(2,1)S(1)}, bf16[2,2,128,256]{3,2,1,0:T(8,128)(2,1)S(1)}, u32[]{:S(2)}, u32[]{:S(2)}) %collective-permute-start.7) | collective-permute-done | bytes 262176 | tf_op jit(solution)/shard_map/ppermute | solution.py:509
  49.8 3.7 %collective-permute-start.6 = (bf16[1,128,256]{2,1,0:T(8,128)(2,1)S(1)}, bf16[1,128,256]{2,1,0:T(8,128)(2,1)S(1)}, u32[]{:S(2)}, u32[]{:S(2)}) collective-permute-start(bf16[1,128,256]{2,1,0:T(8,128)(2,1)S(1)} %get-tuple-element.49), channel_id=1, source_target_pairs={{0,11},{1,10},{2,9},{3,8},{4,15},{5,14},{6,13},{7,12},{8,3},{9,2},... | collective-permute-start | bytes 196616 | tf_op jit(solution)/shard_map/ppermute | solution.py:509
  54.2 3.7 %collective-permute-start.9 = (bf16[1,128,256]{2,1,0:T(8,128)(2,1)S(1)}, bf16[1,128,256]{2,1,0:T(8,128)(2,1)S(1)}, u32[]{:S(2)}, u32[]{:S(2)}) collective-permute-start(bf16[1,128,256]{2,1,0:T(8,128)(2,1)S(1)} %get-tuple-element.53), channel_id=1, source_target_pairs={{0,10},{1,11},{2,8},{3,9},{4,14},{5,15},{6,12},{7,13},{8,2},{9,3},... | collective-permute-start | bytes 196616 | tf_op jit(solution)/shard_map/ppermute | solution.py:509
  57.9 1.0 %own_surfaces.1.part_ref = f32[2,256,1024]{2,1,0:T(8,128)S(1)} custom-call(s32[1]{0:T(128)} %bitcast.half_ref, bf16[4,2,128,256]{3,2,1,0:T(8,128)(2,1)S(1)} %all-to-all-done.1.own_ref, bf16[1024,1024]{1,0:T(8,128)(2,1)S(1)} %copy-done), custom_call_target="tpu_custom_call" | custom-call | flops 536870912 | bytes 2097152 | tf_op jit(solution)/shard_map/own_surfaces/pallas_call | solution.py:428
  58.9 2.0 %collective-permute-done.6.refs_1_ = bf16[1,128,256]{2,1,0:T(8,128)(2,1)S(1)} collective-permute-done((bf16[1,128,256]{2,1,0:T(8,128)(2,1)S(1)}, bf16[1,128,256]{2,1,0:T(8,128)(2,1)S(1)}, u32[]{:S(2)}, u32[]{:S(2)}) %collective-permute-start.6) | collective-permute-done | bytes 65568 | tf_op jit(solution)/shard_map/ppermute | solution.py:509
  60.8 1.5 %surface.2.refs_3_ = f32[2,256,1024]{2,1,0:T(8,128)} custom-call(s32[1]{0:T(128)} %bitcast.half_ref, s32[1]{0:T(128)} %bitcast.1.me_ref, s32[1]{0:T(128)S(6)} %copy.10.counts_ref, f32[2,256,1024]{2,1,0:T(8,128)S(1)} %own_surfaces.1.part_ref, bf16[2,2,128,256]{3,2,1,0:T(8,128)(2,1)S(1)} %collective-permute-done.7.near_ref, ...), custom_call_target="tpu_custom_call" | custom-call | flops 268435456 | bytes 2097152 | tf_op jit(solution)/shard_map/surface/pallas_call | solution.py:467
  62.3 1.3 %collective-permute-done.10.refs_1_ = bf16[1,128,256]{2,1,0:T(8,128)(2,1)S(1)} collective-permute-done((bf16[1,128,256]{2,1,0:T(8,128)(2,1)S(1)}, bf16[1,128,256]{2,1,0:T(8,128)(2,1)S(1)}, u32[]{:S(2)}, u32[]{:S(2)}) %collective-permute-start.10) | collective-permute-done | bytes 65568 | tf_op jit(solution)/shard_map/ppermute | solution.py:509
  63.6 1.4 %collective-permute-done.9.refs_0_ = bf16[1,128,256]{2,1,0:T(8,128)(2,1)S(1)} collective-permute-done((bf16[1,128,256]{2,1,0:T(8,128)(2,1)S(1)}, bf16[1,128,256]{2,1,0:T(8,128)(2,1)S(1)}, u32[]{:S(2)}, u32[]{:S(2)}) %collective-permute-start.9) | collective-permute-done | bytes 65568 | tf_op jit(solution)/shard_map/ppermute | solution.py:509
  65.1 1.5 %surface.3 = f32[2,256,1024]{2,1,0:T(8,128)} custom-call(s32[1]{0:T(128)} %bitcast.half_ref, s32[1]{0:T(128)} %bitcast.1.me_ref, s32[1]{0:T(128)S(6)} %copy.10.counts_ref, f32[2,256,1024]{2,1,0:T(8,128)S(1)} %own_surfaces.1.part_ref, bf16[2,2,128,256]{3,2,1,0:T(8,128)(2,1)S(1)} %collective-permute-done.7.near_ref, ...), custom_call_target="tpu_custom_call", output_to_operand_aliasing={{}: (9, {})} | custom-call | flops 268435456 | bytes 2097152 | tf_op jit(solution)/shard_map/surface/pallas_call | solution.py:467
  (28 shorter events, 1.7 us)
Async XLA Ops:
  0.0 7.6 %copy-start = (bf16[1024,1024]{1,0:T(8,128)(2,1)S(1)}, bf16[1024,1024]{1,0:T(8,128)(2,1)}, u32[]{:S(2)}) copy-start(bf16[1024,1024]{1,0:T(8,128)(2,1)} %constant.29.clone.table_hbm.table_ref.refs_2_) | copy-start | bytes 6291460
  0.0 7.6 %copy-start.1 = (f32[2,256,1024]{2,1,0:T(8,128)S(1)}, f32[2,256,1024]{2,1,0:T(8,128)}, u32[]{:S(2)}) copy-start(f32[2,256,1024]{2,1,0:T(8,128)} %tile_ref.1) | copy-start | bytes 6291460
  0.0 7.6 %copy-start.2 = (f32[8,1024]{1,0:T(8,128)S(1)}, f32[8,1024]{1,0:T(8,128)}, u32[]{:S(2)}) copy-start(f32[8,1024]{1,0:T(8,128)} %constant.30.clone.down_hbm.down_ref) | copy-start | bytes 98308
  0.0 7.6 %copy-start.3 = (f32[1,1024]{1,0:T(1,128)S(1)}, f32[1,1024]{1,0:T(1,128)}, u32[]{:S(2)}) copy-start(f32[1,1024]{1,0:T(1,128)} %constant.31.clone.across_hbm.across_ref) | copy-start | bytes 12292
  3.5 18.2 %collective-permute-start = (bf16[2,128,256]{2,1,0:T(8,128)(2,1)}, bf16[2,128,256]{2,1,0:T(8,128)(2,1)S(1)}, u32[]{:S(2)}, u32[]{:S(2)}) collective-permute-start(bf16[2,128,256]{2,1,0:T(8,128)(2,1)} %get-tuple-element.31), channel_id=1, source_target_pairs={{0,8},{1,9},{2,10},{3,11},{4,12},{5,13},{6,14},{7,15},{8,0},{9,1},... | collective-permute-start | bytes 393224 | tf_op jit(solution)/shard_map/ppermute | solution.py:509
  7.6 14.1 %collective-permute-start.1 = (bf16[2,128,256]{2,1,0:T(8,128)(2,1)}, bf16[2,128,256]{2,1,0:T(8,128)(2,1)S(1)}, u32[]{:S(2)}, u32[]{:S(2)}) collective-permute-start(bf16[2,128,256]{2,1,0:T(8,128)(2,1)} %get-tuple-element.32), channel_id=1, source_target_pairs={{0,9},{1,8},{2,11},{3,10},{4,13},{5,12},{6,15},{7,14},{8,1},{9,0},... | collective-permute-start | bytes 393224 | tf_op jit(solution)/shard_map/ppermute | solution.py:509
  7.6 9.6 %copy-start.4 = (s32[1,2,2]{2,1,0:T(2,128)S(1)}, s32[1,2,2]{2,1,0:T(2,128)}, u32[]{:S(2)}) copy-start(s32[1,2,2]{2,1,0:T(2,128)} %pairs_ref) | copy-start | bytes 52
  10.1 12.3 %all-to-all-start = ((bf16[4,2,128,256]{3,2,1,0:T(8,128)(2,1)}), bf16[4,2,128,256]{3,2,1,0:T(8,128)(2,1)S(1)}, u32[]{:S(2)}, u32[]{:S(2)}) async-start(bf16[4,2,128,256]{3,2,1,0:T(8,128)(2,1)} %get-tuple-element.38), calls=%async_computation | async-start | bytes 1048576 | tf_op jit(solution)/shard_map/all_to_all | solution.py:512
  13.6 17.4 %collective-permute-start.3 = (bf16[2,128,256]{2,1,0:T(8,128)(2,1)S(1)}, bf16[2,128,256]{2,1,0:T(8,128)(2,1)S(1)}, u32[]{:S(2)}, u32[]{:S(2)}) collective-permute-start(bf16[2,128,256]{2,1,0:T(8,128)(2,1)S(1)} %get-tuple-element.40), channel_id=1, source_target_pairs={{0,10},{1,11},{2,8},{3,9},{4,14},{5,15},{6,12},{7,13},{8,2},{9,3},... | collective-permute-start | bytes 393224 | tf_op jit(solution)/shard_map/ppermute | solution.py:509
  17.1 14.0 %collective-permute-start.4 = (bf16[2,128,256]{2,1,0:T(8,128)(2,1)S(1)}, bf16[2,128,256]{2,1,0:T(8,128)(2,1)S(1)}, u32[]{:S(2)}, u32[]{:S(2)}) collective-permute-start(bf16[2,128,256]{2,1,0:T(8,128)(2,1)S(1)} %get-tuple-element.41), channel_id=1, source_target_pairs={{0,11},{1,10},{2,9},{3,8},{4,15},{5,14},{6,13},{7,12},{8,3},{9,2},... | collective-permute-start | bytes 393224 | tf_op jit(solution)/shard_map/ppermute | solution.py:509
  17.3 13.7 %collective-permute-start.2 = (s32[1,2,2]{2,1,0:T(2,128)S(1)}, s32[1,2,2]{2,1,0:T(2,128)S(1)}, u32[]{:S(2)}, u32[]{:S(2)}) collective-permute-start(s32[1,2,2]{2,1,0:T(2,128)S(1)} %copy-done.4), channel_id=1, source_target_pairs={{0,8},{1,9},{2,10},{3,11},{4,12},{5,13},{6,14},{7,15},{8,0},{9,1},... | collective-permute-start | bytes 56 | tf_op jit(solution)/shard_map/ppermute | solution.py:509
  19.8 1.0 %copy-start.5 = (f32[128,1024]{1,0:T(8,128)S(1)}, f32[128,1024]{1,0:T(8,128)}, u32[]{:S(2)}) copy-start(f32[128,1024]{1,0:T(8,128)} %constant.32.clone.short_ref) | copy-start | bytes 1572868
  20.9 0.8 %copy-start.6 = (f32[128,1024]{1,0:T(8,128)}, f32[128,1024]{1,0:T(8,128)S(1)}, u32[]{:S(2)}) copy-start(f32[128,1024]{1,0:T(8,128)S(1)} %scaled_tables.1.short_ref) | copy-start | bytes 1572868
  22.4 1.0 %copy-start.7 = (f32[128,1024]{1,0:T(8,128)S(1)}, f32[128,1024]{1,0:T(8,128)}, u32[]{:S(2)}) copy-start(f32[128,1024]{1,0:T(8,128)} %copy-done.6) | copy-start | bytes 1572868
  33.5 15.6 %collective-permute-start.7 = (bf16[2,2,128,256]{3,2,1,0:T(8,128)(2,1)S(1)}, bf16[2,2,128,256]{3,2,1,0:T(8,128)(2,1)S(1)}, u32[]{:S(2)}, u32[]{:S(2)}) collective-permute-start(bf16[2,2,128,256]{3,2,1,0:T(8,128)(2,1)S(1)} %get-tuple-element.52), channel_id=1, source_target_pairs={{0,8},{1,9},{2,10},{3,11},{4,12},{5,13},{6,14},{7,15},{8,0},{9,1},... | collective-permute-start | bytes 786440 | tf_op jit(solution)/shard_map/ppermute | solution.py:509
  39.8 18.1 %all-to-all-start.1 = ((bf16[4,2,128,256]{3,2,1,0:T(8,128)(2,1)}), bf16[4,2,128,256]{3,2,1,0:T(8,128)(2,1)S(1)}, u32[]{:S(2)}, u32[]{:S(2)}) async-start(bf16[4,2,128,256]{3,2,1,0:T(8,128)(2,1)} %get-tuple-element.50), calls=%async_computation.1 | async-start | bytes 1048576 | tf_op jit(solution)/shard_map/all_to_all | solution.py:512
  49.8 11.1 %collective-permute-start.8 = (bf16[2,128,256]{2,1,0:T(8,128)(2,1)}, bf16[2,128,256]{2,1,0:T(8,128)(2,1)S(1)}, u32[]{:S(2)}, u32[]{:S(2)}) collective-permute-start(bf16[2,128,256]{2,1,0:T(8,128)(2,1)} %slice_bitcast_fusion), channel_id=1, source_target_pairs={{0,1},{1,0},{2,3},{3,2},{4,5},{5,4},{6,7},{7,6},{8,9},{9,8},{10,11... | collective-permute-start | bytes 393224 | tf_op jit(solution)/shard_map/ppermute | solution.py:515
  49.8 9.1 %collective-permute-start.5 = (bf16[1,128,256]{2,1,0:T(8,128)(2,1)S(1)}, bf16[1,128,256]{2,1,0:T(8,128)(2,1)S(1)}, u32[]{:S(2)}, u32[]{:S(2)}) collective-permute-start(bf16[1,128,256]{2,1,0:T(8,128)(2,1)S(1)} %get-tuple-element.48), channel_id=1, source_target_pairs={{0,10},{1,11},{2,8},{3,9},{4,14},{5,15},{6,12},{7,13},{8,2},{9,3},... | collective-permute-start | bytes 196616 | tf_op jit(solution)/shard_map/ppermute | solution.py:509
  49.8 11.1 %collective-permute-start.6 = (bf16[1,128,256]{2,1,0:T(8,128)(2,1)S(1)}, bf16[1,128,256]{2,1,0:T(8,128)(2,1)S(1)}, u32[]{:S(2)}, u32[]{:S(2)}) collective-permute-start(bf16[1,128,256]{2,1,0:T(8,128)(2,1)S(1)} %get-tuple-element.49), channel_id=1, source_target_pairs={{0,11},{1,10},{2,9},{3,8},{4,15},{5,14},{6,13},{7,12},{8,3},{9,2},... | collective-permute-start | bytes 196616 | tf_op jit(solution)/shard_map/ppermute | solution.py:509
  54.1 9.6 %collective-permute-start.10 = (bf16[1,128,256]{2,1,0:T(8,128)(2,1)S(1)}, bf16[1,128,256]{2,1,0:T(8,128)(2,1)S(1)}, u32[]{:S(2)}, u32[]{:S(2)}) collective-permute-start(bf16[1,128,256]{2,1,0:T(8,128)(2,1)S(1)} %get-tuple-element.54), channel_id=1, source_target_pairs={{0,11},{1,10},{2,9},{3,8},{4,15},{5,14},{6,13},{7,12},{8,3},{9,2},... | collective-permute-start | bytes 196616 | tf_op jit(solution)/shard_map/ppermute | solution.py:509
  54.2 10.9 %collective-permute-start.9 = (bf16[1,128,256]{2,1,0:T(8,128)(2,1)S(1)}, bf16[1,128,256]{2,1,0:T(8,128)(2,1)S(1)}, u32[]{:S(2)}, u32[]{:S(2)}) collective-permute-start(bf16[1,128,256]{2,1,0:T(8,128)(2,1)S(1)} %get-tuple-element.53), channel_id=1, source_target_pairs={{0,10},{1,11},{2,8},{3,9},{4,14},{5,15},{6,12},{7,13},{8,2},{9,3},... | collective-permute-start | bytes 196616 | tf_op jit(solution)/shard_map/ppermute | solution.py:509

commit v19 on v16

--- a/solution.py
+++ b/solution.py
@@ -36,41 +36,48 @@
 FINE = 32
 
 
+LANES = 128
+
+
 def short_tables(height):
+    coarse = height // FINE
     column = np.arange(height)[None, :]
-    rough = 2.0 * math.pi / height * (np.arange(height // FINE)[:, None] * FINE * column % height)
+    rough = 2.0 * math.pi / height * (np.arange(coarse)[:, None] * FINE * column % height)
     small = 2.0 * math.pi / height * (np.arange(FINE)[:, None] * column % height)
-    short = [np.cos(small), np.sin(small), np.cos(rough), np.sin(rough)]
-    return jnp.asarray(np.concatenate(short), jnp.float32)
-
-
-def scaled_tables(height, after):
+    rough = rough[:, :LANES]
+    return (
+        jnp.asarray(np.concatenate([np.cos(small), np.sin(small)]), jnp.float32),
+        jnp.asarray(np.concatenate([np.cos(rough), np.sin(rough)]), jnp.float32),
+    )
+
+
+def scaled_tables(height):
     factor = 1.0 / math.sqrt(height)
 
-    def body(short_ref, *refs):
-        refs[-1][: 2 * FINE] = short_ref[: 2 * FINE]
-        refs[-1][2 * FINE :] = short_ref[2 * FINE :] * factor
+    def body(fine_ref, rough_ref, fine_out, rough_out):
+        fine_out[...] = fine_ref[...]
+        rough_out[...] = rough_ref[...] * factor
 
     short = short_tables(height)
     return pl.pallas_call(
         body,
-        in_specs=[pl.BlockSpec(memory_space=pltpu.VMEM)]
-        + [pl.BlockSpec(memory_space=pl.ANY)] * len(after),
-        out_specs=pl.BlockSpec(memory_space=pltpu.VMEM),
-        out_shape=jax.ShapeDtypeStruct(short.shape, short.dtype),
-        compiler_params=params(),
-        cost_estimate=cost(1 << 33, 8 * short.size),
+        in_specs=[pl.BlockSpec(memory_space=pltpu.VMEM)] * 2,
+        out_specs=[pl.BlockSpec(memory_space=pltpu.VMEM)] * 2,
+        out_shape=[jax.ShapeDtypeStruct(table.shape, table.dtype) for table in short],
+        compiler_params=params(),
+        cost_estimate=cost(1 << 33, 8 * short[0].size),
         name="scaled_tables",
-    )(short, *after)
-
-
-def make_table(short_ref, out_ref, first, rows):
-    height = short_ref.shape[1]
+    )(*short)
+
+
+def make_table(fine_ref, rough_ref, out_ref, first, rows):
+    height = fine_ref.shape[1]
     coarse = height // FINE
-    sc, ss = short_ref[:FINE], short_ref[FINE : 2 * FINE]
+    copies = height // LANES
+    sc, ss = fine_ref[:FINE], fine_ref[FINE:]
     for j in range(first // FINE, (first + rows) // FINE):
-        a = 2 * FINE + j
-        rc, rs = short_ref[a : a + 1, :], short_ref[a + coarse : a + coarse + 1, :]
+        rc = jnp.concatenate([rough_ref[j : j + 1, :]] * copies, axis=1)
+        rs = jnp.concatenate([rough_ref[coarse + j : coarse + j + 1, :]] * copies, axis=1)
         here = slice(j * FINE, (j + 1) * FINE)
         out_ref[here, :height] = (rc * sc - rs * ss).astype(jnp.bfloat16)
         out_ref[here, height:] = (rs * sc + rc * ss).astype(jnp.bfloat16)
@@ -309,10 +316,11 @@
     peers, count, double, rows = pieces.shape
     height = peers * rows
 
-    def body(half_ref, me_ref, pieces_ref, near_a, near_b, short_ref, spectra, edge, share, table_ref):
+    def body(half_ref, me_ref, pieces_ref, near_a, near_b, *refs):
+        fine_ref, rough_ref, spectra, edge, share, table_ref = refs
         total = None
         for k in range(peers):
-            make_table(short_ref, table_ref, k * rows, rows)
+            make_table(fine_ref, rough_ref, table_ref, k * rows, rows)
             term = jnp.dot(
                 pieces_ref[k].reshape(count * double, rows),
                 table_ref[k * rows : (k + 1) * rows],
@@ -325,7 +333,7 @@
     return pl.pallas_call(
         body,
         in_specs=[pl.BlockSpec(memory_space=pltpu.SMEM)] * 2
-        + [pl.BlockSpec(memory_space=pltpu.VMEM)] * 4,
+        + [pl.BlockSpec(memory_space=pltpu.VMEM)] * 5,
         out_specs=[pl.BlockSpec(memory_space=pltpu.VMEM)] * 4,
         out_shape=[
             jax.ShapeDtypeStruct((count, 2, double // 2, height), jnp.bfloat16),
@@ -336,7 +344,7 @@
         compiler_params=params(),
         cost_estimate=cost(6 * count * double * height * height, 8 * height * height),
         name="own_spectra",
-    )(*place, pieces, *near, short)
+    )(*place, pieces, *near, *short)
 
 
 def partner_slots(place, theirs, pieces, share, table, spectra, edge):
@@ -527,7 +535,7 @@
     theirs = across(pairs, 0)
     place = (scalar(half), scalar(me))
     spectra, edge, share, table_h = own_spectra(
-        place, mine, arrived[:2], scaled_tables(height, [])
+        place, mine, arrived[:2], scaled_tables(height)
     )
     near, spectra, edge, phases = partner_slots(
         place, theirs, arrived[2:], share, table_h, spectra, edge

time: 61.9 us -> 61.9 us (level)
    unnamed x16 -> x18, local copies, waits for them, and re-layouts: 2.9 us -> 2.62 us
where the time goes in v19:
time: 61.9 us; the launch traced here: 61.4 us
  starting transfers between devices  23.4 us (38%)
  waiting for transfers between devices  17.6 us (28%)
  Pallas kernels  17 us (27%)
  local copies, waits for them, and re-layouts  2.63 us (4%)
  between operations  0.77 us (1%)
    ppermute x8, starting transfers between devices, across(): return lax.ppermute(value, axes, moves)  16.4 us
    ppermute x8, waiting for transfers between devices, across(): return lax.ppermute(value, axes, moves)  13.7 us
    all_to_all x2, starting transfers between devices, along(): return lax.all_to_all(blocks, 'rows', split_axis=0, concat_axis=0)  6.94 us
    all_to_all x2, waiting for transfers between devices, along(): return lax.all_to_all(blocks, 'rows', split_axis=0, concat_axis=0)  3.85 us
    pallas_call x1, Pallas kernels, own_slots(): pl.pallas_call(body, in_specs=[pl.BlockSpec(memory_space=pltpu.SMEM)] * 3...  3.58 us
    pallas_call x1, Pallas kernels, near_columns(): pl.pallas_call(body, grid_spec=pltpu.PrefetchScalarGridSpec(num_scalar_pr...  3.44 us
    unnamed x18, local copies, waits for them, and re-layouts  2.62 us
    pallas_call x1, Pallas kernels, partner_slots(): pl.pallas_call(body, in_specs=[pl.BlockSpec(memory_space=pltpu.SMEM)] * 3...  2.53 us
  transfers between devices with their start and end apart: 11, of which 6 were waited for; matrix products, arithmetic and copies ran while one was open for 0% of the time, Pallas kernels for 15%

profile of v19, /device:TPU:0, one launch (start us, length us, event | category | flops | bytes accessed | tf_op | source)
XLA Modules:
  0.0 61.4 jit_solution(14133205359196464856)
XLA Ops:
  0.0 3.4 %near_columns.1 = (bf16[2,128,256]{2,1,0:T(8,128)(2,1)}, bf16[2,128,256]{2,1,0:T(8,128)(2,1)}) custom-call(s32[1]{0:T(128)} %bitcast.half_ref, s32[1]{0:T(128)} %bitcast.1.me_ref, f32[2,256,1024]{2,1,0:T(8,128)} %tile_ref.1, f32[8,1024]{1,0:T(8,128)} %constant.32.clone.down_hbm.down_ref, f32[1,1024]{1,0:T(1,128)} %constant.33.clone.across_hbm.across_ref, ...), custom_call_target="tpu_custom_call" | custom-call | flops 268435456 | bytes 2621440 | tf_op jit(solution)/shard_map/near_columns/pallas_call | solution.py:151
  3.5 4.1 %collective-permute-start = (bf16[2,128,256]{2,1,0:T(8,128)(2,1)}, bf16[2,128,256]{2,1,0:T(8,128)(2,1)S(1)}, u32[]{:S(2)}, u32[]{:S(2)}) collective-permute-start(bf16[2,128,256]{2,1,0:T(8,128)(2,1)} %get-tuple-element.31), channel_id=1, source_target_pairs={{0,8},{1,9},{2,10},{3,11},{4,12},{5,13},{6,14},{7,15},{8,0},{9,1},... | collective-permute-start | bytes 393224 | tf_op jit(solution)/shard_map/ppermute | solution.py:515
  7.6 2.4 %rest_columns.1 = (bf16[4,2,128,256]{3,2,1,0:T(8,128)(2,1)}, bf16[2,128,256]{2,1,0:T(8,128)(2,1)S(1)}, bf16[2,128,256]{2,1,0:T(8,128)(2,1)S(1)}) custom-call(s32[1]{0:T(128)} %bitcast.2.half_ref, s32[1]{0:T(128)} %bitcast.1.me_ref, f32[2,256,1024]{2,1,0:T(8,128)S(1)} %copy-done.1, f32[8,1024]{1,0:T(8,128)S(1)} %copy-done.2, f32[1,1024]{1,0:T(1,128)S(1)} %copy-done.3, ...), custom_call_target="tpu_custom_call" | custom-call | flops 805306368 | bytes 4194304 | tf_op jit(solution)/shard_map/rest_columns/pallas_call | solution.py:199
  10.1 3.5 %all-to-all-start = ((bf16[4,2,128,256]{3,2,1,0:T(8,128)(2,1)}), bf16[4,2,128,256]{3,2,1,0:T(8,128)(2,1)S(1)}, u32[]{:S(2)}, u32[]{:S(2)}) async-start(bf16[4,2,128,256]{3,2,1,0:T(8,128)(2,1)} %get-tuple-element.38), calls=%async_computation | async-start | bytes 1048576 | tf_op jit(solution)/shard_map/all_to_all | solution.py:518
  13.5 3.5 %collective-permute-start.3 = (bf16[2,128,256]{2,1,0:T(8,128)(2,1)S(1)}, bf16[2,128,256]{2,1,0:T(8,128)(2,1)S(1)}, u32[]{:S(2)}, u32[]{:S(2)}) collective-permute-start(bf16[2,128,256]{2,1,0:T(8,128)(2,1)S(1)} %get-tuple-element.42), channel_id=1, source_target_pairs={{0,10},{1,11},{2,8},{3,9},{4,14},{5,15},{6,12},{7,13},{8,2},{9,3},... | collective-permute-start | bytes 393224 | tf_op jit(solution)/shard_map/ppermute | solution.py:515
  17.3 2.5 %collective-permute-start.2 = (s32[1,2,2]{2,1,0:T(2,128)S(1)}, s32[1,2,2]{2,1,0:T(2,128)S(1)}, u32[]{:S(2)}, u32[]{:S(2)}) collective-permute-start(s32[1,2,2]{2,1,0:T(2,128)S(1)} %copy-done.4), channel_id=1, source_target_pairs={{0,8},{1,9},{2,10},{3,11},{4,12},{5,13},{6,14},{7,15},{8,0},{9,1},... | collective-permute-start | bytes 56 | tf_op jit(solution)/shard_map/ppermute | solution.py:515
  19.8 0.9 %copy-done.5 = f32[64,1024]{1,0:T(8,128)S(1)} copy-done((f32[64,1024]{1,0:T(8,128)S(1)}, f32[64,1024]{1,0:T(8,128)}, u32[]{:S(2)}) %copy-start.5) | copy-done | bytes 262168
  20.8 0.7 %copy-done.7 = f32[64,1024]{1,0:T(8,128)} copy-done((f32[64,1024]{1,0:T(8,128)}, f32[64,1024]{1,0:T(8,128)S(1)}, u32[]{:S(2)}) %copy-start.7) | copy-done | bytes 262168
  21.5 0.9 %all-to-all-done.pieces_ref = bf16[4,2,128,256]{3,2,1,0:T(8,128)(2,1)S(1)} async-done(((bf16[4,2,128,256]{3,2,1,0:T(8,128)(2,1)}), bf16[4,2,128,256]{3,2,1,0:T(8,128)(2,1)S(1)}, u32[]{:S(2)}, u32[]{:S(2)}) %all-to-all-start) | async-done | bytes 524320 | tf_op jit(solution)/shard_map/all_to_all | solution.py:518
  22.4 0.9 %copy-done.8 = f32[64,1024]{1,0:T(8,128)S(1)} copy-done((f32[64,1024]{1,0:T(8,128)S(1)}, f32[64,1024]{1,0:T(8,128)}, u32[]{:S(2)}) %copy-start.8) | copy-done | bytes 262168
  23.3 2.0 %own_spectra.1 = (bf16[2,2,64,1024]{3,2,1,0:T(8,128)(2,1)S(1)}, bf16[2,2,16,1024]{3,2,1,0:T(8,128)(2,1)S(1)}, f32[256,2048]{1,0:T(8,128)S(1)}, bf16[1024,2048]{1,0:T(8,128)(2,1)S(1)}) custom-call(s32[1]{0:T(128)} %bitcast.half_ref, s32[1]{0:T(128)} %bitcast.1.me_ref, bf16[4,2,128,256]{3,2,1,0:T(8,128)(2,1)S(1)} %all-to-all-done.pieces_ref, ...), custom_call_target="tpu_custom_call" | custom-call | flops 1610612736 | bytes 8388608 | tf_op jit(solution)/shard_map/own_spectra/pallas_call | solution.py:333
  25.3 5.6 %collective-permute-done.2.theirs_ref = s32[1,2,2]{2,1,0:T(2,128)S(1)} collective-permute-done((s32[1,2,2]{2,1,0:T(2,128)S(1)}, s32[1,2,2]{2,1,0:T(2,128)S(1)}, u32[]{:S(2)}, u32[]{:S(2)}) %collective-permute-start.2) | collective-permute-done | bytes 48 | tf_op jit(solution)/shard_map/ppermute | solution.py:515
  31.0 2.5 %partner_slots.1 = (bf16[2,2,128,256]{3,2,1,0:T(8,128)(2,1)S(1)}, bf16[4,2,64,1024]{3,2,1,0:T(8,128)(2,1)S(1)}, bf16[4,2,16,1024]{3,2,1,0:T(8,128)(2,1)S(1)}, bf16[4,64,1024]{2,1,0:T(8,128)(2,1)S(1)}) custom-call(s32[1]{0:T(128)} %bitcast.half_ref, s32[1]{0:T(128)} %bitcast.1.me_ref, s32[1,2,2]{2,1,0:T(2,128)S(1)} %collective-permute-done.2.theirs_ref, ...), custom_call_target="tpu_custom_call" | custom-call | flops 2147483648 | bytes 8388608 | tf_op jit(solution)/shard_map/partner_slots/pallas_call | solution.py:372
  33.5 2.4 %collective-permute-start.7 = (bf16[2,2,128,256]{3,2,1,0:T(8,128)(2,1)S(1)}, bf16[2,2,128,256]{3,2,1,0:T(8,128)(2,1)S(1)}, u32[]{:S(2)}, u32[]{:S(2)}) collective-permute-start(bf16[2,2,128,256]{3,2,1,0:T(8,128)(2,1)S(1)} %get-tuple-element.54), channel_id=1, source_target_pairs={{0,8},{1,9},{2,10},{3,11},{4,12},{5,13},{6,14},{7,15},{8,0},{9,1},... | collective-permute-start | bytes 786440 | tf_op jit(solution)/shard_map/ppermute | solution.py:515
  35.9 3.6 %own_slots.1 = (bf16[4,2,128,256]{3,2,1,0:T(8,128)(2,1)}, bf16[2,128,256]{2,1,0:T(8,128)(2,1)}, bf16[2,128,256]{2,1,0:T(8,128)(2,1)S(1)}) custom-call(s32[1]{0:T(128)} %bitcast.half_ref, s32[1]{0:T(128)} %bitcast.1.me_ref, s32[1,2,2]{2,1,0:T(2,128)S(1)} %copy-done.4, bf16[1024,2048]{1,0:T(8,128)(2,1)S(1)} %get-tuple-element.41.refs_3_.table_ref, ...), custom_call_target="tpu_custom_call" | custom-call | flops 1073741824 | bytes 8388608 | tf_op jit(solution)/shard_map/own_slots/pallas_call | solution.py:404
  39.5 3.5 %all-to-all-start.1 = ((bf16[4,2,128,256]{3,2,1,0:T(8,128)(2,1)}), bf16[4,2,128,256]{3,2,1,0:T(8,128)(2,1)S(1)}, u32[]{:S(2)}, u32[]{:S(2)}) async-start(bf16[4,2,128,256]{3,2,1,0:T(8,128)(2,1)} %get-tuple-element.52), calls=%async_computation.1 | async-start | bytes 1048576 | tf_op jit(solution)/shard_map/all_to_all | solution.py:518
  43.0 2.0 %collective-permute-start.5 = (bf16[2,128,256]{2,1,0:T(8,128)(2,1)}, bf16[2,128,256]{2,1,0:T(8,128)(2,1)S(1)}, u32[]{:S(2)}, u32[]{:S(2)}) collective-permute-start(bf16[2,128,256]{2,1,0:T(8,128)(2,1)} %get-tuple-element.50), channel_id=1, source_target_pairs={{0,10},{1,11},{2,8},{3,9},{4,14},{5,15},{6,12},{7,13},{8,2},{9,3},... | collective-permute-start | bytes 393224 | tf_op jit(solution)/shard_map/ppermute | solution.py:515
  45.0 1.6 %collective-permute-start.6 = (bf16[2,128,256]{2,1,0:T(8,128)(2,1)S(1)}, bf16[2,128,256]{2,1,0:T(8,128)(2,1)S(1)}, u32[]{:S(2)}, u32[]{:S(2)}) collective-permute-start(bf16[2,128,256]{2,1,0:T(8,128)(2,1)S(1)} %get-tuple-element.51), channel_id=1, source_target_pairs={{0,11},{1,10},{2,9},{3,8},{4,15},{5,14},{6,13},{7,12},{8,3},{9,2},... | collective-permute-start | bytes 393224 | tf_op jit(solution)/shard_map/ppermute | solution.py:515
  46.6 2.6 %collective-permute-done.7.refs_0_ = bf16[2,2,128,256]{3,2,1,0:T(8,128)(2,1)S(1)} collective-permute-done((bf16[2,2,128,256]{3,2,1,0:T(8,128)(2,1)S(1)}, bf16[2,2,128,256]{3,2,1,0:T(8,128)(2,1)S(1)}, u32[]{:S(2)}, u32[]{:S(2)}) %collective-permute-start.7) | collective-permute-done | bytes 262176 | tf_op jit(solution)/shard_map/ppermute | solution.py:515
  50.0 2.9 %all-to-all-done.1.own_ref = bf16[4,2,128,256]{3,2,1,0:T(8,128)(2,1)S(1)} async-done(((bf16[4,2,128,256]{3,2,1,0:T(8,128)(2,1)}), bf16[4,2,128,256]{3,2,1,0:T(8,128)(2,1)S(1)}, u32[]{:S(2)}, u32[]{:S(2)}) %all-to-all-start.1) | async-done | bytes 524320 | tf_op jit(solution)/shard_map/all_to_all | solution.py:518
  53.0 1.0 %own_surfaces.1.part_ref = f32[2,256,1024]{2,1,0:T(8,128)S(1)} custom-call(s32[1]{0:T(128)} %bitcast.half_ref, bf16[4,2,128,256]{3,2,1,0:T(8,128)(2,1)S(1)} %all-to-all-done.1.own_ref, bf16[1024,1024]{1,0:T(8,128)(2,1)S(1)} %copy-done), custom_call_target="tpu_custom_call" | custom-call | flops 536870912 | bytes 2097152 | tf_op jit(solution)/shard_map/own_surfaces/pallas_call | solution.py:433
  54.0 4.3 %collective-permute-done.5.refs_2_ = bf16[2,128,256]{2,1,0:T(8,128)(2,1)S(1)} collective-permute-done((bf16[2,128,256]{2,1,0:T(8,128)(2,1)}, bf16[2,128,256]{2,1,0:T(8,128)(2,1)S(1)}, u32[]{:S(2)}, u32[]{:S(2)}) %collective-permute-start.5) | collective-permute-done | bytes 131104 | tf_op jit(solution)/shard_map/ppermute | solution.py:515
  58.3 1.1 %collective-permute-done.6.refs_3_ = bf16[2,128,256]{2,1,0:T(8,128)(2,1)S(1)} collective-permute-done((bf16[2,128,256]{2,1,0:T(8,128)(2,1)S(1)}, bf16[2,128,256]{2,1,0:T(8,128)(2,1)S(1)}, u32[]{:S(2)}, u32[]{:S(2)}) %collective-permute-start.6) | collective-permute-done | bytes 131104 | tf_op jit(solution)/shard_map/ppermute | solution.py:515
  59.4 2.0 %surfaces.1 = f32[2,256,1024]{2,1,0:T(8,128)} custom-call(s32[1]{0:T(128)} %bitcast.half_ref, s32[1]{0:T(128)} %bitcast.1.me_ref, s32[1]{0:T(128)S(6)} %copy.9.counts_ref, f32[2,256,1024]{2,1,0:T(8,128)S(1)} %own_surfaces.1.part_ref, bf16[2,2,128,256]{3,2,1,0:T(8,128)(2,1)S(1)} %collective-permute-done.7.refs_0_, ...), custom_call_target="tpu_custom_call" | custom-call | flops 536870912 | bytes 4194304 | tf_op jit(solution)/shard_map/surfaces/pallas_call | solution.py:477
  (25 shorter events, 0.4 us)
Async XLA Ops:
  0.0 7.6 %copy-start = (bf16[1024,1024]{1,0:T(8,128)(2,1)S(1)}, bf16[1024,1024]{1,0:T(8,128)(2,1)}, u32[]{:S(2)}) copy-start(bf16[1024,1024]{1,0:T(8,128)(2,1)} %constant.31.clone.table_hbm.table_ref.refs_4_) | copy-start | bytes 6291460
  0.0 7.6 %copy-start.1 = (f32[2,256,1024]{2,1,0:T(8,128)S(1)}, f32[2,256,1024]{2,1,0:T(8,128)}, u32[]{:S(2)}) copy-start(f32[2,256,1024]{2,1,0:T(8,128)} %tile_ref.1) | copy-start | bytes 6291460
  0.0 7.6 %copy-start.2 = (f32[8,1024]{1,0:T(8,128)S(1)}, f32[8,1024]{1,0:T(8,128)}, u32[]{:S(2)}) copy-start(f32[8,1024]{1,0:T(8,128)} %constant.32.clone.down_hbm.down_ref) | copy-start | bytes 98308
  0.0 7.6 %copy-start.3 = (f32[1,1024]{1,0:T(1,128)S(1)}, f32[1,1024]{1,0:T(1,128)}, u32[]{:S(2)}) copy-start(f32[1,1024]{1,0:T(1,128)} %constant.33.clone.across_hbm.across_ref) | copy-start | bytes 12292
  3.5 18.0 %collective-permute-start = (bf16[2,128,256]{2,1,0:T(8,128)(2,1)}, bf16[2,128,256]{2,1,0:T(8,128)(2,1)S(1)}, u32[]{:S(2)}, u32[]{:S(2)}) collective-permute-start(bf16[2,128,256]{2,1,0:T(8,128)(2,1)} %get-tuple-element.31), channel_id=1, source_target_pairs={{0,8},{1,9},{2,10},{3,11},{4,12},{5,13},{6,14},{7,15},{8,0},{9,1},... | collective-permute-start | bytes 393224 | tf_op jit(solution)/shard_map/ppermute | solution.py:515
  7.6 13.9 %collective-permute-start.1 = (bf16[2,128,256]{2,1,0:T(8,128)(2,1)}, bf16[2,128,256]{2,1,0:T(8,128)(2,1)S(1)}, u32[]{:S(2)}, u32[]{:S(2)}) collective-permute-start(bf16[2,128,256]{2,1,0:T(8,128)(2,1)} %get-tuple-element.32), channel_id=1, source_target_pairs={{0,9},{1,8},{2,11},{3,10},{4,13},{5,12},{6,15},{7,14},{8,1},{9,0},... | collective-permute-start | bytes 393224 | tf_op jit(solution)/shard_map/ppermute | solution.py:515
  7.6 9.6 %copy-start.4 = (s32[1,2,2]{2,1,0:T(2,128)S(1)}, s32[1,2,2]{2,1,0:T(2,128)}, u32[]{:S(2)}) copy-start(s32[1,2,2]{2,1,0:T(2,128)} %pairs_ref) | copy-start | bytes 52
  7.6 12.2 %copy-start.6 = (f32[64,128]{1,0:T(8,128)S(1)}, f32[64,128]{1,0:T(8,128)}, u32[]{:S(2)}) copy-start(f32[64,128]{1,0:T(8,128)} %constant.35.clone.rough_ref) | copy-start | bytes 98308
  10.1 12.3 %all-to-all-start = ((bf16[4,2,128,256]{3,2,1,0:T(8,128)(2,1)}), bf16[4,2,128,256]{3,2,1,0:T(8,128)(2,1)S(1)}, u32[]{:S(2)}, u32[]{:S(2)}) async-start(bf16[4,2,128,256]{3,2,1,0:T(8,128)(2,1)} %get-tuple-element.38), calls=%async_computation | async-start | bytes 1048576 | tf_op jit(solution)/shard_map/all_to_all | solution.py:518
  13.5 17.4 %collective-permute-start.3 = (bf16[2,128,256]{2,1,0:T(8,128)(2,1)S(1)}, bf16[2,128,256]{2,1,0:T(8,128)(2,1)S(1)}, u32[]{:S(2)}, u32[]{:S(2)}) collective-permute-start(bf16[2,128,256]{2,1,0:T(8,128)(2,1)S(1)} %get-tuple-element.42), channel_id=1, source_target_pairs={{0,10},{1,11},{2,8},{3,9},{4,14},{5,15},{6,12},{7,13},{8,2},{9,3},... | collective-permute-start | bytes 393224 | tf_op jit(solution)/shard_map/ppermute | solution.py:515
  17.0 14.0 %collective-permute-start.4 = (bf16[2,128,256]{2,1,0:T(8,128)(2,1)S(1)}, bf16[2,128,256]{2,1,0:T(8,128)(2,1)S(1)}, u32[]{:S(2)}, u32[]{:S(2)}) collective-permute-start(bf16[2,128,256]{2,1,0:T(8,128)(2,1)S(1)} %get-tuple-element.43), channel_id=1, source_target_pairs={{0,11},{1,10},{2,9},{3,8},{4,15},{5,14},{6,13},{7,12},{8,3},{9,2},... | collective-permute-start | bytes 393224 | tf_op jit(solution)/shard_map/ppermute | solution.py:515
  17.3 13.7 %collective-permute-start.2 = (s32[1,2,2]{2,1,0:T(2,128)S(1)}, s32[1,2,2]{2,1,0:T(2,128)S(1)}, u32[]{:S(2)}, u32[]{:S(2)}) collective-permute-start(s32[1,2,2]{2,1,0:T(2,128)S(1)} %copy-done.4), channel_id=1, source_target_pairs={{0,8},{1,9},{2,10},{3,11},{4,12},{5,13},{6,14},{7,15},{8,0},{9,1},... | collective-permute-start | bytes 56 | tf_op jit(solution)/shard_map/ppermute | solution.py:515
  19.8 1.0 %copy-start.5 = (f32[64,1024]{1,0:T(8,128)S(1)}, f32[64,1024]{1,0:T(8,128)}, u32[]{:S(2)}) copy-start(f32[64,1024]{1,0:T(8,128)} %constant.34.clone.fine_ref) | copy-start | bytes 786436
  20.8 0.7 %copy-start.7 = (f32[64,1024]{1,0:T(8,128)}, f32[64,1024]{1,0:T(8,128)S(1)}, u32[]{:S(2)}) copy-start(f32[64,1024]{1,0:T(8,128)S(1)} %get-tuple-element.39.refs_0_) | copy-start | bytes 786436
  22.4 1.0 %copy-start.8 = (f32[64,1024]{1,0:T(8,128)S(1)}, f32[64,1024]{1,0:T(8,128)}, u32[]{:S(2)}) copy-start(f32[64,1024]{1,0:T(8,128)} %copy-done.7) | copy-start | bytes 786436
  33.5 15.8 %collective-permute-start.7 = (bf16[2,2,128,256]{3,2,1,0:T(8,128)(2,1)S(1)}, bf16[2,2,128,256]{3,2,1,0:T(8,128)(2,1)S(1)}, u32[]{:S(2)}, u32[]{:S(2)}) collective-permute-start(bf16[2,2,128,256]{3,2,1,0:T(8,128)(2,1)S(1)} %get-tuple-element.54), channel_id=1, source_target_pairs={{0,8},{1,9},{2,10},{3,11},{4,12},{5,13},{6,14},{7,15},{8,0},{9,1},... | collective-permute-start | bytes 786440 | tf_op jit(solution)/shard_map/ppermute | solution.py:515
  39.5 13.5 %all-to-all-start.1 = ((bf16[4,2,128,256]{3,2,1,0:T(8,128)(2,1)}), bf16[4,2,128,256]{3,2,1,0:T(8,128)(2,1)S(1)}, u32[]{:S(2)}, u32[]{:S(2)}) async-start(bf16[4,2,128,256]{3,2,1,0:T(8,128)(2,1)} %get-tuple-element.52), calls=%async_computation.1 | async-start | bytes 1048576 | tf_op jit(solution)/shard_map/all_to_all | solution.py:518
  43.0 15.3 %collective-permute-start.5 = (bf16[2,128,256]{2,1,0:T(8,128)(2,1)}, bf16[2,128,256]{2,1,0:T(8,128)(2,1)S(1)}, u32[]{:S(2)}, u32[]{:S(2)}) collective-permute-start(bf16[2,128,256]{2,1,0:T(8,128)(2,1)} %get-tuple-element.50), channel_id=1, source_target_pairs={{0,10},{1,11},{2,8},{3,9},{4,14},{5,15},{6,12},{7,13},{8,2},{9,3},... | collective-permute-start | bytes 393224 | tf_op jit(solution)/shard_map/ppermute | solution.py:515
  45.0 14.4 %collective-permute-start.6 = (bf16[2,128,256]{2,1,0:T(8,128)(2,1)S(1)}, bf16[2,128,256]{2,1,0:T(8,128)(2,1)S(1)}, u32[]{:S(2)}, u32[]{:S(2)}) collective-permute-start(bf16[2,128,256]{2,1,0:T(8,128)(2,1)S(1)} %get-tuple-element.51), channel_id=1, source_target_pairs={{0,11},{1,10},{2,9},{3,8},{4,15},{5,14},{6,13},{7,12},{8,3},{9,2},... | collective-permute-start | bytes 393224 | tf_op jit(solution)/shard_map/ppermute | solution.py:515
  49.3 10.1 %collective-permute-start.8 = (bf16[2,128,256]{2,1,0:T(8,128)(2,1)S(1)}, bf16[2,128,256]{2,1,0:T(8,128)(2,1)S(1)}, u32[]{:S(2)}, u32[]{:S(2)}) collective-permute-start(bf16[2,128,256]{2,1,0:T(8,128)(2,1)S(1)} %slice_bitcast_fusion), channel_id=1, source_target_pairs={{0,1},{1,0},{2,3},{3,2},{4,5},{5,4},{6,7},{7,6},{8,9},{9,8},{10,11... | collective-permute-start | bytes 393224 | tf_op jit(solution)/shard_map/ppermute | solution.py:521

commit v20 on v19

--- a/solution.py
+++ b/solution.py
@@ -336,8 +336,8 @@
         + [pl.BlockSpec(memory_space=pltpu.VMEM)] * 5,
         out_specs=[pl.BlockSpec(memory_space=pltpu.VMEM)] * 4,
         out_shape=[
-            jax.ShapeDtypeStruct((count, 2, double // 2, height), jnp.bfloat16),
-            jax.ShapeDtypeStruct((count, 2, 16, height), jnp.bfloat16),
+            jax.ShapeDtypeStruct((2 * count, 2, double // 2, height), jnp.bfloat16),
+            jax.ShapeDtypeStruct((2 * count, 2, 16, height), jnp.bfloat16),
             jax.ShapeDtypeStruct((count * double, 2 * height), jnp.float32),
             jax.ShapeDtypeStruct((height, 2 * height), jnp.bfloat16),
         ],
@@ -361,9 +361,7 @@
             [(theirs_ref[0, p, i] + count) % (2 * count) for i in range(2)] for p in range(slots)
         ]
         inputs = refs[:distant]
-        share_ref, table_ref, own_ref, own_edge, near, every, edges, phases = refs[distant:]
-        every[:count] = own_ref[...]
-        edges[:count] = own_edge[...]
+        share_ref, table_ref, _, _, near, every, edges, phases = refs[distant:]
         total = gather_rows(inputs, table_ref, me, 2, share_ref[...])
         store_spectra(s_ref, total, every, edges, count)
         correlate(s_ref, picks, every, edges, phases)
@@ -380,6 +378,7 @@
             jax.ShapeDtypeStruct((2 * count, 2, 16, height), jnp.bfloat16),
             jax.ShapeDtypeStruct((2 * slots, block, height), jnp.bfloat16),
         ],
+        input_output_aliases={5 + distant: 1, 6 + distant: 2},
         compiler_params=params(),
         cost_estimate=cost(4 * (count + slots) * double * height * height, 8 * height * height),
         name="partner_slots",

time: 61.9 us -> 61.8 us (level)
  no operation moved by 1% of the time
where the time goes in v20:
time: 61.8 us; the launch traced here: 61.3 us
  starting transfers between devices  23.4 us (38%)
  waiting for transfers between devices  17.6 us (28%)
  Pallas kernels  16.9 us (27%)
  local copies, waits for them, and re-layouts  2.63 us (4%)
  between operations  0.77 us (1%)
    ppermute x8, starting transfers between devices, across(): return lax.ppermute(value, axes, moves)  16.4 us
    ppermute x8, waiting for transfers between devices, across(): return lax.ppermute(value, axes, moves)  13.7 us
    all_to_all x2, starting transfers between devices, along(): return lax.all_to_all(blocks, 'rows', split_axis=0, concat_axis=0)  6.94 us
    all_to_all x2, waiting for transfers between devices, along(): return lax.all_to_all(blocks, 'rows', split_axis=0, concat_axis=0)  3.86 us
    pallas_call x1, Pallas kernels, own_slots(): pl.pallas_call(body, in_specs=[pl.BlockSpec(memory_space=pltpu.SMEM)] * 3...  3.58 us
    pallas_call x1, Pallas kernels, near_columns(): pl.pallas_call(body, grid_spec=pltpu.PrefetchScalarGridSpec(num_scalar_pr...  3.44 us
    unnamed x18, local copies, waits for them, and re-layouts  2.62 us
    pallas_call x1, Pallas kernels, partner_slots(): pl.pallas_call(body, in_specs=[pl.BlockSpec(memory_space=pltpu.SMEM)] * 3...  2.48 us
  transfers between devices with their start and end apart: 11, of which 6 were waited for; matrix products, arithmetic and copies ran while one was open for 0% of the time, Pallas kernels for 15%

profile of v20, /device:TPU:0, one launch (start us, length us, event | category | flops | bytes accessed | tf_op | source)
XLA Modules:
  0.0 61.3 jit_solution(13730071496090850757)
XLA Ops:
  0.0 3.4 %near_columns.1 = (bf16[2,128,256]{2,1,0:T(8,128)(2,1)}, bf16[2,128,256]{2,1,0:T(8,128)(2,1)}) custom-call(s32[1]{0:T(128)} %bitcast.half_ref, s32[1]{0:T(128)} %bitcast.1.me_ref, f32[2,256,1024]{2,1,0:T(8,128)} %tile_ref.1, f32[8,1024]{1,0:T(8,128)} %constant.32.clone.down_hbm.down_ref, f32[1,1024]{1,0:T(1,128)} %constant.33.clone.across_hbm.across_ref, ...), custom_call_target="tpu_custom_call" | custom-call | flops 268435456 | bytes 2621440 | tf_op jit(solution)/shard_map/near_columns/pallas_call | solution.py:151
  3.5 4.1 %collective-permute-start = (bf16[2,128,256]{2,1,0:T(8,128)(2,1)}, bf16[2,128,256]{2,1,0:T(8,128)(2,1)S(1)}, u32[]{:S(2)}, u32[]{:S(2)}) collective-permute-start(bf16[2,128,256]{2,1,0:T(8,128)(2,1)} %get-tuple-element.31), channel_id=1, source_target_pairs={{0,8},{1,9},{2,10},{3,11},{4,12},{5,13},{6,14},{7,15},{8,0},{9,1},... | collective-permute-start | bytes 393224 | tf_op jit(solution)/shard_map/ppermute | solution.py:514
  7.6 2.4 %rest_columns.1 = (bf16[4,2,128,256]{3,2,1,0:T(8,128)(2,1)}, bf16[2,128,256]{2,1,0:T(8,128)(2,1)S(1)}, bf16[2,128,256]{2,1,0:T(8,128)(2,1)S(1)}) custom-call(s32[1]{0:T(128)} %bitcast.2.half_ref, s32[1]{0:T(128)} %bitcast.1.me_ref, f32[2,256,1024]{2,1,0:T(8,128)S(1)} %copy-done.1, f32[8,1024]{1,0:T(8,128)S(1)} %copy-done.2, f32[1,1024]{1,0:T(1,128)S(1)} %copy-done.3, ...), custom_call_target="tpu_custom_call" | custom-call | flops 805306368 | bytes 4194304 | tf_op jit(solution)/shard_map/rest_columns/pallas_call | solution.py:199
  10.1 3.5 %all-to-all-start = ((bf16[4,2,128,256]{3,2,1,0:T(8,128)(2,1)}), bf16[4,2,128,256]{3,2,1,0:T(8,128)(2,1)S(1)}, u32[]{:S(2)}, u32[]{:S(2)}) async-start(bf16[4,2,128,256]{3,2,1,0:T(8,128)(2,1)} %get-tuple-element.38), calls=%async_computation | async-start | bytes 1048576 | tf_op jit(solution)/shard_map/all_to_all | solution.py:517
  13.5 3.5 %collective-permute-start.3 = (bf16[2,128,256]{2,1,0:T(8,128)(2,1)S(1)}, bf16[2,128,256]{2,1,0:T(8,128)(2,1)S(1)}, u32[]{:S(2)}, u32[]{:S(2)}) collective-permute-start(bf16[2,128,256]{2,1,0:T(8,128)(2,1)S(1)} %get-tuple-element.42), channel_id=1, source_target_pairs={{0,10},{1,11},{2,8},{3,9},{4,14},{5,15},{6,12},{7,13},{8,2},{9,3},... | collective-permute-start | bytes 393224 | tf_op jit(solution)/shard_map/ppermute | solution.py:514
  17.3 2.5 %collective-permute-start.2 = (s32[1,2,2]{2,1,0:T(2,128)S(1)}, s32[1,2,2]{2,1,0:T(2,128)S(1)}, u32[]{:S(2)}, u32[]{:S(2)}) collective-permute-start(s32[1,2,2]{2,1,0:T(2,128)S(1)} %copy-done.4), channel_id=1, source_target_pairs={{0,8},{1,9},{2,10},{3,11},{4,12},{5,13},{6,14},{7,15},{8,0},{9,1},... | collective-permute-start | bytes 56 | tf_op jit(solution)/shard_map/ppermute | solution.py:514
  19.8 0.9 %copy-done.5 = f32[64,1024]{1,0:T(8,128)S(1)} copy-done((f32[64,1024]{1,0:T(8,128)S(1)}, f32[64,1024]{1,0:T(8,128)}, u32[]{:S(2)}) %copy-start.5) | copy-done | bytes 262168
  20.8 0.7 %copy-done.7 = f32[64,1024]{1,0:T(8,128)} copy-done((f32[64,1024]{1,0:T(8,128)}, f32[64,1024]{1,0:T(8,128)S(1)}, u32[]{:S(2)}) %copy-start.7) | copy-done | bytes 262168
  21.5 0.9 %all-to-all-done.pieces_ref = bf16[4,2,128,256]{3,2,1,0:T(8,128)(2,1)S(1)} async-done(((bf16[4,2,128,256]{3,2,1,0:T(8,128)(2,1)}), bf16[4,2,128,256]{3,2,1,0:T(8,128)(2,1)S(1)}, u32[]{:S(2)}, u32[]{:S(2)}) %all-to-all-start) | async-done | bytes 524320 | tf_op jit(solution)/shard_map/all_to_all | solution.py:517
  22.4 0.9 %copy-done.8 = f32[64,1024]{1,0:T(8,128)S(1)} copy-done((f32[64,1024]{1,0:T(8,128)S(1)}, f32[64,1024]{1,0:T(8,128)}, u32[]{:S(2)}) %copy-start.8) | copy-done | bytes 262168
  23.3 2.0 %own_spectra.1 = (bf16[4,2,64,1024]{3,2,1,0:T(8,128)(2,1)S(1)}, bf16[4,2,16,1024]{3,2,1,0:T(8,128)(2,1)S(1)}, f32[256,2048]{1,0:T(8,128)S(1)}, bf16[1024,2048]{1,0:T(8,128)(2,1)S(1)}) custom-call(s32[1]{0:T(128)} %bitcast.half_ref, s32[1]{0:T(128)} %bitcast.1.me_ref, bf16[4,2,128,256]{3,2,1,0:T(8,128)(2,1)S(1)} %all-to-all-done.pieces_ref, ...), custom_call_target="tpu_custom_call" | custom-call | flops 1610612736 | bytes 8388608 | tf_op jit(solution)/shard_map/own_spectra/pallas_call | solution.py:333
  25.3 5.6 %collective-permute-done.2.theirs_ref = s32[1,2,2]{2,1,0:T(2,128)S(1)} collective-permute-done((s32[1,2,2]{2,1,0:T(2,128)S(1)}, s32[1,2,2]{2,1,0:T(2,128)S(1)}, u32[]{:S(2)}, u32[]{:S(2)}) %collective-permute-start.2) | collective-permute-done | bytes 48 | tf_op jit(solution)/shard_map/ppermute | solution.py:514
  31.0 2.5 %partner_slots.1 = (bf16[2,2,128,256]{3,2,1,0:T(8,128)(2,1)S(1)}, bf16[4,2,64,1024]{3,2,1,0:T(8,128)(2,1)S(1)}, bf16[4,2,16,1024]{3,2,1,0:T(8,128)(2,1)S(1)}, bf16[4,64,1024]{2,1,0:T(8,128)(2,1)S(1)}) custom-call(s32[1]{0:T(128)} %bitcast.half_ref, s32[1]{0:T(128)} %bitcast.1.me_ref, ...), custom_call_target="tpu_custom_call", output_to_operand_aliasing={{1}: (7, {}), {2}: (8, {})} | custom-call | flops 2147483648 | bytes 8388608 | tf_op jit(solution)/shard_map/partner_slots/pallas_call | solution.py:370
  33.5 2.4 %collective-permute-start.7 = (bf16[2,2,128,256]{3,2,1,0:T(8,128)(2,1)S(1)}, bf16[2,2,128,256]{3,2,1,0:T(8,128)(2,1)S(1)}, u32[]{:S(2)}, u32[]{:S(2)}) collective-permute-start(bf16[2,2,128,256]{3,2,1,0:T(8,128)(2,1)S(1)} %get-tuple-element.54), channel_id=1, source_target_pairs={{0,8},{1,9},{2,10},{3,11},{4,12},{5,13},{6,14},{7,15},{8,0},{9,1},... | collective-permute-start | bytes 786440 | tf_op jit(solution)/shard_map/ppermute | solution.py:514
  35.9 3.6 %own_slots.1 = (bf16[4,2,128,256]{3,2,1,0:T(8,128)(2,1)}, bf16[2,128,256]{2,1,0:T(8,128)(2,1)}, bf16[2,128,256]{2,1,0:T(8,128)(2,1)S(1)}) custom-call(s32[1]{0:T(128)} %bitcast.half_ref, s32[1]{0:T(128)} %bitcast.1.me_ref, s32[1,2,2]{2,1,0:T(2,128)S(1)} %copy-done.4, bf16[1024,2048]{1,0:T(8,128)(2,1)S(1)} %get-tuple-element.41.refs_3_.table_ref, ...), custom_call_target="tpu_custom_call" | custom-call | flops 1073741824 | bytes 8388608 | tf_op jit(solution)/shard_map/own_slots/pallas_call | solution.py:403
  39.5 3.5 %all-to-all-start.1 = ((bf16[4,2,128,256]{3,2,1,0:T(8,128)(2,1)}), bf16[4,2,128,256]{3,2,1,0:T(8,128)(2,1)S(1)}, u32[]{:S(2)}, u32[]{:S(2)}) async-start(bf16[4,2,128,256]{3,2,1,0:T(8,128)(2,1)} %get-tuple-element.52), calls=%async_computation.1 | async-start | bytes 1048576 | tf_op jit(solution)/shard_map/all_to_all | solution.py:517
  43.0 2.0 %collective-permute-start.5 = (bf16[2,128,256]{2,1,0:T(8,128)(2,1)}, bf16[2,128,256]{2,1,0:T(8,128)(2,1)S(1)}, u32[]{:S(2)}, u32[]{:S(2)}) collective-permute-start(bf16[2,128,256]{2,1,0:T(8,128)(2,1)} %get-tuple-element.50), channel_id=1, source_target_pairs={{0,10},{1,11},{2,8},{3,9},{4,14},{5,15},{6,12},{7,13},{8,2},{9,3},... | collective-permute-start | bytes 393224 | tf_op jit(solution)/shard_map/ppermute | solution.py:514
  45.0 1.7 %collective-permute-start.6 = (bf16[2,128,256]{2,1,0:T(8,128)(2,1)S(1)}, bf16[2,128,256]{2,1,0:T(8,128)(2,1)S(1)}, u32[]{:S(2)}, u32[]{:S(2)}) collective-permute-start(bf16[2,128,256]{2,1,0:T(8,128)(2,1)S(1)} %get-tuple-element.51), channel_id=1, source_target_pairs={{0,11},{1,10},{2,9},{3,8},{4,15},{5,14},{6,13},{7,12},{8,3},{9,2},... | collective-permute-start | bytes 393224 | tf_op jit(solution)/shard_map/ppermute | solution.py:514
  46.6 2.6 %collective-permute-done.7.refs_0_ = bf16[2,2,128,256]{3,2,1,0:T(8,128)(2,1)S(1)} collective-permute-done((bf16[2,2,128,256]{3,2,1,0:T(8,128)(2,1)S(1)}, bf16[2,2,128,256]{3,2,1,0:T(8,128)(2,1)S(1)}, u32[]{:S(2)}, u32[]{:S(2)}) %collective-permute-start.7) | collective-permute-done | bytes 262176 | tf_op jit(solution)/shard_map/ppermute | solution.py:514
  50.0 3.0 %all-to-all-done.1.own_ref = bf16[4,2,128,256]{3,2,1,0:T(8,128)(2,1)S(1)} async-done(((bf16[4,2,128,256]{3,2,1,0:T(8,128)(2,1)}), bf16[4,2,128,256]{3,2,1,0:T(8,128)(2,1)S(1)}, u32[]{:S(2)}, u32[]{:S(2)}) %all-to-all-start.1) | async-done | bytes 524320 | tf_op jit(solution)/shard_map/all_to_all | solution.py:517
  52.9 1.0 %own_surfaces.1.part_ref = f32[2,256,1024]{2,1,0:T(8,128)S(1)} custom-call(s32[1]{0:T(128)} %bitcast.half_ref, bf16[4,2,128,256]{3,2,1,0:T(8,128)(2,1)S(1)} %all-to-all-done.1.own_ref, bf16[1024,1024]{1,0:T(8,128)(2,1)S(1)} %copy-done), custom_call_target="tpu_custom_call" | custom-call | flops 536870912 | bytes 2097152 | tf_op jit(solution)/shard_map/own_surfaces/pallas_call | solution.py:432
  53.9 4.3 %collective-permute-done.5.refs_2_ = bf16[2,128,256]{2,1,0:T(8,128)(2,1)S(1)} collective-permute-done((bf16[2,128,256]{2,1,0:T(8,128)(2,1)}, bf16[2,128,256]{2,1,0:T(8,128)(2,1)S(1)}, u32[]{:S(2)}, u32[]{:S(2)}) %collective-permute-start.5) | collective-permute-done | bytes 131104 | tf_op jit(solution)/shard_map/ppermute | solution.py:514
  58.3 1.1 %collective-permute-done.6.refs_3_ = bf16[2,128,256]{2,1,0:T(8,128)(2,1)S(1)} collective-permute-done((bf16[2,128,256]{2,1,0:T(8,128)(2,1)S(1)}, bf16[2,128,256]{2,1,0:T(8,128)(2,1)S(1)}, u32[]{:S(2)}, u32[]{:S(2)}) %collective-permute-start.6) | collective-permute-done | bytes 131104 | tf_op jit(solution)/shard_map/ppermute | solution.py:514
  59.4 2.0 %surfaces.1 = f32[2,256,1024]{2,1,0:T(8,128)} custom-call(s32[1]{0:T(128)} %bitcast.half_ref, s32[1]{0:T(128)} %bitcast.1.me_ref, s32[1]{0:T(128)S(6)} %copy.13.counts_ref, f32[2,256,1024]{2,1,0:T(8,128)S(1)} %own_surfaces.1.part_ref, bf16[2,2,128,256]{3,2,1,0:T(8,128)(2,1)S(1)} %collective-permute-done.7.refs_0_, ...), custom_call_target="tpu_custom_call" | custom-call | flops 536870912 | bytes 4194304 | tf_op jit(solution)/shard_map/surfaces/pallas_call | solution.py:476
  (25 shorter events, 0.4 us)
Async XLA Ops:
  0.0 7.6 %copy-start = (bf16[1024,1024]{1,0:T(8,128)(2,1)S(1)}, bf16[1024,1024]{1,0:T(8,128)(2,1)}, u32[]{:S(2)}) copy-start(bf16[1024,1024]{1,0:T(8,128)(2,1)} %constant.31.clone.table_hbm.table_ref.refs_4_) | copy-start | bytes 6291460
  0.0 7.6 %copy-start.1 = (f32[2,256,1024]{2,1,0:T(8,128)S(1)}, f32[2,256,1024]{2,1,0:T(8,128)}, u32[]{:S(2)}) copy-start(f32[2,256,1024]{2,1,0:T(8,128)} %tile_ref.1) | copy-start | bytes 6291460
  0.0 7.6 %copy-start.2 = (f32[8,1024]{1,0:T(8,128)S(1)}, f32[8,1024]{1,0:T(8,128)}, u32[]{:S(2)}) copy-start(f32[8,1024]{1,0:T(8,128)} %constant.32.clone.down_hbm.down_ref) | copy-start | bytes 98308
  0.0 7.6 %copy-start.3 = (f32[1,1024]{1,0:T(1,128)S(1)}, f32[1,1024]{1,0:T(1,128)}, u32[]{:S(2)}) copy-start(f32[1,1024]{1,0:T(1,128)} %constant.33.clone.across_hbm.across_ref) | copy-start | bytes 12292
  3.5 18.0 %collective-permute-start = (bf16[2,128,256]{2,1,0:T(8,128)(2,1)}, bf16[2,128,256]{2,1,0:T(8,128)(2,1)S(1)}, u32[]{:S(2)}, u32[]{:S(2)}) collective-permute-start(bf16[2,128,256]{2,1,0:T(8,128)(2,1)} %get-tuple-element.31), channel_id=1, source_target_pairs={{0,8},{1,9},{2,10},{3,11},{4,12},{5,13},{6,14},{7,15},{8,0},{9,1},... | collective-permute-start | bytes 393224 | tf_op jit(solution)/shard_map/ppermute | solution.py:514
  7.6 13.9 %collective-permute-start.1 = (bf16[2,128,256]{2,1,0:T(8,128)(2,1)}, bf16[2,128,256]{2,1,0:T(8,128)(2,1)S(1)}, u32[]{:S(2)}, u32[]{:S(2)}) collective-permute-start(bf16[2,128,256]{2,1,0:T(8,128)(2,1)} %get-tuple-element.32), channel_id=1, source_target_pairs={{0,9},{1,8},{2,11},{3,10},{4,13},{5,12},{6,15},{7,14},{8,1},{9,0},... | collective-permute-start | bytes 393224 | tf_op jit(solution)/shard_map/ppermute | solution.py:514
  7.6 9.6 %copy-start.4 = (s32[1,2,2]{2,1,0:T(2,128)S(1)}, s32[1,2,2]{2,1,0:T(2,128)}, u32[]{:S(2)}) copy-start(s32[1,2,2]{2,1,0:T(2,128)} %pairs_ref) | copy-start | bytes 52
  7.6 12.2 %copy-start.6 = (f32[64,128]{1,0:T(8,128)S(1)}, f32[64,128]{1,0:T(8,128)}, u32[]{:S(2)}) copy-start(f32[64,128]{1,0:T(8,128)} %constant.35.clone.rough_ref) | copy-start | bytes 98308
  10.1 12.3 %all-to-all-start = ((bf16[4,2,128,256]{3,2,1,0:T(8,128)(2,1)}), bf16[4,2,128,256]{3,2,1,0:T(8,128)(2,1)S(1)}, u32[]{:S(2)}, u32[]{:S(2)}) async-start(bf16[4,2,128,256]{3,2,1,0:T(8,128)(2,1)} %get-tuple-element.38), calls=%async_computation | async-start | bytes 1048576 | tf_op jit(solution)/shard_map/all_to_all | solution.py:517
  13.5 17.4 %collective-permute-start.3 = (bf16[2,128,256]{2,1,0:T(8,128)(2,1)S(1)}, bf16[2,128,256]{2,1,0:T(8,128)(2,1)S(1)}, u32[]{:S(2)}, u32[]{:S(2)}) collective-permute-start(bf16[2,128,256]{2,1,0:T(8,128)(2,1)S(1)} %get-tuple-element.42), channel_id=1, source_target_pairs={{0,10},{1,11},{2,8},{3,9},{4,14},{5,15},{6,12},{7,13},{8,2},{9,3},... | collective-permute-start | bytes 393224 | tf_op jit(solution)/shard_map/ppermute | solution.py:514
  17.0 14.0 %collective-permute-start.4 = (bf16[2,128,256]{2,1,0:T(8,128)(2,1)S(1)}, bf16[2,128,256]{2,1,0:T(8,128)(2,1)S(1)}, u32[]{:S(2)}, u32[]{:S(2)}) collective-permute-start(bf16[2,128,256]{2,1,0:T(8,128)(2,1)S(1)} %get-tuple-element.43), channel_id=1, source_target_pairs={{0,11},{1,10},{2,9},{3,8},{4,15},{5,14},{6,13},{7,12},{8,3},{9,2},... | collective-permute-start | bytes 393224 | tf_op jit(solution)/shard_map/ppermute | solution.py:514
  17.3 13.7 %collective-permute-start.2 = (s32[1,2,2]{2,1,0:T(2,128)S(1)}, s32[1,2,2]{2,1,0:T(2,128)S(1)}, u32[]{:S(2)}, u32[]{:S(2)}) collective-permute-start(s32[1,2,2]{2,1,0:T(2,128)S(1)} %copy-done.4), channel_id=1, source_target_pairs={{0,8},{1,9},{2,10},{3,11},{4,12},{5,13},{6,14},{7,15},{8,0},{9,1},... | collective-permute-start | bytes 56 | tf_op jit(solution)/shard_map/ppermute | solution.py:514
  19.8 1.0 %copy-start.5 = (f32[64,1024]{1,0:T(8,128)S(1)}, f32[64,1024]{1,0:T(8,128)}, u32[]{:S(2)}) copy-start(f32[64,1024]{1,0:T(8,128)} %constant.34.clone.fine_ref) | copy-start | bytes 786436
  20.8 0.7 %copy-start.7 = (f32[64,1024]{1,0:T(8,128)}, f32[64,1024]{1,0:T(8,128)S(1)}, u32[]{:S(2)}) copy-start(f32[64,1024]{1,0:T(8,128)S(1)} %get-tuple-element.39.refs_0_) | copy-start | bytes 786436
  22.4 1.0 %copy-start.8 = (f32[64,1024]{1,0:T(8,128)S(1)}, f32[64,1024]{1,0:T(8,128)}, u32[]{:S(2)}) copy-start(f32[64,1024]{1,0:T(8,128)} %copy-done.7) | copy-start | bytes 786436
  33.5 15.8 %collective-permute-start.7 = (bf16[2,2,128,256]{3,2,1,0:T(8,128)(2,1)S(1)}, bf16[2,2,128,256]{3,2,1,0:T(8,128)(2,1)S(1)}, u32[]{:S(2)}, u32[]{:S(2)}) collective-permute-start(bf16[2,2,128,256]{3,2,1,0:T(8,128)(2,1)S(1)} %get-tuple-element.54), channel_id=1, source_target_pairs={{0,8},{1,9},{2,10},{3,11},{4,12},{5,13},{6,14},{7,15},{8,0},{9,1},... | collective-permute-start | bytes 786440 | tf_op jit(solution)/shard_map/ppermute | solution.py:514
  39.5 13.5 %all-to-all-start.1 = ((bf16[4,2,128,256]{3,2,1,0:T(8,128)(2,1)}), bf16[4,2,128,256]{3,2,1,0:T(8,128)(2,1)S(1)}, u32[]{:S(2)}, u32[]{:S(2)}) async-start(bf16[4,2,128,256]{3,2,1,0:T(8,128)(2,1)} %get-tuple-element.52), calls=%async_computation.1 | async-start | bytes 1048576 | tf_op jit(solution)/shard_map/all_to_all | solution.py:517
  43.0 15.3 %collective-permute-start.5 = (bf16[2,128,256]{2,1,0:T(8,128)(2,1)}, bf16[2,128,256]{2,1,0:T(8,128)(2,1)S(1)}, u32[]{:S(2)}, u32[]{:S(2)}) collective-permute-start(bf16[2,128,256]{2,1,0:T(8,128)(2,1)} %get-tuple-element.50), channel_id=1, source_target_pairs={{0,10},{1,11},{2,8},{3,9},{4,14},{5,15},{6,12},{7,13},{8,2},{9,3},... | collective-permute-start | bytes 393224 | tf_op jit(solution)/shard_map/ppermute | solution.py:514
  45.0 14.4 %collective-permute-start.6 = (bf16[2,128,256]{2,1,0:T(8,128)(2,1)S(1)}, bf16[2,128,256]{2,1,0:T(8,128)(2,1)S(1)}, u32[]{:S(2)}, u32[]{:S(2)}) collective-permute-start(bf16[2,128,256]{2,1,0:T(8,128)(2,1)S(1)} %get-tuple-element.51), channel_id=1, source_target_pairs={{0,11},{1,10},{2,9},{3,8},{4,15},{5,14},{6,13},{7,12},{8,3},{9,2},... | collective-permute-start | bytes 393224 | tf_op jit(solution)/shard_map/ppermute | solution.py:514
  49.3 10.1 %collective-permute-start.8 = (bf16[2,128,256]{2,1,0:T(8,128)(2,1)S(1)}, bf16[2,128,256]{2,1,0:T(8,128)(2,1)S(1)}, u32[]{:S(2)}, u32[]{:S(2)}) collective-permute-start(bf16[2,128,256]{2,1,0:T(8,128)(2,1)S(1)} %slice_bitcast_fusion), channel_id=1, source_target_pairs={{0,1},{1,0},{2,3},{3,2},{4,5},{5,4},{6,7},{7,6},{8,9},{9,8},{10,11... | collective-permute-start | bytes 393224 | tf_op jit(solution)/shard_map/ppermute | solution.py:520
